TPU v7x, 256 devices: a 8x8x2 block of a 8x8x16 slice. The times are simulated.
256 devices in a mesh: groups: 2 (over z), dev: 128 (over x, y, core).
Axes of the slice: x: 8, y: 8, z: 2, core: 2. Of those that a mesh axis runs over, the one named last changes fastest.
The devices are a block of a 8x8x16 slice.
Arguments:
- tokens: bfloat16 [1024, 6144], P(('groups', 'dev')), parts along dimension 0, may hold values from -6 to 6
- queries: bfloat16 [1024, 6144], P(('groups', 'dev')), parts along dimension 0, may hold values from -250 to 250
- token_kv: bfloat16 [1024, 2048], P(('groups', 'dev')), parts along dimension 0, may hold values from -6 to 6
- kv_cache: bfloat16 [1024, 64, 2048], P(('groups', 'dev')), parts along dimension 0, may hold values from -6.5 to 6.5, as said below
- context_lengths: int32 [1024], P(('groups', 'dev')), parts along dimension 0, may hold values from 2 to 64
- fresh_kv: bfloat16 [16384, 2048], P(('groups', 'dev')), parts along dimension 0, may hold values from -6 to 6
- block_counts: int32 [256], P('groups'), parts along dimension 0, may hold values from 0 to 8, as said below
- expert_ids: int32 [1024, 2], P(('groups', 'dev')), parts along dimension 0, may hold values from 0 to 3, all different within a row; in each aligned block of 4 rows (0 to 3, 4 to 7, ...) at most 3 rows name the same one
- route_weights: float32 [1024, 2], P(('groups', 'dev')), parts along dimension 0, may hold values from 0.25 to 1
- norm_gain: float32 [6144], replicated, may hold values from 0.1 to 1.9
- w_gate: bfloat16 [6144, 32768], P(None, 'dev'), may hold values from -0.078125 to 0.078125
- w_up: bfloat16 [6144, 32768], P(None, 'dev'), may hold values from -0.078125 to 0.078125
- w_down: bfloat16 [32768, 6144], P('dev'), may hold values from -0.0625 to 0.0625
Outputs:
- layer_out: bfloat16 [1024, 6144], P(('groups', 'dev')), parts along dimension 0
There are 2 independent parts, one for each index of `groups`. A program takes and returns all parts, laid end to end along the dimension named above; an argument that names none is the same for every part. Nothing has to cross between parts.
Inputs may be any that keep to these rules, and one draw needn't show every extreme that they name: `kv_cache`: each request's cached keys and values; the table of arrays gives their range. `block_counts`: the counts sum to 512; for every device d > 0 the exclusive prefix sum before it lies between d * 4 + 1 and (d + 1) * 4; the first device takes 2 * 4 blocks. `expert_ids`: among the rows of one device no expert is named more than 3 times, and in some devices one expert is named exactly 3 times.
All inputs are finite; a program needn't handle non-finite values.
Results may differ from a plain program's by a relative error of at most 0.008.
Values may be sent and summed in bfloat16 or wider, within the bound.
No kernel may reach another device: no remote copies, remote signals or barrier semaphores. Data moves between devices by JAX's collectives and lax.ppermute only.
A program may use at most 128 MiB of HBM per device.

v0:
```python
import math

import jax
import jax.numpy as jnp
from jax import lax
from jax.experimental import pallas as pl
from jax.experimental.pallas import tpu as pltpu
from jax.sharding import Mesh
from jax.sharding import PartitionSpec as P


QH = 48
KVH = 8
HD = 128
EXPERTS = 4
BLOCK = 16
MOST = 3
DEV = ("dev_0", "dev_1", "dev_2")
GROUPS_DEV = ("groups", "dev_0", "dev_1", "dev_2")


EPS = 1e-05
NEG = -1e30

PIECES = 16
CUT_K = 8
CUT_N = 4


def passed_along(value, axis, steps):
    count = lax.axis_size(axis)
    leading, last = (max(0, -steps), min(count, count - steps))
    return lax.ppermute(value, axis, [(source, source + steps) for source in range(leading, last)])


def shifted(value, axis, steps):
    count = lax.axis_size(axis)
    return lax.ppermute(value, axis, [(place, (place + steps) % count) for place in range(count)])


def swapped(value):
    return shifted(value, "dev_2", 1)


def passed_on(value):
    chips, cores = lax.axis_size("dev_1"), lax.axis_size("dev_2")
    pairs = []
    for chip in range(chips):
        for core in range(cores):
            pairs.append((chip * cores + core, (chip + 1 - 2 * core) % chips * cores + core))
    return lax.ppermute(value, ("dev_1", "dev_2"), pairs)


def added(*terms):
    total = terms[0].astype(jnp.float32)
    for term in terms[1:]:
        total = total + term.astype(jnp.float32)
    return total


def gathered(own):
    other = swapped(own)
    far = lax.axis_size("dev_1") // 2
    came, theirs = {}, {}
    block = {0: own, 1: other}
    for step in range(1, far + 1):
        for part in (0, 1) if step < far else (0,):
            block[part] = passed_on(block[part])
            came[step, part] = block[part]
        for part in (0, 1) if step < far else (0,):
            theirs[step, part] = swapped(came[step, part])
    return own, other, came, theirs


def chain_order(far):
    return [(far - i, 0) for i in range(far)], [(far - i, 1) for i in range(1, far)]


def scattered(far, each, own, other, kept, sent):
    got = [swapped(sent[part]) for part in (0, 1)]
    moving = {}
    for step in range(far, 0, -1):
        for part in (0, 1) if step < far else (0,):
            at = (far - part - step) * each
            terms = [x[at : at + each] for x in (kept[part], got[part])]
            parcel = added(*terms, *moving.get(part, ())).astype(jnp.bfloat16)
            moving[part] = (passed_on(parcel),)
    leaving = added(other, *moving[0]).astype(jnp.bfloat16)
    return added(own, *moving[1], swapped(leaving)).astype(jnp.bfloat16)


def experts_kernel(*refs):
    pieces = refs[:PIECES]
    gate_hbm, up_hbm, down_hbm = refs[PIECES : PIECES + 3]
    outs = refs[PIECES + 3 : PIECES + 9]
    gate, up, down, sems = refs[PIECES + 9 :]
    depth = gate.shape[0] // CUT_K
    span = down.shape[1] // CUT_N
    copies = []
    for k in range(CUT_K):
        rows = pl.ds(k * depth, depth)
        copies.append(
            (
                pltpu.make_async_copy(gate_hbm.at[rows], gate.at[rows], sems.at[2 * k]),
                pltpu.make_async_copy(up_hbm.at[rows], up.at[rows], sems.at[2 * k + 1]),
            )
        )
    last = pltpu.make_async_copy(down_hbm, down, sems.at[2 * CUT_K])
    for pair in copies:
        pair[0].start()
        pair[1].start()
    last.start()
    gate_v = up_v = None
    for k in range(CUT_K):
        cols = pl.ds(k * depth, depth)
        x = jnp.concatenate([p[:, cols] for p in pieces], 0)
        copies[k][0].wait()
        copies[k][1].wait()
        g = jnp.dot(x, gate[cols, :], preferred_element_type=jnp.float32)
        u = jnp.dot(x, up[cols, :], preferred_element_type=jnp.float32)
        gate_v = g if gate_v is None else gate_v + g
        up_v = u if up_v is None else up_v + u
    act = (gate_v / (1.0 + jnp.exp(-gate_v)) * up_v).astype(jnp.bfloat16)
    last.wait()
    for n in range(CUT_N):
        cols = pl.ds(n * span, span)
        part = jnp.dot(act, down[:, cols], preferred_element_type=jnp.float32).astype(jnp.bfloat16)
        at = 0
        for out in outs:
            rows = out.shape[0]
            out[:, cols] = part[at : at + rows]
            at += rows


def experts(pieces, w_gate, w_up, w_down, sizes):
    width = w_gate.shape[0]
    hidden = w_gate.shape[1]
    vm = pl.BlockSpec(memory_space=pltpu.VMEM)
    anyspec = pl.BlockSpec(memory_space=pl.ANY)
    total = sum(sizes)
    return pl.pallas_call(
        experts_kernel,
        out_shape=[jax.ShapeDtypeStruct((s, width), jnp.bfloat16) for s in sizes],
        in_specs=[vm] * PIECES + [anyspec] * 3,
        out_specs=[vm] * len(sizes),
        scratch_shapes=[
            pltpu.VMEM((width, hidden), jnp.bfloat16),
            pltpu.VMEM((width, hidden), jnp.bfloat16),
            pltpu.VMEM((hidden, width), jnp.bfloat16),
            pltpu.SemaphoreType.DMA((2 * CUT_K + 1,)),
        ],
        compiler_params=pltpu.CompilerParams(vmem_limit_bytes=40 * 1024 * 1024),
        cost_estimate=pl.CostEstimate(flops=6 * total * width * hidden, bytes_accessed=6 * width * hidden, transcendentals=total * hidden),
        name="experts",
    )(*pieces, w_gate, w_up, w_down)


def attend(query, cache, lens, own, window, first, last):
    reqs = query.shape[0]
    length = cache.shape[1]
    group = QH // KVH
    half = KVH * HD
    scale = 1.0 / math.sqrt(HD)
    q_all = query.reshape(reqs, KVH, group, HD)
    keys_c = cache[:, :, :half].reshape(reqs, length, KVH, HD)
    vals_c = cache[:, :, half:].reshape(reqs, length, KVH, HD)
    keys_w = window[:, :half].reshape(-1, KVH, HD)
    vals_w = window[:, half:].reshape(-1, KVH, HD)
    keys_o = own[:, :half].reshape(reqs, KVH, HD)
    vals_o = own[:, half:].astype(jnp.float32).reshape(reqs, KVH, HD)
    s_cache = (
        jnp.einsum("rkgh,rpkh->rkgp", q_all, keys_c, preferred_element_type=jnp.float32) * scale
    )
    places = jnp.arange(length, dtype=jnp.int32)
    s_cache = jnp.where(places[None, None, None, :] < lens[:, None, None, None], s_cache, NEG)
    s_win = jnp.einsum("rkgh,pkh->rkgp", q_all, keys_w, preferred_element_type=jnp.float32) * scale
    rows = jnp.arange(window.shape[0], dtype=jnp.int32)
    live = (rows >= first) & (rows < last)
    leader = jnp.arange(reqs, dtype=jnp.int32) == 0
    usable = leader[:, None] & live[None, :]
    s_win = jnp.where(usable[:, None, None, :], s_win, NEG)
    s_own = jnp.einsum("rkgh,rkh->rkg", q_all, keys_o, preferred_element_type=jnp.float32) * scale
    top = jnp.maximum(jnp.maximum(jnp.max(s_cache, -1), jnp.max(s_win, -1)), s_own)
    e_cache = jnp.exp(s_cache - top[..., None])
    e_win = jnp.exp(s_win - top[..., None])
    e_own = jnp.exp(s_own - top)
    total = jnp.sum(e_cache, -1) + jnp.sum(e_win, -1) + e_own
    p_cache = (e_cache / total[..., None]).astype(jnp.bfloat16)
    p_win = (e_win / total[..., None]).astype(jnp.bfloat16)
    p_own = (e_own / total).astype(jnp.bfloat16).astype(jnp.float32)
    mixed = jnp.einsum("rkgp,rpkh->rkgh", p_cache, vals_c, preferred_element_type=jnp.float32)
    mixed = mixed + jnp.einsum("rkgp,pkh->rkgh", p_win, vals_w, preferred_element_type=jnp.float32)
    mixed = mixed + p_own[..., None] * vals_o[:, :, None, :]
    return mixed.reshape(reqs, QH * HD)


def layer(
    tokens,
    queries,
    token_kv,
    kv_cache,
    context_lengths,
    fresh_kv,
    block_counts,
    expert_ids,
    route_weights,
    norm_gain,
    w_gate,
    w_up,
    w_down,
):
    me = lax.axis_index(DEV)
    reqs = tokens.shape[0]
    width = tokens.shape[1]
    span = fresh_kv.shape[0]
    following = passed_along(fresh_kv, DEV, -1)
    window = jnp.concatenate([fresh_kv, following], 0)
    offsets = jnp.cumsum(block_counts) - block_counts
    mine = lax.dynamic_index_in_dim(offsets, me, 0, keepdims=False)
    taken = lax.dynamic_index_in_dim(block_counts, me, 0, keepdims=False)
    first = (mine - me * (span // BLOCK)) * BLOCK
    last = first + taken * BLOCK
    attn = attend(queries, kv_cache, context_lengths, token_kv, window, first, last)
    hidden_state = tokens.astype(jnp.float32) + attn
    spread = jnp.mean(hidden_state * hidden_state, -1, keepdims=True)
    normed = (hidden_state * lax.rsqrt(spread + EPS) * norm_gain).astype(jnp.bfloat16)
    labels = jnp.arange(EXPERTS, dtype=jnp.int32)
    flat_ids = expert_ids.reshape(-1)
    picks = (flat_ids[:, None] == labels[None, :]).astype(jnp.int32)
    slots = jnp.sum((jnp.cumsum(picks, 0) - picks) * picks, 1).reshape(reqs, 2)
    rows_x = lax.axis_size("dev_0")
    per_expert = rows_x // EXPERTS
    expert_of = jnp.arange(rows_x, dtype=jnp.int32) // per_expert
    slot_ids = jnp.arange(MOST, dtype=jnp.int32)
    named = (expert_ids[None, None, :, :] == expert_of[:, None, None, None]) & (
        slots[None, None, :, :] == slot_ids[None, :, None, None]
    )
    taking = jnp.sum(named.astype(jnp.float32), 3)
    weights = jnp.sum(named.astype(jnp.float32) * route_weights[None, None, :, :], 3)
    leaving = jnp.einsum(
        "xmt,td->xmd", taking.astype(jnp.bfloat16), normed, preferred_element_type=jnp.float32
    ).astype(jnp.bfloat16)
    came = lax.all_to_all(leaving, "dev_0", 0, 0, tiled=True)
    own_block = came.reshape(rows_x * MOST, width)
    own, other, came, theirs = gathered(own_block)
    far = lax.axis_size("dev_1") // 2
    chains = chain_order(far)
    each = rows_x * MOST
    pieces = [own, other]
    for group in (theirs, came):
        for chain in chains:
            pieces += [group[key] for key in chain]
    sizes = [each, each] + 2 * [len(chain) * each for chain in chains]
    home_own, home_other, kept_0, kept_1, sent_0, sent_1 = experts(pieces, w_gate, w_up, w_down, sizes)
    summed = scattered(far, each, home_own, home_other, (kept_0, kept_1), (sent_0, sent_1))
    home = lax.all_to_all(summed.reshape(rows_x, MOST, width), "dev_0", 0, 0, tiled=True)
    moe = jnp.einsum(
        "xmt,xmd->td", weights, home.astype(jnp.float32), precision=lax.Precision.HIGHEST
    )
    return (hidden_state + moe).astype(jnp.bfloat16)


def solution(mesh):
    split = Mesh(
        mesh.devices.reshape(mesh.shape["groups"], 8, 8, 2), ("groups", "dev_0", "dev_1", "dev_2")
    )
    return jax.shard_map(
        layer,
        mesh=split,
        in_specs=(
            P(GROUPS_DEV, None),
            P(GROUPS_DEV, None),
            P(GROUPS_DEV, None),
            P(GROUPS_DEV, None, None),
            P(GROUPS_DEV),
            P(GROUPS_DEV, None),
            P("groups"),
            P(GROUPS_DEV, None),
            P(GROUPS_DEV, None),
            P(),
            P(None, DEV),
            P(None, DEV),
            P(DEV, None),
        ),
        out_specs=P(GROUPS_DEV, None),
        check_vma=False,
    )
```

profile of v0, /device:TPU:514, one launch (start us, length us, event | category | flops | bytes accessed | tf_op | source)
XLA Modules:
  0.0 152.6 jit_solution(9541935425904700170)
XLA Ops:
  0.0 1.3 copy.78
  1.3 13.2 %collective-permute-start = (bf16[64,2048]{0,1:T(8,128)(2,1)S(1)}, bf16[64,2048]{0,1:T(8,128)(2,1)S(1)}, u32[]{:S(2)}, u32[]{:S(2)}) collective-permute-start(bf16[64,2048]{0,1:T(8,128)(2,1)S(1)} %copy.78), channel_id=1, source_target_pairs={{1,0},{2,1},{3,2},{4,3},{5,4},{6,5},{7,6},{8,7},{9,8},{10,9},{11,1... | collective-permute-start | bytes 786440 | tf_op jit(solution)/shard_map/ppermute | solution.py:33
  14.5 0.7 iota_compare_fusion.2
  15.2 0.8 copy.88
  16.0 0.8 broadcast_compare_fusion
  16.9 0.2 reduce_window_sum.18
  17.2 0.7 convert_bitcast_fusion
  18.0 0.9 reshape.153
  18.9 1.3 dynamic_slice.8
  20.2 0.8 copy.76
  20.9 0.2 reduce-window.9
  21.2 0.6 dynamic_slice.7
  23.3 0.1 fusion.34
  23.6 0.5 fusion.32
  24.1 0.3 pad_maximum_fusion
  24.4 0.3 fusion.33
  24.7 0.2 fusion.14
  24.9 0.2 fusion.15
  25.2 0.3 fusion.7
  25.5 0.3 fusion.4
  26.0 0.2 multiply_reduce_fusion
  26.1 0.3 convolution_convert_fusion
  26.4 0.3 copy.90
  26.7 25.2 %all_to_all.10 = bf16[8,3,6144]{2,1,0:T(4,128)(2,1)} all-to-all(bf16[8,3,6144]{2,1,0:T(4,128)(2,1)S(1)} %copy.90), channel_id=1, replica_groups=mesh['groups'=2,'dev_0'=8,'dev_1'=8,'dev_2'=2] {'dev_0'}, dimensions={0} | all-to-all | bytes 589824 | tf_op jit(solution)/shard_map/all_to_all | solution.py:243
  51.9 1.2 reshape.162.refs_0_
  53.1 0.1 collective-permute-start.2
  53.2 0.2 collective-permute-start.1
  53.5 7.7 %collective-permute-done.2.refs_12_ = bf16[24,6144]{1,0:T(8,128)(2,1)S(1)} collective-permute-done((bf16[24,6144]{1,0:T(8,128)(2,1)S(1)}, bf16[24,6144]{1,0:T(8,128)(2,1)S(1)}, u32[]{:S(2)}, u32[]{:S(2)}) %collective-permute-start.2) | collective-permute-done | bytes 294944 | tf_op jit(solution)/shard_map/ppermute | solution.py:51
  61.2 7.9 %collective-permute-done.3.refs_11_ = bf16[24,6144]{1,0:T(8,128)(2,1)S(1)} collective-permute-done((bf16[24,6144]{1,0:T(8,128)(2,1)S(1)}, bf16[24,6144]{1,0:T(8,128)(2,1)S(1)}, u32[]{:S(2)}, u32[]{:S(2)}) %collective-permute-start.3) | collective-permute-done | bytes 294944 | tf_op jit(solution)/shard_map/ppermute | solution.py:51
  69.1 3.2 %collective-permute-done.10.refs_15_ = bf16[24,6144]{1,0:T(8,128)(2,1)S(1)} collective-permute-done((bf16[24,6144]{1,0:T(8,128)(2,1)S(1)}, bf16[24,6144]{1,0:T(8,128)(2,1)S(1)}, u32[]{:S(2)}, u32[]{:S(2)}) %collective-permute-start.10) | collective-permute-done | bytes 294944 | tf_op jit(solution)/shard_map/ppermute | solution.py:51
  72.3 0.5 collective-permute-start.8
  72.8 4.3 %collective-permute-done.4.refs_10_ = bf16[24,6144]{1,0:T(8,128)(2,1)S(1)} collective-permute-done((bf16[24,6144]{1,0:T(8,128)(2,1)S(1)}, bf16[24,6144]{1,0:T(8,128)(2,1)S(1)}, u32[]{:S(2)}, u32[]{:S(2)}) %collective-permute-start.4) | collective-permute-done | bytes 294944 | tf_op jit(solution)/shard_map/ppermute | solution.py:51
  77.0 3.2 %collective-permute-done.11.refs_14_ = bf16[24,6144]{1,0:T(8,128)(2,1)S(1)} collective-permute-done((bf16[24,6144]{1,0:T(8,128)(2,1)S(1)}, bf16[24,6144]{1,0:T(8,128)(2,1)S(1)}, u32[]{:S(2)}, u32[]{:S(2)}) %collective-permute-start.11) | collective-permute-done | bytes 294944 | tf_op jit(solution)/shard_map/ppermute | solution.py:51
  80.2 0.5 collective-permute-start.7
  80.7 0.3 collective-permute-start.14
  81.0 3.9 %collective-permute-done.5.refs_9_ = bf16[24,6144]{1,0:T(8,128)(2,1)S(1)} collective-permute-done((bf16[24,6144]{1,0:T(8,128)(2,1)S(1)}, bf16[24,6144]{1,0:T(8,128)(2,1)S(1)}, u32[]{:S(2)}, u32[]{:S(2)}) %collective-permute-start.5) | collective-permute-done | bytes 294944 | tf_op jit(solution)/shard_map/ppermute | solution.py:51
  85.0 3.2 %collective-permute-done.12.refs_13_ = bf16[24,6144]{1,0:T(8,128)(2,1)S(1)} collective-permute-done((bf16[24,6144]{1,0:T(8,128)(2,1)S(1)}, bf16[24,6144]{1,0:T(8,128)(2,1)S(1)}, u32[]{:S(2)}, u32[]{:S(2)}) %collective-permute-start.12) | collective-permute-done | bytes 294944 | tf_op jit(solution)/shard_map/ppermute | solution.py:51
  88.1 1.5 %collective-permute-done.13.refs_6_ = bf16[24,6144]{1,0:T(8,128)(2,1)S(1)} collective-permute-done((bf16[24,6144]{1,0:T(8,128)(2,1)S(1)}, bf16[24,6144]{1,0:T(8,128)(2,1)S(1)}, u32[]{:S(2)}, u32[]{:S(2)}) %collective-permute-start.13) | collective-permute-done | bytes 294944 | tf_op jit(solution)/shard_map/ppermute | solution.py:38
  89.7 6.4 %experts.1 = (bf16[24,6144]{1,0:T(8,128)(2,1)S(1)}, bf16[24,6144]{1,0:T(8,128)(2,1)S(1)}, bf16[96,6144]{1,0:T(8,128)(2,1)S(1)}, bf16[72,6144]{1,0:T(8,128)(2,1)S...) custom-call(bf16[24,6144]{1,0:T(8,128)(2,1)S(1)} %reshape.162.refs_0_, ...), custom_call_target="tpu_custom_call" | custom-call | flops 3623878656 | bytes 9437184 | tf_op jit(solution)/shard_map/experts/pallas_call | solution.py:141
  96.1 0.3 collective-permute-start.20
  96.4 2.7 %collective-permute-done.20 = bf16[96,6144]{1,0:T(8,128)(2,1)S(1)} collective-permute-done((bf16[96,6144]{1,0:T(8,128)(2,1)S(1)}, bf16[96,6144]{1,0:T(8,128)(2,1)S(1)}, u32[]{:S(2)}, u32[]{:S(2)}) %collective-permute-start.20) | collective-permute-done | bytes 1179680 | tf_op jit(solution)/shard_map/ppermute | solution.py:38
  99.2 0.1 collective-permute-start.21
  99.3 0.3 collective-permute-start.16
  99.6 7.6 %collective-permute-done.21 = bf16[24,6144]{1,0:T(8,128)(2,1)S(1)} collective-permute-done((bf16[24,6144]{1,0:T(8,128)(2,1)S(1)}, bf16[24,6144]{1,0:T(8,128)(2,1)S(1)}, u32[]{:S(2)}, u32[]{:S(2)}) %collective-permute-start.21) | collective-permute-done | bytes 294944 | tf_op jit(solution)/shard_map/ppermute | solution.py:51
  107.2 0.1 add_convert_fusion.4
  107.3 0.1 collective-permute-start.22
  107.6 0.1 collective-permute-start.17
  107.7 7.7 %collective-permute-done.22 = bf16[24,6144]{1,0:T(8,128)(2,1)S(1)} collective-permute-done((bf16[24,6144]{1,0:T(8,128)(2,1)S(1)}, bf16[24,6144]{1,0:T(8,128)(2,1)S(1)}, u32[]{:S(2)}, u32[]{:S(2)}) %collective-permute-start.22) | collective-permute-done | bytes 294944 | tf_op jit(solution)/shard_map/ppermute | solution.py:51
  115.4 0.1 add_convert_fusion.3
  115.5 0.1 collective-permute-start.23
  115.6 2.9 %collective-permute-done.17 = bf16[24,6144]{1,0:T(8,128)(2,1)S(1)} collective-permute-done((bf16[24,6144]{1,0:T(8,128)(2,1)S(1)}, bf16[24,6144]{1,0:T(8,128)(2,1)S(1)}, u32[]{:S(2)}, u32[]{:S(2)}) %collective-permute-start.17) | collective-permute-done | bytes 294944 | tf_op jit(solution)/shard_map/ppermute | solution.py:51
  118.6 0.1 add_convert_fusion.7
  118.7 0.1 collective-permute-start.18
  118.8 4.7 %collective-permute-done.23 = bf16[24,6144]{1,0:T(8,128)(2,1)S(1)} collective-permute-done((bf16[24,6144]{1,0:T(8,128)(2,1)S(1)}, bf16[24,6144]{1,0:T(8,128)(2,1)S(1)}, u32[]{:S(2)}, u32[]{:S(2)}) %collective-permute-start.23) | collective-permute-done | bytes 294944 | tf_op jit(solution)/shard_map/ppermute | solution.py:51
  123.6 0.1 add_convert_fusion.2
  123.7 0.1 collective-permute-start.24
  123.8 2.9 %collective-permute-done.18 = bf16[24,6144]{1,0:T(8,128)(2,1)S(1)} collective-permute-done((bf16[24,6144]{1,0:T(8,128)(2,1)S(1)}, bf16[24,6144]{1,0:T(8,128)(2,1)S(1)}, u32[]{:S(2)}, u32[]{:S(2)}) %collective-permute-start.18) | collective-permute-done | bytes 294944 | tf_op jit(solution)/shard_map/ppermute | solution.py:51
  126.8 0.1 collective-permute-start.19
  127.0 4.7 %collective-permute-done.24 = bf16[24,6144]{1,0:T(8,128)(2,1)S(1)} collective-permute-done((bf16[24,6144]{1,0:T(8,128)(2,1)S(1)}, bf16[24,6144]{1,0:T(8,128)(2,1)S(1)}, u32[]{:S(2)}, u32[]{:S(2)}) %collective-permute-start.24) | collective-permute-done | bytes 294944 | tf_op jit(solution)/shard_map/ppermute | solution.py:51
  131.8 0.1 collective-permute-start.25
  131.9 2.9 %collective-permute-done.19 = bf16[24,6144]{1,0:T(8,128)(2,1)S(1)} collective-permute-done((bf16[24,6144]{1,0:T(8,128)(2,1)S(1)}, bf16[24,6144]{1,0:T(8,128)(2,1)S(1)}, u32[]{:S(2)}, u32[]{:S(2)}) %collective-permute-start.19) | collective-permute-done | bytes 294944 | tf_op jit(solution)/shard_map/ppermute | solution.py:51
  135.0 0.2 reshape.163
  135.2 16.4 %all_to_all.11 = bf16[8,3,6144]{2,1,0:T(4,128)(2,1)S(1)} all-to-all(bf16[8,3,6144]{2,1,0:T(4,128)(2,1)S(1)} %reshape.163), channel_id=1, replica_groups=mesh['groups'=2,'dev_0'=8,'dev_1'=8,'dev_2'=2] {'dev_0'}, dimensions={0} | all-to-all | bytes 589824 | tf_op jit(solution)/shard_map/all_to_all | solution.py:256
  151.5 1.1 fusion.1
  (61 shorter events, 1.4 us)
Async XLA Ops:
  0.0 21.2 %copy-start.6 = (s32[128]{0:T(128)S(1)}, s32[128]{0:T(128)}, u32[]{:S(2)}) copy-start(s32[128]{0:T(128)} %param.19) | copy-start | bytes 1540
  0.0 23.2 %copy-start.1 = (bf16[4,64,2048]{2,1,0:T(8,128)(2,1)S(1)}, bf16[4,64,2048]{2,1,0:T(8,128)(2,1)}, u32[]{:S(2)}) copy-start(bf16[4,64,2048]{2,1,0:T(8,128)(2,1)} %param.16) | copy-start | bytes 3145732
  1.3 22.8 %collective-permute-start = (bf16[64,2048]{0,1:T(8,128)(2,1)S(1)}, bf16[64,2048]{0,1:T(8,128)(2,1)S(1)}, u32[]{:S(2)}, u32[]{:S(2)}) collective-permute-start(bf16[64,2048]{0,1:T(8,128)(2,1)S(1)} %copy.78), channel_id=1, source_target_pairs={{1,0},{2,1},{3,2},{4,3},{5,4},{6,5},{7,6},{8,7},{9,8},{10,9},{11,1... | collective-permute-start | bytes 786440 | tf_op jit(solution)/shard_map/ppermute | solution.py:33
  21.1 2.4 %copy-start.5 = (f32[4,2]{0,1:T(2,128)S(1)}, f32[4,2]{0,1:T(2,128)}, u32[]{:S(2)}) copy-start(f32[4,2]{0,1:T(2,128)} %param.21) | copy-start | bytes 100
  25.2 0.8 copy-start.2
  25.2 1.0 copy-start.4
  25.5 64.2 %copy-start = (bf16[6144,256]{1,0:T(8,128)(2,1)S(1)}, bf16[6144,256]{1,0:T(8,128)(2,1)}, u32[]{:S(2)}) copy-start(bf16[6144,256]{1,0:T(8,128)(2,1)} %refs_16_.1) | copy-start | bytes 9437188
  53.1 8.0 %collective-permute-start.2 = (bf16[24,6144]{1,0:T(8,128)(2,1)S(1)}, bf16[24,6144]{1,0:T(8,128)(2,1)S(1)}, u32[]{:S(2)}, u32[]{:S(2)}) collective-permute-start(bf16[24,6144]{1,0:T(8,128)(2,1)S(1)} %reshape.162.refs_0_), channel_id=1, source_target_pairs={{0,2},{1,15},{2,4},{3,1},{4,6},{5,3},{6,8},{7,5},{8,10},{9,7},{10,... | collective-permute-start | bytes 884744 | tf_op jit(solution)/shard_map/ppermute | solution.py:51
  53.2 7.9 %collective-permute-start.1 = (bf16[24,6144]{1,0:T(8,128)(2,1)S(1)}, bf16[24,6144]{1,0:T(8,128)(2,1)S(1)}, u32[]{:S(2)}, u32[]{:S(2)}) collective-permute-start(bf16[24,6144]{1,0:T(8,128)(2,1)S(1)} %reshape.162.refs_0_), channel_id=1, source_target_pairs={{0,1},{1,0},{2,3},{3,2},{4,5},{5,4},{6,7},{7,6},{8,9},{9,8},{10,11... | collective-permute-start | bytes 884744 | tf_op jit(solution)/shard_map/ppermute | solution.py:38
  61.2 7.9 %collective-permute-start.3 = (bf16[24,6144]{1,0:T(8,128)(2,1)S(1)}, bf16[24,6144]{1,0:T(8,128)(2,1)S(1)}, u32[]{:S(2)}, u32[]{:S(2)}) collective-permute-start(bf16[24,6144]{1,0:T(8,128)(2,1)S(1)} %collective-permute-done.2.refs_12_), channel_id=1, source_target_pairs={{0,2},{1,15},{2,4},{3,1},{4,6},{5,3},{6,8},{7,5},{8,10},{9,7},{10,... | collective-permute-start | bytes 884744 | tf_op jit(solution)/shard_map/ppermute | solution.py:51
  61.2 11.1 %collective-permute-start.10 = (bf16[24,6144]{1,0:T(8,128)(2,1)S(1)}, bf16[24,6144]{1,0:T(8,128)(2,1)S(1)}, u32[]{:S(2)}, u32[]{:S(2)}) collective-permute-start(bf16[24,6144]{1,0:T(8,128)(2,1)S(1)} %collective-permute-done.1.refs_1_), channel_id=1, source_target_pairs={{0,2},{1,15},{2,4},{3,1},{4,6},{5,3},{6,8},{7,5},{8,10},{9,7},{10,... | collective-permute-start | bytes 884744 | tf_op jit(solution)/shard_map/ppermute | solution.py:51
  69.1 7.9 %collective-permute-start.4 = (bf16[24,6144]{1,0:T(8,128)(2,1)S(1)}, bf16[24,6144]{1,0:T(8,128)(2,1)S(1)}, u32[]{:S(2)}, u32[]{:S(2)}) collective-permute-start(bf16[24,6144]{1,0:T(8,128)(2,1)S(1)} %collective-permute-done.3.refs_11_), channel_id=1, source_target_pairs={{0,2},{1,15},{2,4},{3,1},{4,6},{5,3},{6,8},{7,5},{8,10},{9,7},{10,... | collective-permute-start | bytes 884744 | tf_op jit(solution)/shard_map/ppermute | solution.py:51
  72.2 7.9 %collective-permute-start.11 = (bf16[24,6144]{1,0:T(8,128)(2,1)S(1)}, bf16[24,6144]{1,0:T(8,128)(2,1)S(1)}, u32[]{:S(2)}, u32[]{:S(2)}) collective-permute-start(bf16[24,6144]{1,0:T(8,128)(2,1)S(1)} %collective-permute-done.10.refs_15_), channel_id=1, source_target_pairs={{0,2},{1,15},{2,4},{3,1},{4,6},{5,3},{6,8},{7,5},{8,10},{9,7},{10,... | collective-permute-start | bytes 884744 | tf_op jit(solution)/shard_map/ppermute | solution.py:51
  72.2 7.9 %collective-permute-start.9 = (bf16[24,6144]{1,0:T(8,128)(2,1)S(1)}, bf16[24,6144]{1,0:T(8,128)(2,1)S(1)}, u32[]{:S(2)}, u32[]{:S(2)}) collective-permute-start(bf16[24,6144]{1,0:T(8,128)(2,1)S(1)} %collective-permute-done.2.refs_12_), channel_id=1, source_target_pairs={{0,1},{1,0},{2,3},{3,2},{4,5},{5,4},{6,7},{7,6},{8,9},{9,8},{10,11... | collective-permute-start | bytes 884744 | tf_op jit(solution)/shard_map/ppermute | solution.py:38
  72.3 8.4 %collective-permute-start.8 = (bf16[24,6144]{1,0:T(8,128)(2,1)S(1)}, bf16[24,6144]{1,0:T(8,128)(2,1)S(1)}, u32[]{:S(2)}, u32[]{:S(2)}) collective-permute-start(bf16[24,6144]{1,0:T(8,128)(2,1)S(1)} %collective-permute-done.3.refs_11_), channel_id=1, source_target_pairs={{0,1},{1,0},{2,3},{3,2},{4,5},{5,4},{6,7},{7,6},{8,9},{9,8},{10,11... | collective-permute-start | bytes 884744 | tf_op jit(solution)/shard_map/ppermute | solution.py:38
  77.0 7.9 %collective-permute-start.5 = (bf16[24,6144]{1,0:T(8,128)(2,1)S(1)}, bf16[24,6144]{1,0:T(8,128)(2,1)S(1)}, u32[]{:S(2)}, u32[]{:S(2)}) collective-permute-start(bf16[24,6144]{1,0:T(8,128)(2,1)S(1)} %collective-permute-done.4.refs_10_), channel_id=1, source_target_pairs={{0,2},{1,15},{2,4},{3,1},{4,6},{5,3},{6,8},{7,5},{8,10},{9,7},{10,... | collective-permute-start | bytes 884744 | tf_op jit(solution)/shard_map/ppermute | solution.py:51
  80.2 7.9 %collective-permute-start.12 = (bf16[24,6144]{1,0:T(8,128)(2,1)S(1)}, bf16[24,6144]{1,0:T(8,128)(2,1)S(1)}, u32[]{:S(2)}, u32[]{:S(2)}) collective-permute-start(bf16[24,6144]{1,0:T(8,128)(2,1)S(1)} %collective-permute-done.11.refs_14_), channel_id=1, source_target_pairs={{0,2},{1,15},{2,4},{3,1},{4,6},{5,3},{6,8},{7,5},{8,10},{9,7},{10,... | collective-permute-start | bytes 884744 | tf_op jit(solution)/shard_map/ppermute | solution.py:51
  80.2 7.9 %collective-permute-start.15 = (bf16[24,6144]{1,0:T(8,128)(2,1)S(1)}, bf16[24,6144]{1,0:T(8,128)(2,1)S(1)}, u32[]{:S(2)}, u32[]{:S(2)}) collective-permute-start(bf16[24,6144]{1,0:T(8,128)(2,1)S(1)} %collective-permute-done.10.refs_15_), channel_id=1, source_target_pairs={{0,1},{1,0},{2,3},{3,2},{4,5},{5,4},{6,7},{7,6},{8,9},{9,8},{10,11... | collective-permute-start | bytes 884744 | tf_op jit(solution)/shard_map/ppermute | solution.py:38
  80.2 7.9 %collective-permute-start.7 = (bf16[24,6144]{1,0:T(8,128)(2,1)S(1)}, bf16[24,6144]{1,0:T(8,128)(2,1)S(1)}, u32[]{:S(2)}, u32[]{:S(2)}) collective-permute-start(bf16[24,6144]{1,0:T(8,128)(2,1)S(1)} %collective-permute-done.4.refs_10_), channel_id=1, source_target_pairs={{0,1},{1,0},{2,3},{3,2},{4,5},{5,4},{6,7},{7,6},{8,9},{9,8},{10,11... | collective-permute-start | bytes 884744 | tf_op jit(solution)/shard_map/ppermute | solution.py:38
  80.7 7.4 %collective-permute-start.14 = (bf16[24,6144]{1,0:T(8,128)(2,1)S(1)}, bf16[24,6144]{1,0:T(8,128)(2,1)S(1)}, u32[]{:S(2)}, u32[]{:S(2)}) collective-permute-start(bf16[24,6144]{1,0:T(8,128)(2,1)S(1)} %collective-permute-done.11.refs_14_), channel_id=1, source_target_pairs={{0,1},{1,0},{2,3},{3,2},{4,5},{5,4},{6,7},{7,6},{8,9},{9,8},{10,11... | collective-permute-start | bytes 884744 | tf_op jit(solution)/shard_map/ppermute | solution.py:38
  85.0 3.2 %collective-permute-start.6 = (bf16[24,6144]{1,0:T(8,128)(2,1)S(1)}, bf16[24,6144]{1,0:T(8,128)(2,1)S(1)}, u32[]{:S(2)}, u32[]{:S(2)}) collective-permute-start(bf16[24,6144]{1,0:T(8,128)(2,1)S(1)} %collective-permute-done.5.refs_9_), channel_id=1, source_target_pairs={{0,1},{1,0},{2,3},{3,2},{4,5},{5,4},{6,7},{7,6},{8,9},{9,8},{10,11... | collective-permute-start | bytes 884744 | tf_op jit(solution)/shard_map/ppermute | solution.py:38
  88.1 1.6 %collective-permute-start.13 = (bf16[24,6144]{1,0:T(8,128)(2,1)S(1)}, bf16[24,6144]{1,0:T(8,128)(2,1)S(1)}, u32[]{:S(2)}, u32[]{:S(2)}) collective-permute-start(bf16[24,6144]{1,0:T(8,128)(2,1)S(1)} %collective-permute-done.12.refs_13_), channel_id=1, source_target_pairs={{0,1},{1,0},{2,3},{3,2},{4,5},{5,4},{6,7},{7,6},{8,9},{9,8},{10,11... | collective-permute-start | bytes 884744 | tf_op jit(solution)/shard_map/ppermute | solution.py:38
  96.1 3.0 %collective-permute-start.20 = (bf16[96,6144]{1,0:T(8,128)(2,1)S(1)}, bf16[96,6144]{1,0:T(8,128)(2,1)S(1)}, u32[]{:S(2)}, u32[]{:S(2)}) collective-permute-start(bf16[96,6144]{1,0:T(8,128)(2,1)S(1)} %get-tuple-element.16), channel_id=1, source_target_pairs={{0,1},{1,0},{2,3},{3,2},{4,5},{5,4},{6,7},{7,6},{8,9},{9,8},{10,11... | collective-permute-start | bytes 3538952 | tf_op jit(solution)/shard_map/ppermute | solution.py:38
  99.2 8.0 %collective-permute-start.21 = (bf16[24,6144]{1,0:T(8,128)(2,1)S(1)}, bf16[24,6144]{1,0:T(8,128)(2,1)S(1)}, u32[]{:S(2)}, u32[]{:S(2)}) collective-permute-start(bf16[24,6144]{1,0:T(8,128)(2,1)S(1)} %add_convert_fusion.5), channel_id=1, source_target_pairs={{0,2},{1,15},{2,4},{3,1},{4,6},{5,3},{6,8},{7,5},{8,10},{9,7},{10,... | collective-permute-start | bytes 884744 | tf_op jit(solution)/shard_map/ppermute | solution.py:51
  99.3 8.2 %collective-permute-start.16 = (bf16[72,6144]{1,0:T(8,128)(2,1)S(1)}, bf16[72,6144]{1,0:T(8,128)(2,1)S(1)}, u32[]{:S(2)}, u32[]{:S(2)}) collective-permute-start(bf16[72,6144]{1,0:T(8,128)(2,1)S(1)} %get-tuple-element.13), channel_id=1, source_target_pairs={{0,1},{1,0},{2,3},{3,2},{4,5},{5,4},{6,7},{7,6},{8,9},{9,8},{10,11... | collective-permute-start | bytes 2654216 | tf_op jit(solution)/shard_map/ppermute | solution.py:38
  107.3 8.0 %collective-permute-start.22 = (bf16[24,6144]{1,0:T(8,128)(2,1)S(1)}, bf16[24,6144]{1,0:T(8,128)(2,1)S(1)}, u32[]{:S(2)}, u32[]{:S(2)}) collective-permute-start(bf16[24,6144]{1,0:T(8,128)(2,1)S(1)} %add_convert_fusion.4), channel_id=1, source_target_pairs={{0,2},{1,15},{2,4},{3,1},{4,6},{5,3},{6,8},{7,5},{8,10},{9,7},{10,... | collective-permute-start | bytes 884744 | tf_op jit(solution)/shard_map/ppermute | solution.py:51
  107.6 11.0 %collective-permute-start.17 = (bf16[24,6144]{1,0:T(8,128)(2,1)S(1)}, bf16[24,6144]{1,0:T(8,128)(2,1)S(1)}, u32[]{:S(2)}, u32[]{:S(2)}) collective-permute-start(bf16[24,6144]{1,0:T(8,128)(2,1)S(1)} %add_convert_fusion.8), channel_id=1, source_target_pairs={{0,2},{1,15},{2,4},{3,1},{4,6},{5,3},{6,8},{7,5},{8,10},{9,7},{10,... | collective-permute-start | bytes 884744 | tf_op jit(solution)/shard_map/ppermute | solution.py:51
  115.5 8.0 %collective-permute-start.23 = (bf16[24,6144]{1,0:T(8,128)(2,1)S(1)}, bf16[24,6144]{1,0:T(8,128)(2,1)S(1)}, u32[]{:S(2)}, u32[]{:S(2)}) collective-permute-start(bf16[24,6144]{1,0:T(8,128)(2,1)S(1)} %add_convert_fusion.3), channel_id=1, source_target_pairs={{0,2},{1,15},{2,4},{3,1},{4,6},{5,3},{6,8},{7,5},{8,10},{9,7},{10,... | collective-permute-start | bytes 884744 | tf_op jit(solution)/shard_map/ppermute | solution.py:51
  118.7 8.0 %collective-permute-start.18 = (bf16[24,6144]{1,0:T(8,128)(2,1)S(1)}, bf16[24,6144]{1,0:T(8,128)(2,1)S(1)}, u32[]{:S(2)}, u32[]{:S(2)}) collective-permute-start(bf16[24,6144]{1,0:T(8,128)(2,1)S(1)} %add_convert_fusion.7), channel_id=1, source_target_pairs={{0,2},{1,15},{2,4},{3,1},{4,6},{5,3},{6,8},{7,5},{8,10},{9,7},{10,... | collective-permute-start | bytes 884744 | tf_op jit(solution)/shard_map/ppermute | solution.py:51
  123.7 8.0 %collective-permute-start.24 = (bf16[24,6144]{1,0:T(8,128)(2,1)S(1)}, bf16[24,6144]{1,0:T(8,128)(2,1)S(1)}, u32[]{:S(2)}, u32[]{:S(2)}) collective-permute-start(bf16[24,6144]{1,0:T(8,128)(2,1)S(1)} %add_convert_fusion.2), channel_id=1, source_target_pairs={{0,2},{1,15},{2,4},{3,1},{4,6},{5,3},{6,8},{7,5},{8,10},{9,7},{10,... | collective-permute-start | bytes 884744 | tf_op jit(solution)/shard_map/ppermute | solution.py:51
  126.8 8.0 %collective-permute-start.19 = (bf16[24,6144]{1,0:T(8,128)(2,1)S(1)}, bf16[24,6144]{1,0:T(8,128)(2,1)S(1)}, u32[]{:S(2)}, u32[]{:S(2)}) collective-permute-start(bf16[24,6144]{1,0:T(8,128)(2,1)S(1)} %add_convert_fusion.6), channel_id=1, source_target_pairs={{0,2},{1,15},{2,4},{3,1},{4,6},{5,3},{6,8},{7,5},{8,10},{9,7},{10,... | collective-permute-start | bytes 884744 | tf_op jit(solution)/shard_map/ppermute | solution.py:51
  131.8 3.1 %collective-permute-start.25 = (bf16[24,6144]{1,0:T(8,128)(2,1)S(1)}, bf16[24,6144]{1,0:T(8,128)(2,1)S(1)}, u32[]{:S(2)}, u32[]{:S(2)}) collective-permute-start(bf16[24,6144]{1,0:T(8,128)(2,1)S(1)} %add_convert_fusion.1), channel_id=1, source_target_pairs={{0,1},{1,0},{2,3},{3,2},{4,5},{5,4},{6,7},{7,6},{8,9},{9,8},{10,11... | collective-permute-start | bytes 884744 | tf_op jit(solution)/shard_map/ppermute | solution.py:38
  134.9 16.7 %copy-start.3 = (bf16[4,6144]{1,0:T(4,128)(2,1)S(1)}, bf16[4,6144]{1,0:T(4,128)(2,1)}, u32[]{:S(2)}) copy-start(bf16[4,6144]{1,0:T(4,128)(2,1)} %param.13) | copy-start | bytes 147460
where the time goes:
time: 153 us
  waiting for transfers between devices  71.1 us (46%)
  blocking collectives  41.5 us (27%)
  starting transfers between devices  16.5 us (11%)
  local copies, waits for them, and re-layouts  7.84 us (5%)
  Pallas kernels  6.44 us (4%)
  other arithmetic  4.68 us (3%)
  matrix products  2.85 us (2%)
  between operations  1.74 us (1%)
    ppermute x14, waiting for transfers between devices, passed_on(): return lax.ppermute(value, ('dev_1', 'dev_2'), pairs)  66.8 us
    all_to_all x1, blocking collectives, layer(): came = lax.all_to_all(leaving, 'dev_0', 0, 0, tiled=True)  25.2 us
    all_to_all x1, blocking collectives, layer(): lax.all_to_all(summed.reshape(rows_x, MOST, width), 'dev_0', 0, 0, tiled=...  16.4 us
    ppermute x1, starting transfers between devices, passed_along(): lax.ppermute(value, axis, [(source, source + steps) for source in range(l...  13.2 us
    pallas_call x1, Pallas kernels, experts(): pl.pallas_call(experts_kernel, out_shape=[jax.ShapeDtypeStruct((s, width)...  6.44 us
    ppermute x11, waiting for transfers between devices, shifted(): lax.ppermute(value, axis, [(place, (place + steps) % count) for place in...  4.28 us
  transfers between devices with their start and end apart: 26, of which 16 were waited for; matrix products, arithmetic and copies ran while one was open for 6% of the time, Pallas kernels for 0%

commit v1 on v0

--- a/solution.py
+++ b/solution.py
@@ -86,7 +86,7 @@
             parcel = added(*terms, *moving.get(part, ())).astype(jnp.bfloat16)
             moving[part] = (passed_on(parcel),)
     leaving = added(other, *moving[0]).astype(jnp.bfloat16)
-    return added(own, *moving[1], swapped(leaving)).astype(jnp.bfloat16)
+    return own, *moving[1], swapped(leaving)
 
 
 def experts_kernel(*refs):
@@ -155,43 +155,217 @@
     )(*pieces, w_gate, w_up, w_down)
 
 
-def attend(query, cache, lens, own, window, first, last):
-    reqs = query.shape[0]
-    length = cache.shape[1]
+def slots_of(ids_ref, reqs, top):
+    named = [ids_ref[k, t] for t in range(reqs) for k in range(top)]
+    slots = []
+    for i, one in enumerate(named):
+        slot = jnp.int32(0)
+        for earlier in named[:i]:
+            slot = slot + (earlier == one).astype(jnp.int32)
+        slots.append(slot)
+    return named, slots
+
+
+def attend_kernel(me_ref, *refs):
+    next_ref = refs[0]
+    far_refs, (hidden_ref, leaving_ref, turned, mixed, packed), near_refs = refs[1:10], refs[10:15], refs[15:24]
+    copies = [pltpu.make_async_copy(f, n, refs[24].at[i]) for i, (f, n) in enumerate(zip(far_refs, near_refs))]
+    for copy in copies:
+        copy.start()
+    lens_ref, ids_ref, counts_ref, query_ref, own_ref, cache_ref, fresh_ref, tokens_ref, gain_ref = near_refs
+    reqs, width = tokens_ref.shape
+    length = cache_ref.shape[1]
+    span = fresh_ref.shape[0]
     group = QH // KVH
+    rows = group * reqs
     half = KVH * HD
     scale = 1.0 / math.sqrt(HD)
-    q_all = query.reshape(reqs, KVH, group, HD)
-    keys_c = cache[:, :, :half].reshape(reqs, length, KVH, HD)
-    vals_c = cache[:, :, half:].reshape(reqs, length, KVH, HD)
-    keys_w = window[:, :half].reshape(-1, KVH, HD)
-    vals_w = window[:, half:].reshape(-1, KVH, HD)
-    keys_o = own[:, :half].reshape(reqs, KVH, HD)
-    vals_o = own[:, half:].astype(jnp.float32).reshape(reqs, KVH, HD)
-    s_cache = (
-        jnp.einsum("rkgh,rpkh->rkgp", q_all, keys_c, preferred_element_type=jnp.float32) * scale
-    )
-    places = jnp.arange(length, dtype=jnp.int32)
-    s_cache = jnp.where(places[None, None, None, :] < lens[:, None, None, None], s_cache, NEG)
-    s_win = jnp.einsum("rkgh,pkh->rkgp", q_all, keys_w, preferred_element_type=jnp.float32) * scale
-    rows = jnp.arange(window.shape[0], dtype=jnp.int32)
-    live = (rows >= first) & (rows < last)
-    leader = jnp.arange(reqs, dtype=jnp.int32) == 0
-    usable = leader[:, None] & live[None, :]
-    s_win = jnp.where(usable[:, None, None, :], s_win, NEG)
-    s_own = jnp.einsum("rkgh,rkh->rkg", q_all, keys_o, preferred_element_type=jnp.float32) * scale
-    top = jnp.maximum(jnp.maximum(jnp.max(s_cache, -1), jnp.max(s_win, -1)), s_own)
-    e_cache = jnp.exp(s_cache - top[..., None])
-    e_win = jnp.exp(s_win - top[..., None])
-    e_own = jnp.exp(s_own - top)
-    total = jnp.sum(e_cache, -1) + jnp.sum(e_win, -1) + e_own
-    p_cache = (e_cache / total[..., None]).astype(jnp.bfloat16)
-    p_win = (e_win / total[..., None]).astype(jnp.bfloat16)
-    p_own = (e_own / total).astype(jnp.bfloat16).astype(jnp.float32)
-    mixed = jnp.einsum("rkgp,rpkh->rkgh", p_cache, vals_c, preferred_element_type=jnp.float32)
-    mixed = mixed + jnp.einsum("rkgp,pkh->rkgh", p_win, vals_w, preferred_element_type=jnp.float32)
-    mixed = mixed + p_own[..., None] * vals_o[:, :, None, :]
-    return mixed.reshape(reqs, QH * HD)
+    me = me_ref[0]
+    f32 = jnp.float32
+    for copy in copies:
+        copy.wait()
+    for h in range(QH):
+        turned[h * reqs : (h + 1) * reqs, :] = query_ref[:, h * HD : (h + 1) * HD].astype(f32)
+    counts = counts_ref[...].astype(f32)
+    places = lax.broadcasted_iota(jnp.int32, counts.shape, 1)
+    before = jnp.sum(jnp.where(places < me, counts, 0.0), 1, keepdims=True)
+    taken = jnp.sum(jnp.where(places == me, counts, 0.0), 1, keepdims=True)
+    first = (before - (me * (span // BLOCK)).astype(f32)) * BLOCK
+    last = first + taken * BLOCK
+    row_w = lax.broadcasted_iota(jnp.int32, (rows, 2 * span), 0) % reqs
+    col_w = lax.broadcasted_iota(jnp.int32, (rows, 2 * span), 1).astype(f32)
+    live_w = (row_w == 0) & (col_w >= first) & (col_w < last)
+    row_c = lax.broadcasted_iota(jnp.int32, (rows, reqs * length), 0) % reqs
+    col_c = lax.broadcasted_iota(jnp.int32, (rows, reqs * length), 1)
+    live_c = (row_c < 0)
+    for r in range(reqs):
+        live_c = live_c | ((row_c == r) & (col_c >= r * length) & (col_c < r * length + lens_ref[r]))
+    for g in range(KVH):
+        k_at = slice(g * HD, (g + 1) * HD)
+        v_at = slice(half + g * HD, half + (g + 1) * HD)
+        q32 = turned[g * rows : (g + 1) * rows, :]
+        q = q32.astype(jnp.bfloat16)
+        contract = (((1,), (1,)), ((), ()))
+        key_c = cache_ref[:, :, k_at].reshape(reqs * length, HD)
+        key_w = jnp.concatenate([fresh_ref[:, k_at], next_ref[:, k_at]], 0)
+        key_o = jnp.concatenate([own_ref[:, k_at].astype(f32)] * group, 0)
+        val_o = jnp.concatenate([own_ref[:, v_at].astype(f32)] * group, 0)
+        s_c = lax.dot_general(q, key_c, contract, preferred_element_type=f32) * scale
+        s_w = lax.dot_general(q, key_w, contract, preferred_element_type=f32) * scale
+        s_o = jnp.sum(q32 * key_o, 1, keepdims=True) * scale
+        s_c = jnp.where(live_c, s_c, NEG)
+        s_w = jnp.where(live_w, s_w, NEG)
+        top = jnp.maximum(jnp.maximum(jnp.max(s_c, 1, keepdims=True), jnp.max(s_w, 1, keepdims=True)), s_o)
+        e_c = jnp.exp(s_c - top)
+        e_w = jnp.exp(s_w - top)
+        e_o = jnp.exp(s_o - top)
+        total = jnp.sum(e_c, 1, keepdims=True) + jnp.sum(e_w, 1, keepdims=True) + e_o
+        over = 1.0 / total
+        p_c = (e_c * over).astype(jnp.bfloat16)
+        p_w = (e_w * over).astype(jnp.bfloat16)
+        p_o = (e_o * over).astype(jnp.bfloat16).astype(f32)
+        val_c = cache_ref[:, :, v_at].reshape(reqs * length, HD)
+        val_w = jnp.concatenate([fresh_ref[:, v_at], next_ref[:, v_at]], 0)
+        out = jnp.dot(p_c, val_c, preferred_element_type=f32) + jnp.dot(p_w, val_w, preferred_element_type=f32)
+        mixed[g * rows : (g + 1) * rows, :] = out + p_o * val_o
+    squares = jnp.zeros((reqs, HD), f32)
+    for h in range(QH):
+        cols = slice(h * HD, (h + 1) * HD)
+        hidden = tokens_ref[:, cols].astype(f32) + mixed[h * reqs : (h + 1) * reqs, :]
+        hidden_ref[:, cols] = hidden
+        squares = squares + hidden * hidden
+    norm = lax.rsqrt(jnp.sum(squares, 1, keepdims=True) / width + EPS)
+    normed = (hidden_ref[...] * norm * gain_ref[...]).astype(jnp.bfloat16).astype(f32)
+    named, slots = slots_of(ids_ref, reqs, ids_ref.shape[0])
+    tall = leaving_ref.shape[0] // EXPERTS
+    padded = MOST + 1
+    cell = lax.broadcasted_iota(jnp.int32, (EXPERTS * padded, 1), 0)
+    gone = jnp.zeros((EXPERTS * padded, width), f32)
+    for t in range(reqs):
+        takes = jnp.zeros((EXPERTS * padded, 1), f32)
+        for k in range(ids_ref.shape[0]):
+            i = t * ids_ref.shape[0] + k
+            takes = takes + (cell == named[i] * padded + slots[i]).astype(f32)
+        gone = gone + takes * normed[t : t + 1, :]
+    for j in range(width // HD):
+        packed[pl.ds(j, EXPERTS * padded, stride=width // HD), :] = gone[:, j * HD : (j + 1) * HD]
+    cut = width // HD
+    for x in range(leaving_ref.shape[0]):
+        at = x // tall * padded * cut
+        leaving_ref[x, :, :] = packed[at : at + MOST * cut, :].astype(jnp.bfloat16)
+
+
+def attended(me, lens, ids, counts, query, own, cache, fresh, following, tokens, gain, places):
+    reqs, width = tokens.shape
+    sm = pl.BlockSpec(memory_space=pltpu.SMEM)
+    vm = pl.BlockSpec(memory_space=pltpu.VMEM)
+    far = (lens, ids, counts, query, own, cache, fresh, tokens, gain)
+    far = [pltpu.with_memory_space_constraint(x, pltpu.HBM) for x in far]
+    return pl.pallas_call(
+        attend_kernel,
+        out_shape=[jax.ShapeDtypeStruct((reqs, width), jnp.float32), jax.ShapeDtypeStruct((places, MOST * width // HD, HD), jnp.bfloat16)],
+        in_specs=[sm, vm] + [pl.BlockSpec(memory_space=pltpu.HBM)] * len(far),
+        out_specs=[vm, vm],
+        scratch_shapes=[
+            pltpu.VMEM((QH * reqs, HD), jnp.float32),
+            pltpu.VMEM((QH * reqs, HD), jnp.float32),
+            pltpu.VMEM((EXPERTS * (MOST + 1) * width // HD, HD), jnp.float32),
+            *(pltpu.SMEM(x.shape, x.dtype) for x in far[:2]),
+            *(pltpu.VMEM(x.shape, x.dtype) for x in far[2:]),
+            pltpu.SemaphoreType.DMA((len(far),)),
+        ],
+        compiler_params=pltpu.CompilerParams(vmem_limit_bytes=16 * 1024 * 1024),
+        cost_estimate=pl.CostEstimate(flops=8 * reqs * width * 392, bytes_accessed=2 * 1024 * 1024, transcendentals=0),
+        name="attended",
+    )(me, following, *far)
+
+
+def unpack_kernel(came_ref, block_ref, spread):
+    rows, width = block_ref.shape
+    spread[...] = came_ref[...].astype(jnp.float32).reshape(spread.shape)
+    for j in range(width // HD):
+        block_ref[:, j * HD : (j + 1) * HD] = spread[pl.ds(j, rows, stride=width // HD), :].astype(jnp.bfloat16)
+
+
+def unpacked(came):
+    places, packed, lanes = came.shape
+    vm = pl.BlockSpec(memory_space=pltpu.VMEM)
+    return pl.pallas_call(
+        unpack_kernel,
+        out_shape=jax.ShapeDtypeStruct((places * MOST, packed // MOST * lanes), jnp.bfloat16),
+        in_specs=[vm],
+        out_specs=vm,
+        scratch_shapes=[pltpu.VMEM((places * packed, lanes), jnp.float32)],
+        compiler_params=pltpu.CompilerParams(vmem_limit_bytes=8 * 1024 * 1024),
+        name="unpacked",
+    )(came)
+
+
+def pack_kernel(first_ref, second_ref, third_ref, packed_ref, spread):
+    rows, width = first_ref.shape
+    f32 = jnp.float32
+    for j in range(width // HD):
+        cols = slice(j * HD, (j + 1) * HD)
+        total = first_ref[:, cols].astype(f32) + second_ref[:, cols].astype(f32) + third_ref[:, cols].astype(f32)
+        spread[pl.ds(j, rows, stride=width // HD), :] = total
+    packed_ref[...] = spread[...].astype(jnp.bfloat16).reshape(packed_ref.shape)
+
+
+def packed_sum(first, second, third, places):
+    rows, width = first.shape
+    vm = pl.BlockSpec(memory_space=pltpu.VMEM)
+    return pl.pallas_call(
+        pack_kernel,
+        out_shape=jax.ShapeDtypeStruct((places, rows // places * width // HD, HD), jnp.bfloat16),
+        in_specs=[vm] * 3,
+        out_specs=vm,
+        scratch_shapes=[pltpu.VMEM((rows * width // HD, HD), jnp.float32)],
+        compiler_params=pltpu.CompilerParams(vmem_limit_bytes=8 * 1024 * 1024),
+        name="packed_sum",
+    )(first, second, third)
+
+
+def mix_kernel(ids_ref, weights_ref, home_ref, hidden_ref, out_ref, spread):
+    reqs, width = hidden_ref.shape
+    tall = home_ref.shape[0] // EXPERTS
+    cut = width // HD
+    f32 = jnp.float32
+    named, slots = slots_of(ids_ref, reqs, ids_ref.shape[0])
+    sums = [jnp.zeros((cut, HD), f32) for _ in range(reqs)]
+    for e in range(EXPERTS):
+        for m in range(MOST):
+            at = slice(m * cut, (m + 1) * cut)
+            cell = home_ref[e * tall, at, :].astype(f32)
+            for x in range(1, tall):
+                cell = cell + home_ref[e * tall + x, at, :].astype(f32)
+            for t in range(reqs):
+                weight = jnp.float32(0.0)
+                for k in range(ids_ref.shape[0]):
+                    i = t * ids_ref.shape[0] + k
+                    here = (named[i] == e) & (slots[i] == m)
+                    weight = weight + jnp.where(here, weights_ref[k, t], 0.0)
+                sums[t] = sums[t] + weight * cell
+    for t in range(reqs):
+        spread[t * cut : (t + 1) * cut, :] = sums[t]
+    for j in range(cut):
+        cols = slice(j * HD, (j + 1) * HD)
+        moe = spread[pl.ds(j, reqs, stride=cut), :]
+        out_ref[:, cols] = (hidden_ref[:, cols] + moe).astype(jnp.bfloat16)
+
+
+def mixed_in(ids, weights, home, hidden):
+    reqs, width = hidden.shape
+    sm = pl.BlockSpec(memory_space=pltpu.SMEM)
+    vm = pl.BlockSpec(memory_space=pltpu.VMEM)
+    return pl.pallas_call(
+        mix_kernel,
+        out_shape=jax.ShapeDtypeStruct((reqs, width), jnp.bfloat16),
+        in_specs=[sm, sm, vm, vm],
+        out_specs=vm,
+        scratch_shapes=[pltpu.VMEM((reqs * width // HD, HD), jnp.float32)],
+        compiler_params=pltpu.CompilerParams(vmem_limit_bytes=8 * 1024 * 1024),
+        name="mixed_in",
+    )(ids, weights, home, hidden)
 
 
 def layer(
@@ -210,38 +384,24 @@
     w_down,
 ):
     me = lax.axis_index(DEV)
-    reqs = tokens.shape[0]
-    width = tokens.shape[1]
-    span = fresh_kv.shape[0]
     following = passed_along(fresh_kv, DEV, -1)
-    window = jnp.concatenate([fresh_kv, following], 0)
-    offsets = jnp.cumsum(block_counts) - block_counts
-    mine = lax.dynamic_index_in_dim(offsets, me, 0, keepdims=False)
-    taken = lax.dynamic_index_in_dim(block_counts, me, 0, keepdims=False)
-    first = (mine - me * (span // BLOCK)) * BLOCK
-    last = first + taken * BLOCK
-    attn = attend(queries, kv_cache, context_lengths, token_kv, window, first, last)
-    hidden_state = tokens.astype(jnp.float32) + attn
-    spread = jnp.mean(hidden_state * hidden_state, -1, keepdims=True)
-    normed = (hidden_state * lax.rsqrt(spread + EPS) * norm_gain).astype(jnp.bfloat16)
-    labels = jnp.arange(EXPERTS, dtype=jnp.int32)
-    flat_ids = expert_ids.reshape(-1)
-    picks = (flat_ids[:, None] == labels[None, :]).astype(jnp.int32)
-    slots = jnp.sum((jnp.cumsum(picks, 0) - picks) * picks, 1).reshape(reqs, 2)
     rows_x = lax.axis_size("dev_0")
-    per_expert = rows_x // EXPERTS
-    expert_of = jnp.arange(rows_x, dtype=jnp.int32) // per_expert
-    slot_ids = jnp.arange(MOST, dtype=jnp.int32)
-    named = (expert_ids[None, None, :, :] == expert_of[:, None, None, None]) & (
-        slots[None, None, :, :] == slot_ids[None, :, None, None]
+    me = lax.axis_index(DEV).astype(jnp.int32)[None]
+    hidden_state, leaving = attended(
+        me,
+        context_lengths,
+        expert_ids.T,
+        block_counts[None],
+        queries,
+        token_kv,
+        kv_cache,
+        fresh_kv,
+        following,
+        tokens,
+        norm_gain[None],
+        rows_x,
     )
-    taking = jnp.sum(named.astype(jnp.float32), 3)
-    weights = jnp.sum(named.astype(jnp.float32) * route_weights[None, None, :, :], 3)
-    leaving = jnp.einsum(
-        "xmt,td->xmd", taking.astype(jnp.bfloat16), normed, preferred_element_type=jnp.float32
-    ).astype(jnp.bfloat16)
-    came = lax.all_to_all(leaving, "dev_0", 0, 0, tiled=True)
-    own_block = came.reshape(rows_x * MOST, width)
+    own_block = unpacked(lax.all_to_all(leaving, "dev_0", 0, 0, tiled=True))
     own, other, came, theirs = gathered(own_block)
     far = lax.axis_size("dev_1") // 2
     chains = chain_order(far)
@@ -252,12 +412,9 @@
             pieces += [group[key] for key in chain]
     sizes = [each, each] + 2 * [len(chain) * each for chain in chains]
     home_own, home_other, kept_0, kept_1, sent_0, sent_1 = experts(pieces, w_gate, w_up, w_down, sizes)
-    summed = scattered(far, each, home_own, home_other, (kept_0, kept_1), (sent_0, sent_1))
-    home = lax.all_to_all(summed.reshape(rows_x, MOST, width), "dev_0", 0, 0, tiled=True)
-    moe = jnp.einsum(
-        "xmt,xmd->td", weights, home.astype(jnp.float32), precision=lax.Precision.HIGHEST
-    )
-    return (hidden_state + moe).astype(jnp.bfloat16)
+    last_terms = scattered(far, each, home_own, home_other, (kept_0, kept_1), (sent_0, sent_1))
+    home = lax.all_to_all(packed_sum(*last_terms, rows_x), "dev_0", 0, 0, tiled=True)
+    return mixed_in(expert_ids.T, route_weights.T, home, hidden_state)
 
 
 def solution(mesh):

time: 153 us -> 142 us (0.928)
  blocking collectives: 41.5 us -> 34.1 us
  Pallas kernels: 6.44 us -> 12.9 us
  local copies, waits for them, and re-layouts: 7.84 us -> 1.9 us
  waiting for transfers between devices: 71.1 us -> 75.3 us
  other arithmetic: 4.68 us -> 0.75 us
  matrix products: 2.85 us -> 0 us
  between operations: 1.74 us -> 0.21 us
    all_to_all x2, blocking collectives: 41.5 us -> 34.1 us  [the longest x1 19.9 us: layer(): own_block = unpacked(lax.all_to_all(leaving, 'dev_0', 0, 0, tiled=True))]
    pallas_call x0 -> x4, Pallas kernels: none -> 6.47 us  [the longest x1 4.61 us: attended(): pl.pallas_call(attend_kernel, out_shape=[jax.ShapeDtypeStruct((reqs, widt...]
    ppermute x1, waiting for transfers between devices: 0.01 us -> 4.18 us  [passed_along(): lax.ppermute(value, axis, [(source, source + steps) for source in range(l...]
    dot_general x7 -> x0, matrix products: 2.85 us -> none  [the longest x1 1.08 us: layer(): jnp.einsum('xmt,xmd->td', weights, home.astype(jnp.float32), precision=la...]
    reshape x5 -> x0, local copies, waits for them, and re-layouts: 2.35 us -> none  [the longest x1 1.25 us: layer(): own_block = came.reshape(rows_x * MOST, width)]
    dynamic_slice x2 -> x0, local copies, waits for them, and re-layouts: 1.9 us -> none  [the longest x1 1.31 us: layer(): taken = lax.dynamic_index_in_dim(block_counts, me, 0, keepdims=False)]
  transfers between devices with their start and end apart: 26 -> 26, of which waited for: 16 -> 17; matrix products, arithmetic and copies ran while one was open for 6% -> 0% of each run, Pallas kernels for 0% -> 0%
where the time goes in v1:
time: 142 us
  waiting for transfers between devices  75.3 us (53%)
  blocking collectives  34.1 us (24%)
  starting transfers between devices  16.4 us (12%)
  Pallas kernels  12.9 us (9%)
  local copies, waits for them, and re-layouts  1.9 us (1%)
    ppermute x14, waiting for transfers between devices, passed_on(): return lax.ppermute(value, ('dev_1', 'dev_2'), pairs)  66.9 us
    all_to_all x1, blocking collectives, layer(): own_block = unpacked(lax.all_to_all(leaving, 'dev_0', 0, 0, tiled=True))  19.9 us
    all_to_all x1, blocking collectives, layer(): lax.all_to_all(packed_sum(*last_terms, rows_x), 'dev_0', 0, 0, tiled=True)  14.2 us
    ppermute x1, starting transfers between devices, passed_along(): lax.ppermute(value, axis, [(source, source + steps) for source in range(l...  13.1 us
    pallas_call x1, Pallas kernels, experts(): pl.pallas_call(experts_kernel, out_shape=[jax.ShapeDtypeStruct((s, width)...  6.44 us
    pallas_call x1, Pallas kernels, attended(): pl.pallas_call(attend_kernel, out_shape=[jax.ShapeDtypeStruct((reqs, widt...  4.61 us
    ppermute x11, waiting for transfers between devices, shifted(): lax.ppermute(value, axis, [(place, (place + steps) % count) for place in...  4.28 us
    ppermute x1, waiting for transfers between devices, passed_along(): lax.ppermute(value, axis, [(source, source + steps) for source in range(l...  4.18 us
  transfers between devices with their start and end apart: 26, of which 17 were waited for; matrix products, arithmetic and copies ran while one was open for 0% of the time, Pallas kernels for 0%

profile of v1, /device:TPU:514, one launch (start us, length us, event | category | flops | bytes accessed | tf_op | source)
XLA Modules:
  0.0 141.5 jit_solution(1802001158377770481)
XLA Ops:
  0.0 13.1 %collective-permute-start = (bf16[64,2048]{1,0:T(8,128)(2,1)}, bf16[64,2048]{1,0:T(8,128)(2,1)S(1)}, u32[]{:S(2)}, u32[]{:S(2)}) collective-permute-start(bf16[64,2048]{1,0:T(8,128)(2,1)} %refs_7_.1), channel_id=1, source_target_pairs={{1,0},{2,1},{3,2},{4,3},{5,4},{6,5},{7,6},{8,7},{9,8},{10,9},{11,1... | collective-permute-start | bytes 786440 | tf_op jit(solution)/shard_map/ppermute | solution.py:33
  13.2 4.2 %collective-permute-done.refs_0_ = bf16[64,2048]{1,0:T(8,128)(2,1)S(1)} collective-permute-done((bf16[64,2048]{1,0:T(8,128)(2,1)}, bf16[64,2048]{1,0:T(8,128)(2,1)S(1)}, u32[]{:S(2)}, u32[]{:S(2)}) %collective-permute-start) | collective-permute-done | bytes 262176 | tf_op jit(solution)/shard_map/ppermute | solution.py:33
  17.3 4.6 %attended.1 = (f32[4,6144]{1,0:T(4,128)S(1)}, bf16[8,144,128]{2,1,0:T(8,128)(2,1)S(1)}) custom-call(s32[1]{0:T(128)} %bitcast.2.me_ref, bf16[64,2048]{1,0:T(8,128)(2,1)S(1)} %collective-permute-done.refs_0_, s32[4]{0:T(128)} %refs_1_.1, s32[2,4]{1,0:T(2,128)} %bitcast.5, s32[1,128]{1,0:T(1,128)} %bitcast.9, bf16[4,6144]{1,0:T(4,128)(2,1)} %refs_4_.1, ...), custom_call_target="tpu_custom_call" | custom-call | flops 77070336 | bytes 2097152 | tf_op jit(solution)/shard_map/attended/pallas_call | solution.py:264
  21.9 19.9 %all_to_all.10.came_ref = bf16[8,144,128]{2,1,0:T(8,128)(2,1)S(1)} all-to-all(bf16[8,144,128]{2,1,0:T(8,128)(2,1)S(1)} %get-tuple-element.13), channel_id=1, replica_groups=mesh['groups'=2,'dev_0'=8,'dev_1'=8,'dev_2'=2] {'dev_0'}, dimensions={0} | all-to-all | bytes 589824 | tf_op jit(solution)/shard_map/all_to_all | solution.py:404
  41.8 0.2 unpacked.1.refs_0_
  42.0 0.1 collective-permute-start.2
  42.2 0.4 collective-permute-start.1
  42.5 7.5 %collective-permute-done.2.refs_12_ = bf16[24,6144]{1,0:T(8,128)(2,1)S(1)} collective-permute-done((bf16[24,6144]{1,0:T(8,128)(2,1)S(1)}, bf16[24,6144]{1,0:T(8,128)(2,1)S(1)}, u32[]{:S(2)}, u32[]{:S(2)}) %collective-permute-start.2) | collective-permute-done | bytes 294944 | tf_op jit(solution)/shard_map/ppermute | solution.py:51
  50.1 0.0 collective-permute-start.3
  50.1 0.0 collective-permute-done.1.refs_1_
  50.1 0.0 collective-permute-start.10
  50.1 7.9 %collective-permute-done.3.refs_11_ = bf16[24,6144]{1,0:T(8,128)(2,1)S(1)} collective-permute-done((bf16[24,6144]{1,0:T(8,128)(2,1)S(1)}, bf16[24,6144]{1,0:T(8,128)(2,1)S(1)}, u32[]{:S(2)}, u32[]{:S(2)}) %collective-permute-start.3) | collective-permute-done | bytes 294944 | tf_op jit(solution)/shard_map/ppermute | solution.py:51
  58.0 0.0 collective-permute-start.4
  58.0 3.2 %collective-permute-done.10.refs_15_ = bf16[24,6144]{1,0:T(8,128)(2,1)S(1)} collective-permute-done((bf16[24,6144]{1,0:T(8,128)(2,1)S(1)}, bf16[24,6144]{1,0:T(8,128)(2,1)S(1)}, u32[]{:S(2)}, u32[]{:S(2)}) %collective-permute-start.10) | collective-permute-done | bytes 294944 | tf_op jit(solution)/shard_map/ppermute | solution.py:51
  61.2 0.0 collective-permute-start.11
  61.2 0.0 collective-permute-start.9
  61.2 0.5 collective-permute-start.8
  61.7 4.3 %collective-permute-done.4.refs_10_ = bf16[24,6144]{1,0:T(8,128)(2,1)S(1)} collective-permute-done((bf16[24,6144]{1,0:T(8,128)(2,1)S(1)}, bf16[24,6144]{1,0:T(8,128)(2,1)S(1)}, u32[]{:S(2)}, u32[]{:S(2)}) %collective-permute-start.4) | collective-permute-done | bytes 294944 | tf_op jit(solution)/shard_map/ppermute | solution.py:51
  66.0 0.0 collective-permute-start.5
  66.0 3.2 %collective-permute-done.11.refs_14_ = bf16[24,6144]{1,0:T(8,128)(2,1)S(1)} collective-permute-done((bf16[24,6144]{1,0:T(8,128)(2,1)S(1)}, bf16[24,6144]{1,0:T(8,128)(2,1)S(1)}, u32[]{:S(2)}, u32[]{:S(2)}) %collective-permute-start.11) | collective-permute-done | bytes 294944 | tf_op jit(solution)/shard_map/ppermute | solution.py:51
  69.1 0.0 collective-permute-start.12
  69.1 0.0 collective-permute-start.15
  69.1 0.0 collective-permute-done.9.refs_5_
  69.1 0.5 collective-permute-start.7
  69.6 0.0 collective-permute-done.8.refs_4_
  69.6 0.1 collective-permute-start.14
  69.8 4.1 %collective-permute-done.5.refs_9_ = bf16[24,6144]{1,0:T(8,128)(2,1)S(1)} collective-permute-done((bf16[24,6144]{1,0:T(8,128)(2,1)S(1)}, bf16[24,6144]{1,0:T(8,128)(2,1)S(1)}, u32[]{:S(2)}, u32[]{:S(2)}) %collective-permute-start.5) | collective-permute-done | bytes 294944 | tf_op jit(solution)/shard_map/ppermute | solution.py:51
  73.9 0.0 collective-permute-start.6
  73.9 3.2 %collective-permute-done.12.refs_13_ = bf16[24,6144]{1,0:T(8,128)(2,1)S(1)} collective-permute-done((bf16[24,6144]{1,0:T(8,128)(2,1)S(1)}, bf16[24,6144]{1,0:T(8,128)(2,1)S(1)}, u32[]{:S(2)}, u32[]{:S(2)}) %collective-permute-start.12) | collective-permute-done | bytes 294944 | tf_op jit(solution)/shard_map/ppermute | solution.py:51
  77.0 0.0 collective-permute-start.13
  77.1 0.0 collective-permute-done.14.refs_7_
  77.1 1.5 %collective-permute-done.13.refs_6_ = bf16[24,6144]{1,0:T(8,128)(2,1)S(1)} collective-permute-done((bf16[24,6144]{1,0:T(8,128)(2,1)S(1)}, bf16[24,6144]{1,0:T(8,128)(2,1)S(1)}, u32[]{:S(2)}, u32[]{:S(2)}) %collective-permute-start.13) | collective-permute-done | bytes 294944 | tf_op jit(solution)/shard_map/ppermute | solution.py:38
  78.6 1.9 %copy-done = bf16[6144,256]{1,0:T(8,128)(2,1)S(1)} copy-done((bf16[6144,256]{1,0:T(8,128)(2,1)S(1)}, bf16[6144,256]{1,0:T(8,128)(2,1)}, u32[]{:S(2)}) %copy-start) | copy-done | bytes 3145752
  80.5 6.4 %experts.1 = (bf16[24,6144]{1,0:T(8,128)(2,1)S(1)}, bf16[24,6144]{1,0:T(8,128)(2,1)S(1)}, bf16[96,6144]{1,0:T(8,128)(2,1)S(1)}, bf16[72,6144]{1,0:T(8,128)(2,1)S...) custom-call(bf16[24,6144]{1,0:T(8,128)(2,1)S(1)} %unpacked.1.refs_0_, ...), custom_call_target="tpu_custom_call" | custom-call | flops 3623878656 | bytes 9437184 | tf_op jit(solution)/shard_map/experts/pallas_call | solution.py:141
  87.0 0.3 collective-permute-start.20
  87.2 2.7 %collective-permute-done.20 = bf16[96,6144]{1,0:T(8,128)(2,1)S(1)} collective-permute-done((bf16[96,6144]{1,0:T(8,128)(2,1)S(1)}, bf16[96,6144]{1,0:T(8,128)(2,1)S(1)}, u32[]{:S(2)}, u32[]{:S(2)}) %collective-permute-start.20) | collective-permute-done | bytes 1179680 | tf_op jit(solution)/shard_map/ppermute | solution.py:38
  89.9 0.1 add_convert_fusion.4
  90.0 0.1 collective-permute-start.21
  90.2 0.3 collective-permute-start.16
  90.4 7.6 %collective-permute-done.21 = bf16[24,6144]{1,0:T(8,128)(2,1)S(1)} collective-permute-done((bf16[24,6144]{1,0:T(8,128)(2,1)S(1)}, bf16[24,6144]{1,0:T(8,128)(2,1)S(1)}, u32[]{:S(2)}, u32[]{:S(2)}) %collective-permute-start.21) | collective-permute-done | bytes 294944 | tf_op jit(solution)/shard_map/ppermute | solution.py:51
  98.1 0.1 add_convert_fusion.3
  98.2 0.1 collective-permute-start.22
  98.3 0.1 add_convert_fusion.7
  98.4 0.1 collective-permute-start.17
  98.5 7.7 %collective-permute-done.22 = bf16[24,6144]{1,0:T(8,128)(2,1)S(1)} collective-permute-done((bf16[24,6144]{1,0:T(8,128)(2,1)S(1)}, bf16[24,6144]{1,0:T(8,128)(2,1)S(1)}, u32[]{:S(2)}, u32[]{:S(2)}) %collective-permute-start.22) | collective-permute-done | bytes 294944 | tf_op jit(solution)/shard_map/ppermute | solution.py:51
  106.2 0.1 add_convert_fusion.2
  106.3 0.1 collective-permute-start.23
  106.5 2.9 %collective-permute-done.17 = bf16[24,6144]{1,0:T(8,128)(2,1)S(1)} collective-permute-done((bf16[24,6144]{1,0:T(8,128)(2,1)S(1)}, bf16[24,6144]{1,0:T(8,128)(2,1)S(1)}, u32[]{:S(2)}, u32[]{:S(2)}) %collective-permute-start.17) | collective-permute-done | bytes 294944 | tf_op jit(solution)/shard_map/ppermute | solution.py:51
  109.4 0.1 add_convert_fusion.6
  109.5 0.1 collective-permute-start.18
  109.6 4.7 %collective-permute-done.23 = bf16[24,6144]{1,0:T(8,128)(2,1)S(1)} collective-permute-done((bf16[24,6144]{1,0:T(8,128)(2,1)S(1)}, bf16[24,6144]{1,0:T(8,128)(2,1)S(1)}, u32[]{:S(2)}, u32[]{:S(2)}) %collective-permute-start.23) | collective-permute-done | bytes 294944 | tf_op jit(solution)/shard_map/ppermute | solution.py:51
  114.4 0.1 add_convert_fusion.1
  114.5 0.1 collective-permute-start.24
  114.6 2.9 %collective-permute-done.18 = bf16[24,6144]{1,0:T(8,128)(2,1)S(1)} collective-permute-done((bf16[24,6144]{1,0:T(8,128)(2,1)S(1)}, bf16[24,6144]{1,0:T(8,128)(2,1)S(1)}, u32[]{:S(2)}, u32[]{:S(2)}) %collective-permute-start.18) | collective-permute-done | bytes 294944 | tf_op jit(solution)/shard_map/ppermute | solution.py:51
  117.5 0.1 add_convert_fusion.5
  117.7 0.1 collective-permute-start.19
  117.8 4.7 %collective-permute-done.24 = bf16[24,6144]{1,0:T(8,128)(2,1)S(1)} collective-permute-done((bf16[24,6144]{1,0:T(8,128)(2,1)S(1)}, bf16[24,6144]{1,0:T(8,128)(2,1)S(1)}, u32[]{:S(2)}, u32[]{:S(2)}) %collective-permute-start.24) | collective-permute-done | bytes 294944 | tf_op jit(solution)/shard_map/ppermute | solution.py:51
  122.5 0.1 add_convert_fusion
  122.6 0.1 collective-permute-start.25
  122.8 2.9 %collective-permute-done.19.second_ref = bf16[24,6144]{1,0:T(8,128)(2,1)S(1)} collective-permute-done((bf16[24,6144]{1,0:T(8,128)(2,1)S(1)}, bf16[24,6144]{1,0:T(8,128)(2,1)S(1)}, u32[]{:S(2)}, u32[]{:S(2)}) %collective-permute-start.19) | collective-permute-done | bytes 294944 | tf_op jit(solution)/shard_map/ppermute | solution.py:51
  125.7 0.0 collective-permute-done.25.third_ref
  125.7 0.3 packed_sum.1
  126.0 14.2 %all_to_all.11.home_ref = bf16[8,144,128]{2,1,0:T(8,128)(2,1)S(1)} all-to-all(bf16[8,144,128]{2,1,0:T(8,128)(2,1)S(1)} %packed_sum.1), channel_id=1, replica_groups=mesh['groups'=2,'dev_0'=8,'dev_1'=8,'dev_2'=2] {'dev_0'}, dimensions={0} | all-to-all | bytes 589824 | tf_op jit(solution)/shard_map/all_to_all | solution.py:416
  140.2 1.4 mixed_in.1
  (9 shorter events, 0.0 us)
Async XLA Ops:
  0.0 17.3 %collective-permute-start = (bf16[64,2048]{1,0:T(8,128)(2,1)}, bf16[64,2048]{1,0:T(8,128)(2,1)S(1)}, u32[]{:S(2)}, u32[]{:S(2)}) collective-permute-start(bf16[64,2048]{1,0:T(8,128)(2,1)} %refs_7_.1), channel_id=1, source_target_pairs={{1,0},{2,1},{3,2},{4,3},{5,4},{6,5},{7,6},{8,7},{9,8},{10,9},{11,1... | collective-permute-start | bytes 786440 | tf_op jit(solution)/shard_map/ppermute | solution.py:33
  42.0 8.0 %collective-permute-start.2 = (bf16[24,6144]{1,0:T(8,128)(2,1)S(1)}, bf16[24,6144]{1,0:T(8,128)(2,1)S(1)}, u32[]{:S(2)}, u32[]{:S(2)}) collective-permute-start(bf16[24,6144]{1,0:T(8,128)(2,1)S(1)} %unpacked.1.refs_0_), channel_id=1, source_target_pairs={{0,2},{1,15},{2,4},{3,1},{4,6},{5,3},{6,8},{7,5},{8,10},{9,7},{10,... | collective-permute-start | bytes 884744 | tf_op jit(solution)/shard_map/ppermute | solution.py:51
  42.2 7.9 %collective-permute-start.1 = (bf16[24,6144]{1,0:T(8,128)(2,1)S(1)}, bf16[24,6144]{1,0:T(8,128)(2,1)S(1)}, u32[]{:S(2)}, u32[]{:S(2)}) collective-permute-start(bf16[24,6144]{1,0:T(8,128)(2,1)S(1)} %unpacked.1.refs_0_), channel_id=1, source_target_pairs={{0,1},{1,0},{2,3},{3,2},{4,5},{5,4},{6,7},{7,6},{8,9},{9,8},{10,11... | collective-permute-start | bytes 884744 | tf_op jit(solution)/shard_map/ppermute | solution.py:38
  50.1 7.9 %collective-permute-start.3 = (bf16[24,6144]{1,0:T(8,128)(2,1)S(1)}, bf16[24,6144]{1,0:T(8,128)(2,1)S(1)}, u32[]{:S(2)}, u32[]{:S(2)}) collective-permute-start(bf16[24,6144]{1,0:T(8,128)(2,1)S(1)} %collective-permute-done.2.refs_12_), channel_id=1, source_target_pairs={{0,2},{1,15},{2,4},{3,1},{4,6},{5,3},{6,8},{7,5},{8,10},{9,7},{10,... | collective-permute-start | bytes 884744 | tf_op jit(solution)/shard_map/ppermute | solution.py:51
  50.1 11.1 %collective-permute-start.10 = (bf16[24,6144]{1,0:T(8,128)(2,1)S(1)}, bf16[24,6144]{1,0:T(8,128)(2,1)S(1)}, u32[]{:S(2)}, u32[]{:S(2)}) collective-permute-start(bf16[24,6144]{1,0:T(8,128)(2,1)S(1)} %collective-permute-done.1.refs_1_), channel_id=1, source_target_pairs={{0,2},{1,15},{2,4},{3,1},{4,6},{5,3},{6,8},{7,5},{8,10},{9,7},{10,... | collective-permute-start | bytes 884744 | tf_op jit(solution)/shard_map/ppermute | solution.py:51
  58.0 7.9 %collective-permute-start.4 = (bf16[24,6144]{1,0:T(8,128)(2,1)S(1)}, bf16[24,6144]{1,0:T(8,128)(2,1)S(1)}, u32[]{:S(2)}, u32[]{:S(2)}) collective-permute-start(bf16[24,6144]{1,0:T(8,128)(2,1)S(1)} %collective-permute-done.3.refs_11_), channel_id=1, source_target_pairs={{0,2},{1,15},{2,4},{3,1},{4,6},{5,3},{6,8},{7,5},{8,10},{9,7},{10,... | collective-permute-start | bytes 884744 | tf_op jit(solution)/shard_map/ppermute | solution.py:51
  61.2 7.9 %collective-permute-start.11 = (bf16[24,6144]{1,0:T(8,128)(2,1)S(1)}, bf16[24,6144]{1,0:T(8,128)(2,1)S(1)}, u32[]{:S(2)}, u32[]{:S(2)}) collective-permute-start(bf16[24,6144]{1,0:T(8,128)(2,1)S(1)} %collective-permute-done.10.refs_15_), channel_id=1, source_target_pairs={{0,2},{1,15},{2,4},{3,1},{4,6},{5,3},{6,8},{7,5},{8,10},{9,7},{10,... | collective-permute-start | bytes 884744 | tf_op jit(solution)/shard_map/ppermute | solution.py:51
  61.2 7.9 %collective-permute-start.9 = (bf16[24,6144]{1,0:T(8,128)(2,1)S(1)}, bf16[24,6144]{1,0:T(8,128)(2,1)S(1)}, u32[]{:S(2)}, u32[]{:S(2)}) collective-permute-start(bf16[24,6144]{1,0:T(8,128)(2,1)S(1)} %collective-permute-done.2.refs_12_), channel_id=1, source_target_pairs={{0,1},{1,0},{2,3},{3,2},{4,5},{5,4},{6,7},{7,6},{8,9},{9,8},{10,11... | collective-permute-start | bytes 884744 | tf_op jit(solution)/shard_map/ppermute | solution.py:38
  61.2 8.4 %collective-permute-start.8 = (bf16[24,6144]{1,0:T(8,128)(2,1)S(1)}, bf16[24,6144]{1,0:T(8,128)(2,1)S(1)}, u32[]{:S(2)}, u32[]{:S(2)}) collective-permute-start(bf16[24,6144]{1,0:T(8,128)(2,1)S(1)} %collective-permute-done.3.refs_11_), channel_id=1, source_target_pairs={{0,1},{1,0},{2,3},{3,2},{4,5},{5,4},{6,7},{7,6},{8,9},{9,8},{10,11... | collective-permute-start | bytes 884744 | tf_op jit(solution)/shard_map/ppermute | solution.py:38
  66.0 7.9 %collective-permute-start.5 = (bf16[24,6144]{1,0:T(8,128)(2,1)S(1)}, bf16[24,6144]{1,0:T(8,128)(2,1)S(1)}, u32[]{:S(2)}, u32[]{:S(2)}) collective-permute-start(bf16[24,6144]{1,0:T(8,128)(2,1)S(1)} %collective-permute-done.4.refs_10_), channel_id=1, source_target_pairs={{0,2},{1,15},{2,4},{3,1},{4,6},{5,3},{6,8},{7,5},{8,10},{9,7},{10,... | collective-permute-start | bytes 884744 | tf_op jit(solution)/shard_map/ppermute | solution.py:51
  69.1 7.9 %collective-permute-start.12 = (bf16[24,6144]{1,0:T(8,128)(2,1)S(1)}, bf16[24,6144]{1,0:T(8,128)(2,1)S(1)}, u32[]{:S(2)}, u32[]{:S(2)}) collective-permute-start(bf16[24,6144]{1,0:T(8,128)(2,1)S(1)} %collective-permute-done.11.refs_14_), channel_id=1, source_target_pairs={{0,2},{1,15},{2,4},{3,1},{4,6},{5,3},{6,8},{7,5},{8,10},{9,7},{10,... | collective-permute-start | bytes 884744 | tf_op jit(solution)/shard_map/ppermute | solution.py:51
  69.1 7.9 %collective-permute-start.15 = (bf16[24,6144]{1,0:T(8,128)(2,1)S(1)}, bf16[24,6144]{1,0:T(8,128)(2,1)S(1)}, u32[]{:S(2)}, u32[]{:S(2)}) collective-permute-start(bf16[24,6144]{1,0:T(8,128)(2,1)S(1)} %collective-permute-done.10.refs_15_), channel_id=1, source_target_pairs={{0,1},{1,0},{2,3},{3,2},{4,5},{5,4},{6,7},{7,6},{8,9},{9,8},{10,11... | collective-permute-start | bytes 884744 | tf_op jit(solution)/shard_map/ppermute | solution.py:38
  69.1 7.9 %collective-permute-start.7 = (bf16[24,6144]{1,0:T(8,128)(2,1)S(1)}, bf16[24,6144]{1,0:T(8,128)(2,1)S(1)}, u32[]{:S(2)}, u32[]{:S(2)}) collective-permute-start(bf16[24,6144]{1,0:T(8,128)(2,1)S(1)} %collective-permute-done.4.refs_10_), channel_id=1, source_target_pairs={{0,1},{1,0},{2,3},{3,2},{4,5},{5,4},{6,7},{7,6},{8,9},{9,8},{10,11... | collective-permute-start | bytes 884744 | tf_op jit(solution)/shard_map/ppermute | solution.py:38
  69.6 7.4 %collective-permute-start.14 = (bf16[24,6144]{1,0:T(8,128)(2,1)S(1)}, bf16[24,6144]{1,0:T(8,128)(2,1)S(1)}, u32[]{:S(2)}, u32[]{:S(2)}) collective-permute-start(bf16[24,6144]{1,0:T(8,128)(2,1)S(1)} %collective-permute-done.11.refs_14_), channel_id=1, source_target_pairs={{0,1},{1,0},{2,3},{3,2},{4,5},{5,4},{6,7},{7,6},{8,9},{9,8},{10,11... | collective-permute-start | bytes 884744 | tf_op jit(solution)/shard_map/ppermute | solution.py:38
  73.9 3.2 %collective-permute-start.6 = (bf16[24,6144]{1,0:T(8,128)(2,1)S(1)}, bf16[24,6144]{1,0:T(8,128)(2,1)S(1)}, u32[]{:S(2)}, u32[]{:S(2)}) collective-permute-start(bf16[24,6144]{1,0:T(8,128)(2,1)S(1)} %collective-permute-done.5.refs_9_), channel_id=1, source_target_pairs={{0,1},{1,0},{2,3},{3,2},{4,5},{5,4},{6,7},{7,6},{8,9},{9,8},{10,11... | collective-permute-start | bytes 884744 | tf_op jit(solution)/shard_map/ppermute | solution.py:38
  77.0 1.6 %collective-permute-start.13 = (bf16[24,6144]{1,0:T(8,128)(2,1)S(1)}, bf16[24,6144]{1,0:T(8,128)(2,1)S(1)}, u32[]{:S(2)}, u32[]{:S(2)}) collective-permute-start(bf16[24,6144]{1,0:T(8,128)(2,1)S(1)} %collective-permute-done.12.refs_13_), channel_id=1, source_target_pairs={{0,1},{1,0},{2,3},{3,2},{4,5},{5,4},{6,7},{7,6},{8,9},{9,8},{10,11... | collective-permute-start | bytes 884744 | tf_op jit(solution)/shard_map/ppermute | solution.py:38
  78.6 1.9 %copy-start = (bf16[6144,256]{1,0:T(8,128)(2,1)S(1)}, bf16[6144,256]{1,0:T(8,128)(2,1)}, u32[]{:S(2)}) copy-start(bf16[6144,256]{1,0:T(8,128)(2,1)} %refs_16_.1) | copy-start | bytes 9437188
  87.0 3.0 %collective-permute-start.20 = (bf16[96,6144]{1,0:T(8,128)(2,1)S(1)}, bf16[96,6144]{1,0:T(8,128)(2,1)S(1)}, u32[]{:S(2)}, u32[]{:S(2)}) collective-permute-start(bf16[96,6144]{1,0:T(8,128)(2,1)S(1)} %get-tuple-element.19), channel_id=1, source_target_pairs={{0,1},{1,0},{2,3},{3,2},{4,5},{5,4},{6,7},{7,6},{8,9},{9,8},{10,11... | collective-permute-start | bytes 3538952 | tf_op jit(solution)/shard_map/ppermute | solution.py:38
  90.0 8.0 %collective-permute-start.21 = (bf16[24,6144]{1,0:T(8,128)(2,1)S(1)}, bf16[24,6144]{1,0:T(8,128)(2,1)S(1)}, u32[]{:S(2)}, u32[]{:S(2)}) collective-permute-start(bf16[24,6144]{1,0:T(8,128)(2,1)S(1)} %add_convert_fusion.4), channel_id=1, source_target_pairs={{0,2},{1,15},{2,4},{3,1},{4,6},{5,3},{6,8},{7,5},{8,10},{9,7},{10,... | collective-permute-start | bytes 884744 | tf_op jit(solution)/shard_map/ppermute | solution.py:51
  90.2 8.2 %collective-permute-start.16 = (bf16[72,6144]{1,0:T(8,128)(2,1)S(1)}, bf16[72,6144]{1,0:T(8,128)(2,1)S(1)}, u32[]{:S(2)}, u32[]{:S(2)}) collective-permute-start(bf16[72,6144]{1,0:T(8,128)(2,1)S(1)} %get-tuple-element.16), channel_id=1, source_target_pairs={{0,1},{1,0},{2,3},{3,2},{4,5},{5,4},{6,7},{7,6},{8,9},{9,8},{10,11... | collective-permute-start | bytes 2654216 | tf_op jit(solution)/shard_map/ppermute | solution.py:38
  98.2 8.0 %collective-permute-start.22 = (bf16[24,6144]{1,0:T(8,128)(2,1)S(1)}, bf16[24,6144]{1,0:T(8,128)(2,1)S(1)}, u32[]{:S(2)}, u32[]{:S(2)}) collective-permute-start(bf16[24,6144]{1,0:T(8,128)(2,1)S(1)} %add_convert_fusion.3), channel_id=1, source_target_pairs={{0,2},{1,15},{2,4},{3,1},{4,6},{5,3},{6,8},{7,5},{8,10},{9,7},{10,... | collective-permute-start | bytes 884744 | tf_op jit(solution)/shard_map/ppermute | solution.py:51
  98.4 11.0 %collective-permute-start.17 = (bf16[24,6144]{1,0:T(8,128)(2,1)S(1)}, bf16[24,6144]{1,0:T(8,128)(2,1)S(1)}, u32[]{:S(2)}, u32[]{:S(2)}) collective-permute-start(bf16[24,6144]{1,0:T(8,128)(2,1)S(1)} %add_convert_fusion.7), channel_id=1, source_target_pairs={{0,2},{1,15},{2,4},{3,1},{4,6},{5,3},{6,8},{7,5},{8,10},{9,7},{10,... | collective-permute-start | bytes 884744 | tf_op jit(solution)/shard_map/ppermute | solution.py:51
  106.3 8.0 %collective-permute-start.23 = (bf16[24,6144]{1,0:T(8,128)(2,1)S(1)}, bf16[24,6144]{1,0:T(8,128)(2,1)S(1)}, u32[]{:S(2)}, u32[]{:S(2)}) collective-permute-start(bf16[24,6144]{1,0:T(8,128)(2,1)S(1)} %add_convert_fusion.2), channel_id=1, source_target_pairs={{0,2},{1,15},{2,4},{3,1},{4,6},{5,3},{6,8},{7,5},{8,10},{9,7},{10,... | collective-permute-start | bytes 884744 | tf_op jit(solution)/shard_map/ppermute | solution.py:51
  109.5 8.0 %collective-permute-start.18 = (bf16[24,6144]{1,0:T(8,128)(2,1)S(1)}, bf16[24,6144]{1,0:T(8,128)(2,1)S(1)}, u32[]{:S(2)}, u32[]{:S(2)}) collective-permute-start(bf16[24,6144]{1,0:T(8,128)(2,1)S(1)} %add_convert_fusion.6), channel_id=1, source_target_pairs={{0,2},{1,15},{2,4},{3,1},{4,6},{5,3},{6,8},{7,5},{8,10},{9,7},{10,... | collective-permute-start | bytes 884744 | tf_op jit(solution)/shard_map/ppermute | solution.py:51
  114.5 8.0 %collective-permute-start.24 = (bf16[24,6144]{1,0:T(8,128)(2,1)S(1)}, bf16[24,6144]{1,0:T(8,128)(2,1)S(1)}, u32[]{:S(2)}, u32[]{:S(2)}) collective-permute-start(bf16[24,6144]{1,0:T(8,128)(2,1)S(1)} %add_convert_fusion.1), channel_id=1, source_target_pairs={{0,2},{1,15},{2,4},{3,1},{4,6},{5,3},{6,8},{7,5},{8,10},{9,7},{10,... | collective-permute-start | bytes 884744 | tf_op jit(solution)/shard_map/ppermute | solution.py:51
  117.7 8.0 %collective-permute-start.19 = (bf16[24,6144]{1,0:T(8,128)(2,1)S(1)}, bf16[24,6144]{1,0:T(8,128)(2,1)S(1)}, u32[]{:S(2)}, u32[]{:S(2)}) collective-permute-start(bf16[24,6144]{1,0:T(8,128)(2,1)S(1)} %add_convert_fusion.5), channel_id=1, source_target_pairs={{0,2},{1,15},{2,4},{3,1},{4,6},{5,3},{6,8},{7,5},{8,10},{9,7},{10,... | collective-permute-start | bytes 884744 | tf_op jit(solution)/shard_map/ppermute | solution.py:51
  122.5 17.6 %copy-start.1 = (s32[4,2]{0,1:T(2,128)S(1)}, s32[4,2]{0,1:T(2,128)}, u32[]{:S(2)}) copy-start(s32[4,2]{0,1:T(2,128)} %param.20) | copy-start | bytes 100
  122.5 17.6 %copy-start.2 = (f32[4,2]{0,1:T(2,128)S(1)}, f32[4,2]{0,1:T(2,128)}, u32[]{:S(2)}) copy-start(f32[4,2]{0,1:T(2,128)} %param.21) | copy-start | bytes 100
  122.6 3.1 %collective-permute-start.25 = (bf16[24,6144]{1,0:T(8,128)(2,1)S(1)}, bf16[24,6144]{1,0:T(8,128)(2,1)S(1)}, u32[]{:S(2)}, u32[]{:S(2)}) collective-permute-start(bf16[24,6144]{1,0:T(8,128)(2,1)S(1)} %add_convert_fusion), channel_id=1, source_target_pairs={{0,1},{1,0},{2,3},{3,2},{4,5},{5,4},{6,7},{7,6},{8,9},{9,8},{10,11... | collective-permute-start | bytes 884744 | tf_op jit(solution)/shard_map/ppermute | solution.py:38

commit v2 on v1

--- a/solution.py
+++ b/solution.py
@@ -1,3 +1,4 @@
+import functools
 import math
 
 import jax
@@ -22,7 +23,6 @@
 EPS = 1e-05
 NEG = -1e30
 
-PIECES = 16
 CUT_K = 8
 CUT_N = 4
 
@@ -69,59 +69,34 @@
             came[step, part] = block[part]
         for part in (0, 1) if step < far else (0,):
             theirs[step, part] = swapped(came[step, part])
-    return own, other, came, theirs
-
-
-def chain_order(far):
-    return [(far - i, 0) for i in range(far)], [(far - i, 1) for i in range(1, far)]
-
-
-def scattered(far, each, own, other, kept, sent):
-    got = [swapped(sent[part]) for part in (0, 1)]
+    return other, came, theirs
+
+
+def scattered(far, own, other, kept, got):
     moving = {}
     for step in range(far, 0, -1):
-        for part in (0, 1) if step < far else (0,):
-            at = (far - part - step) * each
-            terms = [x[at : at + each] for x in (kept[part], got[part])]
+        for part in (0, 1) if step < far else (1,):
+            terms = [kept[step, part], got[step, part]]
             parcel = added(*terms, *moving.get(part, ())).astype(jnp.bfloat16)
             moving[part] = (passed_on(parcel),)
     leaving = added(other, *moving[0]).astype(jnp.bfloat16)
     return own, *moving[1], swapped(leaving)
 
 
-def experts_kernel(*refs):
-    pieces = refs[:PIECES]
-    gate_hbm, up_hbm, down_hbm = refs[PIECES : PIECES + 3]
-    outs = refs[PIECES + 3 : PIECES + 9]
-    gate, up, down, sems = refs[PIECES + 9 :]
+def multiplied(pieces, gate, up, down, outs, ready):
     depth = gate.shape[0] // CUT_K
     span = down.shape[1] // CUT_N
-    copies = []
-    for k in range(CUT_K):
-        rows = pl.ds(k * depth, depth)
-        copies.append(
-            (
-                pltpu.make_async_copy(gate_hbm.at[rows], gate.at[rows], sems.at[2 * k]),
-                pltpu.make_async_copy(up_hbm.at[rows], up.at[rows], sems.at[2 * k + 1]),
-            )
-        )
-    last = pltpu.make_async_copy(down_hbm, down, sems.at[2 * CUT_K])
-    for pair in copies:
-        pair[0].start()
-        pair[1].start()
-    last.start()
     gate_v = up_v = None
     for k in range(CUT_K):
         cols = pl.ds(k * depth, depth)
         x = jnp.concatenate([p[:, cols] for p in pieces], 0)
-        copies[k][0].wait()
-        copies[k][1].wait()
+        ready(k)
         g = jnp.dot(x, gate[cols, :], preferred_element_type=jnp.float32)
         u = jnp.dot(x, up[cols, :], preferred_element_type=jnp.float32)
         gate_v = g if gate_v is None else gate_v + g
         up_v = u if up_v is None else up_v + u
     act = (gate_v / (1.0 + jnp.exp(-gate_v)) * up_v).astype(jnp.bfloat16)
-    last.wait()
+    ready(CUT_K)
     for n in range(CUT_N):
         cols = pl.ds(n * span, span)
         part = jnp.dot(act, down[:, cols], preferred_element_type=jnp.float32).astype(jnp.bfloat16)
@@ -132,27 +107,69 @@
             at += rows
 
 
-def experts(pieces, w_gate, w_up, w_down, sizes):
-    width = w_gate.shape[0]
-    hidden = w_gate.shape[1]
-    vm = pl.BlockSpec(memory_space=pltpu.VMEM)
-    anyspec = pl.BlockSpec(memory_space=pl.ANY)
-    total = sum(sizes)
-    return pl.pallas_call(
-        experts_kernel,
+def early_kernel(count, *refs):
+    pieces, (gate_far, up_far, down_far) = refs[:count], refs[count : count + 3]
+    outs, (gate, up, down, sems) = refs[count + 3 : -4], refs[-4:]
+    depth = gate.shape[0] // CUT_K
+    copies = []
+    for k in range(CUT_K):
+        rows = pl.ds(k * depth, depth)
+        copies.append(
+            (
+                pltpu.make_async_copy(gate_far.at[rows], gate.at[rows], sems.at[2 * k]),
+                pltpu.make_async_copy(up_far.at[rows], up.at[rows], sems.at[2 * k + 1]),
+            )
+        )
+    copies.append((pltpu.make_async_copy(down_far, down, sems.at[2 * CUT_K]),))
+    for group in copies:
+        for copy in group:
+            copy.start()
+
+    def ready(k):
+        for copy in copies[k]:
+            copy.wait()
+
+    multiplied(pieces, gate, up, down, outs, ready)
+
+
+def late_kernel(count, *refs):
+    multiplied(refs[:count], *refs[count : count + 3], refs[count + 3 :], lambda k: None)
+
+
+def product_cost(rows, width, hidden):
+    return pl.CostEstimate(flops=6 * rows * width * hidden, bytes_accessed=6 * width * hidden, transcendentals=rows * hidden)
+
+
+def early_products(pieces, weights, sizes):
+    width, hidden = weights[0].shape
+    vm = pl.BlockSpec(memory_space=pltpu.VMEM)
+    far = pl.BlockSpec(memory_space=pltpu.HBM)
+    outs = [jax.ShapeDtypeStruct((s, width), jnp.bfloat16) for s in sizes]
+    held = [pltpu.VMEM(w.shape, w.dtype) for w in weights]
+    return pl.pallas_call(
+        functools.partial(early_kernel, len(pieces)),
+        out_shape=outs + held,
+        in_specs=[vm] * len(pieces) + [far] * 3,
+        out_specs=[vm] * (len(sizes) + 3),
+        scratch_shapes=[pltpu.SemaphoreType.DMA((2 * CUT_K + 1,))],
+        compiler_params=pltpu.CompilerParams(vmem_limit_bytes=24 * 1024 * 1024),
+        cost_estimate=product_cost(sum(sizes), width, hidden),
+        name="early",
+    )(*pieces, *[pltpu.with_memory_space_constraint(w, pltpu.HBM) for w in weights])
+
+
+def late_products(pieces, weights, sizes):
+    width, hidden = weights[0].shape
+    vm = pl.BlockSpec(memory_space=pltpu.VMEM)
+    return pl.pallas_call(
+        functools.partial(late_kernel, len(pieces)),
         out_shape=[jax.ShapeDtypeStruct((s, width), jnp.bfloat16) for s in sizes],
-        in_specs=[vm] * PIECES + [anyspec] * 3,
+        in_specs=[vm] * (len(pieces) + 3),
         out_specs=[vm] * len(sizes),
-        scratch_shapes=[
-            pltpu.VMEM((width, hidden), jnp.bfloat16),
-            pltpu.VMEM((width, hidden), jnp.bfloat16),
-            pltpu.VMEM((hidden, width), jnp.bfloat16),
-            pltpu.SemaphoreType.DMA((2 * CUT_K + 1,)),
-        ],
-        compiler_params=pltpu.CompilerParams(vmem_limit_bytes=40 * 1024 * 1024),
-        cost_estimate=pl.CostEstimate(flops=6 * total * width * hidden, bytes_accessed=6 * width * hidden, transcendentals=total * hidden),
-        name="experts",
-    )(*pieces, w_gate, w_up, w_down)
+        compiler_params=pltpu.CompilerParams(vmem_limit_bytes=24 * 1024 * 1024),
+        cost_estimate=product_cost(sum(sizes), width, hidden),
+        name="late",
+    )(*pieces, *weights)
 
 
 def slots_of(ids_ref, reqs, top):
@@ -402,17 +419,38 @@
         rows_x,
     )
     own_block = unpacked(lax.all_to_all(leaving, "dev_0", 0, 0, tiled=True))
-    own, other, came, theirs = gathered(own_block)
+    other, came, theirs = gathered(own_block)
     far = lax.axis_size("dev_1") // 2
-    chains = chain_order(far)
     each = rows_x * MOST
-    pieces = [own, other]
+    near = range(far - 2, 0, -1)
+    pieces = [own_block, other]
     for group in (theirs, came):
-        for chain in chains:
-            pieces += [group[key] for key in chain]
-    sizes = [each, each] + 2 * [len(chain) * each for chain in chains]
-    home_own, home_other, kept_0, kept_1, sent_0, sent_1 = experts(pieces, w_gate, w_up, w_down, sizes)
-    last_terms = scattered(far, each, home_own, home_other, (kept_0, kept_1), (sent_0, sent_1))
+        for part in (0, 1):
+            pieces += [group[step, part] for step in near]
+    home_own, home_other, *groups, gate, up, down = early_products(
+        pieces, (w_gate, w_up, w_down), [each, each] + [len(near) * each] * 4
+    )
+    last = far - 1
+    pieces = [
+        came[far, 0],
+        theirs[last, 1],
+        theirs[last, 0],
+        theirs[far, 0],
+        came[last, 1],
+        came[last, 0],
+    ]
+    kept, got = {}, {}
+    sent = [swapped(groups[2 + part]) for part in (0, 1)]
+    for part in (0, 1):
+        for i, step in enumerate(near):
+            kept[step, part] = groups[part][i * each : (i + 1) * each]
+            got[step, part] = sent[part][i * each : (i + 1) * each]
+    kept[far, 1], kept[last, 1], kept[last, 0], *sent = late_products(
+        pieces, (gate, up, down), [each, each, each, 2 * each, each]
+    )
+    sent = [swapped(x) for x in sent]
+    got[far, 1], got[last, 1], got[last, 0] = sent[0][:each], sent[0][each:], sent[1]
+    last_terms = scattered(far, home_own, home_other, kept, got)
     home = lax.all_to_all(packed_sum(*last_terms, rows_x), "dev_0", 0, 0, tiled=True)
     return mixed_in(expert_ids.T, route_weights.T, home, hidden_state)
 

time: 142 us -> 136 us (0.958)
  waiting for transfers between devices: 75.3 us -> 71.9 us
  local copies, waits for them, and re-layouts: 1.9 us -> 0.01 us
    ppermute x14, waiting for transfers between devices: 66.9 us -> 64.8 us  [passed_on(): return lax.ppermute(value, ('dev_1', 'dev_2'), pairs)]
    unnamed x6 -> x4, local copies, waits for them, and re-layouts: 1.9 us -> 0.01 us
    ppermute x11 -> x13, waiting for transfers between devices: 4.28 us -> 2.89 us  [shifted(): lax.ppermute(value, axis, [(place, (place + steps) % count) for place in...]
    ppermute x11 -> x13, starting transfers between devices: 2.18 us -> 2.93 us  [shifted(): lax.ppermute(value, axis, [(place, (place + steps) % count) for place in...]
    pallas_call x1 -> x2, Pallas kernels: 6.44 us -> 6.58 us  [the longest x1 4.9 us: early_products(): pl.pallas_call(functools.partial(early_kernel, len(pieces)), out_shape=ou...]
  transfers between devices with their start and end apart: 26 -> 28, of which waited for: 17 -> 17; matrix products, arithmetic and copies ran while one was open for 0% -> 1% of each run, Pallas kernels for 0% -> 4%
where the time goes in v2:
time: 136 us
  waiting for transfers between devices  71.9 us (53%)
  blocking collectives  33.1 us (24%)
  starting transfers between devices  17.2 us (13%)
  Pallas kernels  13 us (10%)
    ppermute x14, waiting for transfers between devices, passed_on(): return lax.ppermute(value, ('dev_1', 'dev_2'), pairs)  64.8 us
    all_to_all x1, blocking collectives, layer(): own_block = unpacked(lax.all_to_all(leaving, 'dev_0', 0, 0, tiled=True))  19.9 us
    all_to_all x1, blocking collectives, layer(): lax.all_to_all(packed_sum(*last_terms, rows_x), 'dev_0', 0, 0, tiled=True)  13.3 us
    ppermute x1, starting transfers between devices, passed_along(): lax.ppermute(value, axis, [(source, source + steps) for source in range(l...  13.1 us
    pallas_call x1, Pallas kernels, early_products(): pl.pallas_call(functools.partial(early_kernel, len(pieces)), out_shape=ou...  4.9 us
    pallas_call x1, Pallas kernels, attended(): pl.pallas_call(attend_kernel, out_shape=[jax.ShapeDtypeStruct((reqs, widt...  4.61 us
    ppermute x1, waiting for transfers between devices, passed_along(): lax.ppermute(value, axis, [(source, source + steps) for source in range(l...  4.18 us
    ppermute x13, starting transfers between devices, shifted(): lax.ppermute(value, axis, [(place, (place + steps) % count) for place in...  2.93 us
  transfers between devices with their start and end apart: 28, of which 17 were waited for; matrix products, arithmetic and copies ran while one was open for 1% of the time, Pallas kernels for 4%

profile of v2, /device:TPU:514, one launch (start us, length us, event | category | flops | bytes accessed | tf_op | source)
XLA Modules:
  0.0 136.2 jit_solution(15221634087540123819)
XLA Ops:
  0.0 13.1 %collective-permute-start = (bf16[64,2048]{1,0:T(8,128)(2,1)}, bf16[64,2048]{1,0:T(8,128)(2,1)S(1)}, u32[]{:S(2)}, u32[]{:S(2)}) collective-permute-start(bf16[64,2048]{1,0:T(8,128)(2,1)} %refs_7_.1), channel_id=1, source_target_pairs={{1,0},{2,1},{3,2},{4,3},{5,4},{6,5},{7,6},{8,7},{9,8},{10,9},{11,1... | collective-permute-start | bytes 786440 | tf_op jit(solution)/shard_map/ppermute | solution.py:33
  13.2 4.2 %collective-permute-done.refs_0_ = bf16[64,2048]{1,0:T(8,128)(2,1)S(1)} collective-permute-done((bf16[64,2048]{1,0:T(8,128)(2,1)}, bf16[64,2048]{1,0:T(8,128)(2,1)S(1)}, u32[]{:S(2)}, u32[]{:S(2)}) %collective-permute-start) | collective-permute-done | bytes 262176 | tf_op jit(solution)/shard_map/ppermute | solution.py:33
  17.3 4.6 %attended.1 = (f32[4,6144]{1,0:T(4,128)S(1)}, bf16[8,144,128]{2,1,0:T(8,128)(2,1)S(1)}) custom-call(s32[1]{0:T(128)} %bitcast.2.me_ref, bf16[64,2048]{1,0:T(8,128)(2,1)S(1)} %collective-permute-done.refs_0_, s32[4]{0:T(128)} %refs_1_.1, s32[2,4]{1,0:T(2,128)} %bitcast.5, s32[1,128]{1,0:T(1,128)} %bitcast.9, bf16[4,6144]{1,0:T(4,128)(2,1)} %refs_4_.1, ...), custom_call_target="tpu_custom_call" | custom-call | flops 77070336 | bytes 2097152 | tf_op jit(solution)/shard_map/attended/pallas_call | solution.py:281
  21.9 19.9 %all_to_all.10.came_ref = bf16[8,144,128]{2,1,0:T(8,128)(2,1)S(1)} all-to-all(bf16[8,144,128]{2,1,0:T(8,128)(2,1)S(1)} %get-tuple-element.21), channel_id=1, replica_groups=mesh['groups'=2,'dev_0'=8,'dev_1'=8,'dev_2'=2] {'dev_0'}, dimensions={0} | all-to-all | bytes 589824 | tf_op jit(solution)/shard_map/all_to_all | solution.py:421
  41.8 0.2 unpacked.1.refs_0_
  42.0 0.1 collective-permute-start.2
  42.2 0.4 collective-permute-start.1
  42.5 7.5 %collective-permute-done.2.refs_7_ = bf16[24,6144]{1,0:T(8,128)(2,1)S(1)} collective-permute-done((bf16[24,6144]{1,0:T(8,128)(2,1)S(1)}, bf16[24,6144]{1,0:T(8,128)(2,1)S(1)}, u32[]{:S(2)}, u32[]{:S(2)}) %collective-permute-start.2) | collective-permute-done | bytes 294944 | tf_op jit(solution)/shard_map/ppermute | solution.py:51
  50.1 0.0 collective-permute-start.3
  50.1 0.0 collective-permute-done.1.refs_1_
  50.1 0.0 collective-permute-start.6
  50.1 7.9 %collective-permute-done.3.refs_6_ = bf16[24,6144]{1,0:T(8,128)(2,1)S(1)} collective-permute-done((bf16[24,6144]{1,0:T(8,128)(2,1)S(1)}, bf16[24,6144]{1,0:T(8,128)(2,1)S(1)}, u32[]{:S(2)}, u32[]{:S(2)}) %collective-permute-start.3) | collective-permute-done | bytes 294944 | tf_op jit(solution)/shard_map/ppermute | solution.py:51
  58.0 3.2 %collective-permute-done.6.refs_9_ = bf16[24,6144]{1,0:T(8,128)(2,1)S(1)} collective-permute-done((bf16[24,6144]{1,0:T(8,128)(2,1)S(1)}, bf16[24,6144]{1,0:T(8,128)(2,1)S(1)}, u32[]{:S(2)}, u32[]{:S(2)}) %collective-permute-start.6) | collective-permute-done | bytes 294944 | tf_op jit(solution)/shard_map/ppermute | solution.py:51
  61.2 0.0 collective-permute-start.5
  61.2 0.5 collective-permute-start.4
  61.7 4.3 %collective-permute-done.11.refs_5_ = bf16[24,6144]{1,0:T(8,128)(2,1)S(1)} collective-permute-done((bf16[24,6144]{1,0:T(8,128)(2,1)S(1)}, bf16[24,6144]{1,0:T(8,128)(2,1)S(1)}, u32[]{:S(2)}, u32[]{:S(2)}) %collective-permute-start.11) | collective-permute-done | bytes 294944 | tf_op jit(solution)/shard_map/ppermute | solution.py:51
  66.0 0.0 collective-permute-start.12
  66.0 3.2 %collective-permute-done.7.refs_8_ = bf16[24,6144]{1,0:T(8,128)(2,1)S(1)} collective-permute-done((bf16[24,6144]{1,0:T(8,128)(2,1)S(1)}, bf16[24,6144]{1,0:T(8,128)(2,1)S(1)}, u32[]{:S(2)}, u32[]{:S(2)}) %collective-permute-start.7) | collective-permute-done | bytes 294944 | tf_op jit(solution)/shard_map/ppermute | solution.py:51
  69.1 0.0 collective-permute-start.13
  69.1 0.0 collective-permute-start.9
  69.1 0.5 collective-permute-start.8
  69.6 0.0 collective-permute-done.4.refs_2_
  69.6 0.1 collective-permute-start.15
  69.8 4.1 %collective-permute-done.12.refs_0_ = bf16[24,6144]{1,0:T(8,128)(2,1)S(1)} collective-permute-done((bf16[24,6144]{1,0:T(8,128)(2,1)S(1)}, bf16[24,6144]{1,0:T(8,128)(2,1)S(1)}, u32[]{:S(2)}, u32[]{:S(2)}) %collective-permute-start.12) | collective-permute-done | bytes 294944 | tf_op jit(solution)/shard_map/ppermute | solution.py:51
  73.9 3.2 %collective-permute-done.13.refs_4_ = bf16[24,6144]{1,0:T(8,128)(2,1)S(1)} collective-permute-done((bf16[24,6144]{1,0:T(8,128)(2,1)S(1)}, bf16[24,6144]{1,0:T(8,128)(2,1)S(1)}, u32[]{:S(2)}, u32[]{:S(2)}) %collective-permute-start.13) | collective-permute-done | bytes 294944 | tf_op jit(solution)/shard_map/ppermute | solution.py:51
  77.0 0.0 collective-permute-start.14
  77.1 4.9 %early.1 = (bf16[24,6144]{1,0:T(8,128)(2,1)S(1)}, bf16[24,6144]{1,0:T(8,128)(2,1)S(1)}, bf16[48,6144]{1,0:T(8,128)(2,1)S(1)}, bf16[48,6144]{1,0:T(8,128)(2,1)S(1...) custom-call(bf16[24,6144]{1,0:T(8,128)(2,1)S(1)} %unpacked.1.refs_0_, ...), custom_call_target="tpu_custom_call" | custom-call | flops 2264924160 | bytes 9437184 | tf_op jit(solution)/shard_map/early/pallas_call | solution.py:149
  82.0 0.0 collective-permute-done.15.refs_2_
  82.0 1.7 %late.1 = (bf16[24,6144]{1,0:T(8,128)(2,1)S(1)}, bf16[24,6144]{1,0:T(8,128)(2,1)S(1)}, bf16[24,6144]{1,0:T(8,128)(2,1)S(1)}, bf16[48,6144]{1,0:T(8,128)(2,1)S(1)}, bf16[24,6144]{1,0:T(8,128)(2,1)S(1)}) custom-call(bf16[24,6144]{1,0:T(8,128)(2,1)S(1)} %collective-permute-done.12.refs_0_, bf16[24,6144]{1,0:T(8,128)(2,1)S(1)} %collective-permute-done.14.refs_1_, ...), custom_call_target="tpu_custom_call" | custom-call | flops 1358954496 | bytes 9437184 | tf_op jit(solution)/shard_map/late/pallas_call | solution.py:164
  83.7 0.6 collective-permute-start.23
  84.3 0.1 collective-permute-start.22
  84.4 0.4 collective-permute-start.10
  84.8 0.1 collective-permute-start.17
  85.0 0.5 collective-permute-done.23
  85.5 0.1 add_convert_fusion.3
  85.6 0.1 collective-permute-start.24
  85.7 2.3 %collective-permute-done.17 = bf16[48,6144]{1,0:T(8,128)(2,1)S(1)} collective-permute-done((bf16[48,6144]{1,0:T(8,128)(2,1)S(1)}, bf16[48,6144]{1,0:T(8,128)(2,1)S(1)}, u32[]{:S(2)}, u32[]{:S(2)}) %collective-permute-start.17) | collective-permute-done | bytes 589856 | tf_op jit(solution)/shard_map/ppermute | solution.py:38
  88.0 0.1 add_convert_fusion.7
  88.1 0.1 collective-permute-start.18
  88.3 5.4 %collective-permute-done.24 = bf16[24,6144]{1,0:T(8,128)(2,1)S(1)} collective-permute-done((bf16[24,6144]{1,0:T(8,128)(2,1)S(1)}, bf16[24,6144]{1,0:T(8,128)(2,1)S(1)}, u32[]{:S(2)}, u32[]{:S(2)}) %collective-permute-start.24) | collective-permute-done | bytes 294944 | tf_op jit(solution)/shard_map/ppermute | solution.py:51
  93.6 0.1 add_convert_fusion.2
  93.7 0.1 collective-permute-start.25
  93.9 2.9 %collective-permute-done.18 = bf16[24,6144]{1,0:T(8,128)(2,1)S(1)} collective-permute-done((bf16[24,6144]{1,0:T(8,128)(2,1)S(1)}, bf16[24,6144]{1,0:T(8,128)(2,1)S(1)}, u32[]{:S(2)}, u32[]{:S(2)}) %collective-permute-start.18) | collective-permute-done | bytes 294944 | tf_op jit(solution)/shard_map/ppermute | solution.py:51
  96.8 0.1 add_convert_fusion.6
  96.9 0.0 copy-start
  96.9 0.0 copy-start.1
  96.9 0.1 collective-permute-start.19
  97.1 4.7 %collective-permute-done.25 = bf16[24,6144]{1,0:T(8,128)(2,1)S(1)} collective-permute-done((bf16[24,6144]{1,0:T(8,128)(2,1)S(1)}, bf16[24,6144]{1,0:T(8,128)(2,1)S(1)}, u32[]{:S(2)}, u32[]{:S(2)}) %collective-permute-start.25) | collective-permute-done | bytes 294944 | tf_op jit(solution)/shard_map/ppermute | solution.py:51
  101.8 0.1 add_convert_fusion.1
  101.9 0.1 collective-permute-start.26
  102.1 2.9 %collective-permute-done.19 = bf16[24,6144]{1,0:T(8,128)(2,1)S(1)} collective-permute-done((bf16[24,6144]{1,0:T(8,128)(2,1)S(1)}, bf16[24,6144]{1,0:T(8,128)(2,1)S(1)}, u32[]{:S(2)}, u32[]{:S(2)}) %collective-permute-start.19) | collective-permute-done | bytes 294944 | tf_op jit(solution)/shard_map/ppermute | solution.py:51
  105.0 0.1 add_convert_fusion.5
  105.1 0.1 collective-permute-start.20
  105.2 4.7 %collective-permute-done.26 = bf16[24,6144]{1,0:T(8,128)(2,1)S(1)} collective-permute-done((bf16[24,6144]{1,0:T(8,128)(2,1)S(1)}, bf16[24,6144]{1,0:T(8,128)(2,1)S(1)}, u32[]{:S(2)}, u32[]{:S(2)}) %collective-permute-start.26) | collective-permute-done | bytes 294944 | tf_op jit(solution)/shard_map/ppermute | solution.py:51
  109.9 0.1 add_convert_fusion
  110.0 0.1 collective-permute-start.27
  110.2 3.0 %collective-permute-done.20 = bf16[24,6144]{1,0:T(8,128)(2,1)S(1)} collective-permute-done((bf16[24,6144]{1,0:T(8,128)(2,1)S(1)}, bf16[24,6144]{1,0:T(8,128)(2,1)S(1)}, u32[]{:S(2)}, u32[]{:S(2)}) %collective-permute-start.20) | collective-permute-done | bytes 294944 | tf_op jit(solution)/shard_map/ppermute | solution.py:51
  113.1 0.1 add_convert_fusion.4
  113.2 0.1 collective-permute-start.21
  113.4 0.0 collective-permute-done.27.third_ref
  113.4 7.9 %collective-permute-done.21.second_ref = bf16[24,6144]{1,0:T(8,128)(2,1)S(1)} collective-permute-done((bf16[24,6144]{1,0:T(8,128)(2,1)S(1)}, bf16[24,6144]{1,0:T(8,128)(2,1)S(1)}, u32[]{:S(2)}, u32[]{:S(2)}) %collective-permute-start.21) | collective-permute-done | bytes 294944 | tf_op jit(solution)/shard_map/ppermute | solution.py:51
  121.3 0.3 packed_sum.1
  121.6 13.3 %all_to_all.11.home_ref = bf16[8,144,128]{2,1,0:T(8,128)(2,1)S(1)} all-to-all(bf16[8,144,128]{2,1,0:T(8,128)(2,1)S(1)} %packed_sum.1), channel_id=1, replica_groups=mesh['groups'=2,'dev_0'=8,'dev_1'=8,'dev_2'=2] {'dev_0'}, dimensions={0} | all-to-all | bytes 589824 | tf_op jit(solution)/shard_map/all_to_all | solution.py:454
  134.8 1.4 %mixed_in.1 = bf16[4,6144]{1,0:T(4,128)(2,1)} custom-call(s32[2,4]{1,0:T(2,128)S(1)} %bitcast.6, f32[2,4]{1,0:T(2,128)S(1)} %bitcast.7, bf16[8,144,128]{2,1,0:T(8,128)(2,1)S(1)} %all_to_all.11.home_ref, f32[4,6144]{1,0:T(4,128)S(1)} %get-tuple-element.36.hidden_ref), custom_call_target="tpu_custom_call" | custom-call | tf_op jit(solution)/shard_map/mixed_in/pallas_call | solution.py:377
  (12 shorter events, 0.0 us)
Async XLA Ops:
  0.0 17.3 %collective-permute-start = (bf16[64,2048]{1,0:T(8,128)(2,1)}, bf16[64,2048]{1,0:T(8,128)(2,1)S(1)}, u32[]{:S(2)}, u32[]{:S(2)}) collective-permute-start(bf16[64,2048]{1,0:T(8,128)(2,1)} %refs_7_.1), channel_id=1, source_target_pairs={{1,0},{2,1},{3,2},{4,3},{5,4},{6,5},{7,6},{8,7},{9,8},{10,9},{11,1... | collective-permute-start | bytes 786440 | tf_op jit(solution)/shard_map/ppermute | solution.py:33
  42.0 8.0 %collective-permute-start.2 = (bf16[24,6144]{1,0:T(8,128)(2,1)S(1)}, bf16[24,6144]{1,0:T(8,128)(2,1)S(1)}, u32[]{:S(2)}, u32[]{:S(2)}) collective-permute-start(bf16[24,6144]{1,0:T(8,128)(2,1)S(1)} %unpacked.1.refs_0_), channel_id=1, source_target_pairs={{0,2},{1,15},{2,4},{3,1},{4,6},{5,3},{6,8},{7,5},{8,10},{9,7},{10,... | collective-permute-start | bytes 884744 | tf_op jit(solution)/shard_map/ppermute | solution.py:51
  42.2 7.9 %collective-permute-start.1 = (bf16[24,6144]{1,0:T(8,128)(2,1)S(1)}, bf16[24,6144]{1,0:T(8,128)(2,1)S(1)}, u32[]{:S(2)}, u32[]{:S(2)}) collective-permute-start(bf16[24,6144]{1,0:T(8,128)(2,1)S(1)} %unpacked.1.refs_0_), channel_id=1, source_target_pairs={{0,1},{1,0},{2,3},{3,2},{4,5},{5,4},{6,7},{7,6},{8,9},{9,8},{10,11... | collective-permute-start | bytes 884744 | tf_op jit(solution)/shard_map/ppermute | solution.py:38
  50.1 7.9 %collective-permute-start.3 = (bf16[24,6144]{1,0:T(8,128)(2,1)S(1)}, bf16[24,6144]{1,0:T(8,128)(2,1)S(1)}, u32[]{:S(2)}, u32[]{:S(2)}) collective-permute-start(bf16[24,6144]{1,0:T(8,128)(2,1)S(1)} %collective-permute-done.2.refs_7_), channel_id=1, source_target_pairs={{0,2},{1,15},{2,4},{3,1},{4,6},{5,3},{6,8},{7,5},{8,10},{9,7},{10,... | collective-permute-start | bytes 884744 | tf_op jit(solution)/shard_map/ppermute | solution.py:51
  50.1 11.1 %collective-permute-start.6 = (bf16[24,6144]{1,0:T(8,128)(2,1)S(1)}, bf16[24,6144]{1,0:T(8,128)(2,1)S(1)}, u32[]{:S(2)}, u32[]{:S(2)}) collective-permute-start(bf16[24,6144]{1,0:T(8,128)(2,1)S(1)} %collective-permute-done.1.refs_1_), channel_id=1, source_target_pairs={{0,2},{1,15},{2,4},{3,1},{4,6},{5,3},{6,8},{7,5},{8,10},{9,7},{10,... | collective-permute-start | bytes 884744 | tf_op jit(solution)/shard_map/ppermute | solution.py:51
  58.0 7.9 %collective-permute-start.11 = (bf16[24,6144]{1,0:T(8,128)(2,1)S(1)}, bf16[24,6144]{1,0:T(8,128)(2,1)S(1)}, u32[]{:S(2)}, u32[]{:S(2)}) collective-permute-start(bf16[24,6144]{1,0:T(8,128)(2,1)S(1)} %collective-permute-done.3.refs_6_), channel_id=1, source_target_pairs={{0,2},{1,15},{2,4},{3,1},{4,6},{5,3},{6,8},{7,5},{8,10},{9,7},{10,... | collective-permute-start | bytes 884744 | tf_op jit(solution)/shard_map/ppermute | solution.py:51
  61.2 7.9 %collective-permute-start.7 = (bf16[24,6144]{1,0:T(8,128)(2,1)S(1)}, bf16[24,6144]{1,0:T(8,128)(2,1)S(1)}, u32[]{:S(2)}, u32[]{:S(2)}) collective-permute-start(bf16[24,6144]{1,0:T(8,128)(2,1)S(1)} %collective-permute-done.6.refs_9_), channel_id=1, source_target_pairs={{0,2},{1,15},{2,4},{3,1},{4,6},{5,3},{6,8},{7,5},{8,10},{9,7},{10,... | collective-permute-start | bytes 884744 | tf_op jit(solution)/shard_map/ppermute | solution.py:51
  61.2 7.9 %collective-permute-start.5 = (bf16[24,6144]{1,0:T(8,128)(2,1)S(1)}, bf16[24,6144]{1,0:T(8,128)(2,1)S(1)}, u32[]{:S(2)}, u32[]{:S(2)}) collective-permute-start(bf16[24,6144]{1,0:T(8,128)(2,1)S(1)} %collective-permute-done.2.refs_7_), channel_id=1, source_target_pairs={{0,1},{1,0},{2,3},{3,2},{4,5},{5,4},{6,7},{7,6},{8,9},{9,8},{10,11... | collective-permute-start | bytes 884744 | tf_op jit(solution)/shard_map/ppermute | solution.py:38
  61.2 8.4 %collective-permute-start.4 = (bf16[24,6144]{1,0:T(8,128)(2,1)S(1)}, bf16[24,6144]{1,0:T(8,128)(2,1)S(1)}, u32[]{:S(2)}, u32[]{:S(2)}) collective-permute-start(bf16[24,6144]{1,0:T(8,128)(2,1)S(1)} %collective-permute-done.3.refs_6_), channel_id=1, source_target_pairs={{0,1},{1,0},{2,3},{3,2},{4,5},{5,4},{6,7},{7,6},{8,9},{9,8},{10,11... | collective-permute-start | bytes 884744 | tf_op jit(solution)/shard_map/ppermute | solution.py:38
  66.0 7.9 %collective-permute-start.12 = (bf16[24,6144]{1,0:T(8,128)(2,1)S(1)}, bf16[24,6144]{1,0:T(8,128)(2,1)S(1)}, u32[]{:S(2)}, u32[]{:S(2)}) collective-permute-start(bf16[24,6144]{1,0:T(8,128)(2,1)S(1)} %collective-permute-done.11.refs_5_), channel_id=1, source_target_pairs={{0,2},{1,15},{2,4},{3,1},{4,6},{5,3},{6,8},{7,5},{8,10},{9,7},{10,... | collective-permute-start | bytes 884744 | tf_op jit(solution)/shard_map/ppermute | solution.py:51
  69.1 7.9 %collective-permute-start.13 = (bf16[24,6144]{1,0:T(8,128)(2,1)S(1)}, bf16[24,6144]{1,0:T(8,128)(2,1)S(1)}, u32[]{:S(2)}, u32[]{:S(2)}) collective-permute-start(bf16[24,6144]{1,0:T(8,128)(2,1)S(1)} %collective-permute-done.7.refs_8_), channel_id=1, source_target_pairs={{0,2},{1,15},{2,4},{3,1},{4,6},{5,3},{6,8},{7,5},{8,10},{9,7},{10,... | collective-permute-start | bytes 884744 | tf_op jit(solution)/shard_map/ppermute | solution.py:51
  69.1 7.9 %collective-permute-start.9 = (bf16[24,6144]{1,0:T(8,128)(2,1)S(1)}, bf16[24,6144]{1,0:T(8,128)(2,1)S(1)}, u32[]{:S(2)}, u32[]{:S(2)}) collective-permute-start(bf16[24,6144]{1,0:T(8,128)(2,1)S(1)} %collective-permute-done.6.refs_9_), channel_id=1, source_target_pairs={{0,1},{1,0},{2,3},{3,2},{4,5},{5,4},{6,7},{7,6},{8,9},{9,8},{10,11... | collective-permute-start | bytes 884744 | tf_op jit(solution)/shard_map/ppermute | solution.py:38
  69.1 7.9 %collective-permute-start.8 = (bf16[24,6144]{1,0:T(8,128)(2,1)S(1)}, bf16[24,6144]{1,0:T(8,128)(2,1)S(1)}, u32[]{:S(2)}, u32[]{:S(2)}) collective-permute-start(bf16[24,6144]{1,0:T(8,128)(2,1)S(1)} %collective-permute-done.7.refs_8_), channel_id=1, source_target_pairs={{0,1},{1,0},{2,3},{3,2},{4,5},{5,4},{6,7},{7,6},{8,9},{9,8},{10,11... | collective-permute-start | bytes 884744 | tf_op jit(solution)/shard_map/ppermute | solution.py:38
  69.6 12.3 %collective-permute-start.15 = (bf16[24,6144]{1,0:T(8,128)(2,1)S(1)}, bf16[24,6144]{1,0:T(8,128)(2,1)S(1)}, u32[]{:S(2)}, u32[]{:S(2)}) collective-permute-start(bf16[24,6144]{1,0:T(8,128)(2,1)S(1)} %collective-permute-done.11.refs_5_), channel_id=1, source_target_pairs={{0,1},{1,0},{2,3},{3,2},{4,5},{5,4},{6,7},{7,6},{8,9},{9,8},{10,11... | collective-permute-start | bytes 884744 | tf_op jit(solution)/shard_map/ppermute | solution.py:38
  73.9 8.1 %collective-permute-start.16 = (bf16[24,6144]{1,0:T(8,128)(2,1)S(1)}, bf16[24,6144]{1,0:T(8,128)(2,1)S(1)}, u32[]{:S(2)}, u32[]{:S(2)}) collective-permute-start(bf16[24,6144]{1,0:T(8,128)(2,1)S(1)} %collective-permute-done.12.refs_0_), channel_id=1, source_target_pairs={{0,1},{1,0},{2,3},{3,2},{4,5},{5,4},{6,7},{7,6},{8,9},{9,8},{10,11... | collective-permute-start | bytes 884744 | tf_op jit(solution)/shard_map/ppermute | solution.py:38
  77.0 4.9 %collective-permute-start.14 = (bf16[24,6144]{1,0:T(8,128)(2,1)S(1)}, bf16[24,6144]{1,0:T(8,128)(2,1)S(1)}, u32[]{:S(2)}, u32[]{:S(2)}) collective-permute-start(bf16[24,6144]{1,0:T(8,128)(2,1)S(1)} %collective-permute-done.13.refs_4_), channel_id=1, source_target_pairs={{0,1},{1,0},{2,3},{3,2},{4,5},{5,4},{6,7},{7,6},{8,9},{9,8},{10,11... | collective-permute-start | bytes 884744 | tf_op jit(solution)/shard_map/ppermute | solution.py:38
  83.7 1.8 %collective-permute-start.23 = (bf16[24,6144]{1,0:T(8,128)(2,1)S(1)}, bf16[24,6144]{1,0:T(8,128)(2,1)S(1)}, u32[]{:S(2)}, u32[]{:S(2)}) collective-permute-start(bf16[24,6144]{1,0:T(8,128)(2,1)S(1)} %get-tuple-element.35), channel_id=1, source_target_pairs={{0,1},{1,0},{2,3},{3,2},{4,5},{5,4},{6,7},{7,6},{8,9},{9,8},{10,11... | collective-permute-start | bytes 884744 | tf_op jit(solution)/shard_map/ppermute | solution.py:38
  84.3 4.0 %collective-permute-start.22 = (bf16[48,6144]{1,0:T(8,128)(2,1)S(1)}, bf16[48,6144]{1,0:T(8,128)(2,1)S(1)}, u32[]{:S(2)}, u32[]{:S(2)}) collective-permute-start(bf16[48,6144]{1,0:T(8,128)(2,1)S(1)} %get-tuple-element.33), channel_id=1, source_target_pairs={{0,1},{1,0},{2,3},{3,2},{4,5},{5,4},{6,7},{7,6},{8,9},{9,8},{10,11... | collective-permute-start | bytes 1769480 | tf_op jit(solution)/shard_map/ppermute | solution.py:38
  84.4 17.6 %collective-permute-start.10 = (bf16[48,6144]{1,0:T(8,128)(2,1)S(1)}, bf16[48,6144]{1,0:T(8,128)(2,1)S(1)}, u32[]{:S(2)}, u32[]{:S(2)}) collective-permute-start(bf16[48,6144]{1,0:T(8,128)(2,1)S(1)} %get-tuple-element.24), channel_id=1, source_target_pairs={{0,1},{1,0},{2,3},{3,2},{4,5},{5,4},{6,7},{7,6},{8,9},{9,8},{10,11... | collective-permute-start | bytes 1769480 | tf_op jit(solution)/shard_map/ppermute | solution.py:38
  84.8 3.2 %collective-permute-start.17 = (bf16[48,6144]{1,0:T(8,128)(2,1)S(1)}, bf16[48,6144]{1,0:T(8,128)(2,1)S(1)}, u32[]{:S(2)}, u32[]{:S(2)}) collective-permute-start(bf16[48,6144]{1,0:T(8,128)(2,1)S(1)} %get-tuple-element.29), channel_id=1, source_target_pairs={{0,1},{1,0},{2,3},{3,2},{4,5},{5,4},{6,7},{7,6},{8,9},{9,8},{10,11... | collective-permute-start | bytes 1769480 | tf_op jit(solution)/shard_map/ppermute | solution.py:38
  85.6 8.0 %collective-permute-start.24 = (bf16[24,6144]{1,0:T(8,128)(2,1)S(1)}, bf16[24,6144]{1,0:T(8,128)(2,1)S(1)}, u32[]{:S(2)}, u32[]{:S(2)}) collective-permute-start(bf16[24,6144]{1,0:T(8,128)(2,1)S(1)} %add_convert_fusion.3), channel_id=1, source_target_pairs={{0,2},{1,15},{2,4},{3,1},{4,6},{5,3},{6,8},{7,5},{8,10},{9,7},{10,... | collective-permute-start | bytes 884744 | tf_op jit(solution)/shard_map/ppermute | solution.py:51
  88.1 8.7 %collective-permute-start.18 = (bf16[24,6144]{1,0:T(8,128)(2,1)S(1)}, bf16[24,6144]{1,0:T(8,128)(2,1)S(1)}, u32[]{:S(2)}, u32[]{:S(2)}) collective-permute-start(bf16[24,6144]{1,0:T(8,128)(2,1)S(1)} %add_convert_fusion.7), channel_id=1, source_target_pairs={{0,2},{1,15},{2,4},{3,1},{4,6},{5,3},{6,8},{7,5},{8,10},{9,7},{10,... | collective-permute-start | bytes 884744 | tf_op jit(solution)/shard_map/ppermute | solution.py:51
  93.7 8.0 %collective-permute-start.25 = (bf16[24,6144]{1,0:T(8,128)(2,1)S(1)}, bf16[24,6144]{1,0:T(8,128)(2,1)S(1)}, u32[]{:S(2)}, u32[]{:S(2)}) collective-permute-start(bf16[24,6144]{1,0:T(8,128)(2,1)S(1)} %add_convert_fusion.2), channel_id=1, source_target_pairs={{0,2},{1,15},{2,4},{3,1},{4,6},{5,3},{6,8},{7,5},{8,10},{9,7},{10,... | collective-permute-start | bytes 884744 | tf_op jit(solution)/shard_map/ppermute | solution.py:51
  96.9 37.9 %copy-start = (s32[4,2]{0,1:T(2,128)S(1)}, s32[4,2]{0,1:T(2,128)}, u32[]{:S(2)}) copy-start(s32[4,2]{0,1:T(2,128)} %param.20) | copy-start | bytes 100
  96.9 37.9 %copy-start.1 = (f32[4,2]{0,1:T(2,128)S(1)}, f32[4,2]{0,1:T(2,128)}, u32[]{:S(2)}) copy-start(f32[4,2]{0,1:T(2,128)} %param.21) | copy-start | bytes 100
  96.9 8.0 %collective-permute-start.19 = (bf16[24,6144]{1,0:T(8,128)(2,1)S(1)}, bf16[24,6144]{1,0:T(8,128)(2,1)S(1)}, u32[]{:S(2)}, u32[]{:S(2)}) collective-permute-start(bf16[24,6144]{1,0:T(8,128)(2,1)S(1)} %add_convert_fusion.6), channel_id=1, source_target_pairs={{0,2},{1,15},{2,4},{3,1},{4,6},{5,3},{6,8},{7,5},{8,10},{9,7},{10,... | collective-permute-start | bytes 884744 | tf_op jit(solution)/shard_map/ppermute | solution.py:51
  101.9 8.0 %collective-permute-start.26 = (bf16[24,6144]{1,0:T(8,128)(2,1)S(1)}, bf16[24,6144]{1,0:T(8,128)(2,1)S(1)}, u32[]{:S(2)}, u32[]{:S(2)}) collective-permute-start(bf16[24,6144]{1,0:T(8,128)(2,1)S(1)} %add_convert_fusion.1), channel_id=1, source_target_pairs={{0,2},{1,15},{2,4},{3,1},{4,6},{5,3},{6,8},{7,5},{8,10},{9,7},{10,... | collective-permute-start | bytes 884744 | tf_op jit(solution)/shard_map/ppermute | solution.py:51
  105.1 8.0 %collective-permute-start.20 = (bf16[24,6144]{1,0:T(8,128)(2,1)S(1)}, bf16[24,6144]{1,0:T(8,128)(2,1)S(1)}, u32[]{:S(2)}, u32[]{:S(2)}) collective-permute-start(bf16[24,6144]{1,0:T(8,128)(2,1)S(1)} %add_convert_fusion.5), channel_id=1, source_target_pairs={{0,2},{1,15},{2,4},{3,1},{4,6},{5,3},{6,8},{7,5},{8,10},{9,7},{10,... | collective-permute-start | bytes 884744 | tf_op jit(solution)/shard_map/ppermute | solution.py:51
  110.0 3.4 %collective-permute-start.27 = (bf16[24,6144]{1,0:T(8,128)(2,1)S(1)}, bf16[24,6144]{1,0:T(8,128)(2,1)S(1)}, u32[]{:S(2)}, u32[]{:S(2)}) collective-permute-start(bf16[24,6144]{1,0:T(8,128)(2,1)S(1)} %add_convert_fusion), channel_id=1, source_target_pairs={{0,1},{1,0},{2,3},{3,2},{4,5},{5,4},{6,7},{7,6},{8,9},{9,8},{10,11... | collective-permute-start | bytes 884744 | tf_op jit(solution)/shard_map/ppermute | solution.py:38
  113.2 8.0 %collective-permute-start.21 = (bf16[24,6144]{1,0:T(8,128)(2,1)S(1)}, bf16[24,6144]{1,0:T(8,128)(2,1)S(1)}, u32[]{:S(2)}, u32[]{:S(2)}) collective-permute-start(bf16[24,6144]{1,0:T(8,128)(2,1)S(1)} %add_convert_fusion.4), channel_id=1, source_target_pairs={{0,2},{1,15},{2,4},{3,1},{4,6},{5,3},{6,8},{7,5},{8,10},{9,7},{10,... | collective-permute-start | bytes 884744 | tf_op jit(solution)/shard_map/ppermute | solution.py:51

commit v3 on v2

--- a/solution.py
+++ b/solution.py
@@ -49,13 +49,6 @@
         for core in range(cores):
             pairs.append((chip * cores + core, (chip + 1 - 2 * core) % chips * cores + core))
     return lax.ppermute(value, ("dev_1", "dev_2"), pairs)
-
-
-def added(*terms):
-    total = terms[0].astype(jnp.float32)
-    for term in terms[1:]:
-        total = total + term.astype(jnp.float32)
-    return total
 
 
 def gathered(own):
@@ -72,15 +65,58 @@
     return other, came, theirs
 
 
-def scattered(far, own, other, kept, got):
+def hop_kernel(parts, *refs):
+    out = refs[-1]
+    total = None
+    for ref, (row, col) in zip(refs, parts):
+        term = ref[row : row + out.shape[0], col : col + out.shape[1]].astype(jnp.float32)
+        total = term if total is None else total + term
+    out[...] = total.astype(out.dtype)
+
+
+def hop_sum(rows, cols, *terms):
+    vm = pl.BlockSpec(memory_space=pltpu.VMEM)
+    return pl.pallas_call(
+        functools.partial(hop_kernel, [at for _, at in terms]),
+        out_shape=jax.ShapeDtypeStruct((rows, cols), jnp.bfloat16),
+        in_specs=[vm] * len(terms),
+        out_specs=vm,
+        compiler_params=pltpu.CompilerParams(vmem_limit_bytes=8 * 1024 * 1024),
+        name="hop_sum",
+    )(*[x for x, _ in terms])
+
+
+def scattered(far, each, own, other, kept, got):
+    half = own.shape[1] // 2
     moving = {}
     for step in range(far, 0, -1):
         for part in (0, 1) if step < far else (1,):
-            terms = [kept[step, part], got[step, part]]
-            parcel = added(*terms, *moving.get(part, ())).astype(jnp.bfloat16)
-            moving[part] = (passed_on(parcel),)
-    leaving = added(other, *moving[0]).astype(jnp.bfloat16)
-    return own, *moving[1], swapped(leaving)
+            for side in (0, 1):
+                terms = [(x, (row, side * half)) for x, row in (kept[step, part], got[step, part])]
+                if (part, side) in moving:
+                    terms.append((moving[part, side], (0, 0)))
+                parcel = hop_sum(each, half, *terms)
+                moving[part, side] = passed_on(parcel)
+    return own, moving[1, 0], moving[1, 1], swapped(two_sum(other, moving[0, 0], moving[0, 1]))
+
+
+def two_kernel(whole_ref, left_ref, right_ref, out_ref):
+    half = left_ref.shape[1]
+    for side, ref in enumerate((left_ref, right_ref)):
+        cols = slice(side * half, (side + 1) * half)
+        out_ref[:, cols] = (whole_ref[:, cols].astype(jnp.float32) + ref[...].astype(jnp.float32)).astype(out_ref.dtype)
+
+
+def two_sum(whole, left, right):
+    vm = pl.BlockSpec(memory_space=pltpu.VMEM)
+    return pl.pallas_call(
+        two_kernel,
+        out_shape=jax.ShapeDtypeStruct(whole.shape, whole.dtype),
+        in_specs=[vm] * 3,
+        out_specs=vm,
+        compiler_params=pltpu.CompilerParams(vmem_limit_bytes=8 * 1024 * 1024),
+        name="two_sum",
+    )(whole, left, right)
 
 
 def multiplied(pieces, gate, up, down, outs, ready):
@@ -318,28 +354,31 @@
     )(came)
 
 
-def pack_kernel(first_ref, second_ref, third_ref, packed_ref, spread):
+def pack_kernel(first_ref, left_ref, right_ref, third_ref, packed_ref, spread):
     rows, width = first_ref.shape
     f32 = jnp.float32
+    half = left_ref.shape[1]
     for j in range(width // HD):
         cols = slice(j * HD, (j + 1) * HD)
-        total = first_ref[:, cols].astype(f32) + second_ref[:, cols].astype(f32) + third_ref[:, cols].astype(f32)
+        side = left_ref if j * HD < half else right_ref
+        came = side[:, j * HD % half : j * HD % half + HD].astype(f32)
+        total = first_ref[:, cols].astype(f32) + came + third_ref[:, cols].astype(f32)
         spread[pl.ds(j, rows, stride=width // HD), :] = total
     packed_ref[...] = spread[...].astype(jnp.bfloat16).reshape(packed_ref.shape)
 
 
-def packed_sum(first, second, third, places):
+def packed_sum(first, left, right, third, places):
     rows, width = first.shape
     vm = pl.BlockSpec(memory_space=pltpu.VMEM)
     return pl.pallas_call(
         pack_kernel,
         out_shape=jax.ShapeDtypeStruct((places, rows // places * width // HD, HD), jnp.bfloat16),
-        in_specs=[vm] * 3,
+        in_specs=[vm] * 4,
         out_specs=vm,
         scratch_shapes=[pltpu.VMEM((rows * width // HD, HD), jnp.float32)],
         compiler_params=pltpu.CompilerParams(vmem_limit_bytes=8 * 1024 * 1024),
         name="packed_sum",
-    )(first, second, third)
+    )(first, left, right, third)
 
 
 def mix_kernel(ids_ref, weights_ref, home_ref, hidden_ref, out_ref, spread):
@@ -443,14 +482,13 @@
     sent = [swapped(groups[2 + part]) for part in (0, 1)]
     for part in (0, 1):
         for i, step in enumerate(near):
-            kept[step, part] = groups[part][i * each : (i + 1) * each]
-            got[step, part] = sent[part][i * each : (i + 1) * each]
-    kept[far, 1], kept[last, 1], kept[last, 0], *sent = late_products(
-        pieces, (gate, up, down), [each, each, each, 2 * each, each]
-    )
-    sent = [swapped(x) for x in sent]
-    got[far, 1], got[last, 1], got[last, 0] = sent[0][:each], sent[0][each:], sent[1]
-    last_terms = scattered(far, home_own, home_other, kept, got)
+            kept[step, part] = (groups[part], i * each)
+            got[step, part] = (sent[part], i * each)
+    *stay, sent_1, sent_0 = late_products(pieces, (gate, up, down), [each, each, each, 2 * each, each])
+    kept[far, 1], kept[last, 1], kept[last, 0] = [(x, 0) for x in stay]
+    first = swapped(sent_1)
+    got[far, 1], got[last, 1], got[last, 0] = (first, 0), (first, each), (swapped(sent_0), 0)
+    last_terms = scattered(far, each, home_own, home_other, kept, got)
     home = lax.all_to_all(packed_sum(*last_terms, rows_x), "dev_0", 0, 0, tiled=True)
     return mixed_in(expert_ids.T, route_weights.T, home, hidden_state)
 

time: 136 us -> 140 us (1.029)
  waiting for transfers between devices: 71.9 us -> 73.6 us
    ppermute x14 -> x21, waiting for transfers between devices: 64.8 us -> 67.6 us  [passed_on(): return lax.ppermute(value, ('dev_1', 'dev_2'), pairs)]
  transfers between devices with their start and end apart: 28 -> 35, of which waited for: 17 -> 23; matrix products, arithmetic and copies ran while one was open for 1% -> 0% of each run, Pallas kernels for 4% -> 5%
where the time goes in v3:
time: 140 us; the launch traced here: 139 us
  waiting for transfers between devices  73.6 us (53%)
  blocking collectives  33.1 us (24%)
  starting transfers between devices  18.4 us (13%)
  Pallas kernels  13.8 us (10%)
    ppermute x21, waiting for transfers between devices, passed_on(): return lax.ppermute(value, ('dev_1', 'dev_2'), pairs)  67.6 us
    all_to_all x1, blocking collectives, layer(): own_block = unpacked(lax.all_to_all(leaving, 'dev_0', 0, 0, tiled=True))  19.9 us
    all_to_all x1, blocking collectives, layer(): lax.all_to_all(packed_sum(*last_terms, rows_x), 'dev_0', 0, 0, tiled=True)  13.2 us
    ppermute x1, starting transfers between devices, passed_along(): lax.ppermute(value, axis, [(source, source + steps) for source in range(l...  13.1 us
    pallas_call x1, Pallas kernels, early_products(): pl.pallas_call(functools.partial(early_kernel, len(pieces)), out_shape=ou...  4.9 us
    pallas_call x1, Pallas kernels, attended(): pl.pallas_call(attend_kernel, out_shape=[jax.ShapeDtypeStruct((reqs, widt...  4.61 us
    ppermute x1, waiting for transfers between devices, passed_along(): lax.ppermute(value, axis, [(source, source + steps) for source in range(l...  4.18 us
    ppermute x13, starting transfers between devices, shifted(): lax.ppermute(value, axis, [(place, (place + steps) % count) for place in...  3.06 us
  transfers between devices with their start and end apart: 35, of which 23 were waited for; matrix products, arithmetic and copies ran while one was open for 0% of the time, Pallas kernels for 5%

profile of v3, /device:TPU:514, one launch (start us, length us, event | category | flops | bytes accessed | tf_op | source)
XLA Modules:
  0.0 139.3 jit_solution(9791015304100032528)
XLA Ops:
  0.0 13.1 %collective-permute-start = (bf16[64,2048]{1,0:T(8,128)(2,1)}, bf16[64,2048]{1,0:T(8,128)(2,1)S(1)}, u32[]{:S(2)}, u32[]{:S(2)}) collective-permute-start(bf16[64,2048]{1,0:T(8,128)(2,1)} %refs_7_.1), channel_id=1, source_target_pairs={{1,0},{2,1},{3,2},{4,3},{5,4},{6,5},{7,6},{8,7},{9,8},{10,9},{11,1... | collective-permute-start | bytes 786440 | tf_op jit(solution)/shard_map/ppermute | solution.py:33
  13.2 4.2 %collective-permute-done.refs_0_ = bf16[64,2048]{1,0:T(8,128)(2,1)S(1)} collective-permute-done((bf16[64,2048]{1,0:T(8,128)(2,1)}, bf16[64,2048]{1,0:T(8,128)(2,1)S(1)}, u32[]{:S(2)}, u32[]{:S(2)}) %collective-permute-start) | collective-permute-done | bytes 262176 | tf_op jit(solution)/shard_map/ppermute | solution.py:33
  17.3 4.6 %attended.1 = (f32[4,6144]{1,0:T(4,128)S(1)}, bf16[8,144,128]{2,1,0:T(8,128)(2,1)S(1)}) custom-call(s32[1]{0:T(128)} %bitcast.2.me_ref, bf16[64,2048]{1,0:T(8,128)(2,1)S(1)} %collective-permute-done.refs_0_, s32[4]{0:T(128)} %refs_1_.1, s32[2,4]{1,0:T(2,128)} %bitcast.5, s32[1,128]{1,0:T(1,128)} %bitcast.9, bf16[4,6144]{1,0:T(4,128)(2,1)} %refs_4_.1, ...), custom_call_target="tpu_custom_call" | custom-call | flops 77070336 | bytes 2097152 | tf_op jit(solution)/shard_map/attended/pallas_call | solution.py:317
  21.9 19.9 %all_to_all.10.came_ref = bf16[8,144,128]{2,1,0:T(8,128)(2,1)S(1)} all-to-all(bf16[8,144,128]{2,1,0:T(8,128)(2,1)S(1)} %get-tuple-element.21), channel_id=1, replica_groups=mesh['groups'=2,'dev_0'=8,'dev_1'=8,'dev_2'=2] {'dev_0'}, dimensions={0} | all-to-all | bytes 589824 | tf_op jit(solution)/shard_map/all_to_all | solution.py:460
  41.8 0.2 unpacked.1.refs_0_
  42.0 0.1 collective-permute-start.2
  42.2 0.4 collective-permute-start.1
  42.5 7.5 %collective-permute-done.2.refs_7_ = bf16[24,6144]{1,0:T(8,128)(2,1)S(1)} collective-permute-done((bf16[24,6144]{1,0:T(8,128)(2,1)S(1)}, bf16[24,6144]{1,0:T(8,128)(2,1)S(1)}, u32[]{:S(2)}, u32[]{:S(2)}) %collective-permute-start.2) | collective-permute-done | bytes 294944 | tf_op jit(solution)/shard_map/ppermute | solution.py:51
  50.1 7.9 %collective-permute-done.3.refs_6_ = bf16[24,6144]{1,0:T(8,128)(2,1)S(1)} collective-permute-done((bf16[24,6144]{1,0:T(8,128)(2,1)S(1)}, bf16[24,6144]{1,0:T(8,128)(2,1)S(1)}, u32[]{:S(2)}, u32[]{:S(2)}) %collective-permute-start.3) | collective-permute-done | bytes 294944 | tf_op jit(solution)/shard_map/ppermute | solution.py:51
  58.0 3.2 %collective-permute-done.6.refs_9_ = bf16[24,6144]{1,0:T(8,128)(2,1)S(1)} collective-permute-done((bf16[24,6144]{1,0:T(8,128)(2,1)S(1)}, bf16[24,6144]{1,0:T(8,128)(2,1)S(1)}, u32[]{:S(2)}, u32[]{:S(2)}) %collective-permute-start.6) | collective-permute-done | bytes 294944 | tf_op jit(solution)/shard_map/ppermute | solution.py:51
  61.2 0.5 collective-permute-start.4
  61.7 4.3 %collective-permute-done.11.refs_5_ = bf16[24,6144]{1,0:T(8,128)(2,1)S(1)} collective-permute-done((bf16[24,6144]{1,0:T(8,128)(2,1)S(1)}, bf16[24,6144]{1,0:T(8,128)(2,1)S(1)}, u32[]{:S(2)}, u32[]{:S(2)}) %collective-permute-start.11) | collective-permute-done | bytes 294944 | tf_op jit(solution)/shard_map/ppermute | solution.py:51
  66.0 3.2 %collective-permute-done.7.refs_8_ = bf16[24,6144]{1,0:T(8,128)(2,1)S(1)} collective-permute-done((bf16[24,6144]{1,0:T(8,128)(2,1)S(1)}, bf16[24,6144]{1,0:T(8,128)(2,1)S(1)}, u32[]{:S(2)}, u32[]{:S(2)}) %collective-permute-start.7) | collective-permute-done | bytes 294944 | tf_op jit(solution)/shard_map/ppermute | solution.py:51
  69.1 0.5 collective-permute-start.8
  69.6 0.1 collective-permute-start.15
  69.8 4.1 %collective-permute-done.12.refs_0_ = bf16[24,6144]{1,0:T(8,128)(2,1)S(1)} collective-permute-done((bf16[24,6144]{1,0:T(8,128)(2,1)S(1)}, bf16[24,6144]{1,0:T(8,128)(2,1)S(1)}, u32[]{:S(2)}, u32[]{:S(2)}) %collective-permute-start.12) | collective-permute-done | bytes 294944 | tf_op jit(solution)/shard_map/ppermute | solution.py:51
  73.9 3.2 %collective-permute-done.13.refs_4_ = bf16[24,6144]{1,0:T(8,128)(2,1)S(1)} collective-permute-done((bf16[24,6144]{1,0:T(8,128)(2,1)S(1)}, bf16[24,6144]{1,0:T(8,128)(2,1)S(1)}, u32[]{:S(2)}, u32[]{:S(2)}) %collective-permute-start.13) | collective-permute-done | bytes 294944 | tf_op jit(solution)/shard_map/ppermute | solution.py:51
  77.1 4.9 %early.1 = (bf16[24,6144]{1,0:T(8,128)(2,1)S(1)}, bf16[24,6144]{1,0:T(8,128)(2,1)S(1)}, bf16[48,6144]{1,0:T(8,128)(2,1)S(1)}, bf16[48,6144]{1,0:T(8,128)(2,1)S(1...) custom-call(bf16[24,6144]{1,0:T(8,128)(2,1)S(1)} %unpacked.1.refs_0_, ...), custom_call_target="tpu_custom_call" | custom-call | flops 2264924160 | bytes 9437184 | tf_op jit(solution)/shard_map/early/pallas_call | solution.py:185
  82.0 0.6 collective-permute-start.26
  82.6 1.7 %late.1 = (bf16[24,6144]{1,0:T(8,128)(2,1)S(1)}, bf16[24,6144]{1,0:T(8,128)(2,1)S(1)}, bf16[24,6144]{1,0:T(8,128)(2,1)S(1)}, bf16[48,6144]{1,0:T(8,128)(2,1)S(1)}, bf16[24,6144]{1,0:T(8,128)(2,1)S(1)}) custom-call(bf16[24,6144]{1,0:T(8,128)(2,1)S(1)} %collective-permute-done.12.refs_0_, bf16[24,6144]{1,0:T(8,128)(2,1)S(1)} %collective-permute-done.14.refs_1_, ...), custom_call_target="tpu_custom_call" | custom-call | flops 1358954496 | bytes 9437184 | tf_op jit(solution)/shard_map/late/pallas_call | solution.py:200
  84.3 0.2 collective-permute-start.17
  84.5 0.5 collective-permute-start.27
  84.9 0.1 collective-permute-start.10
  85.1 1.8 %collective-permute-done.27.refs_1_ = bf16[24,6144]{1,0:T(8,128)(2,1)S(1)} collective-permute-done((bf16[24,6144]{1,0:T(8,128)(2,1)S(1)}, bf16[24,6144]{1,0:T(8,128)(2,1)S(1)}, u32[]{:S(2)}, u32[]{:S(2)}) %collective-permute-start.27) | collective-permute-done | bytes 294944 | tf_op jit(solution)/shard_map/ppermute | solution.py:38
  86.9 0.1 collective-permute-start.31
  87.1 0.1 collective-permute-start.28
  87.2 6.1 %collective-permute-done.31.refs_2_ = bf16[24,3072]{1,0:T(8,128)(2,1)S(1)} collective-permute-done((bf16[24,3072]{1,0:T(8,128)(2,1)S(1)}, bf16[24,3072]{1,0:T(8,128)(2,1)S(1)}, u32[]{:S(2)}, u32[]{:S(2)}) %collective-permute-start.31) | collective-permute-done | bytes 147488 | tf_op jit(solution)/shard_map/ppermute | solution.py:51
  93.3 0.1 hop_sum.26
  93.4 0.1 collective-permute-start.32
  93.5 1.4 collective-permute-done.28.refs_2_
  94.9 0.1 hop_sum.23
  95.0 0.1 collective-permute-start.29
  95.2 0.1 collective-permute-start.22
  95.4 0.1 collective-permute-start.18
  95.5 4.4 %collective-permute-done.32.refs_2_ = bf16[24,3072]{1,0:T(8,128)(2,1)S(1)} collective-permute-done((bf16[24,3072]{1,0:T(8,128)(2,1)S(1)}, bf16[24,3072]{1,0:T(8,128)(2,1)S(1)}, u32[]{:S(2)}, u32[]{:S(2)}) %collective-permute-start.32) | collective-permute-done | bytes 147488 | tf_op jit(solution)/shard_map/ppermute | solution.py:51
  99.9 0.1 hop_sum.27
  99.9 0.1 collective-permute-start.33
  100.1 1.4 collective-permute-done.29.refs_2_
  101.4 0.1 hop_sum.24
  101.5 0.4 collective-permute-start.30
  101.9 1.2 collective-permute-done.22.refs_2_
  103.0 0.1 hop_sum.19
  103.1 0.1 collective-permute-start.23
  103.2 1.4 collective-permute-done.18.refs_2_
  104.6 0.1 hop_sum.15
  104.7 0.1 collective-permute-start.19
  104.8 1.6 %collective-permute-done.33.right_ref = bf16[24,3072]{1,0:T(8,128)(2,1)S(1)} collective-permute-done((bf16[24,3072]{1,0:T(8,128)(2,1)S(1)}, bf16[24,3072]{1,0:T(8,128)(2,1)S(1)}, u32[]{:S(2)}, u32[]{:S(2)}) %collective-permute-start.33) | collective-permute-done | bytes 147488 | tf_op jit(solution)/shard_map/ppermute | solution.py:51
  106.4 1.8 %collective-permute-done.30.left_ref = bf16[24,3072]{1,0:T(8,128)(2,1)S(1)} collective-permute-done((bf16[24,3072]{1,0:T(8,128)(2,1)S(1)}, bf16[24,3072]{1,0:T(8,128)(2,1)S(1)}, u32[]{:S(2)}, u32[]{:S(2)}) %collective-permute-start.30) | collective-permute-done | bytes 147488 | tf_op jit(solution)/shard_map/ppermute | solution.py:51
  108.2 0.1 two_sum.1
  108.3 0.1 collective-permute-start.34
  108.4 1.3 collective-permute-done.23.refs_2_
  109.8 0.1 hop_sum.20
  109.9 0.1 collective-permute-start.24
  110.0 1.4 collective-permute-done.19.refs_2_
  111.4 0.1 collective-permute-start.20
  111.6 4.8 %collective-permute-done.24.refs_2_ = bf16[24,3072]{1,0:T(8,128)(2,1)S(1)} collective-permute-done((bf16[24,3072]{1,0:T(8,128)(2,1)S(1)}, bf16[24,3072]{1,0:T(8,128)(2,1)S(1)}, u32[]{:S(2)}, u32[]{:S(2)}) %collective-permute-start.24) | collective-permute-done | bytes 147488 | tf_op jit(solution)/shard_map/ppermute | solution.py:51
  116.4 0.1 collective-permute-start.25
  116.5 1.4 collective-permute-done.20.refs_2_
  118.0 0.1 collective-permute-start.21
  118.1 4.7 %collective-permute-done.25.right_ref = bf16[24,3072]{1,0:T(8,128)(2,1)S(1)} collective-permute-done((bf16[24,3072]{1,0:T(8,128)(2,1)S(1)}, bf16[24,3072]{1,0:T(8,128)(2,1)S(1)}, u32[]{:S(2)}, u32[]{:S(2)}) %collective-permute-start.25) | collective-permute-done | bytes 147488 | tf_op jit(solution)/shard_map/ppermute | solution.py:51
  122.9 1.6 %collective-permute-done.21.left_ref = bf16[24,3072]{1,0:T(8,128)(2,1)S(1)} collective-permute-done((bf16[24,3072]{1,0:T(8,128)(2,1)S(1)}, bf16[24,3072]{1,0:T(8,128)(2,1)S(1)}, u32[]{:S(2)}, u32[]{:S(2)}) %collective-permute-start.21) | collective-permute-done | bytes 147488 | tf_op jit(solution)/shard_map/ppermute | solution.py:51
  124.4 0.3 packed_sum.1
  124.7 13.2 %all_to_all.11.home_ref = bf16[8,144,128]{2,1,0:T(8,128)(2,1)S(1)} all-to-all(bf16[8,144,128]{2,1,0:T(8,128)(2,1)S(1)} %packed_sum.1), channel_id=1, replica_groups=mesh['groups'=2,'dev_0'=8,'dev_1'=8,'dev_2'=2] {'dev_0'}, dimensions={0} | all-to-all | bytes 589824 | tf_op jit(solution)/shard_map/all_to_all | solution.py:492
  138.0 1.4 mixed_in.1
  (33 shorter events, 0.4 us)
Async XLA Ops:
  0.0 17.3 %collective-permute-start = (bf16[64,2048]{1,0:T(8,128)(2,1)}, bf16[64,2048]{1,0:T(8,128)(2,1)S(1)}, u32[]{:S(2)}, u32[]{:S(2)}) collective-permute-start(bf16[64,2048]{1,0:T(8,128)(2,1)} %refs_7_.1), channel_id=1, source_target_pairs={{1,0},{2,1},{3,2},{4,3},{5,4},{6,5},{7,6},{8,7},{9,8},{10,9},{11,1... | collective-permute-start | bytes 786440 | tf_op jit(solution)/shard_map/ppermute | solution.py:33
  42.0 8.0 %collective-permute-start.2 = (bf16[24,6144]{1,0:T(8,128)(2,1)S(1)}, bf16[24,6144]{1,0:T(8,128)(2,1)S(1)}, u32[]{:S(2)}, u32[]{:S(2)}) collective-permute-start(bf16[24,6144]{1,0:T(8,128)(2,1)S(1)} %unpacked.1.refs_0_), channel_id=1, source_target_pairs={{0,2},{1,15},{2,4},{3,1},{4,6},{5,3},{6,8},{7,5},{8,10},{9,7},{10,... | collective-permute-start | bytes 884744 | tf_op jit(solution)/shard_map/ppermute | solution.py:51
  42.2 7.9 %collective-permute-start.1 = (bf16[24,6144]{1,0:T(8,128)(2,1)S(1)}, bf16[24,6144]{1,0:T(8,128)(2,1)S(1)}, u32[]{:S(2)}, u32[]{:S(2)}) collective-permute-start(bf16[24,6144]{1,0:T(8,128)(2,1)S(1)} %unpacked.1.refs_0_), channel_id=1, source_target_pairs={{0,1},{1,0},{2,3},{3,2},{4,5},{5,4},{6,7},{7,6},{8,9},{9,8},{10,11... | collective-permute-start | bytes 884744 | tf_op jit(solution)/shard_map/ppermute | solution.py:38
  50.1 7.9 %collective-permute-start.3 = (bf16[24,6144]{1,0:T(8,128)(2,1)S(1)}, bf16[24,6144]{1,0:T(8,128)(2,1)S(1)}, u32[]{:S(2)}, u32[]{:S(2)}) collective-permute-start(bf16[24,6144]{1,0:T(8,128)(2,1)S(1)} %collective-permute-done.2.refs_7_), channel_id=1, source_target_pairs={{0,2},{1,15},{2,4},{3,1},{4,6},{5,3},{6,8},{7,5},{8,10},{9,7},{10,... | collective-permute-start | bytes 884744 | tf_op jit(solution)/shard_map/ppermute | solution.py:51
  50.1 11.1 %collective-permute-start.6 = (bf16[24,6144]{1,0:T(8,128)(2,1)S(1)}, bf16[24,6144]{1,0:T(8,128)(2,1)S(1)}, u32[]{:S(2)}, u32[]{:S(2)}) collective-permute-start(bf16[24,6144]{1,0:T(8,128)(2,1)S(1)} %collective-permute-done.1.refs_1_), channel_id=1, source_target_pairs={{0,2},{1,15},{2,4},{3,1},{4,6},{5,3},{6,8},{7,5},{8,10},{9,7},{10,... | collective-permute-start | bytes 884744 | tf_op jit(solution)/shard_map/ppermute | solution.py:51
  58.0 7.9 %collective-permute-start.11 = (bf16[24,6144]{1,0:T(8,128)(2,1)S(1)}, bf16[24,6144]{1,0:T(8,128)(2,1)S(1)}, u32[]{:S(2)}, u32[]{:S(2)}) collective-permute-start(bf16[24,6144]{1,0:T(8,128)(2,1)S(1)} %collective-permute-done.3.refs_6_), channel_id=1, source_target_pairs={{0,2},{1,15},{2,4},{3,1},{4,6},{5,3},{6,8},{7,5},{8,10},{9,7},{10,... | collective-permute-start | bytes 884744 | tf_op jit(solution)/shard_map/ppermute | solution.py:51
  61.2 7.9 %collective-permute-start.7 = (bf16[24,6144]{1,0:T(8,128)(2,1)S(1)}, bf16[24,6144]{1,0:T(8,128)(2,1)S(1)}, u32[]{:S(2)}, u32[]{:S(2)}) collective-permute-start(bf16[24,6144]{1,0:T(8,128)(2,1)S(1)} %collective-permute-done.6.refs_9_), channel_id=1, source_target_pairs={{0,2},{1,15},{2,4},{3,1},{4,6},{5,3},{6,8},{7,5},{8,10},{9,7},{10,... | collective-permute-start | bytes 884744 | tf_op jit(solution)/shard_map/ppermute | solution.py:51
  61.2 7.9 %collective-permute-start.5 = (bf16[24,6144]{1,0:T(8,128)(2,1)S(1)}, bf16[24,6144]{1,0:T(8,128)(2,1)S(1)}, u32[]{:S(2)}, u32[]{:S(2)}) collective-permute-start(bf16[24,6144]{1,0:T(8,128)(2,1)S(1)} %collective-permute-done.2.refs_7_), channel_id=1, source_target_pairs={{0,1},{1,0},{2,3},{3,2},{4,5},{5,4},{6,7},{7,6},{8,9},{9,8},{10,11... | collective-permute-start | bytes 884744 | tf_op jit(solution)/shard_map/ppermute | solution.py:38
  61.2 8.4 %collective-permute-start.4 = (bf16[24,6144]{1,0:T(8,128)(2,1)S(1)}, bf16[24,6144]{1,0:T(8,128)(2,1)S(1)}, u32[]{:S(2)}, u32[]{:S(2)}) collective-permute-start(bf16[24,6144]{1,0:T(8,128)(2,1)S(1)} %collective-permute-done.3.refs_6_), channel_id=1, source_target_pairs={{0,1},{1,0},{2,3},{3,2},{4,5},{5,4},{6,7},{7,6},{8,9},{9,8},{10,11... | collective-permute-start | bytes 884744 | tf_op jit(solution)/shard_map/ppermute | solution.py:38
  66.0 7.9 %collective-permute-start.12 = (bf16[24,6144]{1,0:T(8,128)(2,1)S(1)}, bf16[24,6144]{1,0:T(8,128)(2,1)S(1)}, u32[]{:S(2)}, u32[]{:S(2)}) collective-permute-start(bf16[24,6144]{1,0:T(8,128)(2,1)S(1)} %collective-permute-done.11.refs_5_), channel_id=1, source_target_pairs={{0,2},{1,15},{2,4},{3,1},{4,6},{5,3},{6,8},{7,5},{8,10},{9,7},{10,... | collective-permute-start | bytes 884744 | tf_op jit(solution)/shard_map/ppermute | solution.py:51
  69.1 7.9 %collective-permute-start.13 = (bf16[24,6144]{1,0:T(8,128)(2,1)S(1)}, bf16[24,6144]{1,0:T(8,128)(2,1)S(1)}, u32[]{:S(2)}, u32[]{:S(2)}) collective-permute-start(bf16[24,6144]{1,0:T(8,128)(2,1)S(1)} %collective-permute-done.7.refs_8_), channel_id=1, source_target_pairs={{0,2},{1,15},{2,4},{3,1},{4,6},{5,3},{6,8},{7,5},{8,10},{9,7},{10,... | collective-permute-start | bytes 884744 | tf_op jit(solution)/shard_map/ppermute | solution.py:51
  69.1 7.9 %collective-permute-start.9 = (bf16[24,6144]{1,0:T(8,128)(2,1)S(1)}, bf16[24,6144]{1,0:T(8,128)(2,1)S(1)}, u32[]{:S(2)}, u32[]{:S(2)}) collective-permute-start(bf16[24,6144]{1,0:T(8,128)(2,1)S(1)} %collective-permute-done.6.refs_9_), channel_id=1, source_target_pairs={{0,1},{1,0},{2,3},{3,2},{4,5},{5,4},{6,7},{7,6},{8,9},{9,8},{10,11... | collective-permute-start | bytes 884744 | tf_op jit(solution)/shard_map/ppermute | solution.py:38
  69.1 7.9 %collective-permute-start.8 = (bf16[24,6144]{1,0:T(8,128)(2,1)S(1)}, bf16[24,6144]{1,0:T(8,128)(2,1)S(1)}, u32[]{:S(2)}, u32[]{:S(2)}) collective-permute-start(bf16[24,6144]{1,0:T(8,128)(2,1)S(1)} %collective-permute-done.7.refs_8_), channel_id=1, source_target_pairs={{0,1},{1,0},{2,3},{3,2},{4,5},{5,4},{6,7},{7,6},{8,9},{9,8},{10,11... | collective-permute-start | bytes 884744 | tf_op jit(solution)/shard_map/ppermute | solution.py:38
  69.6 13.0 %collective-permute-start.15 = (bf16[24,6144]{1,0:T(8,128)(2,1)S(1)}, bf16[24,6144]{1,0:T(8,128)(2,1)S(1)}, u32[]{:S(2)}, u32[]{:S(2)}) collective-permute-start(bf16[24,6144]{1,0:T(8,128)(2,1)S(1)} %collective-permute-done.11.refs_5_), channel_id=1, source_target_pairs={{0,1},{1,0},{2,3},{3,2},{4,5},{5,4},{6,7},{7,6},{8,9},{9,8},{10,11... | collective-permute-start | bytes 884744 | tf_op jit(solution)/shard_map/ppermute | solution.py:38
  73.9 8.7 %collective-permute-start.16 = (bf16[24,6144]{1,0:T(8,128)(2,1)S(1)}, bf16[24,6144]{1,0:T(8,128)(2,1)S(1)}, u32[]{:S(2)}, u32[]{:S(2)}) collective-permute-start(bf16[24,6144]{1,0:T(8,128)(2,1)S(1)} %collective-permute-done.12.refs_0_), channel_id=1, source_target_pairs={{0,1},{1,0},{2,3},{3,2},{4,5},{5,4},{6,7},{7,6},{8,9},{9,8},{10,11... | collective-permute-start | bytes 884744 | tf_op jit(solution)/shard_map/ppermute | solution.py:38
  77.0 5.5 %collective-permute-start.14 = (bf16[24,6144]{1,0:T(8,128)(2,1)S(1)}, bf16[24,6144]{1,0:T(8,128)(2,1)S(1)}, u32[]{:S(2)}, u32[]{:S(2)}) collective-permute-start(bf16[24,6144]{1,0:T(8,128)(2,1)S(1)} %collective-permute-done.13.refs_4_), channel_id=1, source_target_pairs={{0,1},{1,0},{2,3},{3,2},{4,5},{5,4},{6,7},{7,6},{8,9},{9,8},{10,11... | collective-permute-start | bytes 884744 | tf_op jit(solution)/shard_map/ppermute | solution.py:38
  82.0 5.2 %collective-permute-start.26 = (bf16[48,6144]{1,0:T(8,128)(2,1)S(1)}, bf16[48,6144]{1,0:T(8,128)(2,1)S(1)}, u32[]{:S(2)}, u32[]{:S(2)}) collective-permute-start(bf16[48,6144]{1,0:T(8,128)(2,1)S(1)} %get-tuple-element.33), channel_id=1, source_target_pairs={{0,1},{1,0},{2,3},{3,2},{4,5},{5,4},{6,7},{7,6},{8,9},{9,8},{10,11... | collective-permute-start | bytes 1769480 | tf_op jit(solution)/shard_map/ppermute | solution.py:38
  84.3 10.8 %collective-permute-start.17 = (bf16[48,6144]{1,0:T(8,128)(2,1)S(1)}, bf16[48,6144]{1,0:T(8,128)(2,1)S(1)}, u32[]{:S(2)}, u32[]{:S(2)}) collective-permute-start(bf16[48,6144]{1,0:T(8,128)(2,1)S(1)} %get-tuple-element.29), channel_id=1, source_target_pairs={{0,1},{1,0},{2,3},{3,2},{4,5},{5,4},{6,7},{7,6},{8,9},{9,8},{10,11... | collective-permute-start | bytes 1769480 | tf_op jit(solution)/shard_map/ppermute | solution.py:38
  84.5 2.4 %collective-permute-start.27 = (bf16[24,6144]{1,0:T(8,128)(2,1)S(1)}, bf16[24,6144]{1,0:T(8,128)(2,1)S(1)}, u32[]{:S(2)}, u32[]{:S(2)}) collective-permute-start(bf16[24,6144]{1,0:T(8,128)(2,1)S(1)} %get-tuple-element.35), channel_id=1, source_target_pairs={{0,1},{1,0},{2,3},{3,2},{4,5},{5,4},{6,7},{7,6},{8,9},{9,8},{10,11... | collective-permute-start | bytes 884744 | tf_op jit(solution)/shard_map/ppermute | solution.py:38
  84.9 23.5 %collective-permute-start.10 = (bf16[48,6144]{1,0:T(8,128)(2,1)S(1)}, bf16[48,6144]{1,0:T(8,128)(2,1)S(1)}, u32[]{:S(2)}, u32[]{:S(2)}) collective-permute-start(bf16[48,6144]{1,0:T(8,128)(2,1)S(1)} %get-tuple-element.24), channel_id=1, source_target_pairs={{0,1},{1,0},{2,3},{3,2},{4,5},{5,4},{6,7},{7,6},{8,9},{9,8},{10,11... | collective-permute-start | bytes 1769480 | tf_op jit(solution)/shard_map/ppermute | solution.py:38
  86.9 6.5 %collective-permute-start.31 = (bf16[24,3072]{1,0:T(8,128)(2,1)S(1)}, bf16[24,3072]{1,0:T(8,128)(2,1)S(1)}, u32[]{:S(2)}, u32[]{:S(2)}) collective-permute-start(bf16[24,3072]{1,0:T(8,128)(2,1)S(1)} %hop_sum.25), channel_id=1, source_target_pairs={{0,2},{1,15},{2,4},{3,1},{4,6},{5,3},{6,8},{7,5},{8,10},{9,7},{10,... | collective-permute-start | bytes 442376 | tf_op jit(solution)/shard_map/ppermute | solution.py:51
  87.1 7.9 %collective-permute-start.28 = (bf16[24,3072]{1,0:T(8,128)(2,1)S(1)}, bf16[24,3072]{1,0:T(8,128)(2,1)S(1)}, u32[]{:S(2)}, u32[]{:S(2)}) collective-permute-start(bf16[24,3072]{1,0:T(8,128)(2,1)S(1)} %hop_sum.22), channel_id=1, source_target_pairs={{0,2},{1,15},{2,4},{3,1},{4,6},{5,3},{6,8},{7,5},{8,10},{9,7},{10,... | collective-permute-start | bytes 442376 | tf_op jit(solution)/shard_map/ppermute | solution.py:51
  93.4 6.5 %collective-permute-start.32 = (bf16[24,3072]{1,0:T(8,128)(2,1)S(1)}, bf16[24,3072]{1,0:T(8,128)(2,1)S(1)}, u32[]{:S(2)}, u32[]{:S(2)}) collective-permute-start(bf16[24,3072]{1,0:T(8,128)(2,1)S(1)} %hop_sum.26), channel_id=1, source_target_pairs={{0,2},{1,15},{2,4},{3,1},{4,6},{5,3},{6,8},{7,5},{8,10},{9,7},{10,... | collective-permute-start | bytes 442376 | tf_op jit(solution)/shard_map/ppermute | solution.py:51
  95.0 6.5 %collective-permute-start.29 = (bf16[24,3072]{1,0:T(8,128)(2,1)S(1)}, bf16[24,3072]{1,0:T(8,128)(2,1)S(1)}, u32[]{:S(2)}, u32[]{:S(2)}) collective-permute-start(bf16[24,3072]{1,0:T(8,128)(2,1)S(1)} %hop_sum.23), channel_id=1, source_target_pairs={{0,2},{1,15},{2,4},{3,1},{4,6},{5,3},{6,8},{7,5},{8,10},{9,7},{10,... | collective-permute-start | bytes 442376 | tf_op jit(solution)/shard_map/ppermute | solution.py:51
  95.2 7.9 %collective-permute-start.22 = (bf16[24,3072]{1,0:T(8,128)(2,1)S(1)}, bf16[24,3072]{1,0:T(8,128)(2,1)S(1)}, u32[]{:S(2)}, u32[]{:S(2)}) collective-permute-start(bf16[24,3072]{1,0:T(8,128)(2,1)S(1)} %hop_sum.18), channel_id=1, source_target_pairs={{0,2},{1,15},{2,4},{3,1},{4,6},{5,3},{6,8},{7,5},{8,10},{9,7},{10,... | collective-permute-start | bytes 442376 | tf_op jit(solution)/shard_map/ppermute | solution.py:51
  95.4 9.2 %collective-permute-start.18 = (bf16[24,3072]{1,0:T(8,128)(2,1)S(1)}, bf16[24,3072]{1,0:T(8,128)(2,1)S(1)}, u32[]{:S(2)}, u32[]{:S(2)}) collective-permute-start(bf16[24,3072]{1,0:T(8,128)(2,1)S(1)} %hop_sum.14), channel_id=1, source_target_pairs={{0,2},{1,15},{2,4},{3,1},{4,6},{5,3},{6,8},{7,5},{8,10},{9,7},{10,... | collective-permute-start | bytes 442376 | tf_op jit(solution)/shard_map/ppermute | solution.py:51
  99.9 6.5 %collective-permute-start.33 = (bf16[24,3072]{1,0:T(8,128)(2,1)S(1)}, bf16[24,3072]{1,0:T(8,128)(2,1)S(1)}, u32[]{:S(2)}, u32[]{:S(2)}) collective-permute-start(bf16[24,3072]{1,0:T(8,128)(2,1)S(1)} %hop_sum.27), channel_id=1, source_target_pairs={{0,2},{1,15},{2,4},{3,1},{4,6},{5,3},{6,8},{7,5},{8,10},{9,7},{10,... | collective-permute-start | bytes 442376 | tf_op jit(solution)/shard_map/ppermute | solution.py:51
  101.5 6.7 %collective-permute-start.30 = (bf16[24,3072]{1,0:T(8,128)(2,1)S(1)}, bf16[24,3072]{1,0:T(8,128)(2,1)S(1)}, u32[]{:S(2)}, u32[]{:S(2)}) collective-permute-start(bf16[24,3072]{1,0:T(8,128)(2,1)S(1)} %hop_sum.24), channel_id=1, source_target_pairs={{0,2},{1,15},{2,4},{3,1},{4,6},{5,3},{6,8},{7,5},{8,10},{9,7},{10,... | collective-permute-start | bytes 442376 | tf_op jit(solution)/shard_map/ppermute | solution.py:51
  103.1 6.7 %collective-permute-start.23 = (bf16[24,3072]{1,0:T(8,128)(2,1)S(1)}, bf16[24,3072]{1,0:T(8,128)(2,1)S(1)}, u32[]{:S(2)}, u32[]{:S(2)}) collective-permute-start(bf16[24,3072]{1,0:T(8,128)(2,1)S(1)} %hop_sum.19), channel_id=1, source_target_pairs={{0,2},{1,15},{2,4},{3,1},{4,6},{5,3},{6,8},{7,5},{8,10},{9,7},{10,... | collective-permute-start | bytes 442376 | tf_op jit(solution)/shard_map/ppermute | solution.py:51
  104.7 6.7 %collective-permute-start.19 = (bf16[24,3072]{1,0:T(8,128)(2,1)S(1)}, bf16[24,3072]{1,0:T(8,128)(2,1)S(1)}, u32[]{:S(2)}, u32[]{:S(2)}) collective-permute-start(bf16[24,3072]{1,0:T(8,128)(2,1)S(1)} %hop_sum.15), channel_id=1, source_target_pairs={{0,2},{1,15},{2,4},{3,1},{4,6},{5,3},{6,8},{7,5},{8,10},{9,7},{10,... | collective-permute-start | bytes 442376 | tf_op jit(solution)/shard_map/ppermute | solution.py:51
  108.3 9.8 %collective-permute-start.34 = (bf16[24,6144]{1,0:T(8,128)(2,1)S(1)}, bf16[24,6144]{1,0:T(8,128)(2,1)S(1)}, u32[]{:S(2)}, u32[]{:S(2)}) collective-permute-start(bf16[24,6144]{1,0:T(8,128)(2,1)S(1)} %two_sum.1), channel_id=1, source_target_pairs={{0,1},{1,0},{2,3},{3,2},{4,5},{5,4},{6,7},{7,6},{8,9},{9,8},{10,11... | collective-permute-start | bytes 884744 | tf_op jit(solution)/shard_map/ppermute | solution.py:38
  109.8 28.1 %copy-start = (s32[4,2]{0,1:T(2,128)S(1)}, s32[4,2]{0,1:T(2,128)}, u32[]{:S(2)}) copy-start(s32[4,2]{0,1:T(2,128)} %param.20) | copy-start | bytes 100
  109.8 28.1 %copy-start.1 = (f32[4,2]{0,1:T(2,128)S(1)}, f32[4,2]{0,1:T(2,128)}, u32[]{:S(2)}) copy-start(f32[4,2]{0,1:T(2,128)} %param.21) | copy-start | bytes 100
  109.9 6.5 %collective-permute-start.24 = (bf16[24,3072]{1,0:T(8,128)(2,1)S(1)}, bf16[24,3072]{1,0:T(8,128)(2,1)S(1)}, u32[]{:S(2)}, u32[]{:S(2)}) collective-permute-start(bf16[24,3072]{1,0:T(8,128)(2,1)S(1)} %hop_sum.20), channel_id=1, source_target_pairs={{0,2},{1,15},{2,4},{3,1},{4,6},{5,3},{6,8},{7,5},{8,10},{9,7},{10,... | collective-permute-start | bytes 442376 | tf_op jit(solution)/shard_map/ppermute | solution.py:51
  111.4 6.5 %collective-permute-start.20 = (bf16[24,3072]{1,0:T(8,128)(2,1)S(1)}, bf16[24,3072]{1,0:T(8,128)(2,1)S(1)}, u32[]{:S(2)}, u32[]{:S(2)}) collective-permute-start(bf16[24,3072]{1,0:T(8,128)(2,1)S(1)} %hop_sum.16), channel_id=1, source_target_pairs={{0,2},{1,15},{2,4},{3,1},{4,6},{5,3},{6,8},{7,5},{8,10},{9,7},{10,... | collective-permute-start | bytes 442376 | tf_op jit(solution)/shard_map/ppermute | solution.py:51
  116.4 6.5 %collective-permute-start.25 = (bf16[24,3072]{1,0:T(8,128)(2,1)S(1)}, bf16[24,3072]{1,0:T(8,128)(2,1)S(1)}, u32[]{:S(2)}, u32[]{:S(2)}) collective-permute-start(bf16[24,3072]{1,0:T(8,128)(2,1)S(1)} %hop_sum.21), channel_id=1, source_target_pairs={{0,2},{1,15},{2,4},{3,1},{4,6},{5,3},{6,8},{7,5},{8,10},{9,7},{10,... | collective-permute-start | bytes 442376 | tf_op jit(solution)/shard_map/ppermute | solution.py:51
  118.0 6.5 %collective-permute-start.21 = (bf16[24,3072]{1,0:T(8,128)(2,1)S(1)}, bf16[24,3072]{1,0:T(8,128)(2,1)S(1)}, u32[]{:S(2)}, u32[]{:S(2)}) collective-permute-start(bf16[24,3072]{1,0:T(8,128)(2,1)S(1)} %hop_sum.17), channel_id=1, source_target_pairs={{0,2},{1,15},{2,4},{3,1},{4,6},{5,3},{6,8},{7,5},{8,10},{9,7},{10,... | collective-permute-start | bytes 442376 | tf_op jit(solution)/shard_map/ppermute | solution.py:51

commit v4 on v3

--- a/solution.py
+++ b/solution.py
@@ -470,24 +470,20 @@
         pieces, (w_gate, w_up, w_down), [each, each] + [len(near) * each] * 4
     )
     last = far - 1
-    pieces = [
-        came[far, 0],
-        theirs[last, 1],
-        theirs[last, 0],
-        theirs[far, 0],
-        came[last, 1],
-        came[last, 0],
-    ]
     kept, got = {}, {}
-    sent = [swapped(groups[2 + part]) for part in (0, 1)]
+    near_sent = [swapped(groups[2 + part]) for part in (0, 1)]
     for part in (0, 1):
         for i, step in enumerate(near):
             kept[step, part] = (groups[part], i * each)
-            got[step, part] = (sent[part], i * each)
-    *stay, sent_1, sent_0 = late_products(pieces, (gate, up, down), [each, each, each, 2 * each, each])
-    kept[far, 1], kept[last, 1], kept[last, 0] = [(x, 0) for x in stay]
-    first = swapped(sent_1)
-    got[far, 1], got[last, 1], got[last, 0] = (first, 0), (first, each), (swapped(sent_0), 0)
+            got[step, part] = (near_sent[part], i * each)
+    pieces = [theirs[last, 0], theirs[last, 1], came[last, 0], came[last, 1]]
+    results = late_products(pieces, (gate, up, down), [each] * 4)
+    for part in (0, 1):
+        kept[last, part] = (results[part], 0)
+        got[last, part] = (swapped(results[2 + part]), 0)
+    results = late_products([came[far, 0], theirs[far, 0]], (gate, up, down), [each] * 2)
+    kept[far, 1] = (results[0], 0)
+    got[far, 1] = (swapped(results[1]), 0)
     last_terms = scattered(far, each, home_own, home_other, kept, got)
     home = lax.all_to_all(packed_sum(*last_terms, rows_x), "dev_0", 0, 0, tiled=True)
     return mixed_in(expert_ids.T, route_weights.T, home, hidden_state)

time: 140 us -> 132 us (0.943)
  waiting for transfers between devices: 73.6 us -> 64.4 us
  Pallas kernels: 13.8 us -> 15.7 us
    ppermute x21, waiting for transfers between devices: 67.6 us -> 58.3 us  [passed_on(): return lax.ppermute(value, ('dev_1', 'dev_2'), pairs)]
    pallas_call x1 -> x2, Pallas kernels: 1.68 us -> 3.56 us  [late_products(): pl.pallas_call(functools.partial(late_kernel, len(pieces)), out_shape=[ja...]
    ppermute x13 -> x14, starting transfers between devices: 3.06 us -> 3.32 us  [shifted(): lax.ppermute(value, axis, [(place, (place + steps) % count) for place in...]
  transfers between devices with their start and end apart: 35 -> 36, of which waited for: 23 -> 24; matrix products, arithmetic and copies ran while one was open for 0% -> 0% of each run, Pallas kernels for 5% -> 7%
where the time goes in v4:
time: 132 us
  waiting for transfers between devices  64.4 us (49%)
  blocking collectives  33.1 us (25%)
  starting transfers between devices  18.3 us (14%)
  Pallas kernels  15.7 us (12%)
    ppermute x21, waiting for transfers between devices, passed_on(): return lax.ppermute(value, ('dev_1', 'dev_2'), pairs)  58.3 us
    all_to_all x1, blocking collectives, layer(): own_block = unpacked(lax.all_to_all(leaving, 'dev_0', 0, 0, tiled=True))  19.9 us
    all_to_all x1, blocking collectives, layer(): lax.all_to_all(packed_sum(*last_terms, rows_x), 'dev_0', 0, 0, tiled=True)  13.2 us
    ppermute x1, starting transfers between devices, passed_along(): lax.ppermute(value, axis, [(source, source + steps) for source in range(l...  13.1 us
    pallas_call x1, Pallas kernels, early_products(): pl.pallas_call(functools.partial(early_kernel, len(pieces)), out_shape=ou...  4.9 us
    pallas_call x1, Pallas kernels, attended(): pl.pallas_call(attend_kernel, out_shape=[jax.ShapeDtypeStruct((reqs, widt...  4.61 us
    ppermute x1, waiting for transfers between devices, passed_along(): lax.ppermute(value, axis, [(source, source + steps) for source in range(l...  4.18 us
    pallas_call x2, Pallas kernels, late_products(): pl.pallas_call(functools.partial(late_kernel, len(pieces)), out_shape=[ja...  3.56 us
  transfers between devices with their start and end apart: 36, of which 24 were waited for; matrix products, arithmetic and copies ran while one was open for 0% of the time, Pallas kernels for 7%

profile of v4, /device:TPU:514, one launch (start us, length us, event | category | flops | bytes accessed | tf_op | source)
XLA Modules:
  0.0 131.7 jit_solution(16475660993681451953)
XLA Ops:
  0.0 13.1 %collective-permute-start = (bf16[64,2048]{1,0:T(8,128)(2,1)}, bf16[64,2048]{1,0:T(8,128)(2,1)S(1)}, u32[]{:S(2)}, u32[]{:S(2)}) collective-permute-start(bf16[64,2048]{1,0:T(8,128)(2,1)} %refs_7_.1), channel_id=1, source_target_pairs={{1,0},{2,1},{3,2},{4,3},{5,4},{6,5},{7,6},{8,7},{9,8},{10,9},{11,1... | collective-permute-start | bytes 786440 | tf_op jit(solution)/shard_map/ppermute | solution.py:33
  13.2 4.2 %collective-permute-done.refs_0_ = bf16[64,2048]{1,0:T(8,128)(2,1)S(1)} collective-permute-done((bf16[64,2048]{1,0:T(8,128)(2,1)}, bf16[64,2048]{1,0:T(8,128)(2,1)S(1)}, u32[]{:S(2)}, u32[]{:S(2)}) %collective-permute-start) | collective-permute-done | bytes 262176 | tf_op jit(solution)/shard_map/ppermute | solution.py:33
  17.3 4.6 %attended.1 = (f32[4,6144]{1,0:T(4,128)S(1)}, bf16[8,144,128]{2,1,0:T(8,128)(2,1)S(1)}) custom-call(s32[1]{0:T(128)} %bitcast.2.me_ref, bf16[64,2048]{1,0:T(8,128)(2,1)S(1)} %collective-permute-done.refs_0_, s32[4]{0:T(128)} %refs_1_.1, s32[2,4]{1,0:T(2,128)} %bitcast.5, s32[1,128]{1,0:T(1,128)} %bitcast.9, bf16[4,6144]{1,0:T(4,128)(2,1)} %refs_4_.1, ...), custom_call_target="tpu_custom_call" | custom-call | flops 77070336 | bytes 2097152 | tf_op jit(solution)/shard_map/attended/pallas_call | solution.py:317
  21.9 19.9 %all_to_all.10.came_ref = bf16[8,144,128]{2,1,0:T(8,128)(2,1)S(1)} all-to-all(bf16[8,144,128]{2,1,0:T(8,128)(2,1)S(1)} %get-tuple-element.22), channel_id=1, replica_groups=mesh['groups'=2,'dev_0'=8,'dev_1'=8,'dev_2'=2] {'dev_0'}, dimensions={0} | all-to-all | bytes 589824 | tf_op jit(solution)/shard_map/all_to_all | solution.py:460
  41.8 0.2 unpacked.1.refs_0_
  42.0 0.1 collective-permute-start.1
  42.2 0.1 collective-permute-start.2
  42.3 1.4 %collective-permute-done.1.refs_1_ = bf16[24,6144]{1,0:T(8,128)(2,1)S(1)} collective-permute-done((bf16[24,6144]{1,0:T(8,128)(2,1)S(1)}, bf16[24,6144]{1,0:T(8,128)(2,1)S(1)}, u32[]{:S(2)}, u32[]{:S(2)}) %collective-permute-start.1) | collective-permute-done | bytes 294944 | tf_op jit(solution)/shard_map/ppermute | solution.py:38
  43.7 6.5 %collective-permute-done.2.refs_7_ = bf16[24,6144]{1,0:T(8,128)(2,1)S(1)} collective-permute-done((bf16[24,6144]{1,0:T(8,128)(2,1)S(1)}, bf16[24,6144]{1,0:T(8,128)(2,1)S(1)}, u32[]{:S(2)}, u32[]{:S(2)}) %collective-permute-start.2) | collective-permute-done | bytes 294944 | tf_op jit(solution)/shard_map/ppermute | solution.py:51
  50.2 3.2 %collective-permute-done.6.refs_9_ = bf16[24,6144]{1,0:T(8,128)(2,1)S(1)} collective-permute-done((bf16[24,6144]{1,0:T(8,128)(2,1)S(1)}, bf16[24,6144]{1,0:T(8,128)(2,1)S(1)}, u32[]{:S(2)}, u32[]{:S(2)}) %collective-permute-start.6) | collective-permute-done | bytes 294944 | tf_op jit(solution)/shard_map/ppermute | solution.py:51
  53.4 4.8 %collective-permute-done.3.refs_6_ = bf16[24,6144]{1,0:T(8,128)(2,1)S(1)} collective-permute-done((bf16[24,6144]{1,0:T(8,128)(2,1)S(1)}, bf16[24,6144]{1,0:T(8,128)(2,1)S(1)}, u32[]{:S(2)}, u32[]{:S(2)}) %collective-permute-start.3) | collective-permute-done | bytes 294944 | tf_op jit(solution)/shard_map/ppermute | solution.py:51
  58.2 0.5 collective-permute-start.4
  58.7 2.6 %collective-permute-done.7.refs_8_ = bf16[24,6144]{1,0:T(8,128)(2,1)S(1)} collective-permute-done((bf16[24,6144]{1,0:T(8,128)(2,1)S(1)}, bf16[24,6144]{1,0:T(8,128)(2,1)S(1)}, u32[]{:S(2)}, u32[]{:S(2)}) %collective-permute-start.7) | collective-permute-done | bytes 294944 | tf_op jit(solution)/shard_map/ppermute | solution.py:51
  61.3 4.8 %collective-permute-done.11.refs_2_ = bf16[24,6144]{1,0:T(8,128)(2,1)S(1)} collective-permute-done((bf16[24,6144]{1,0:T(8,128)(2,1)S(1)}, bf16[24,6144]{1,0:T(8,128)(2,1)S(1)}, u32[]{:S(2)}, u32[]{:S(2)}) %collective-permute-start.11) | collective-permute-done | bytes 294944 | tf_op jit(solution)/shard_map/ppermute | solution.py:51
  66.1 0.5 collective-permute-start.8
  66.6 0.1 collective-permute-start.12
  66.8 2.5 %collective-permute-done.13.refs_3_ = bf16[24,6144]{1,0:T(8,128)(2,1)S(1)} collective-permute-done((bf16[24,6144]{1,0:T(8,128)(2,1)S(1)}, bf16[24,6144]{1,0:T(8,128)(2,1)S(1)}, u32[]{:S(2)}, u32[]{:S(2)}) %collective-permute-start.13) | collective-permute-done | bytes 294944 | tf_op jit(solution)/shard_map/ppermute | solution.py:51
  69.3 4.8 %collective-permute-done.16.refs_0_ = bf16[24,6144]{1,0:T(8,128)(2,1)S(1)} collective-permute-done((bf16[24,6144]{1,0:T(8,128)(2,1)S(1)}, bf16[24,6144]{1,0:T(8,128)(2,1)S(1)}, u32[]{:S(2)}, u32[]{:S(2)}) %collective-permute-start.16) | collective-permute-done | bytes 294944 | tf_op jit(solution)/shard_map/ppermute | solution.py:51
  74.1 4.9 %early.1 = (bf16[24,6144]{1,0:T(8,128)(2,1)S(1)}, bf16[24,6144]{1,0:T(8,128)(2,1)S(1)}, bf16[48,6144]{1,0:T(8,128)(2,1)S(1)}, bf16[48,6144]{1,0:T(8,128)(2,1)S(1...) custom-call(bf16[24,6144]{1,0:T(8,128)(2,1)S(1)} %unpacked.1.refs_0_, ...), custom_call_target="tpu_custom_call" | custom-call | flops 2264924160 | bytes 9437184 | tf_op jit(solution)/shard_map/early/pallas_call | solution.py:185
  79.0 0.6 collective-permute-start.27
  79.6 1.7 %late.2 = (bf16[24,6144]{1,0:T(8,128)(2,1)S(1)}, bf16[24,6144]{1,0:T(8,128)(2,1)S(1)}, bf16[24,6144]{1,0:T(8,128)(2,1)S(1)}, bf16[24,6144]{1,0:T(8,128)(2,1)S(1)}) custom-call(bf16[24,6144]{1,0:T(8,128)(2,1)S(1)} %collective-permute-done.12.refs_0_, bf16[24,6144]{1,0:T(8,128)(2,1)S(1)} %collective-permute-done.14.refs_1_, ...), custom_call_target="tpu_custom_call" | custom-call | flops 905969664 | bytes 9437184 | tf_op jit(solution)/shard_map/late/pallas_call | solution.py:200
  81.3 0.2 collective-permute-start.28
  81.5 1.8 %late.3 = (bf16[24,6144]{1,0:T(8,128)(2,1)S(1)}, bf16[24,6144]{1,0:T(8,128)(2,1)S(1)}) custom-call(bf16[24,6144]{1,0:T(8,128)(2,1)S(1)} %collective-permute-done.16.refs_0_, bf16[24,6144]{1,0:T(8,128)(2,1)S(1)} %collective-permute-done.17.refs_1_, bf16[6144,256]{1,0:T(8,128)(2,1)S(1)} %get-tuple-element.26.refs_4_.refs_2_, ...), custom_call_target="tpu_custom_call" | custom-call | flops 452984832 | bytes 9437184 | tf_op jit(solution)/shard_map/late/pallas_call | solution.py:200
  83.3 0.6 collective-permute-start.18
  83.9 0.1 collective-permute-start.10
  84.1 0.4 collective-permute-start.15
  84.5 0.1 collective-permute-start.32
  84.6 0.5 collective-permute-done.18.refs_1_
  85.2 0.1 collective-permute-start.23
  85.4 5.6 %collective-permute-done.32.refs_2_ = bf16[24,3072]{1,0:T(8,128)(2,1)S(1)} collective-permute-done((bf16[24,3072]{1,0:T(8,128)(2,1)S(1)}, bf16[24,3072]{1,0:T(8,128)(2,1)S(1)}, u32[]{:S(2)}, u32[]{:S(2)}) %collective-permute-start.32) | collective-permute-done | bytes 147488 | tf_op jit(solution)/shard_map/ppermute | solution.py:51
  90.9 0.1 hop_sum.26
  91.0 1.5 %collective-permute-done.29.refs_2_ = bf16[24,3072]{1,0:T(8,128)(2,1)S(1)} collective-permute-done((bf16[24,3072]{1,0:T(8,128)(2,1)S(1)}, bf16[24,3072]{1,0:T(8,128)(2,1)S(1)}, u32[]{:S(2)}, u32[]{:S(2)}) %collective-permute-start.29) | collective-permute-done | bytes 147488 | tf_op jit(solution)/shard_map/ppermute | solution.py:51
  92.5 0.1 hop_sum.23
  92.6 0.4 collective-permute-start.30
  92.9 1.1 collective-permute-done.23.refs_2_
  94.1 0.1 hop_sum.19
  94.1 0.1 collective-permute-start.24
  94.3 3.0 %collective-permute-done.19.refs_2_ = bf16[24,3072]{1,0:T(8,128)(2,1)S(1)} collective-permute-done((bf16[24,3072]{1,0:T(8,128)(2,1)S(1)}, bf16[24,3072]{1,0:T(8,128)(2,1)S(1)}, u32[]{:S(2)}, u32[]{:S(2)}) %collective-permute-start.19) | collective-permute-done | bytes 147488 | tf_op jit(solution)/shard_map/ppermute | solution.py:51
  97.3 0.1 hop_sum.15
  97.3 0.1 collective-permute-start.20
  97.5 1.4 %collective-permute-done.33.refs_2_ = bf16[24,3072]{1,0:T(8,128)(2,1)S(1)} collective-permute-done((bf16[24,3072]{1,0:T(8,128)(2,1)S(1)}, bf16[24,3072]{1,0:T(8,128)(2,1)S(1)}, u32[]{:S(2)}, u32[]{:S(2)}) %collective-permute-start.33) | collective-permute-done | bytes 147488 | tf_op jit(solution)/shard_map/ppermute | solution.py:51
  98.9 0.1 hop_sum.27
  98.9 0.1 collective-permute-start.34
  99.1 1.4 %collective-permute-done.30.refs_2_ = bf16[24,3072]{1,0:T(8,128)(2,1)S(1)} collective-permute-done((bf16[24,3072]{1,0:T(8,128)(2,1)S(1)}, bf16[24,3072]{1,0:T(8,128)(2,1)S(1)}, u32[]{:S(2)}, u32[]{:S(2)}) %collective-permute-start.30) | collective-permute-done | bytes 147488 | tf_op jit(solution)/shard_map/ppermute | solution.py:51
  100.4 0.1 hop_sum.24
  100.5 0.1 collective-permute-start.31
  100.7 1.4 %collective-permute-done.24.refs_2_ = bf16[24,3072]{1,0:T(8,128)(2,1)S(1)} collective-permute-done((bf16[24,3072]{1,0:T(8,128)(2,1)S(1)}, bf16[24,3072]{1,0:T(8,128)(2,1)S(1)}, u32[]{:S(2)}, u32[]{:S(2)}) %collective-permute-start.24) | collective-permute-done | bytes 147488 | tf_op jit(solution)/shard_map/ppermute | solution.py:51
  102.0 0.1 hop_sum.20
  102.1 0.1 collective-permute-start.25
  102.2 1.6 %collective-permute-done.20.refs_2_ = bf16[24,3072]{1,0:T(8,128)(2,1)S(1)} collective-permute-done((bf16[24,3072]{1,0:T(8,128)(2,1)S(1)}, bf16[24,3072]{1,0:T(8,128)(2,1)S(1)}, u32[]{:S(2)}, u32[]{:S(2)}) %collective-permute-start.20) | collective-permute-done | bytes 147488 | tf_op jit(solution)/shard_map/ppermute | solution.py:51
  103.9 0.1 collective-permute-start.21
  104.0 1.4 %collective-permute-done.34.right_ref = bf16[24,3072]{1,0:T(8,128)(2,1)S(1)} collective-permute-done((bf16[24,3072]{1,0:T(8,128)(2,1)S(1)}, bf16[24,3072]{1,0:T(8,128)(2,1)S(1)}, u32[]{:S(2)}, u32[]{:S(2)}) %collective-permute-start.34) | collective-permute-done | bytes 147488 | tf_op jit(solution)/shard_map/ppermute | solution.py:51
  105.4 1.6 %collective-permute-done.31.left_ref = bf16[24,3072]{1,0:T(8,128)(2,1)S(1)} collective-permute-done((bf16[24,3072]{1,0:T(8,128)(2,1)S(1)}, bf16[24,3072]{1,0:T(8,128)(2,1)S(1)}, u32[]{:S(2)}, u32[]{:S(2)}) %collective-permute-start.31) | collective-permute-done | bytes 147488 | tf_op jit(solution)/shard_map/ppermute | solution.py:51
  107.0 0.1 two_sum.1
  107.0 0.1 collective-permute-start.35
  107.2 1.4 %collective-permute-done.25.refs_2_ = bf16[24,3072]{1,0:T(8,128)(2,1)S(1)} collective-permute-done((bf16[24,3072]{1,0:T(8,128)(2,1)S(1)}, bf16[24,3072]{1,0:T(8,128)(2,1)S(1)}, u32[]{:S(2)}, u32[]{:S(2)}) %collective-permute-start.25) | collective-permute-done | bytes 147488 | tf_op jit(solution)/shard_map/ppermute | solution.py:51
  108.6 0.1 collective-permute-start.26
  108.7 1.6 %collective-permute-done.21.refs_2_ = bf16[24,3072]{1,0:T(8,128)(2,1)S(1)} collective-permute-done((bf16[24,3072]{1,0:T(8,128)(2,1)S(1)}, bf16[24,3072]{1,0:T(8,128)(2,1)S(1)}, u32[]{:S(2)}, u32[]{:S(2)}) %collective-permute-start.21) | collective-permute-done | bytes 147488 | tf_op jit(solution)/shard_map/ppermute | solution.py:51
  110.4 0.1 collective-permute-start.22
  110.6 4.5 %collective-permute-done.26.right_ref = bf16[24,3072]{1,0:T(8,128)(2,1)S(1)} collective-permute-done((bf16[24,3072]{1,0:T(8,128)(2,1)S(1)}, bf16[24,3072]{1,0:T(8,128)(2,1)S(1)}, u32[]{:S(2)}, u32[]{:S(2)}) %collective-permute-start.26) | collective-permute-done | bytes 147488 | tf_op jit(solution)/shard_map/ppermute | solution.py:51
  115.1 1.8 %collective-permute-done.22.left_ref = bf16[24,3072]{1,0:T(8,128)(2,1)S(1)} collective-permute-done((bf16[24,3072]{1,0:T(8,128)(2,1)S(1)}, bf16[24,3072]{1,0:T(8,128)(2,1)S(1)}, u32[]{:S(2)}, u32[]{:S(2)}) %collective-permute-start.22) | collective-permute-done | bytes 147488 | tf_op jit(solution)/shard_map/ppermute | solution.py:51
  116.9 0.3 packed_sum.1
  117.2 13.2 %all_to_all.11.home_ref = bf16[8,144,128]{2,1,0:T(8,128)(2,1)S(1)} all-to-all(bf16[8,144,128]{2,1,0:T(8,128)(2,1)S(1)} %packed_sum.1), channel_id=1, replica_groups=mesh['groups'=2,'dev_0'=8,'dev_1'=8,'dev_2'=2] {'dev_0'}, dimensions={0} | all-to-all | bytes 589824 | tf_op jit(solution)/shard_map/all_to_all | solution.py:488
  130.4 1.4 %mixed_in.1 = bf16[4,6144]{1,0:T(4,128)(2,1)} custom-call(s32[2,4]{1,0:T(2,128)S(1)} %bitcast.6, f32[2,4]{1,0:T(2,128)S(1)} %bitcast.7, bf16[8,144,128]{2,1,0:T(8,128)(2,1)S(1)} %all_to_all.11.home_ref, f32[4,6144]{1,0:T(4,128)S(1)} %get-tuple-element.38.hidden_ref), custom_call_target="tpu_custom_call" | custom-call | tf_op jit(solution)/shard_map/mixed_in/pallas_call | solution.py:416
  (36 shorter events, 0.4 us)
Async XLA Ops:
  0.0 17.3 %collective-permute-start = (bf16[64,2048]{1,0:T(8,128)(2,1)}, bf16[64,2048]{1,0:T(8,128)(2,1)S(1)}, u32[]{:S(2)}, u32[]{:S(2)}) collective-permute-start(bf16[64,2048]{1,0:T(8,128)(2,1)} %refs_7_.1), channel_id=1, source_target_pairs={{1,0},{2,1},{3,2},{4,3},{5,4},{6,5},{7,6},{8,7},{9,8},{10,9},{11,1... | collective-permute-start | bytes 786440 | tf_op jit(solution)/shard_map/ppermute | solution.py:33
  42.0 1.7 %collective-permute-start.1 = (bf16[24,6144]{1,0:T(8,128)(2,1)S(1)}, bf16[24,6144]{1,0:T(8,128)(2,1)S(1)}, u32[]{:S(2)}, u32[]{:S(2)}) collective-permute-start(bf16[24,6144]{1,0:T(8,128)(2,1)S(1)} %unpacked.1.refs_0_), channel_id=1, source_target_pairs={{0,1},{1,0},{2,3},{3,2},{4,5},{5,4},{6,7},{7,6},{8,9},{9,8},{10,11... | collective-permute-start | bytes 884744 | tf_op jit(solution)/shard_map/ppermute | solution.py:38
  42.2 8.0 %collective-permute-start.2 = (bf16[24,6144]{1,0:T(8,128)(2,1)S(1)}, bf16[24,6144]{1,0:T(8,128)(2,1)S(1)}, u32[]{:S(2)}, u32[]{:S(2)}) collective-permute-start(bf16[24,6144]{1,0:T(8,128)(2,1)S(1)} %unpacked.1.refs_0_), channel_id=1, source_target_pairs={{0,2},{1,15},{2,4},{3,1},{4,6},{5,3},{6,8},{7,5},{8,10},{9,7},{10,... | collective-permute-start | bytes 884744 | tf_op jit(solution)/shard_map/ppermute | solution.py:51
  43.7 9.7 %collective-permute-start.6 = (bf16[24,6144]{1,0:T(8,128)(2,1)S(1)}, bf16[24,6144]{1,0:T(8,128)(2,1)S(1)}, u32[]{:S(2)}, u32[]{:S(2)}) collective-permute-start(bf16[24,6144]{1,0:T(8,128)(2,1)S(1)} %collective-permute-done.1.refs_1_), channel_id=1, source_target_pairs={{0,2},{1,15},{2,4},{3,1},{4,6},{5,3},{6,8},{7,5},{8,10},{9,7},{10,... | collective-permute-start | bytes 884744 | tf_op jit(solution)/shard_map/ppermute | solution.py:51
  50.2 7.9 %collective-permute-start.3 = (bf16[24,6144]{1,0:T(8,128)(2,1)S(1)}, bf16[24,6144]{1,0:T(8,128)(2,1)S(1)}, u32[]{:S(2)}, u32[]{:S(2)}) collective-permute-start(bf16[24,6144]{1,0:T(8,128)(2,1)S(1)} %collective-permute-done.2.refs_7_), channel_id=1, source_target_pairs={{0,2},{1,15},{2,4},{3,1},{4,6},{5,3},{6,8},{7,5},{8,10},{9,7},{10,... | collective-permute-start | bytes 884744 | tf_op jit(solution)/shard_map/ppermute | solution.py:51
  53.4 7.9 %collective-permute-start.7 = (bf16[24,6144]{1,0:T(8,128)(2,1)S(1)}, bf16[24,6144]{1,0:T(8,128)(2,1)S(1)}, u32[]{:S(2)}, u32[]{:S(2)}) collective-permute-start(bf16[24,6144]{1,0:T(8,128)(2,1)S(1)} %collective-permute-done.6.refs_9_), channel_id=1, source_target_pairs={{0,2},{1,15},{2,4},{3,1},{4,6},{5,3},{6,8},{7,5},{8,10},{9,7},{10,... | collective-permute-start | bytes 884744 | tf_op jit(solution)/shard_map/ppermute | solution.py:51
  58.2 7.9 %collective-permute-start.11 = (bf16[24,6144]{1,0:T(8,128)(2,1)S(1)}, bf16[24,6144]{1,0:T(8,128)(2,1)S(1)}, u32[]{:S(2)}, u32[]{:S(2)}) collective-permute-start(bf16[24,6144]{1,0:T(8,128)(2,1)S(1)} %collective-permute-done.3.refs_6_), channel_id=1, source_target_pairs={{0,2},{1,15},{2,4},{3,1},{4,6},{5,3},{6,8},{7,5},{8,10},{9,7},{10,... | collective-permute-start | bytes 884744 | tf_op jit(solution)/shard_map/ppermute | solution.py:51
  58.2 7.9 %collective-permute-start.5 = (bf16[24,6144]{1,0:T(8,128)(2,1)S(1)}, bf16[24,6144]{1,0:T(8,128)(2,1)S(1)}, u32[]{:S(2)}, u32[]{:S(2)}) collective-permute-start(bf16[24,6144]{1,0:T(8,128)(2,1)S(1)} %collective-permute-done.2.refs_7_), channel_id=1, source_target_pairs={{0,1},{1,0},{2,3},{3,2},{4,5},{5,4},{6,7},{7,6},{8,9},{9,8},{10,11... | collective-permute-start | bytes 884744 | tf_op jit(solution)/shard_map/ppermute | solution.py:38
  58.2 8.4 %collective-permute-start.4 = (bf16[24,6144]{1,0:T(8,128)(2,1)S(1)}, bf16[24,6144]{1,0:T(8,128)(2,1)S(1)}, u32[]{:S(2)}, u32[]{:S(2)}) collective-permute-start(bf16[24,6144]{1,0:T(8,128)(2,1)S(1)} %collective-permute-done.3.refs_6_), channel_id=1, source_target_pairs={{0,1},{1,0},{2,3},{3,2},{4,5},{5,4},{6,7},{7,6},{8,9},{9,8},{10,11... | collective-permute-start | bytes 884744 | tf_op jit(solution)/shard_map/ppermute | solution.py:38
  61.3 7.9 %collective-permute-start.13 = (bf16[24,6144]{1,0:T(8,128)(2,1)S(1)}, bf16[24,6144]{1,0:T(8,128)(2,1)S(1)}, u32[]{:S(2)}, u32[]{:S(2)}) collective-permute-start(bf16[24,6144]{1,0:T(8,128)(2,1)S(1)} %collective-permute-done.7.refs_8_), channel_id=1, source_target_pairs={{0,2},{1,15},{2,4},{3,1},{4,6},{5,3},{6,8},{7,5},{8,10},{9,7},{10,... | collective-permute-start | bytes 884744 | tf_op jit(solution)/shard_map/ppermute | solution.py:51
  66.1 7.9 %collective-permute-start.16 = (bf16[24,6144]{1,0:T(8,128)(2,1)S(1)}, bf16[24,6144]{1,0:T(8,128)(2,1)S(1)}, u32[]{:S(2)}, u32[]{:S(2)}) collective-permute-start(bf16[24,6144]{1,0:T(8,128)(2,1)S(1)} %collective-permute-done.11.refs_2_), channel_id=1, source_target_pairs={{0,2},{1,15},{2,4},{3,1},{4,6},{5,3},{6,8},{7,5},{8,10},{9,7},{10,... | collective-permute-start | bytes 884744 | tf_op jit(solution)/shard_map/ppermute | solution.py:51
  66.1 7.9 %collective-permute-start.9 = (bf16[24,6144]{1,0:T(8,128)(2,1)S(1)}, bf16[24,6144]{1,0:T(8,128)(2,1)S(1)}, u32[]{:S(2)}, u32[]{:S(2)}) collective-permute-start(bf16[24,6144]{1,0:T(8,128)(2,1)S(1)} %collective-permute-done.6.refs_9_), channel_id=1, source_target_pairs={{0,1},{1,0},{2,3},{3,2},{4,5},{5,4},{6,7},{7,6},{8,9},{9,8},{10,11... | collective-permute-start | bytes 884744 | tf_op jit(solution)/shard_map/ppermute | solution.py:38
  66.1 7.9 %collective-permute-start.8 = (bf16[24,6144]{1,0:T(8,128)(2,1)S(1)}, bf16[24,6144]{1,0:T(8,128)(2,1)S(1)}, u32[]{:S(2)}, u32[]{:S(2)}) collective-permute-start(bf16[24,6144]{1,0:T(8,128)(2,1)S(1)} %collective-permute-done.7.refs_8_), channel_id=1, source_target_pairs={{0,1},{1,0},{2,3},{3,2},{4,5},{5,4},{6,7},{7,6},{8,9},{9,8},{10,11... | collective-permute-start | bytes 884744 | tf_op jit(solution)/shard_map/ppermute | solution.py:38
  66.6 13.0 %collective-permute-start.12 = (bf16[24,6144]{1,0:T(8,128)(2,1)S(1)}, bf16[24,6144]{1,0:T(8,128)(2,1)S(1)}, u32[]{:S(2)}, u32[]{:S(2)}) collective-permute-start(bf16[24,6144]{1,0:T(8,128)(2,1)S(1)} %collective-permute-done.11.refs_2_), channel_id=1, source_target_pairs={{0,1},{1,0},{2,3},{3,2},{4,5},{5,4},{6,7},{7,6},{8,9},{9,8},{10,11... | collective-permute-start | bytes 884744 | tf_op jit(solution)/shard_map/ppermute | solution.py:38
  69.3 10.3 %collective-permute-start.14 = (bf16[24,6144]{1,0:T(8,128)(2,1)S(1)}, bf16[24,6144]{1,0:T(8,128)(2,1)S(1)}, u32[]{:S(2)}, u32[]{:S(2)}) collective-permute-start(bf16[24,6144]{1,0:T(8,128)(2,1)S(1)} %collective-permute-done.13.refs_3_), channel_id=1, source_target_pairs={{0,1},{1,0},{2,3},{3,2},{4,5},{5,4},{6,7},{7,6},{8,9},{9,8},{10,11... | collective-permute-start | bytes 884744 | tf_op jit(solution)/shard_map/ppermute | solution.py:38
  74.0 7.4 %collective-permute-start.17 = (bf16[24,6144]{1,0:T(8,128)(2,1)S(1)}, bf16[24,6144]{1,0:T(8,128)(2,1)S(1)}, u32[]{:S(2)}, u32[]{:S(2)}) collective-permute-start(bf16[24,6144]{1,0:T(8,128)(2,1)S(1)} %collective-permute-done.16.refs_0_), channel_id=1, source_target_pairs={{0,1},{1,0},{2,3},{3,2},{4,5},{5,4},{6,7},{7,6},{8,9},{9,8},{10,11... | collective-permute-start | bytes 884744 | tf_op jit(solution)/shard_map/ppermute | solution.py:38
  79.0 6.2 %collective-permute-start.27 = (bf16[48,6144]{1,0:T(8,128)(2,1)S(1)}, bf16[48,6144]{1,0:T(8,128)(2,1)S(1)}, u32[]{:S(2)}, u32[]{:S(2)}) collective-permute-start(bf16[48,6144]{1,0:T(8,128)(2,1)S(1)} %get-tuple-element.35), channel_id=1, source_target_pairs={{0,1},{1,0},{2,3},{3,2},{4,5},{5,4},{6,7},{7,6},{8,9},{9,8},{10,11... | collective-permute-start | bytes 1769480 | tf_op jit(solution)/shard_map/ppermute | solution.py:38
  81.3 3.1 %collective-permute-start.28 = (bf16[24,6144]{1,0:T(8,128)(2,1)S(1)}, bf16[24,6144]{1,0:T(8,128)(2,1)S(1)}, u32[]{:S(2)}, u32[]{:S(2)}) collective-permute-start(bf16[24,6144]{1,0:T(8,128)(2,1)S(1)} %get-tuple-element.37), channel_id=1, source_target_pairs={{0,1},{1,0},{2,3},{3,2},{4,5},{5,4},{6,7},{7,6},{8,9},{9,8},{10,11... | collective-permute-start | bytes 884744 | tf_op jit(solution)/shard_map/ppermute | solution.py:38
  83.3 1.8 %collective-permute-start.18 = (bf16[24,6144]{1,0:T(8,128)(2,1)S(1)}, bf16[24,6144]{1,0:T(8,128)(2,1)S(1)}, u32[]{:S(2)}, u32[]{:S(2)}) collective-permute-start(bf16[24,6144]{1,0:T(8,128)(2,1)S(1)} %get-tuple-element.32), channel_id=1, source_target_pairs={{0,1},{1,0},{2,3},{3,2},{4,5},{5,4},{6,7},{7,6},{8,9},{9,8},{10,11... | collective-permute-start | bytes 884744 | tf_op jit(solution)/shard_map/ppermute | solution.py:38
  83.9 16.7 %collective-permute-start.10 = (bf16[48,6144]{1,0:T(8,128)(2,1)S(1)}, bf16[48,6144]{1,0:T(8,128)(2,1)S(1)}, u32[]{:S(2)}, u32[]{:S(2)}) collective-permute-start(bf16[48,6144]{1,0:T(8,128)(2,1)S(1)} %get-tuple-element.25), channel_id=1, source_target_pairs={{0,1},{1,0},{2,3},{3,2},{4,5},{5,4},{6,7},{7,6},{8,9},{9,8},{10,11... | collective-permute-start | bytes 1769480 | tf_op jit(solution)/shard_map/ppermute | solution.py:38
  84.1 8.5 %collective-permute-start.15 = (bf16[24,6144]{1,0:T(8,128)(2,1)S(1)}, bf16[24,6144]{1,0:T(8,128)(2,1)S(1)}, u32[]{:S(2)}, u32[]{:S(2)}) collective-permute-start(bf16[24,6144]{1,0:T(8,128)(2,1)S(1)} %get-tuple-element.30), channel_id=1, source_target_pairs={{0,1},{1,0},{2,3},{3,2},{4,5},{5,4},{6,7},{7,6},{8,9},{9,8},{10,11... | collective-permute-start | bytes 884744 | tf_op jit(solution)/shard_map/ppermute | solution.py:38
  84.5 6.5 %collective-permute-start.32 = (bf16[24,3072]{1,0:T(8,128)(2,1)S(1)}, bf16[24,3072]{1,0:T(8,128)(2,1)S(1)}, u32[]{:S(2)}, u32[]{:S(2)}) collective-permute-start(bf16[24,3072]{1,0:T(8,128)(2,1)S(1)} %hop_sum.25), channel_id=1, source_target_pairs={{0,2},{1,15},{2,4},{3,1},{4,6},{5,3},{6,8},{7,5},{8,10},{9,7},{10,... | collective-permute-start | bytes 442376 | tf_op jit(solution)/shard_map/ppermute | solution.py:51
  85.1 7.4 %collective-permute-start.29 = (bf16[24,3072]{1,0:T(8,128)(2,1)S(1)}, bf16[24,3072]{1,0:T(8,128)(2,1)S(1)}, u32[]{:S(2)}, u32[]{:S(2)}) collective-permute-start(bf16[24,3072]{1,0:T(8,128)(2,1)S(1)} %hop_sum.22), channel_id=1, source_target_pairs={{0,2},{1,15},{2,4},{3,1},{4,6},{5,3},{6,8},{7,5},{8,10},{9,7},{10,... | collective-permute-start | bytes 442376 | tf_op jit(solution)/shard_map/ppermute | solution.py:51
  85.2 8.9 %collective-permute-start.23 = (bf16[24,3072]{1,0:T(8,128)(2,1)S(1)}, bf16[24,3072]{1,0:T(8,128)(2,1)S(1)}, u32[]{:S(2)}, u32[]{:S(2)}) collective-permute-start(bf16[24,3072]{1,0:T(8,128)(2,1)S(1)} %hop_sum.18), channel_id=1, source_target_pairs={{0,2},{1,15},{2,4},{3,1},{4,6},{5,3},{6,8},{7,5},{8,10},{9,7},{10,... | collective-permute-start | bytes 442376 | tf_op jit(solution)/shard_map/ppermute | solution.py:51
  90.9 6.4 %collective-permute-start.19 = (bf16[24,3072]{1,0:T(8,128)(2,1)S(1)}, bf16[24,3072]{1,0:T(8,128)(2,1)S(1)}, u32[]{:S(2)}, u32[]{:S(2)}) collective-permute-start(bf16[24,3072]{1,0:T(8,128)(2,1)S(1)} %hop_sum.14), channel_id=1, source_target_pairs={{0,2},{1,15},{2,4},{3,1},{4,6},{5,3},{6,8},{7,5},{8,10},{9,7},{10,... | collective-permute-start | bytes 442376 | tf_op jit(solution)/shard_map/ppermute | solution.py:51
  92.5 6.4 %collective-permute-start.33 = (bf16[24,3072]{1,0:T(8,128)(2,1)S(1)}, bf16[24,3072]{1,0:T(8,128)(2,1)S(1)}, u32[]{:S(2)}, u32[]{:S(2)}) collective-permute-start(bf16[24,3072]{1,0:T(8,128)(2,1)S(1)} %hop_sum.26), channel_id=1, source_target_pairs={{0,2},{1,15},{2,4},{3,1},{4,6},{5,3},{6,8},{7,5},{8,10},{9,7},{10,... | collective-permute-start | bytes 442376 | tf_op jit(solution)/shard_map/ppermute | solution.py:51
  92.6 7.9 %collective-permute-start.30 = (bf16[24,3072]{1,0:T(8,128)(2,1)S(1)}, bf16[24,3072]{1,0:T(8,128)(2,1)S(1)}, u32[]{:S(2)}, u32[]{:S(2)}) collective-permute-start(bf16[24,3072]{1,0:T(8,128)(2,1)S(1)} %hop_sum.23), channel_id=1, source_target_pairs={{0,2},{1,15},{2,4},{3,1},{4,6},{5,3},{6,8},{7,5},{8,10},{9,7},{10,... | collective-permute-start | bytes 442376 | tf_op jit(solution)/shard_map/ppermute | solution.py:51
  94.1 7.9 %collective-permute-start.24 = (bf16[24,3072]{1,0:T(8,128)(2,1)S(1)}, bf16[24,3072]{1,0:T(8,128)(2,1)S(1)}, u32[]{:S(2)}, u32[]{:S(2)}) collective-permute-start(bf16[24,3072]{1,0:T(8,128)(2,1)S(1)} %hop_sum.19), channel_id=1, source_target_pairs={{0,2},{1,15},{2,4},{3,1},{4,6},{5,3},{6,8},{7,5},{8,10},{9,7},{10,... | collective-permute-start | bytes 442376 | tf_op jit(solution)/shard_map/ppermute | solution.py:51
  97.3 6.5 %collective-permute-start.20 = (bf16[24,3072]{1,0:T(8,128)(2,1)S(1)}, bf16[24,3072]{1,0:T(8,128)(2,1)S(1)}, u32[]{:S(2)}, u32[]{:S(2)}) collective-permute-start(bf16[24,3072]{1,0:T(8,128)(2,1)S(1)} %hop_sum.15), channel_id=1, source_target_pairs={{0,2},{1,15},{2,4},{3,1},{4,6},{5,3},{6,8},{7,5},{8,10},{9,7},{10,... | collective-permute-start | bytes 442376 | tf_op jit(solution)/shard_map/ppermute | solution.py:51
  98.9 6.5 %collective-permute-start.34 = (bf16[24,3072]{1,0:T(8,128)(2,1)S(1)}, bf16[24,3072]{1,0:T(8,128)(2,1)S(1)}, u32[]{:S(2)}, u32[]{:S(2)}) collective-permute-start(bf16[24,3072]{1,0:T(8,128)(2,1)S(1)} %hop_sum.27), channel_id=1, source_target_pairs={{0,2},{1,15},{2,4},{3,1},{4,6},{5,3},{6,8},{7,5},{8,10},{9,7},{10,... | collective-permute-start | bytes 442376 | tf_op jit(solution)/shard_map/ppermute | solution.py:51
  100.5 6.5 %collective-permute-start.31 = (bf16[24,3072]{1,0:T(8,128)(2,1)S(1)}, bf16[24,3072]{1,0:T(8,128)(2,1)S(1)}, u32[]{:S(2)}, u32[]{:S(2)}) collective-permute-start(bf16[24,3072]{1,0:T(8,128)(2,1)S(1)} %hop_sum.24), channel_id=1, source_target_pairs={{0,2},{1,15},{2,4},{3,1},{4,6},{5,3},{6,8},{7,5},{8,10},{9,7},{10,... | collective-permute-start | bytes 442376 | tf_op jit(solution)/shard_map/ppermute | solution.py:51
  102.1 6.5 %collective-permute-start.25 = (bf16[24,3072]{1,0:T(8,128)(2,1)S(1)}, bf16[24,3072]{1,0:T(8,128)(2,1)S(1)}, u32[]{:S(2)}, u32[]{:S(2)}) collective-permute-start(bf16[24,3072]{1,0:T(8,128)(2,1)S(1)} %hop_sum.20), channel_id=1, source_target_pairs={{0,2},{1,15},{2,4},{3,1},{4,6},{5,3},{6,8},{7,5},{8,10},{9,7},{10,... | collective-permute-start | bytes 442376 | tf_op jit(solution)/shard_map/ppermute | solution.py:51
  103.9 26.5 %copy-start = (s32[4,2]{0,1:T(2,128)S(1)}, s32[4,2]{0,1:T(2,128)}, u32[]{:S(2)}) copy-start(s32[4,2]{0,1:T(2,128)} %param.20) | copy-start | bytes 100
  103.9 26.5 %copy-start.1 = (f32[4,2]{0,1:T(2,128)S(1)}, f32[4,2]{0,1:T(2,128)}, u32[]{:S(2)}) copy-start(f32[4,2]{0,1:T(2,128)} %param.21) | copy-start | bytes 100
  103.9 6.5 %collective-permute-start.21 = (bf16[24,3072]{1,0:T(8,128)(2,1)S(1)}, bf16[24,3072]{1,0:T(8,128)(2,1)S(1)}, u32[]{:S(2)}, u32[]{:S(2)}) collective-permute-start(bf16[24,3072]{1,0:T(8,128)(2,1)S(1)} %hop_sum.16), channel_id=1, source_target_pairs={{0,2},{1,15},{2,4},{3,1},{4,6},{5,3},{6,8},{7,5},{8,10},{9,7},{10,... | collective-permute-start | bytes 442376 | tf_op jit(solution)/shard_map/ppermute | solution.py:51
  107.0 9.8 %collective-permute-start.35 = (bf16[24,6144]{1,0:T(8,128)(2,1)S(1)}, bf16[24,6144]{1,0:T(8,128)(2,1)S(1)}, u32[]{:S(2)}, u32[]{:S(2)}) collective-permute-start(bf16[24,6144]{1,0:T(8,128)(2,1)S(1)} %two_sum.1), channel_id=1, source_target_pairs={{0,1},{1,0},{2,3},{3,2},{4,5},{5,4},{6,7},{7,6},{8,9},{9,8},{10,11... | collective-permute-start | bytes 884744 | tf_op jit(solution)/shard_map/ppermute | solution.py:38
  108.6 6.5 %collective-permute-start.26 = (bf16[24,3072]{1,0:T(8,128)(2,1)S(1)}, bf16[24,3072]{1,0:T(8,128)(2,1)S(1)}, u32[]{:S(2)}, u32[]{:S(2)}) collective-permute-start(bf16[24,3072]{1,0:T(8,128)(2,1)S(1)} %hop_sum.21), channel_id=1, source_target_pairs={{0,2},{1,15},{2,4},{3,1},{4,6},{5,3},{6,8},{7,5},{8,10},{9,7},{10,... | collective-permute-start | bytes 442376 | tf_op jit(solution)/shard_map/ppermute | solution.py:51
  110.4 6.5 %collective-permute-start.22 = (bf16[24,3072]{1,0:T(8,128)(2,1)S(1)}, bf16[24,3072]{1,0:T(8,128)(2,1)S(1)}, u32[]{:S(2)}, u32[]{:S(2)}) collective-permute-start(bf16[24,3072]{1,0:T(8,128)(2,1)S(1)} %hop_sum.17), channel_id=1, source_target_pairs={{0,2},{1,15},{2,4},{3,1},{4,6},{5,3},{6,8},{7,5},{8,10},{9,7},{10,... | collective-permute-start | bytes 442376 | tf_op jit(solution)/shard_map/ppermute | solution.py:51

commit v5 on v3

--- a/solution.py
+++ b/solution.py
@@ -51,15 +51,36 @@
     return lax.ppermute(value, ("dev_1", "dev_2"), pairs)
 
 
-def gathered(own):
+def join_kernel(left_ref, right_ref, out_ref):
+    half = left_ref.shape[1]
+    out_ref[:, :half] = left_ref[...]
+    out_ref[:, half:] = right_ref[...]
+
+
+def joined(left, right):
+    rows, half = left.shape
+    vm = pl.BlockSpec(memory_space=pltpu.VMEM)
+    return pl.pallas_call(
+        join_kernel,
+        out_shape=jax.ShapeDtypeStruct((rows, 2 * half), left.dtype),
+        in_specs=[vm] * 2,
+        out_specs=vm,
+        compiler_params=pltpu.CompilerParams(vmem_limit_bytes=8 * 1024 * 1024),
+        name="joined",
+    )(left, right)
+
+
+def gathered(own, left, right):
     other = swapped(own)
     far = lax.axis_size("dev_1") // 2
     came, theirs = {}, {}
-    block = {0: own, 1: other}
+    sides, whole = (left, right), other
     for step in range(1, far + 1):
-        for part in (0, 1) if step < far else (0,):
-            block[part] = passed_on(block[part])
-            came[step, part] = block[part]
+        sides = [passed_on(x) for x in sides]
+        came[step, 0] = joined(*sides)
+        if step < far:
+            whole = passed_on(whole)
+            came[step, 1] = whole
         for part in (0, 1) if step < far else (0,):
             theirs[step, part] = swapped(came[step, part])
     return other, came, theirs
@@ -333,11 +354,15 @@
     )(me, following, *far)
 
 
-def unpack_kernel(came_ref, block_ref, spread):
+def unpack_kernel(came_ref, block_ref, left_ref, right_ref, spread):
     rows, width = block_ref.shape
+    half = width // 2
     spread[...] = came_ref[...].astype(jnp.float32).reshape(spread.shape)
     for j in range(width // HD):
-        block_ref[:, j * HD : (j + 1) * HD] = spread[pl.ds(j, rows, stride=width // HD), :].astype(jnp.bfloat16)
+        tile = spread[pl.ds(j, rows, stride=width // HD), :].astype(jnp.bfloat16)
+        block_ref[:, j * HD : (j + 1) * HD] = tile
+        side = left_ref if j * HD < half else right_ref
+        side[:, j * HD % half : j * HD % half + HD] = tile
 
 
 def unpacked(came):
@@ -345,9 +370,11 @@
     vm = pl.BlockSpec(memory_space=pltpu.VMEM)
     return pl.pallas_call(
         unpack_kernel,
-        out_shape=jax.ShapeDtypeStruct((places * MOST, packed // MOST * lanes), jnp.bfloat16),
+        out_shape=[
+            jax.ShapeDtypeStruct((places * MOST, packed // MOST * lanes // cut), jnp.bfloat16) for cut in (1, 2, 2)
+        ],
         in_specs=[vm],
-        out_specs=vm,
+        out_specs=[vm] * 3,
         scratch_shapes=[pltpu.VMEM((places * packed, lanes), jnp.float32)],
         compiler_params=pltpu.CompilerParams(vmem_limit_bytes=8 * 1024 * 1024),
         name="unpacked",
@@ -457,8 +484,8 @@
         norm_gain[None],
         rows_x,
     )
-    own_block = unpacked(lax.all_to_all(leaving, "dev_0", 0, 0, tiled=True))
-    other, came, theirs = gathered(own_block)
+    own_block, *own_sides = unpacked(lax.all_to_all(leaving, "dev_0", 0, 0, tiled=True))
+    other, came, theirs = gathered(own_block, *own_sides)
     far = lax.axis_size("dev_1") // 2
     each = rows_x * MOST
     near = range(far - 2, 0, -1)

time: 140 us -> 140 us (level)
    ppermute x21 -> x25, waiting for transfers between devices: 67.6 us -> 64.9 us  [passed_on(): return lax.ppermute(value, ('dev_1', 'dev_2'), pairs)]
    ppermute x13, waiting for transfers between devices: 1.8 us -> 3.35 us  [shifted(): lax.ppermute(value, axis, [(place, (place + steps) % count) for place in...]
    ppermute x21 -> x25, starting transfers between devices: 2.23 us -> 3.2 us  [passed_on(): return lax.ppermute(value, ('dev_1', 'dev_2'), pairs)]
  transfers between devices with their start and end apart: 35 -> 39, of which waited for: 23 -> 26; matrix products, arithmetic and copies ran while one was open for 0% -> 0% of each run, Pallas kernels for 5% -> 5%
where the time goes in v5:
time: 140 us; the launch traced here: 139 us
  waiting for transfers between devices  72.4 us (52%)
  blocking collectives  33.1 us (24%)
  starting transfers between devices  19.6 us (14%)
  Pallas kernels  13.9 us (10%)
    ppermute x25, waiting for transfers between devices, passed_on(): return lax.ppermute(value, ('dev_1', 'dev_2'), pairs)  64.9 us
    all_to_all x1, blocking collectives, layer(): lax.all_to_all(leaving, 'dev_0', 0, 0, tiled=True)  19.9 us
    all_to_all x1, blocking collectives, layer(): lax.all_to_all(packed_sum(*last_terms, rows_x), 'dev_0', 0, 0, tiled=True)  13.3 us
    ppermute x1, starting transfers between devices, passed_along(): lax.ppermute(value, axis, [(source, source + steps) for source in range(l...  13.1 us
    pallas_call x1, Pallas kernels, early_products(): pl.pallas_call(functools.partial(early_kernel, len(pieces)), out_shape=ou...  4.9 us
    pallas_call x1, Pallas kernels, attended(): pl.pallas_call(attend_kernel, out_shape=[jax.ShapeDtypeStruct((reqs, widt...  4.61 us
    ppermute x1, waiting for transfers between devices, passed_along(): lax.ppermute(value, axis, [(source, source + steps) for source in range(l...  4.18 us
    ppermute x13, waiting for transfers between devices, shifted(): lax.ppermute(value, axis, [(place, (place + steps) % count) for place in...  3.35 us
  transfers between devices with their start and end apart: 39, of which 26 were waited for; matrix products, arithmetic and copies ran while one was open for 0% of the time, Pallas kernels for 5%

profile of v5, /device:TPU:514, one launch (start us, length us, event | category | flops | bytes accessed | tf_op | source)
XLA Modules:
  0.0 139.4 jit_solution(11041484649841583906)
XLA Ops:
  0.0 13.1 %collective-permute-start = (bf16[64,2048]{1,0:T(8,128)(2,1)}, bf16[64,2048]{1,0:T(8,128)(2,1)S(1)}, u32[]{:S(2)}, u32[]{:S(2)}) collective-permute-start(bf16[64,2048]{1,0:T(8,128)(2,1)} %refs_7_.1), channel_id=1, source_target_pairs={{1,0},{2,1},{3,2},{4,3},{5,4},{6,5},{7,6},{8,7},{9,8},{10,9},{11,1... | collective-permute-start | bytes 786440 | tf_op jit(solution)/shard_map/ppermute | solution.py:33
  13.2 4.2 %collective-permute-done.refs_0_ = bf16[64,2048]{1,0:T(8,128)(2,1)S(1)} collective-permute-done((bf16[64,2048]{1,0:T(8,128)(2,1)}, bf16[64,2048]{1,0:T(8,128)(2,1)S(1)}, u32[]{:S(2)}, u32[]{:S(2)}) %collective-permute-start) | collective-permute-done | bytes 262176 | tf_op jit(solution)/shard_map/ppermute | solution.py:33
  17.3 4.6 %attended.1 = (f32[4,6144]{1,0:T(4,128)S(1)}, bf16[8,144,128]{2,1,0:T(8,128)(2,1)S(1)}) custom-call(s32[1]{0:T(128)} %bitcast.2.me_ref, bf16[64,2048]{1,0:T(8,128)(2,1)S(1)} %collective-permute-done.refs_0_, s32[4]{0:T(128)} %refs_1_.1, s32[2,4]{1,0:T(2,128)} %bitcast.5, s32[1,128]{1,0:T(1,128)} %bitcast.9, bf16[4,6144]{1,0:T(4,128)(2,1)} %refs_4_.1, ...), custom_call_target="tpu_custom_call" | custom-call | flops 77070336 | bytes 2097152 | tf_op jit(solution)/shard_map/attended/pallas_call | solution.py:338
  21.9 19.9 %all_to_all.10.came_ref = bf16[8,144,128]{2,1,0:T(8,128)(2,1)S(1)} all-to-all(bf16[8,144,128]{2,1,0:T(8,128)(2,1)S(1)} %get-tuple-element.24), channel_id=1, replica_groups=mesh['groups'=2,'dev_0'=8,'dev_1'=8,'dev_2'=2] {'dev_0'}, dimensions={0} | all-to-all | bytes 589824 | tf_op jit(solution)/shard_map/all_to_all | solution.py:487
  41.8 0.3 unpacked.1
  42.1 0.1 collective-permute-start.1
  42.2 1.6 %collective-permute-done.1.refs_1_ = bf16[24,6144]{1,0:T(8,128)(2,1)S(1)} collective-permute-done((bf16[24,6144]{1,0:T(8,128)(2,1)S(1)}, bf16[24,6144]{1,0:T(8,128)(2,1)S(1)}, u32[]{:S(2)}, u32[]{:S(2)}) %collective-permute-start.1) | collective-permute-done | bytes 294944 | tf_op jit(solution)/shard_map/ppermute | solution.py:38
  43.8 9.5 %collective-permute-done.2.left_ref = bf16[24,3072]{1,0:T(8,128)(2,1)S(1)} collective-permute-done((bf16[24,3072]{1,0:T(8,128)(2,1)S(1)}, bf16[24,3072]{1,0:T(8,128)(2,1)S(1)}, u32[]{:S(2)}, u32[]{:S(2)}) %collective-permute-start.2) | collective-permute-done | bytes 147488 | tf_op jit(solution)/shard_map/ppermute | solution.py:51
  53.3 1.6 %collective-permute-done.4.right_ref = bf16[24,3072]{1,0:T(8,128)(2,1)S(1)} collective-permute-done((bf16[24,3072]{1,0:T(8,128)(2,1)S(1)}, bf16[24,3072]{1,0:T(8,128)(2,1)S(1)}, u32[]{:S(2)}, u32[]{:S(2)}) %collective-permute-start.4) | collective-permute-done | bytes 147488 | tf_op jit(solution)/shard_map/ppermute | solution.py:51
  54.9 4.7 %collective-permute-done.3.left_ref = bf16[24,3072]{1,0:T(8,128)(2,1)S(1)} collective-permute-done((bf16[24,3072]{1,0:T(8,128)(2,1)S(1)}, bf16[24,3072]{1,0:T(8,128)(2,1)S(1)}, u32[]{:S(2)}, u32[]{:S(2)}) %collective-permute-start.3) | collective-permute-done | bytes 147488 | tf_op jit(solution)/shard_map/ppermute | solution.py:51
  59.7 1.6 %collective-permute-done.5.right_ref = bf16[24,3072]{1,0:T(8,128)(2,1)S(1)} collective-permute-done((bf16[24,3072]{1,0:T(8,128)(2,1)S(1)}, bf16[24,3072]{1,0:T(8,128)(2,1)S(1)}, u32[]{:S(2)}, u32[]{:S(2)}) %collective-permute-start.5) | collective-permute-done | bytes 147488 | tf_op jit(solution)/shard_map/ppermute | solution.py:51
  61.2 4.8 %collective-permute-done.13.left_ref = bf16[24,3072]{1,0:T(8,128)(2,1)S(1)} collective-permute-done((bf16[24,3072]{1,0:T(8,128)(2,1)S(1)}, bf16[24,3072]{1,0:T(8,128)(2,1)S(1)}, u32[]{:S(2)}, u32[]{:S(2)}) %collective-permute-start.13) | collective-permute-done | bytes 147488 | tf_op jit(solution)/shard_map/ppermute | solution.py:51
  66.0 1.6 %collective-permute-done.15.right_ref = bf16[24,3072]{1,0:T(8,128)(2,1)S(1)} collective-permute-done((bf16[24,3072]{1,0:T(8,128)(2,1)S(1)}, bf16[24,3072]{1,0:T(8,128)(2,1)S(1)}, u32[]{:S(2)}, u32[]{:S(2)}) %collective-permute-start.15) | collective-permute-done | bytes 147488 | tf_op jit(solution)/shard_map/ppermute | solution.py:51
  67.6 0.1 collective-permute-start.7
  67.8 0.6 collective-permute-start.6
  68.4 4.0 %collective-permute-done.14.left_ref = bf16[24,3072]{1,0:T(8,128)(2,1)S(1)} collective-permute-done((bf16[24,3072]{1,0:T(8,128)(2,1)S(1)}, bf16[24,3072]{1,0:T(8,128)(2,1)S(1)}, u32[]{:S(2)}, u32[]{:S(2)}) %collective-permute-start.14) | collective-permute-done | bytes 147488 | tf_op jit(solution)/shard_map/ppermute | solution.py:51
  72.4 1.6 %collective-permute-done.16.right_ref = bf16[24,3072]{1,0:T(8,128)(2,1)S(1)} collective-permute-done((bf16[24,3072]{1,0:T(8,128)(2,1)S(1)}, bf16[24,3072]{1,0:T(8,128)(2,1)S(1)}, u32[]{:S(2)}, u32[]{:S(2)}) %collective-permute-start.16) | collective-permute-done | bytes 147488 | tf_op jit(solution)/shard_map/ppermute | solution.py:51
  74.0 0.6 collective-permute-start.19
  74.6 0.2 collective-permute-start.20
  74.8 2.3 %collective-permute-done.17.refs_4_ = bf16[24,6144]{1,0:T(8,128)(2,1)S(1)} collective-permute-done((bf16[24,6144]{1,0:T(8,128)(2,1)S(1)}, bf16[24,6144]{1,0:T(8,128)(2,1)S(1)}, u32[]{:S(2)}, u32[]{:S(2)}) %collective-permute-start.17) | collective-permute-done | bytes 294944 | tf_op jit(solution)/shard_map/ppermute | solution.py:51
  77.1 4.9 %early.1 = (bf16[24,6144]{1,0:T(8,128)(2,1)S(1)}, bf16[24,6144]{1,0:T(8,128)(2,1)S(1)}, bf16[48,6144]{1,0:T(8,128)(2,1)S(1)}, bf16[48,6144]{1,0:T(8,128)(2,1)S(1...) custom-call(bf16[24,6144]{1,0:T(8,128)(2,1)S(1)} %get-tuple-element., ...), custom_call_target="tpu_custom_call" | custom-call | flops 2264924160 | bytes 9437184 | tf_op jit(solution)/shard_map/early/pallas_call | solution.py:206
  82.0 0.6 collective-permute-start.30
  82.7 1.7 %late.1 = (bf16[24,6144]{1,0:T(8,128)(2,1)S(1)}, bf16[24,6144]{1,0:T(8,128)(2,1)S(1)}, bf16[24,6144]{1,0:T(8,128)(2,1)S(1)}, bf16[48,6144]{1,0:T(8,128)(2,1)S(1)}, bf16[24,6144]{1,0:T(8,128)(2,1)S(1)}) custom-call(bf16[24,6144]{1,0:T(8,128)(2,1)S(1)} %joined.6.refs_0_, bf16[24,6144]{1,0:T(8,128)(2,1)S(1)} %collective-permute-done.18.refs_1_, ...), custom_call_target="tpu_custom_call" | custom-call | flops 1358954496 | bytes 9437184 | tf_op jit(solution)/shard_map/late/pallas_call | solution.py:221
  84.3 0.2 collective-permute-start.21
  84.5 0.5 collective-permute-start.31
  85.0 0.1 collective-permute-start.12
  85.1 1.8 %collective-permute-done.31.refs_1_ = bf16[24,6144]{1,0:T(8,128)(2,1)S(1)} collective-permute-done((bf16[24,6144]{1,0:T(8,128)(2,1)S(1)}, bf16[24,6144]{1,0:T(8,128)(2,1)S(1)}, u32[]{:S(2)}, u32[]{:S(2)}) %collective-permute-start.31) | collective-permute-done | bytes 294944 | tf_op jit(solution)/shard_map/ppermute | solution.py:38
  86.9 0.1 collective-permute-start.35
  87.1 0.1 collective-permute-start.32
  87.3 6.1 %collective-permute-done.35.refs_2_ = bf16[24,3072]{1,0:T(8,128)(2,1)S(1)} collective-permute-done((bf16[24,3072]{1,0:T(8,128)(2,1)S(1)}, bf16[24,3072]{1,0:T(8,128)(2,1)S(1)}, u32[]{:S(2)}, u32[]{:S(2)}) %collective-permute-start.35) | collective-permute-done | bytes 147488 | tf_op jit(solution)/shard_map/ppermute | solution.py:51
  93.4 0.1 hop_sum.26
  93.4 0.1 collective-permute-start.36
  93.6 1.4 collective-permute-done.32.refs_2_
  95.0 0.1 hop_sum.23
  95.0 0.4 collective-permute-start.33
  95.4 0.1 collective-permute-start.26
  95.6 1.2 collective-permute-start.22
  96.8 3.1 %collective-permute-done.36.refs_2_ = bf16[24,3072]{1,0:T(8,128)(2,1)S(1)} collective-permute-done((bf16[24,3072]{1,0:T(8,128)(2,1)S(1)}, bf16[24,3072]{1,0:T(8,128)(2,1)S(1)}, u32[]{:S(2)}, u32[]{:S(2)}) %collective-permute-start.36) | collective-permute-done | bytes 147488 | tf_op jit(solution)/shard_map/ppermute | solution.py:51
  99.9 0.1 hop_sum.27
  100.0 0.1 collective-permute-start.37
  100.1 1.6 %collective-permute-done.33.refs_2_ = bf16[24,3072]{1,0:T(8,128)(2,1)S(1)} collective-permute-done((bf16[24,3072]{1,0:T(8,128)(2,1)S(1)}, bf16[24,3072]{1,0:T(8,128)(2,1)S(1)}, u32[]{:S(2)}, u32[]{:S(2)}) %collective-permute-start.33) | collective-permute-done | bytes 147488 | tf_op jit(solution)/shard_map/ppermute | solution.py:51
  101.7 0.1 hop_sum.24
  101.8 0.1 collective-permute-start.34
  101.9 1.4 collective-permute-done.26.refs_2_
  103.4 0.1 collective-permute-start.27
  103.5 1.4 collective-permute-done.22.refs_2_
  104.9 0.1 collective-permute-start.23
  105.1 1.4 collective-permute-done.37.right_ref
  106.5 1.8 %collective-permute-done.34.left_ref = bf16[24,3072]{1,0:T(8,128)(2,1)S(1)} collective-permute-done((bf16[24,3072]{1,0:T(8,128)(2,1)S(1)}, bf16[24,3072]{1,0:T(8,128)(2,1)S(1)}, u32[]{:S(2)}, u32[]{:S(2)}) %collective-permute-start.34) | collective-permute-done | bytes 147488 | tf_op jit(solution)/shard_map/ppermute | solution.py:51
  108.2 0.1 two_sum.1
  108.3 0.1 collective-permute-start.38
  108.5 1.3 collective-permute-done.27.refs_2_
  109.9 0.1 collective-permute-start.28
  110.0 1.4 collective-permute-done.23.refs_2_
  111.5 0.1 collective-permute-start.24
  111.6 4.8 %collective-permute-done.28.refs_2_ = bf16[24,3072]{1,0:T(8,128)(2,1)S(1)} collective-permute-done((bf16[24,3072]{1,0:T(8,128)(2,1)S(1)}, bf16[24,3072]{1,0:T(8,128)(2,1)S(1)}, u32[]{:S(2)}, u32[]{:S(2)}) %collective-permute-start.28) | collective-permute-done | bytes 147488 | tf_op jit(solution)/shard_map/ppermute | solution.py:51
  116.4 0.1 collective-permute-start.29
  116.6 1.4 collective-permute-done.24.refs_2_
  118.0 0.1 collective-permute-start.25
  118.2 4.7 %collective-permute-done.29.right_ref = bf16[24,3072]{1,0:T(8,128)(2,1)S(1)} collective-permute-done((bf16[24,3072]{1,0:T(8,128)(2,1)S(1)}, bf16[24,3072]{1,0:T(8,128)(2,1)S(1)}, u32[]{:S(2)}, u32[]{:S(2)}) %collective-permute-start.29) | collective-permute-done | bytes 147488 | tf_op jit(solution)/shard_map/ppermute | solution.py:51
  122.9 1.6 %collective-permute-done.25.left_ref = bf16[24,3072]{1,0:T(8,128)(2,1)S(1)} collective-permute-done((bf16[24,3072]{1,0:T(8,128)(2,1)S(1)}, bf16[24,3072]{1,0:T(8,128)(2,1)S(1)}, u32[]{:S(2)}, u32[]{:S(2)}) %collective-permute-start.25) | collective-permute-done | bytes 147488 | tf_op jit(solution)/shard_map/ppermute | solution.py:51
  124.5 0.3 packed_sum.1
  124.7 13.3 %all_to_all.11.home_ref = bf16[8,144,128]{2,1,0:T(8,128)(2,1)S(1)} all-to-all(bf16[8,144,128]{2,1,0:T(8,128)(2,1)S(1)} %packed_sum.1), channel_id=1, replica_groups=mesh['groups'=2,'dev_0'=8,'dev_1'=8,'dev_2'=2] {'dev_0'}, dimensions={0} | all-to-all | bytes 589824 | tf_op jit(solution)/shard_map/all_to_all | solution.py:519
  138.0 1.4 mixed_in.1
  (45 shorter events, 0.7 us)
Async XLA Ops:
  0.0 17.3 %collective-permute-start = (bf16[64,2048]{1,0:T(8,128)(2,1)}, bf16[64,2048]{1,0:T(8,128)(2,1)S(1)}, u32[]{:S(2)}, u32[]{:S(2)}) collective-permute-start(bf16[64,2048]{1,0:T(8,128)(2,1)} %refs_7_.1), channel_id=1, source_target_pairs={{1,0},{2,1},{3,2},{4,3},{5,4},{6,5},{7,6},{8,7},{9,8},{10,9},{11,1... | collective-permute-start | bytes 786440 | tf_op jit(solution)/shard_map/ppermute | solution.py:33
  42.1 1.7 %collective-permute-start.1 = (bf16[24,6144]{1,0:T(8,128)(2,1)S(1)}, bf16[24,6144]{1,0:T(8,128)(2,1)S(1)}, u32[]{:S(2)}, u32[]{:S(2)}) collective-permute-start(bf16[24,6144]{1,0:T(8,128)(2,1)S(1)} %get-tuple-element.25.refs_0_), channel_id=1, source_target_pairs={{0,1},{1,0},{2,3},{3,2},{4,5},{5,4},{6,7},{7,6},{8,9},{9,8},{10,11... | collective-permute-start | bytes 884744 | tf_op jit(solution)/shard_map/ppermute | solution.py:38
  43.8 11.1 %collective-permute-start.8 = (bf16[24,6144]{1,0:T(8,128)(2,1)S(1)}, bf16[24,6144]{1,0:T(8,128)(2,1)S(1)}, u32[]{:S(2)}, u32[]{:S(2)}) collective-permute-start(bf16[24,6144]{1,0:T(8,128)(2,1)S(1)} %collective-permute-done.1.refs_1_), channel_id=1, source_target_pairs={{0,2},{1,15},{2,4},{3,1},{4,6},{5,3},{6,8},{7,5},{8,10},{9,7},{10,... | collective-permute-start | bytes 884744 | tf_op jit(solution)/shard_map/ppermute | solution.py:51
  43.8 9.5 %collective-permute-start.2 = (bf16[24,3072]{1,0:T(8,128)(2,1)S(1)}, bf16[24,3072]{1,0:T(8,128)(2,1)S(1)}, u32[]{:S(2)}, u32[]{:S(2)}) collective-permute-start(bf16[24,3072]{1,0:T(8,128)(2,1)S(1)} %get-tuple-element.26), channel_id=1, source_target_pairs={{0,2},{1,15},{2,4},{3,1},{4,6},{5,3},{6,8},{7,5},{8,10},{9,7},{10,... | collective-permute-start | bytes 442376 | tf_op jit(solution)/shard_map/ppermute | solution.py:51
  43.8 11.1 %collective-permute-start.4 = (bf16[24,3072]{1,0:T(8,128)(2,1)S(1)}, bf16[24,3072]{1,0:T(8,128)(2,1)S(1)}, u32[]{:S(2)}, u32[]{:S(2)}) collective-permute-start(bf16[24,3072]{1,0:T(8,128)(2,1)S(1)} %get-tuple-element.27), channel_id=1, source_target_pairs={{0,2},{1,15},{2,4},{3,1},{4,6},{5,3},{6,8},{7,5},{8,10},{9,7},{10,... | collective-permute-start | bytes 442376 | tf_op jit(solution)/shard_map/ppermute | solution.py:51
  53.3 6.4 %collective-permute-start.3 = (bf16[24,3072]{1,0:T(8,128)(2,1)S(1)}, bf16[24,3072]{1,0:T(8,128)(2,1)S(1)}, u32[]{:S(2)}, u32[]{:S(2)}) collective-permute-start(bf16[24,3072]{1,0:T(8,128)(2,1)S(1)} %collective-permute-done.2.left_ref), channel_id=1, source_target_pairs={{0,2},{1,15},{2,4},{3,1},{4,6},{5,3},{6,8},{7,5},{8,10},{9,7},{10,... | collective-permute-start | bytes 442376 | tf_op jit(solution)/shard_map/ppermute | solution.py:51
  54.9 6.4 %collective-permute-start.5 = (bf16[24,3072]{1,0:T(8,128)(2,1)S(1)}, bf16[24,3072]{1,0:T(8,128)(2,1)S(1)}, u32[]{:S(2)}, u32[]{:S(2)}) collective-permute-start(bf16[24,3072]{1,0:T(8,128)(2,1)S(1)} %collective-permute-done.4.right_ref), channel_id=1, source_target_pairs={{0,2},{1,15},{2,4},{3,1},{4,6},{5,3},{6,8},{7,5},{8,10},{9,7},{10,... | collective-permute-start | bytes 442376 | tf_op jit(solution)/shard_map/ppermute | solution.py:51
  54.9 13.5 %collective-permute-start.9 = (bf16[24,6144]{1,0:T(8,128)(2,1)S(1)}, bf16[24,6144]{1,0:T(8,128)(2,1)S(1)}, u32[]{:S(2)}, u32[]{:S(2)}) collective-permute-start(bf16[24,6144]{1,0:T(8,128)(2,1)S(1)} %collective-permute-done.8.refs_9_), channel_id=1, source_target_pairs={{0,2},{1,15},{2,4},{3,1},{4,6},{5,3},{6,8},{7,5},{8,10},{9,7},{10,... | collective-permute-start | bytes 884744 | tf_op jit(solution)/shard_map/ppermute | solution.py:51
  59.6 6.4 %collective-permute-start.13 = (bf16[24,3072]{1,0:T(8,128)(2,1)S(1)}, bf16[24,3072]{1,0:T(8,128)(2,1)S(1)}, u32[]{:S(2)}, u32[]{:S(2)}) collective-permute-start(bf16[24,3072]{1,0:T(8,128)(2,1)S(1)} %collective-permute-done.3.left_ref), channel_id=1, source_target_pairs={{0,2},{1,15},{2,4},{3,1},{4,6},{5,3},{6,8},{7,5},{8,10},{9,7},{10,... | collective-permute-start | bytes 442376 | tf_op jit(solution)/shard_map/ppermute | solution.py:51
  61.2 6.4 %collective-permute-start.15 = (bf16[24,3072]{1,0:T(8,128)(2,1)S(1)}, bf16[24,3072]{1,0:T(8,128)(2,1)S(1)}, u32[]{:S(2)}, u32[]{:S(2)}) collective-permute-start(bf16[24,3072]{1,0:T(8,128)(2,1)S(1)} %collective-permute-done.5.right_ref), channel_id=1, source_target_pairs={{0,2},{1,15},{2,4},{3,1},{4,6},{5,3},{6,8},{7,5},{8,10},{9,7},{10,... | collective-permute-start | bytes 442376 | tf_op jit(solution)/shard_map/ppermute | solution.py:51
  66.0 6.4 %collective-permute-start.14 = (bf16[24,3072]{1,0:T(8,128)(2,1)S(1)}, bf16[24,3072]{1,0:T(8,128)(2,1)S(1)}, u32[]{:S(2)}, u32[]{:S(2)}) collective-permute-start(bf16[24,3072]{1,0:T(8,128)(2,1)S(1)} %collective-permute-done.13.left_ref), channel_id=1, source_target_pairs={{0,2},{1,15},{2,4},{3,1},{4,6},{5,3},{6,8},{7,5},{8,10},{9,7},{10,... | collective-permute-start | bytes 442376 | tf_op jit(solution)/shard_map/ppermute | solution.py:51
  67.6 6.4 %collective-permute-start.16 = (bf16[24,3072]{1,0:T(8,128)(2,1)S(1)}, bf16[24,3072]{1,0:T(8,128)(2,1)S(1)}, u32[]{:S(2)}, u32[]{:S(2)}) collective-permute-start(bf16[24,3072]{1,0:T(8,128)(2,1)S(1)} %collective-permute-done.15.right_ref), channel_id=1, source_target_pairs={{0,2},{1,15},{2,4},{3,1},{4,6},{5,3},{6,8},{7,5},{8,10},{9,7},{10,... | collective-permute-start | bytes 442376 | tf_op jit(solution)/shard_map/ppermute | solution.py:51
  67.6 6.4 %collective-permute-start.7 = (bf16[24,6144]{1,0:T(8,128)(2,1)S(1)}, bf16[24,6144]{1,0:T(8,128)(2,1)S(1)}, u32[]{:S(2)}, u32[]{:S(2)}) collective-permute-start(bf16[24,6144]{1,0:T(8,128)(2,1)S(1)} %joined.5.refs_7_), channel_id=1, source_target_pairs={{0,1},{1,0},{2,3},{3,2},{4,5},{5,4},{6,7},{7,6},{8,9},{9,8},{10,11... | collective-permute-start | bytes 884744 | tf_op jit(solution)/shard_map/ppermute | solution.py:38
  67.8 6.8 %collective-permute-start.6 = (bf16[24,6144]{1,0:T(8,128)(2,1)S(1)}, bf16[24,6144]{1,0:T(8,128)(2,1)S(1)}, u32[]{:S(2)}, u32[]{:S(2)}) collective-permute-start(bf16[24,6144]{1,0:T(8,128)(2,1)S(1)} %joined.4.refs_6_), channel_id=1, source_target_pairs={{0,1},{1,0},{2,3},{3,2},{4,5},{5,4},{6,7},{7,6},{8,9},{9,8},{10,11... | collective-permute-start | bytes 884744 | tf_op jit(solution)/shard_map/ppermute | solution.py:38
  68.4 8.7 %collective-permute-start.17 = (bf16[24,6144]{1,0:T(8,128)(2,1)S(1)}, bf16[24,6144]{1,0:T(8,128)(2,1)S(1)}, u32[]{:S(2)}, u32[]{:S(2)}) collective-permute-start(bf16[24,6144]{1,0:T(8,128)(2,1)S(1)} %collective-permute-done.9.refs_8_), channel_id=1, source_target_pairs={{0,2},{1,15},{2,4},{3,1},{4,6},{5,3},{6,8},{7,5},{8,10},{9,7},{10,... | collective-permute-start | bytes 884744 | tf_op jit(solution)/shard_map/ppermute | solution.py:51
  72.4 4.7 %collective-permute-start.11 = (bf16[24,6144]{1,0:T(8,128)(2,1)S(1)}, bf16[24,6144]{1,0:T(8,128)(2,1)S(1)}, u32[]{:S(2)}, u32[]{:S(2)}) collective-permute-start(bf16[24,6144]{1,0:T(8,128)(2,1)S(1)} %collective-permute-done.8.refs_9_), channel_id=1, source_target_pairs={{0,1},{1,0},{2,3},{3,2},{4,5},{5,4},{6,7},{7,6},{8,9},{9,8},{10,11... | collective-permute-start | bytes 884744 | tf_op jit(solution)/shard_map/ppermute | solution.py:38
  73.9 3.2 %collective-permute-start.10 = (bf16[24,6144]{1,0:T(8,128)(2,1)S(1)}, bf16[24,6144]{1,0:T(8,128)(2,1)S(1)}, u32[]{:S(2)}, u32[]{:S(2)}) collective-permute-start(bf16[24,6144]{1,0:T(8,128)(2,1)S(1)} %collective-permute-done.9.refs_8_), channel_id=1, source_target_pairs={{0,1},{1,0},{2,3},{3,2},{4,5},{5,4},{6,7},{7,6},{8,9},{9,8},{10,11... | collective-permute-start | bytes 884744 | tf_op jit(solution)/shard_map/ppermute | solution.py:38
  74.0 8.6 %collective-permute-start.19 = (bf16[24,6144]{1,0:T(8,128)(2,1)S(1)}, bf16[24,6144]{1,0:T(8,128)(2,1)S(1)}, u32[]{:S(2)}, u32[]{:S(2)}) collective-permute-start(bf16[24,6144]{1,0:T(8,128)(2,1)S(1)} %joined.7.refs_5_), channel_id=1, source_target_pairs={{0,1},{1,0},{2,3},{3,2},{4,5},{5,4},{6,7},{7,6},{8,9},{9,8},{10,11... | collective-permute-start | bytes 884744 | tf_op jit(solution)/shard_map/ppermute | solution.py:38
  74.6 8.0 %collective-permute-start.20 = (bf16[24,6144]{1,0:T(8,128)(2,1)S(1)}, bf16[24,6144]{1,0:T(8,128)(2,1)S(1)}, u32[]{:S(2)}, u32[]{:S(2)}) collective-permute-start(bf16[24,6144]{1,0:T(8,128)(2,1)S(1)} %joined.6.refs_0_), channel_id=1, source_target_pairs={{0,1},{1,0},{2,3},{3,2},{4,5},{5,4},{6,7},{7,6},{8,9},{9,8},{10,11... | collective-permute-start | bytes 884744 | tf_op jit(solution)/shard_map/ppermute | solution.py:38
  77.1 5.5 %collective-permute-start.18 = (bf16[24,6144]{1,0:T(8,128)(2,1)S(1)}, bf16[24,6144]{1,0:T(8,128)(2,1)S(1)}, u32[]{:S(2)}, u32[]{:S(2)}) collective-permute-start(bf16[24,6144]{1,0:T(8,128)(2,1)S(1)} %collective-permute-done.17.refs_4_), channel_id=1, source_target_pairs={{0,1},{1,0},{2,3},{3,2},{4,5},{5,4},{6,7},{7,6},{8,9},{9,8},{10,11... | collective-permute-start | bytes 884744 | tf_op jit(solution)/shard_map/ppermute | solution.py:38
  82.0 5.2 %collective-permute-start.30 = (bf16[48,6144]{1,0:T(8,128)(2,1)S(1)}, bf16[48,6144]{1,0:T(8,128)(2,1)S(1)}, u32[]{:S(2)}, u32[]{:S(2)}) collective-permute-start(bf16[48,6144]{1,0:T(8,128)(2,1)S(1)} %get-tuple-element.39), channel_id=1, source_target_pairs={{0,1},{1,0},{2,3},{3,2},{4,5},{5,4},{6,7},{7,6},{8,9},{9,8},{10,11... | collective-permute-start | bytes 1769480 | tf_op jit(solution)/shard_map/ppermute | solution.py:38
  84.3 11.1 %collective-permute-start.21 = (bf16[48,6144]{1,0:T(8,128)(2,1)S(1)}, bf16[48,6144]{1,0:T(8,128)(2,1)S(1)}, u32[]{:S(2)}, u32[]{:S(2)}) collective-permute-start(bf16[48,6144]{1,0:T(8,128)(2,1)S(1)} %get-tuple-element.35), channel_id=1, source_target_pairs={{0,1},{1,0},{2,3},{3,2},{4,5},{5,4},{6,7},{7,6},{8,9},{9,8},{10,11... | collective-permute-start | bytes 1769480 | tf_op jit(solution)/shard_map/ppermute | solution.py:38
  84.5 2.4 %collective-permute-start.31 = (bf16[24,6144]{1,0:T(8,128)(2,1)S(1)}, bf16[24,6144]{1,0:T(8,128)(2,1)S(1)}, u32[]{:S(2)}, u32[]{:S(2)}) collective-permute-start(bf16[24,6144]{1,0:T(8,128)(2,1)S(1)} %get-tuple-element.41), channel_id=1, source_target_pairs={{0,1},{1,0},{2,3},{3,2},{4,5},{5,4},{6,7},{7,6},{8,9},{9,8},{10,11... | collective-permute-start | bytes 884744 | tf_op jit(solution)/shard_map/ppermute | solution.py:38
  85.0 23.5 %collective-permute-start.12 = (bf16[48,6144]{1,0:T(8,128)(2,1)S(1)}, bf16[48,6144]{1,0:T(8,128)(2,1)S(1)}, u32[]{:S(2)}, u32[]{:S(2)}) collective-permute-start(bf16[48,6144]{1,0:T(8,128)(2,1)S(1)} %get-tuple-element.30), channel_id=1, source_target_pairs={{0,1},{1,0},{2,3},{3,2},{4,5},{5,4},{6,7},{7,6},{8,9},{9,8},{10,11... | collective-permute-start | bytes 1769480 | tf_op jit(solution)/shard_map/ppermute | solution.py:38
  86.9 6.5 %collective-permute-start.35 = (bf16[24,3072]{1,0:T(8,128)(2,1)S(1)}, bf16[24,3072]{1,0:T(8,128)(2,1)S(1)}, u32[]{:S(2)}, u32[]{:S(2)}) collective-permute-start(bf16[24,3072]{1,0:T(8,128)(2,1)S(1)} %hop_sum.25), channel_id=1, source_target_pairs={{0,2},{1,15},{2,4},{3,1},{4,6},{5,3},{6,8},{7,5},{8,10},{9,7},{10,... | collective-permute-start | bytes 442376 | tf_op jit(solution)/shard_map/ppermute | solution.py:51
  87.1 7.9 %collective-permute-start.32 = (bf16[24,3072]{1,0:T(8,128)(2,1)S(1)}, bf16[24,3072]{1,0:T(8,128)(2,1)S(1)}, u32[]{:S(2)}, u32[]{:S(2)}) collective-permute-start(bf16[24,3072]{1,0:T(8,128)(2,1)S(1)} %hop_sum.22), channel_id=1, source_target_pairs={{0,2},{1,15},{2,4},{3,1},{4,6},{5,3},{6,8},{7,5},{8,10},{9,7},{10,... | collective-permute-start | bytes 442376 | tf_op jit(solution)/shard_map/ppermute | solution.py:51
  93.4 6.5 %collective-permute-start.36 = (bf16[24,3072]{1,0:T(8,128)(2,1)S(1)}, bf16[24,3072]{1,0:T(8,128)(2,1)S(1)}, u32[]{:S(2)}, u32[]{:S(2)}) collective-permute-start(bf16[24,3072]{1,0:T(8,128)(2,1)S(1)} %hop_sum.26), channel_id=1, source_target_pairs={{0,2},{1,15},{2,4},{3,1},{4,6},{5,3},{6,8},{7,5},{8,10},{9,7},{10,... | collective-permute-start | bytes 442376 | tf_op jit(solution)/shard_map/ppermute | solution.py:51
  95.0 6.7 %collective-permute-start.33 = (bf16[24,3072]{1,0:T(8,128)(2,1)S(1)}, bf16[24,3072]{1,0:T(8,128)(2,1)S(1)}, u32[]{:S(2)}, u32[]{:S(2)}) collective-permute-start(bf16[24,3072]{1,0:T(8,128)(2,1)S(1)} %hop_sum.23), channel_id=1, source_target_pairs={{0,2},{1,15},{2,4},{3,1},{4,6},{5,3},{6,8},{7,5},{8,10},{9,7},{10,... | collective-permute-start | bytes 442376 | tf_op jit(solution)/shard_map/ppermute | solution.py:51
  95.4 7.9 %collective-permute-start.26 = (bf16[24,3072]{1,0:T(8,128)(2,1)S(1)}, bf16[24,3072]{1,0:T(8,128)(2,1)S(1)}, u32[]{:S(2)}, u32[]{:S(2)}) collective-permute-start(bf16[24,3072]{1,0:T(8,128)(2,1)S(1)} %hop_sum.18), channel_id=1, source_target_pairs={{0,2},{1,15},{2,4},{3,1},{4,6},{5,3},{6,8},{7,5},{8,10},{9,7},{10,... | collective-permute-start | bytes 442376 | tf_op jit(solution)/shard_map/ppermute | solution.py:51
  95.6 9.2 %collective-permute-start.22 = (bf16[24,3072]{1,0:T(8,128)(2,1)S(1)}, bf16[24,3072]{1,0:T(8,128)(2,1)S(1)}, u32[]{:S(2)}, u32[]{:S(2)}) collective-permute-start(bf16[24,3072]{1,0:T(8,128)(2,1)S(1)} %hop_sum.14), channel_id=1, source_target_pairs={{0,2},{1,15},{2,4},{3,1},{4,6},{5,3},{6,8},{7,5},{8,10},{9,7},{10,... | collective-permute-start | bytes 442376 | tf_op jit(solution)/shard_map/ppermute | solution.py:51
  100.0 6.5 %collective-permute-start.37 = (bf16[24,3072]{1,0:T(8,128)(2,1)S(1)}, bf16[24,3072]{1,0:T(8,128)(2,1)S(1)}, u32[]{:S(2)}, u32[]{:S(2)}) collective-permute-start(bf16[24,3072]{1,0:T(8,128)(2,1)S(1)} %hop_sum.27), channel_id=1, source_target_pairs={{0,2},{1,15},{2,4},{3,1},{4,6},{5,3},{6,8},{7,5},{8,10},{9,7},{10,... | collective-permute-start | bytes 442376 | tf_op jit(solution)/shard_map/ppermute | solution.py:51
  101.8 6.5 %collective-permute-start.34 = (bf16[24,3072]{1,0:T(8,128)(2,1)S(1)}, bf16[24,3072]{1,0:T(8,128)(2,1)S(1)}, u32[]{:S(2)}, u32[]{:S(2)}) collective-permute-start(bf16[24,3072]{1,0:T(8,128)(2,1)S(1)} %hop_sum.24), channel_id=1, source_target_pairs={{0,2},{1,15},{2,4},{3,1},{4,6},{5,3},{6,8},{7,5},{8,10},{9,7},{10,... | collective-permute-start | bytes 442376 | tf_op jit(solution)/shard_map/ppermute | solution.py:51
  103.4 6.5 %collective-permute-start.27 = (bf16[24,3072]{1,0:T(8,128)(2,1)S(1)}, bf16[24,3072]{1,0:T(8,128)(2,1)S(1)}, u32[]{:S(2)}, u32[]{:S(2)}) collective-permute-start(bf16[24,3072]{1,0:T(8,128)(2,1)S(1)} %hop_sum.19), channel_id=1, source_target_pairs={{0,2},{1,15},{2,4},{3,1},{4,6},{5,3},{6,8},{7,5},{8,10},{9,7},{10,... | collective-permute-start | bytes 442376 | tf_op jit(solution)/shard_map/ppermute | solution.py:51
  104.9 6.5 %collective-permute-start.23 = (bf16[24,3072]{1,0:T(8,128)(2,1)S(1)}, bf16[24,3072]{1,0:T(8,128)(2,1)S(1)}, u32[]{:S(2)}, u32[]{:S(2)}) collective-permute-start(bf16[24,3072]{1,0:T(8,128)(2,1)S(1)} %hop_sum.15), channel_id=1, source_target_pairs={{0,2},{1,15},{2,4},{3,1},{4,6},{5,3},{6,8},{7,5},{8,10},{9,7},{10,... | collective-permute-start | bytes 442376 | tf_op jit(solution)/shard_map/ppermute | solution.py:51
  108.3 9.8 %collective-permute-start.38 = (bf16[24,6144]{1,0:T(8,128)(2,1)S(1)}, bf16[24,6144]{1,0:T(8,128)(2,1)S(1)}, u32[]{:S(2)}, u32[]{:S(2)}) collective-permute-start(bf16[24,6144]{1,0:T(8,128)(2,1)S(1)} %two_sum.1), channel_id=1, source_target_pairs={{0,1},{1,0},{2,3},{3,2},{4,5},{5,4},{6,7},{7,6},{8,9},{9,8},{10,11... | collective-permute-start | bytes 884744 | tf_op jit(solution)/shard_map/ppermute | solution.py:38
  109.9 28.1 %copy-start = (s32[4,2]{0,1:T(2,128)S(1)}, s32[4,2]{0,1:T(2,128)}, u32[]{:S(2)}) copy-start(s32[4,2]{0,1:T(2,128)} %param.20) | copy-start | bytes 100
  109.9 28.1 %copy-start.1 = (f32[4,2]{0,1:T(2,128)S(1)}, f32[4,2]{0,1:T(2,128)}, u32[]{:S(2)}) copy-start(f32[4,2]{0,1:T(2,128)} %param.21) | copy-start | bytes 100
  109.9 6.5 %collective-permute-start.28 = (bf16[24,3072]{1,0:T(8,128)(2,1)S(1)}, bf16[24,3072]{1,0:T(8,128)(2,1)S(1)}, u32[]{:S(2)}, u32[]{:S(2)}) collective-permute-start(bf16[24,3072]{1,0:T(8,128)(2,1)S(1)} %hop_sum.20), channel_id=1, source_target_pairs={{0,2},{1,15},{2,4},{3,1},{4,6},{5,3},{6,8},{7,5},{8,10},{9,7},{10,... | collective-permute-start | bytes 442376 | tf_op jit(solution)/shard_map/ppermute | solution.py:51
  111.5 6.5 %collective-permute-start.24 = (bf16[24,3072]{1,0:T(8,128)(2,1)S(1)}, bf16[24,3072]{1,0:T(8,128)(2,1)S(1)}, u32[]{:S(2)}, u32[]{:S(2)}) collective-permute-start(bf16[24,3072]{1,0:T(8,128)(2,1)S(1)} %hop_sum.16), channel_id=1, source_target_pairs={{0,2},{1,15},{2,4},{3,1},{4,6},{5,3},{6,8},{7,5},{8,10},{9,7},{10,... | collective-permute-start | bytes 442376 | tf_op jit(solution)/shard_map/ppermute | solution.py:51
  116.4 6.5 %collective-permute-start.29 = (bf16[24,3072]{1,0:T(8,128)(2,1)S(1)}, bf16[24,3072]{1,0:T(8,128)(2,1)S(1)}, u32[]{:S(2)}, u32[]{:S(2)}) collective-permute-start(bf16[24,3072]{1,0:T(8,128)(2,1)S(1)} %hop_sum.21), channel_id=1, source_target_pairs={{0,2},{1,15},{2,4},{3,1},{4,6},{5,3},{6,8},{7,5},{8,10},{9,7},{10,... | collective-permute-start | bytes 442376 | tf_op jit(solution)/shard_map/ppermute | solution.py:51
  118.0 6.5 %collective-permute-start.25 = (bf16[24,3072]{1,0:T(8,128)(2,1)S(1)}, bf16[24,3072]{1,0:T(8,128)(2,1)S(1)}, u32[]{:S(2)}, u32[]{:S(2)}) collective-permute-start(bf16[24,3072]{1,0:T(8,128)(2,1)S(1)} %hop_sum.17), channel_id=1, source_target_pairs={{0,2},{1,15},{2,4},{3,1},{4,6},{5,3},{6,8},{7,5},{8,10},{9,7},{10,... | collective-permute-start | bytes 442376 | tf_op jit(solution)/shard_map/ppermute | solution.py:51

commit v6 on v5

--- a/solution.py
+++ b/solution.py
@@ -140,20 +140,18 @@
     )(whole, left, right)
 
 
-def multiplied(pieces, gate, up, down, outs, ready):
+def multiplied(pieces, gate, up, down, outs):
     depth = gate.shape[0] // CUT_K
     span = down.shape[1] // CUT_N
     gate_v = up_v = None
     for k in range(CUT_K):
         cols = pl.ds(k * depth, depth)
         x = jnp.concatenate([p[:, cols] for p in pieces], 0)
-        ready(k)
         g = jnp.dot(x, gate[cols, :], preferred_element_type=jnp.float32)
         u = jnp.dot(x, up[cols, :], preferred_element_type=jnp.float32)
         gate_v = g if gate_v is None else gate_v + g
         up_v = u if up_v is None else up_v + u
     act = (gate_v / (1.0 + jnp.exp(-gate_v)) * up_v).astype(jnp.bfloat16)
-    ready(CUT_K)
     for n in range(CUT_N):
         cols = pl.ds(n * span, span)
         part = jnp.dot(act, down[:, cols], preferred_element_type=jnp.float32).astype(jnp.bfloat16)
@@ -164,68 +162,47 @@
             at += rows
 
 
-def early_kernel(count, *refs):
-    pieces, (gate_far, up_far, down_far) = refs[:count], refs[count : count + 3]
-    outs, (gate, up, down, sems) = refs[count + 3 : -4], refs[-4:]
-    depth = gate.shape[0] // CUT_K
-    copies = []
-    for k in range(CUT_K):
-        rows = pl.ds(k * depth, depth)
-        copies.append(
-            (
-                pltpu.make_async_copy(gate_far.at[rows], gate.at[rows], sems.at[2 * k]),
-                pltpu.make_async_copy(up_far.at[rows], up.at[rows], sems.at[2 * k + 1]),
-            )
-        )
-    copies.append((pltpu.make_async_copy(down_far, down, sems.at[2 * CUT_K]),))
-    for group in copies:
-        for copy in group:
-            copy.start()
-
-    def ready(k):
-        for copy in copies[k]:
-            copy.wait()
-
-    multiplied(pieces, gate, up, down, outs, ready)
-
-
-def late_kernel(count, *refs):
-    multiplied(refs[:count], *refs[count : count + 3], refs[count + 3 :], lambda k: None)
+def hold_kernel(*refs):
+    count = len(refs) // 2
+    copies = [pltpu.make_async_copy(refs[i], refs[count + i], refs[-1].at[i]) for i in range(count)]
+    for copy in copies:
+        copy.start()
+    for copy in copies:
+        copy.wait()
+
+
+def held(weights):
+    return pl.pallas_call(
+        hold_kernel,
+        out_shape=[pltpu.VMEM(w.shape, w.dtype) for w in weights],
+        in_specs=[pl.BlockSpec(memory_space=pltpu.HBM)] * len(weights),
+        out_specs=[pl.BlockSpec(memory_space=pltpu.VMEM)] * len(weights),
+        scratch_shapes=[pltpu.SemaphoreType.DMA((len(weights),))],
+        compiler_params=pltpu.CompilerParams(vmem_limit_bytes=16 * 1024 * 1024),
+        cost_estimate=pl.CostEstimate(flops=1 << 20, bytes_accessed=2 * sum(w.size for w in weights), transcendentals=0),
+        name="held",
+    )(*[pltpu.with_memory_space_constraint(w, pltpu.HBM) for w in weights])
+
+
+def product_kernel(count, *refs):
+    multiplied(refs[:count], *refs[count : count + 3], refs[count + 3 :])
 
 
 def product_cost(rows, width, hidden):
     return pl.CostEstimate(flops=6 * rows * width * hidden, bytes_accessed=6 * width * hidden, transcendentals=rows * hidden)
 
 
-def early_products(pieces, weights, sizes):
+def products(pieces, weights, sizes):
     width, hidden = weights[0].shape
     vm = pl.BlockSpec(memory_space=pltpu.VMEM)
-    far = pl.BlockSpec(memory_space=pltpu.HBM)
-    outs = [jax.ShapeDtypeStruct((s, width), jnp.bfloat16) for s in sizes]
-    held = [pltpu.VMEM(w.shape, w.dtype) for w in weights]
-    return pl.pallas_call(
-        functools.partial(early_kernel, len(pieces)),
-        out_shape=outs + held,
-        in_specs=[vm] * len(pieces) + [far] * 3,
-        out_specs=[vm] * (len(sizes) + 3),
-        scratch_shapes=[pltpu.SemaphoreType.DMA((2 * CUT_K + 1,))],
-        compiler_params=pltpu.CompilerParams(vmem_limit_bytes=24 * 1024 * 1024),
-        cost_estimate=product_cost(sum(sizes), width, hidden),
-        name="early",
-    )(*pieces, *[pltpu.with_memory_space_constraint(w, pltpu.HBM) for w in weights])
-
-
-def late_products(pieces, weights, sizes):
-    width, hidden = weights[0].shape
-    vm = pl.BlockSpec(memory_space=pltpu.VMEM)
-    return pl.pallas_call(
-        functools.partial(late_kernel, len(pieces)),
+    return pl.pallas_call(
+        functools.partial(product_kernel, len(pieces)),
         out_shape=[jax.ShapeDtypeStruct((s, width), jnp.bfloat16) for s in sizes],
         in_specs=[vm] * (len(pieces) + 3),
         out_specs=[vm] * len(sizes),
         compiler_params=pltpu.CompilerParams(vmem_limit_bytes=24 * 1024 * 1024),
         cost_estimate=product_cost(sum(sizes), width, hidden),
-        name="late",
+        name="products",
     )(*pieces, *weights)
 
 
@@ -244,7 +221,7 @@
     next_ref = refs[0]
     far_refs, (hidden_ref, leaving_ref, turned, mixed, packed), near_refs = refs[1:10], refs[10:15], refs[15:24]
     copies = [pltpu.make_async_copy(f, n, refs[24].at[i]) for i, (f, n) in enumerate(zip(far_refs, near_refs))]
-    for copy in copies:
+    for copy in copies[5:7] + copies[:5] + copies[7:]:
         copy.start()
     lens_ref, ids_ref, counts_ref, query_ref, own_ref, cache_ref, fresh_ref, tokens_ref, gain_ref = near_refs
     reqs, width = tokens_ref.shape
@@ -256,7 +233,7 @@
     scale = 1.0 / math.sqrt(HD)
     me = me_ref[0]
     f32 = jnp.float32
-    for copy in copies:
+    for copy in copies[:5]:
         copy.wait()
     for h in range(QH):
         turned[h * reqs : (h + 1) * reqs, :] = query_ref[:, h * HD : (h + 1) * HD].astype(f32)
@@ -274,6 +251,8 @@
     live_c = (row_c < 0)
     for r in range(reqs):
         live_c = live_c | ((row_c == r) & (col_c >= r * length) & (col_c < r * length + lens_ref[r]))
+    for copy in copies[5:7]:
+        copy.wait()
     for g in range(KVH):
         k_at = slice(g * HD, (g + 1) * HD)
         v_at = slice(half + g * HD, half + (g + 1) * HD)
@@ -302,6 +281,8 @@
         val_w = jnp.concatenate([fresh_ref[:, v_at], next_ref[:, v_at]], 0)
         out = jnp.dot(p_c, val_c, preferred_element_type=f32) + jnp.dot(p_w, val_w, preferred_element_type=f32)
         mixed[g * rows : (g + 1) * rows, :] = out + p_o * val_o
+    for copy in copies[7:]:
+        copy.wait()
     squares = jnp.zeros((reqs, HD), f32)
     for h in range(QH):
         cols = slice(h * HD, (h + 1) * HD)
@@ -493,9 +474,8 @@
     for group in (theirs, came):
         for part in (0, 1):
             pieces += [group[step, part] for step in near]
-    home_own, home_other, *groups, gate, up, down = early_products(
-        pieces, (w_gate, w_up, w_down), [each, each] + [len(near) * each] * 4
-    )
+    weights = held((w_gate, w_up, w_down))
+    home_own, home_other, *groups = products(pieces, weights, [each, each] + [len(near) * each] * 4)
     last = far - 1
     pieces = [
         came[far, 0],
@@ -511,7 +491,7 @@
         for i, step in enumerate(near):
             kept[step, part] = (groups[part], i * each)
             got[step, part] = (sent[part], i * each)
-    *stay, sent_1, sent_0 = late_products(pieces, (gate, up, down), [each, each, each, 2 * each, each])
+    *stay, sent_1, sent_0 = products(pieces, weights, [each, each, each, 2 * each, each])
     kept[far, 1], kept[last, 1], kept[last, 0] = [(x, 0) for x in stay]
     first = swapped(sent_1)
     got[far, 1], got[last, 1], got[last, 0] = (first, 0), (first, each), (swapped(sent_0), 0)

time: 140 us -> 141 us (level)
  Pallas kernels: 13.9 us -> 15.4 us
    pallas_call x2 -> x3, Pallas kernels: 6.57 us -> 8.02 us  [the longest x2 4.24 us: products(): pl.pallas_call(functools.partial(product_kernel, len(pieces)), out_shape=...]
  transfers between devices with their start and end apart: 39 -> 39, of which waited for: 26 -> 26; matrix products, arithmetic and copies ran while one was open for 0% -> 0% of each run, Pallas kernels for 5% -> 6%
where the time goes in v6:
time: 141 us
  waiting for transfers between devices  72.4 us (51%)
  blocking collectives  33.1 us (23%)
  starting transfers between devices  19.6 us (14%)
  Pallas kernels  15.4 us (11%)
    ppermute x25, waiting for transfers between devices, passed_on(): return lax.ppermute(value, ('dev_1', 'dev_2'), pairs)  64.9 us
    all_to_all x1, blocking collectives, layer(): lax.all_to_all(leaving, 'dev_0', 0, 0, tiled=True)  19.9 us
    all_to_all x1, blocking collectives, layer(): lax.all_to_all(packed_sum(*last_terms, rows_x), 'dev_0', 0, 0, tiled=True)  13.3 us
    ppermute x1, starting transfers between devices, passed_along(): lax.ppermute(value, axis, [(source, source + steps) for source in range(l...  13.1 us
    pallas_call x1, Pallas kernels, attended(): pl.pallas_call(attend_kernel, out_shape=[jax.ShapeDtypeStruct((reqs, widt...  4.64 us
    pallas_call x2, Pallas kernels, products(): pl.pallas_call(functools.partial(product_kernel, len(pieces)), out_shape=...  4.24 us
    ppermute x1, waiting for transfers between devices, passed_along(): lax.ppermute(value, axis, [(source, source + steps) for source in range(l...  4.18 us
    pallas_call x1, Pallas kernels, held(): pl.pallas_call(hold_kernel, out_shape=[pltpu.VMEM(w.shape, w.dtype) for w...  3.78 us
  transfers between devices with their start and end apart: 39, of which 26 were waited for; matrix products, arithmetic and copies ran while one was open for 0% of the time, Pallas kernels for 6%

profile of v6, /device:TPU:514, one launch (start us, length us, event | category | flops | bytes accessed | tf_op | source)
XLA Modules:
  0.0 140.9 jit_solution(3561580567804123243)
XLA Ops:
  0.0 13.1 %collective-permute-start = (bf16[64,2048]{1,0:T(8,128)(2,1)}, bf16[64,2048]{1,0:T(8,128)(2,1)S(1)}, u32[]{:S(2)}, u32[]{:S(2)}) collective-permute-start(bf16[64,2048]{1,0:T(8,128)(2,1)} %refs_7_.1), channel_id=1, source_target_pairs={{1,0},{2,1},{3,2},{4,3},{5,4},{6,5},{7,6},{8,7},{9,8},{10,9},{11,1... | collective-permute-start | bytes 786440 | tf_op jit(solution)/shard_map/ppermute | solution.py:33
  13.2 4.2 %collective-permute-done.refs_0_ = bf16[64,2048]{1,0:T(8,128)(2,1)S(1)} collective-permute-done((bf16[64,2048]{1,0:T(8,128)(2,1)}, bf16[64,2048]{1,0:T(8,128)(2,1)S(1)}, u32[]{:S(2)}, u32[]{:S(2)}) %collective-permute-start) | collective-permute-done | bytes 262176 | tf_op jit(solution)/shard_map/ppermute | solution.py:33
  17.3 4.6 %attended.1 = (f32[4,6144]{1,0:T(4,128)S(1)}, bf16[8,144,128]{2,1,0:T(8,128)(2,1)S(1)}) custom-call(s32[1]{0:T(128)} %bitcast.2.me_ref, bf16[64,2048]{1,0:T(8,128)(2,1)S(1)} %collective-permute-done.refs_0_, s32[4]{0:T(128)} %refs_1_.2, s32[2,4]{1,0:T(2,128)} %bitcast.5, s32[1,128]{1,0:T(1,128)} %bitcast.9, bf16[4,6144]{1,0:T(4,128)(2,1)} %refs_4_.1, ...), custom_call_target="tpu_custom_call" | custom-call | flops 77070336 | bytes 2097152 | tf_op jit(solution)/shard_map/attended/pallas_call | solution.py:319
  22.0 19.9 %all_to_all.10.came_ref = bf16[8,144,128]{2,1,0:T(8,128)(2,1)S(1)} all-to-all(bf16[8,144,128]{2,1,0:T(8,128)(2,1)S(1)} %get-tuple-element.24), channel_id=1, replica_groups=mesh['groups'=2,'dev_0'=8,'dev_1'=8,'dev_2'=2] {'dev_0'}, dimensions={0} | all-to-all | bytes 589824 | tf_op jit(solution)/shard_map/all_to_all | solution.py:468
  41.8 0.3 unpacked.1
  42.1 0.1 collective-permute-start.1
  42.3 1.6 %collective-permute-done.1.refs_1_ = bf16[24,6144]{1,0:T(8,128)(2,1)S(1)} collective-permute-done((bf16[24,6144]{1,0:T(8,128)(2,1)S(1)}, bf16[24,6144]{1,0:T(8,128)(2,1)S(1)}, u32[]{:S(2)}, u32[]{:S(2)}) %collective-permute-start.1) | collective-permute-done | bytes 294944 | tf_op jit(solution)/shard_map/ppermute | solution.py:38
  43.8 9.5 %collective-permute-done.2.left_ref = bf16[24,3072]{1,0:T(8,128)(2,1)S(1)} collective-permute-done((bf16[24,3072]{1,0:T(8,128)(2,1)S(1)}, bf16[24,3072]{1,0:T(8,128)(2,1)S(1)}, u32[]{:S(2)}, u32[]{:S(2)}) %collective-permute-start.2) | collective-permute-done | bytes 147488 | tf_op jit(solution)/shard_map/ppermute | solution.py:51
  53.3 1.6 %collective-permute-done.4.right_ref = bf16[24,3072]{1,0:T(8,128)(2,1)S(1)} collective-permute-done((bf16[24,3072]{1,0:T(8,128)(2,1)S(1)}, bf16[24,3072]{1,0:T(8,128)(2,1)S(1)}, u32[]{:S(2)}, u32[]{:S(2)}) %collective-permute-start.4) | collective-permute-done | bytes 147488 | tf_op jit(solution)/shard_map/ppermute | solution.py:51
  54.9 4.7 %collective-permute-done.3.left_ref = bf16[24,3072]{1,0:T(8,128)(2,1)S(1)} collective-permute-done((bf16[24,3072]{1,0:T(8,128)(2,1)S(1)}, bf16[24,3072]{1,0:T(8,128)(2,1)S(1)}, u32[]{:S(2)}, u32[]{:S(2)}) %collective-permute-start.3) | collective-permute-done | bytes 147488 | tf_op jit(solution)/shard_map/ppermute | solution.py:51
  59.7 1.6 %collective-permute-done.5.right_ref = bf16[24,3072]{1,0:T(8,128)(2,1)S(1)} collective-permute-done((bf16[24,3072]{1,0:T(8,128)(2,1)S(1)}, bf16[24,3072]{1,0:T(8,128)(2,1)S(1)}, u32[]{:S(2)}, u32[]{:S(2)}) %collective-permute-start.5) | collective-permute-done | bytes 147488 | tf_op jit(solution)/shard_map/ppermute | solution.py:51
  61.3 4.8 %collective-permute-done.13.left_ref = bf16[24,3072]{1,0:T(8,128)(2,1)S(1)} collective-permute-done((bf16[24,3072]{1,0:T(8,128)(2,1)S(1)}, bf16[24,3072]{1,0:T(8,128)(2,1)S(1)}, u32[]{:S(2)}, u32[]{:S(2)}) %collective-permute-start.13) | collective-permute-done | bytes 147488 | tf_op jit(solution)/shard_map/ppermute | solution.py:51
  66.0 1.6 %collective-permute-done.15.right_ref = bf16[24,3072]{1,0:T(8,128)(2,1)S(1)} collective-permute-done((bf16[24,3072]{1,0:T(8,128)(2,1)S(1)}, bf16[24,3072]{1,0:T(8,128)(2,1)S(1)}, u32[]{:S(2)}, u32[]{:S(2)}) %collective-permute-start.15) | collective-permute-done | bytes 147488 | tf_op jit(solution)/shard_map/ppermute | solution.py:51
  67.6 0.1 collective-permute-start.7
  67.8 0.6 collective-permute-start.6
  68.4 4.0 %collective-permute-done.14.left_ref = bf16[24,3072]{1,0:T(8,128)(2,1)S(1)} collective-permute-done((bf16[24,3072]{1,0:T(8,128)(2,1)S(1)}, bf16[24,3072]{1,0:T(8,128)(2,1)S(1)}, u32[]{:S(2)}, u32[]{:S(2)}) %collective-permute-start.14) | collective-permute-done | bytes 147488 | tf_op jit(solution)/shard_map/ppermute | solution.py:51
  72.4 1.6 %collective-permute-done.16.right_ref = bf16[24,3072]{1,0:T(8,128)(2,1)S(1)} collective-permute-done((bf16[24,3072]{1,0:T(8,128)(2,1)S(1)}, bf16[24,3072]{1,0:T(8,128)(2,1)S(1)}, u32[]{:S(2)}, u32[]{:S(2)}) %collective-permute-start.16) | collective-permute-done | bytes 147488 | tf_op jit(solution)/shard_map/ppermute | solution.py:51
  74.0 0.6 collective-permute-start.19
  74.7 0.2 collective-permute-start.20
  74.8 2.3 %collective-permute-done.17.refs_4_ = bf16[24,6144]{1,0:T(8,128)(2,1)S(1)} collective-permute-done((bf16[24,6144]{1,0:T(8,128)(2,1)S(1)}, bf16[24,6144]{1,0:T(8,128)(2,1)S(1)}, u32[]{:S(2)}, u32[]{:S(2)}) %collective-permute-start.17) | collective-permute-done | bytes 294944 | tf_op jit(solution)/shard_map/ppermute | solution.py:51
  77.1 3.8 %held.1 = (bf16[6144,256]{1,0:T(8,128)(2,1)S(1)}, bf16[6144,256]{1,0:T(8,128)(2,1)S(1)}, bf16[256,6144]{1,0:T(8,128)(2,1)S(1)}) custom-call(bf16[6144,256]{1,0:T(8,128)(2,1)} %refs_0_.1, bf16[6144,256]{1,0:T(8,128)(2,1)} %refs_1_.3, bf16[256,6144]{1,0:T(8,128)(2,1)} %refs_2_.1), custom_call_target="tpu_custom_call" | custom-call | flops 1048576 | bytes 9437184 | tf_op jit(solution)/shard_map/held/pallas_call | solution.py:175
  80.9 2.6 %products.2 = (bf16[24,6144]{1,0:T(8,128)(2,1)S(1)}, bf16[24,6144]{1,0:T(8,128)(2,1)S(1)}, bf16[48,6144]{1,0:T(8,128)(2,1)S(1)}, bf16[48,6144]{1,0:T(8,128)(2,1)...) custom-call(bf16[24,6144]{1,0:T(8,128)(2,1)S(1)} %get-tuple-element.25.refs_0_, ...), custom_call_target="tpu_custom_call" | custom-call | flops 2264924160 | bytes 9437184 | tf_op jit(solution)/shard_map/products/pallas_call | solution.py:198
  83.5 0.6 collective-permute-start.30
  84.2 1.7 %products.3 = (bf16[24,6144]{1,0:T(8,128)(2,1)S(1)}, bf16[24,6144]{1,0:T(8,128)(2,1)S(1)}, bf16[24,6144]{1,0:T(8,128)(2,1)S(1)}, bf16[48,6144]{1,0:T(8,128)(2,1)S(1)}, bf16[24,6144]{1,0:T(8,128)(2,1)S(1)}) custom-call(bf16[24,6144]{1,0:T(8,128)(2,1)S(1)} %joined.6.refs_0_, bf16[24,6144]{1,0:T(8,128)(2,1)S(1)} %collective-permute-done.18.refs_1_, ...), custom_call_target="tpu_custom_call" | custom-call | flops 1358954496 | bytes 9437184 | tf_op jit(solution)/shard_map/products/pallas_call | solution.py:198
  85.8 0.2 collective-permute-start.21
  86.0 0.5 collective-permute-start.31
  86.5 0.1 collective-permute-start.12
  86.6 1.8 %collective-permute-done.31.refs_1_ = bf16[24,6144]{1,0:T(8,128)(2,1)S(1)} collective-permute-done((bf16[24,6144]{1,0:T(8,128)(2,1)S(1)}, bf16[24,6144]{1,0:T(8,128)(2,1)S(1)}, u32[]{:S(2)}, u32[]{:S(2)}) %collective-permute-start.31) | collective-permute-done | bytes 294944 | tf_op jit(solution)/shard_map/ppermute | solution.py:38
  88.4 0.1 collective-permute-start.32
  88.6 0.1 collective-permute-start.35
  88.8 6.1 %collective-permute-done.32.refs_2_ = bf16[24,3072]{1,0:T(8,128)(2,1)S(1)} collective-permute-done((bf16[24,3072]{1,0:T(8,128)(2,1)S(1)}, bf16[24,3072]{1,0:T(8,128)(2,1)S(1)}, u32[]{:S(2)}, u32[]{:S(2)}) %collective-permute-start.32) | collective-permute-done | bytes 147488 | tf_op jit(solution)/shard_map/ppermute | solution.py:51
  94.9 0.1 hop_sum.23
  94.9 0.1 collective-permute-start.33
  95.1 1.4 collective-permute-done.35.refs_2_
  96.5 0.1 hop_sum.26
  96.5 0.4 collective-permute-start.36
  96.9 0.1 collective-permute-start.22
  97.1 1.2 collective-permute-start.26
  98.3 3.1 %collective-permute-done.33.refs_2_ = bf16[24,3072]{1,0:T(8,128)(2,1)S(1)} collective-permute-done((bf16[24,3072]{1,0:T(8,128)(2,1)S(1)}, bf16[24,3072]{1,0:T(8,128)(2,1)S(1)}, u32[]{:S(2)}, u32[]{:S(2)}) %collective-permute-start.33) | collective-permute-done | bytes 147488 | tf_op jit(solution)/shard_map/ppermute | solution.py:51
  101.4 0.1 hop_sum.24
  101.5 0.1 collective-permute-start.34
  101.6 1.6 %collective-permute-done.36.refs_2_ = bf16[24,3072]{1,0:T(8,128)(2,1)S(1)} collective-permute-done((bf16[24,3072]{1,0:T(8,128)(2,1)S(1)}, bf16[24,3072]{1,0:T(8,128)(2,1)S(1)}, u32[]{:S(2)}, u32[]{:S(2)}) %collective-permute-start.36) | collective-permute-done | bytes 147488 | tf_op jit(solution)/shard_map/ppermute | solution.py:51
  103.3 0.1 collective-permute-start.37
  103.4 1.4 collective-permute-done.22.refs_2_
  104.9 0.1 collective-permute-start.23
  105.0 1.4 collective-permute-done.26.refs_2_
  106.4 0.1 collective-permute-start.27
  106.6 1.4 collective-permute-done.34.left_ref
  108.0 1.8 %collective-permute-done.37.right_ref = bf16[24,3072]{1,0:T(8,128)(2,1)S(1)} collective-permute-done((bf16[24,3072]{1,0:T(8,128)(2,1)S(1)}, bf16[24,3072]{1,0:T(8,128)(2,1)S(1)}, u32[]{:S(2)}, u32[]{:S(2)}) %collective-permute-start.37) | collective-permute-done | bytes 147488 | tf_op jit(solution)/shard_map/ppermute | solution.py:51
  109.7 0.1 two_sum.1
  109.8 0.1 collective-permute-start.38
  110.0 1.3 collective-permute-done.23.refs_2_
  111.4 0.1 collective-permute-start.24
  111.5 1.4 collective-permute-done.27.refs_2_
  113.0 0.1 collective-permute-start.28
  113.1 4.8 %collective-permute-done.24.refs_2_ = bf16[24,3072]{1,0:T(8,128)(2,1)S(1)} collective-permute-done((bf16[24,3072]{1,0:T(8,128)(2,1)S(1)}, bf16[24,3072]{1,0:T(8,128)(2,1)S(1)}, u32[]{:S(2)}, u32[]{:S(2)}) %collective-permute-start.24) | collective-permute-done | bytes 147488 | tf_op jit(solution)/shard_map/ppermute | solution.py:51
  117.9 0.1 collective-permute-start.25
  118.1 1.4 collective-permute-done.28.refs_2_
  119.5 0.1 collective-permute-start.29
  119.7 4.7 %collective-permute-done.25.left_ref = bf16[24,3072]{1,0:T(8,128)(2,1)S(1)} collective-permute-done((bf16[24,3072]{1,0:T(8,128)(2,1)S(1)}, bf16[24,3072]{1,0:T(8,128)(2,1)S(1)}, u32[]{:S(2)}, u32[]{:S(2)}) %collective-permute-start.25) | collective-permute-done | bytes 147488 | tf_op jit(solution)/shard_map/ppermute | solution.py:51
  124.4 1.6 %collective-permute-done.29.right_ref = bf16[24,3072]{1,0:T(8,128)(2,1)S(1)} collective-permute-done((bf16[24,3072]{1,0:T(8,128)(2,1)S(1)}, bf16[24,3072]{1,0:T(8,128)(2,1)S(1)}, u32[]{:S(2)}, u32[]{:S(2)}) %collective-permute-start.29) | collective-permute-done | bytes 147488 | tf_op jit(solution)/shard_map/ppermute | solution.py:51
  126.0 0.3 packed_sum.1
  126.2 13.3 %all_to_all.11.home_ref = bf16[8,144,128]{2,1,0:T(8,128)(2,1)S(1)} all-to-all(bf16[8,144,128]{2,1,0:T(8,128)(2,1)S(1)} %packed_sum.1), channel_id=1, replica_groups=mesh['groups'=2,'dev_0'=8,'dev_1'=8,'dev_2'=2] {'dev_0'}, dimensions={0} | all-to-all | bytes 589824 | tf_op jit(solution)/shard_map/all_to_all | solution.py:499
  139.5 1.4 mixed_in.1
  (46 shorter events, 0.7 us)
Async XLA Ops:
  0.0 17.3 %collective-permute-start = (bf16[64,2048]{1,0:T(8,128)(2,1)}, bf16[64,2048]{1,0:T(8,128)(2,1)S(1)}, u32[]{:S(2)}, u32[]{:S(2)}) collective-permute-start(bf16[64,2048]{1,0:T(8,128)(2,1)} %refs_7_.1), channel_id=1, source_target_pairs={{1,0},{2,1},{3,2},{4,3},{5,4},{6,5},{7,6},{8,7},{9,8},{10,9},{11,1... | collective-permute-start | bytes 786440 | tf_op jit(solution)/shard_map/ppermute | solution.py:33
  42.1 1.7 %collective-permute-start.1 = (bf16[24,6144]{1,0:T(8,128)(2,1)S(1)}, bf16[24,6144]{1,0:T(8,128)(2,1)S(1)}, u32[]{:S(2)}, u32[]{:S(2)}) collective-permute-start(bf16[24,6144]{1,0:T(8,128)(2,1)S(1)} %get-tuple-element.25.refs_0_), channel_id=1, source_target_pairs={{0,1},{1,0},{2,3},{3,2},{4,5},{5,4},{6,7},{7,6},{8,9},{9,8},{10,11... | collective-permute-start | bytes 884744 | tf_op jit(solution)/shard_map/ppermute | solution.py:38
  43.8 11.1 %collective-permute-start.8 = (bf16[24,6144]{1,0:T(8,128)(2,1)S(1)}, bf16[24,6144]{1,0:T(8,128)(2,1)S(1)}, u32[]{:S(2)}, u32[]{:S(2)}) collective-permute-start(bf16[24,6144]{1,0:T(8,128)(2,1)S(1)} %collective-permute-done.1.refs_1_), channel_id=1, source_target_pairs={{0,2},{1,15},{2,4},{3,1},{4,6},{5,3},{6,8},{7,5},{8,10},{9,7},{10,... | collective-permute-start | bytes 884744 | tf_op jit(solution)/shard_map/ppermute | solution.py:51
  43.8 9.5 %collective-permute-start.2 = (bf16[24,3072]{1,0:T(8,128)(2,1)S(1)}, bf16[24,3072]{1,0:T(8,128)(2,1)S(1)}, u32[]{:S(2)}, u32[]{:S(2)}) collective-permute-start(bf16[24,3072]{1,0:T(8,128)(2,1)S(1)} %get-tuple-element.26), channel_id=1, source_target_pairs={{0,2},{1,15},{2,4},{3,1},{4,6},{5,3},{6,8},{7,5},{8,10},{9,7},{10,... | collective-permute-start | bytes 442376 | tf_op jit(solution)/shard_map/ppermute | solution.py:51
  43.8 11.1 %collective-permute-start.4 = (bf16[24,3072]{1,0:T(8,128)(2,1)S(1)}, bf16[24,3072]{1,0:T(8,128)(2,1)S(1)}, u32[]{:S(2)}, u32[]{:S(2)}) collective-permute-start(bf16[24,3072]{1,0:T(8,128)(2,1)S(1)} %get-tuple-element.27), channel_id=1, source_target_pairs={{0,2},{1,15},{2,4},{3,1},{4,6},{5,3},{6,8},{7,5},{8,10},{9,7},{10,... | collective-permute-start | bytes 442376 | tf_op jit(solution)/shard_map/ppermute | solution.py:51
  53.3 6.4 %collective-permute-start.3 = (bf16[24,3072]{1,0:T(8,128)(2,1)S(1)}, bf16[24,3072]{1,0:T(8,128)(2,1)S(1)}, u32[]{:S(2)}, u32[]{:S(2)}) collective-permute-start(bf16[24,3072]{1,0:T(8,128)(2,1)S(1)} %collective-permute-done.2.left_ref), channel_id=1, source_target_pairs={{0,2},{1,15},{2,4},{3,1},{4,6},{5,3},{6,8},{7,5},{8,10},{9,7},{10,... | collective-permute-start | bytes 442376 | tf_op jit(solution)/shard_map/ppermute | solution.py:51
  54.9 6.4 %collective-permute-start.5 = (bf16[24,3072]{1,0:T(8,128)(2,1)S(1)}, bf16[24,3072]{1,0:T(8,128)(2,1)S(1)}, u32[]{:S(2)}, u32[]{:S(2)}) collective-permute-start(bf16[24,3072]{1,0:T(8,128)(2,1)S(1)} %collective-permute-done.4.right_ref), channel_id=1, source_target_pairs={{0,2},{1,15},{2,4},{3,1},{4,6},{5,3},{6,8},{7,5},{8,10},{9,7},{10,... | collective-permute-start | bytes 442376 | tf_op jit(solution)/shard_map/ppermute | solution.py:51
  54.9 13.5 %collective-permute-start.9 = (bf16[24,6144]{1,0:T(8,128)(2,1)S(1)}, bf16[24,6144]{1,0:T(8,128)(2,1)S(1)}, u32[]{:S(2)}, u32[]{:S(2)}) collective-permute-start(bf16[24,6144]{1,0:T(8,128)(2,1)S(1)} %collective-permute-done.8.refs_9_), channel_id=1, source_target_pairs={{0,2},{1,15},{2,4},{3,1},{4,6},{5,3},{6,8},{7,5},{8,10},{9,7},{10,... | collective-permute-start | bytes 884744 | tf_op jit(solution)/shard_map/ppermute | solution.py:51
  59.7 6.4 %collective-permute-start.13 = (bf16[24,3072]{1,0:T(8,128)(2,1)S(1)}, bf16[24,3072]{1,0:T(8,128)(2,1)S(1)}, u32[]{:S(2)}, u32[]{:S(2)}) collective-permute-start(bf16[24,3072]{1,0:T(8,128)(2,1)S(1)} %collective-permute-done.3.left_ref), channel_id=1, source_target_pairs={{0,2},{1,15},{2,4},{3,1},{4,6},{5,3},{6,8},{7,5},{8,10},{9,7},{10,... | collective-permute-start | bytes 442376 | tf_op jit(solution)/shard_map/ppermute | solution.py:51
  61.3 6.4 %collective-permute-start.15 = (bf16[24,3072]{1,0:T(8,128)(2,1)S(1)}, bf16[24,3072]{1,0:T(8,128)(2,1)S(1)}, u32[]{:S(2)}, u32[]{:S(2)}) collective-permute-start(bf16[24,3072]{1,0:T(8,128)(2,1)S(1)} %collective-permute-done.5.right_ref), channel_id=1, source_target_pairs={{0,2},{1,15},{2,4},{3,1},{4,6},{5,3},{6,8},{7,5},{8,10},{9,7},{10,... | collective-permute-start | bytes 442376 | tf_op jit(solution)/shard_map/ppermute | solution.py:51
  66.0 6.4 %collective-permute-start.14 = (bf16[24,3072]{1,0:T(8,128)(2,1)S(1)}, bf16[24,3072]{1,0:T(8,128)(2,1)S(1)}, u32[]{:S(2)}, u32[]{:S(2)}) collective-permute-start(bf16[24,3072]{1,0:T(8,128)(2,1)S(1)} %collective-permute-done.13.left_ref), channel_id=1, source_target_pairs={{0,2},{1,15},{2,4},{3,1},{4,6},{5,3},{6,8},{7,5},{8,10},{9,7},{10,... | collective-permute-start | bytes 442376 | tf_op jit(solution)/shard_map/ppermute | solution.py:51
  67.6 6.4 %collective-permute-start.16 = (bf16[24,3072]{1,0:T(8,128)(2,1)S(1)}, bf16[24,3072]{1,0:T(8,128)(2,1)S(1)}, u32[]{:S(2)}, u32[]{:S(2)}) collective-permute-start(bf16[24,3072]{1,0:T(8,128)(2,1)S(1)} %collective-permute-done.15.right_ref), channel_id=1, source_target_pairs={{0,2},{1,15},{2,4},{3,1},{4,6},{5,3},{6,8},{7,5},{8,10},{9,7},{10,... | collective-permute-start | bytes 442376 | tf_op jit(solution)/shard_map/ppermute | solution.py:51
  67.6 6.4 %collective-permute-start.7 = (bf16[24,6144]{1,0:T(8,128)(2,1)S(1)}, bf16[24,6144]{1,0:T(8,128)(2,1)S(1)}, u32[]{:S(2)}, u32[]{:S(2)}) collective-permute-start(bf16[24,6144]{1,0:T(8,128)(2,1)S(1)} %joined.5.refs_7_), channel_id=1, source_target_pairs={{0,1},{1,0},{2,3},{3,2},{4,5},{5,4},{6,7},{7,6},{8,9},{9,8},{10,11... | collective-permute-start | bytes 884744 | tf_op jit(solution)/shard_map/ppermute | solution.py:38
  67.8 6.8 %collective-permute-start.6 = (bf16[24,6144]{1,0:T(8,128)(2,1)S(1)}, bf16[24,6144]{1,0:T(8,128)(2,1)S(1)}, u32[]{:S(2)}, u32[]{:S(2)}) collective-permute-start(bf16[24,6144]{1,0:T(8,128)(2,1)S(1)} %joined.4.refs_6_), channel_id=1, source_target_pairs={{0,1},{1,0},{2,3},{3,2},{4,5},{5,4},{6,7},{7,6},{8,9},{9,8},{10,11... | collective-permute-start | bytes 884744 | tf_op jit(solution)/shard_map/ppermute | solution.py:38
  68.4 8.7 %collective-permute-start.17 = (bf16[24,6144]{1,0:T(8,128)(2,1)S(1)}, bf16[24,6144]{1,0:T(8,128)(2,1)S(1)}, u32[]{:S(2)}, u32[]{:S(2)}) collective-permute-start(bf16[24,6144]{1,0:T(8,128)(2,1)S(1)} %collective-permute-done.9.refs_8_), channel_id=1, source_target_pairs={{0,2},{1,15},{2,4},{3,1},{4,6},{5,3},{6,8},{7,5},{8,10},{9,7},{10,... | collective-permute-start | bytes 884744 | tf_op jit(solution)/shard_map/ppermute | solution.py:51
  72.4 8.5 %collective-permute-start.11 = (bf16[24,6144]{1,0:T(8,128)(2,1)S(1)}, bf16[24,6144]{1,0:T(8,128)(2,1)S(1)}, u32[]{:S(2)}, u32[]{:S(2)}) collective-permute-start(bf16[24,6144]{1,0:T(8,128)(2,1)S(1)} %collective-permute-done.8.refs_9_), channel_id=1, source_target_pairs={{0,1},{1,0},{2,3},{3,2},{4,5},{5,4},{6,7},{7,6},{8,9},{9,8},{10,11... | collective-permute-start | bytes 884744 | tf_op jit(solution)/shard_map/ppermute | solution.py:38
  74.0 7.0 %collective-permute-start.10 = (bf16[24,6144]{1,0:T(8,128)(2,1)S(1)}, bf16[24,6144]{1,0:T(8,128)(2,1)S(1)}, u32[]{:S(2)}, u32[]{:S(2)}) collective-permute-start(bf16[24,6144]{1,0:T(8,128)(2,1)S(1)} %collective-permute-done.9.refs_8_), channel_id=1, source_target_pairs={{0,1},{1,0},{2,3},{3,2},{4,5},{5,4},{6,7},{7,6},{8,9},{9,8},{10,11... | collective-permute-start | bytes 884744 | tf_op jit(solution)/shard_map/ppermute | solution.py:38
  74.0 10.1 %collective-permute-start.19 = (bf16[24,6144]{1,0:T(8,128)(2,1)S(1)}, bf16[24,6144]{1,0:T(8,128)(2,1)S(1)}, u32[]{:S(2)}, u32[]{:S(2)}) collective-permute-start(bf16[24,6144]{1,0:T(8,128)(2,1)S(1)} %joined.7.refs_5_), channel_id=1, source_target_pairs={{0,1},{1,0},{2,3},{3,2},{4,5},{5,4},{6,7},{7,6},{8,9},{9,8},{10,11... | collective-permute-start | bytes 884744 | tf_op jit(solution)/shard_map/ppermute | solution.py:38
  74.7 9.5 %collective-permute-start.20 = (bf16[24,6144]{1,0:T(8,128)(2,1)S(1)}, bf16[24,6144]{1,0:T(8,128)(2,1)S(1)}, u32[]{:S(2)}, u32[]{:S(2)}) collective-permute-start(bf16[24,6144]{1,0:T(8,128)(2,1)S(1)} %joined.6.refs_0_), channel_id=1, source_target_pairs={{0,1},{1,0},{2,3},{3,2},{4,5},{5,4},{6,7},{7,6},{8,9},{9,8},{10,11... | collective-permute-start | bytes 884744 | tf_op jit(solution)/shard_map/ppermute | solution.py:38
  77.1 7.0 %collective-permute-start.18 = (bf16[24,6144]{1,0:T(8,128)(2,1)S(1)}, bf16[24,6144]{1,0:T(8,128)(2,1)S(1)}, u32[]{:S(2)}, u32[]{:S(2)}) collective-permute-start(bf16[24,6144]{1,0:T(8,128)(2,1)S(1)} %collective-permute-done.17.refs_4_), channel_id=1, source_target_pairs={{0,1},{1,0},{2,3},{3,2},{4,5},{5,4},{6,7},{7,6},{8,9},{9,8},{10,11... | collective-permute-start | bytes 884744 | tf_op jit(solution)/shard_map/ppermute | solution.py:38
  83.5 5.2 %collective-permute-start.30 = (bf16[48,6144]{1,0:T(8,128)(2,1)S(1)}, bf16[48,6144]{1,0:T(8,128)(2,1)S(1)}, u32[]{:S(2)}, u32[]{:S(2)}) collective-permute-start(bf16[48,6144]{1,0:T(8,128)(2,1)S(1)} %get-tuple-element.39), channel_id=1, source_target_pairs={{0,1},{1,0},{2,3},{3,2},{4,5},{5,4},{6,7},{7,6},{8,9},{9,8},{10,11... | collective-permute-start | bytes 1769480 | tf_op jit(solution)/shard_map/ppermute | solution.py:38
  85.8 11.1 %collective-permute-start.21 = (bf16[48,6144]{1,0:T(8,128)(2,1)S(1)}, bf16[48,6144]{1,0:T(8,128)(2,1)S(1)}, u32[]{:S(2)}, u32[]{:S(2)}) collective-permute-start(bf16[48,6144]{1,0:T(8,128)(2,1)S(1)} %get-tuple-element.35), channel_id=1, source_target_pairs={{0,1},{1,0},{2,3},{3,2},{4,5},{5,4},{6,7},{7,6},{8,9},{9,8},{10,11... | collective-permute-start | bytes 1769480 | tf_op jit(solution)/shard_map/ppermute | solution.py:38
  86.0 2.4 %collective-permute-start.31 = (bf16[24,6144]{1,0:T(8,128)(2,1)S(1)}, bf16[24,6144]{1,0:T(8,128)(2,1)S(1)}, u32[]{:S(2)}, u32[]{:S(2)}) collective-permute-start(bf16[24,6144]{1,0:T(8,128)(2,1)S(1)} %get-tuple-element.41), channel_id=1, source_target_pairs={{0,1},{1,0},{2,3},{3,2},{4,5},{5,4},{6,7},{7,6},{8,9},{9,8},{10,11... | collective-permute-start | bytes 884744 | tf_op jit(solution)/shard_map/ppermute | solution.py:38
  86.5 23.5 %collective-permute-start.12 = (bf16[48,6144]{1,0:T(8,128)(2,1)S(1)}, bf16[48,6144]{1,0:T(8,128)(2,1)S(1)}, u32[]{:S(2)}, u32[]{:S(2)}) collective-permute-start(bf16[48,6144]{1,0:T(8,128)(2,1)S(1)} %get-tuple-element.33), channel_id=1, source_target_pairs={{0,1},{1,0},{2,3},{3,2},{4,5},{5,4},{6,7},{7,6},{8,9},{9,8},{10,11... | collective-permute-start | bytes 1769480 | tf_op jit(solution)/shard_map/ppermute | solution.py:38
  88.4 6.5 %collective-permute-start.32 = (bf16[24,3072]{1,0:T(8,128)(2,1)S(1)}, bf16[24,3072]{1,0:T(8,128)(2,1)S(1)}, u32[]{:S(2)}, u32[]{:S(2)}) collective-permute-start(bf16[24,3072]{1,0:T(8,128)(2,1)S(1)} %hop_sum.22), channel_id=1, source_target_pairs={{0,2},{1,15},{2,4},{3,1},{4,6},{5,3},{6,8},{7,5},{8,10},{9,7},{10,... | collective-permute-start | bytes 442376 | tf_op jit(solution)/shard_map/ppermute | solution.py:51
  88.6 7.9 %collective-permute-start.35 = (bf16[24,3072]{1,0:T(8,128)(2,1)S(1)}, bf16[24,3072]{1,0:T(8,128)(2,1)S(1)}, u32[]{:S(2)}, u32[]{:S(2)}) collective-permute-start(bf16[24,3072]{1,0:T(8,128)(2,1)S(1)} %hop_sum.25), channel_id=1, source_target_pairs={{0,2},{1,15},{2,4},{3,1},{4,6},{5,3},{6,8},{7,5},{8,10},{9,7},{10,... | collective-permute-start | bytes 442376 | tf_op jit(solution)/shard_map/ppermute | solution.py:51
  94.9 6.5 %collective-permute-start.33 = (bf16[24,3072]{1,0:T(8,128)(2,1)S(1)}, bf16[24,3072]{1,0:T(8,128)(2,1)S(1)}, u32[]{:S(2)}, u32[]{:S(2)}) collective-permute-start(bf16[24,3072]{1,0:T(8,128)(2,1)S(1)} %hop_sum.23), channel_id=1, source_target_pairs={{0,2},{1,15},{2,4},{3,1},{4,6},{5,3},{6,8},{7,5},{8,10},{9,7},{10,... | collective-permute-start | bytes 442376 | tf_op jit(solution)/shard_map/ppermute | solution.py:51
  96.5 6.7 %collective-permute-start.36 = (bf16[24,3072]{1,0:T(8,128)(2,1)S(1)}, bf16[24,3072]{1,0:T(8,128)(2,1)S(1)}, u32[]{:S(2)}, u32[]{:S(2)}) collective-permute-start(bf16[24,3072]{1,0:T(8,128)(2,1)S(1)} %hop_sum.26), channel_id=1, source_target_pairs={{0,2},{1,15},{2,4},{3,1},{4,6},{5,3},{6,8},{7,5},{8,10},{9,7},{10,... | collective-permute-start | bytes 442376 | tf_op jit(solution)/shard_map/ppermute | solution.py:51
  96.9 7.9 %collective-permute-start.22 = (bf16[24,3072]{1,0:T(8,128)(2,1)S(1)}, bf16[24,3072]{1,0:T(8,128)(2,1)S(1)}, u32[]{:S(2)}, u32[]{:S(2)}) collective-permute-start(bf16[24,3072]{1,0:T(8,128)(2,1)S(1)} %hop_sum.14), channel_id=1, source_target_pairs={{0,2},{1,15},{2,4},{3,1},{4,6},{5,3},{6,8},{7,5},{8,10},{9,7},{10,... | collective-permute-start | bytes 442376 | tf_op jit(solution)/shard_map/ppermute | solution.py:51
  97.1 9.2 %collective-permute-start.26 = (bf16[24,3072]{1,0:T(8,128)(2,1)S(1)}, bf16[24,3072]{1,0:T(8,128)(2,1)S(1)}, u32[]{:S(2)}, u32[]{:S(2)}) collective-permute-start(bf16[24,3072]{1,0:T(8,128)(2,1)S(1)} %hop_sum.18), channel_id=1, source_target_pairs={{0,2},{1,15},{2,4},{3,1},{4,6},{5,3},{6,8},{7,5},{8,10},{9,7},{10,... | collective-permute-start | bytes 442376 | tf_op jit(solution)/shard_map/ppermute | solution.py:51
  101.5 6.5 %collective-permute-start.34 = (bf16[24,3072]{1,0:T(8,128)(2,1)S(1)}, bf16[24,3072]{1,0:T(8,128)(2,1)S(1)}, u32[]{:S(2)}, u32[]{:S(2)}) collective-permute-start(bf16[24,3072]{1,0:T(8,128)(2,1)S(1)} %hop_sum.24), channel_id=1, source_target_pairs={{0,2},{1,15},{2,4},{3,1},{4,6},{5,3},{6,8},{7,5},{8,10},{9,7},{10,... | collective-permute-start | bytes 442376 | tf_op jit(solution)/shard_map/ppermute | solution.py:51
  103.3 6.5 %collective-permute-start.37 = (bf16[24,3072]{1,0:T(8,128)(2,1)S(1)}, bf16[24,3072]{1,0:T(8,128)(2,1)S(1)}, u32[]{:S(2)}, u32[]{:S(2)}) collective-permute-start(bf16[24,3072]{1,0:T(8,128)(2,1)S(1)} %hop_sum.27), channel_id=1, source_target_pairs={{0,2},{1,15},{2,4},{3,1},{4,6},{5,3},{6,8},{7,5},{8,10},{9,7},{10,... | collective-permute-start | bytes 442376 | tf_op jit(solution)/shard_map/ppermute | solution.py:51
  104.9 6.5 %collective-permute-start.23 = (bf16[24,3072]{1,0:T(8,128)(2,1)S(1)}, bf16[24,3072]{1,0:T(8,128)(2,1)S(1)}, u32[]{:S(2)}, u32[]{:S(2)}) collective-permute-start(bf16[24,3072]{1,0:T(8,128)(2,1)S(1)} %hop_sum.15), channel_id=1, source_target_pairs={{0,2},{1,15},{2,4},{3,1},{4,6},{5,3},{6,8},{7,5},{8,10},{9,7},{10,... | collective-permute-start | bytes 442376 | tf_op jit(solution)/shard_map/ppermute | solution.py:51
  106.4 6.5 %collective-permute-start.27 = (bf16[24,3072]{1,0:T(8,128)(2,1)S(1)}, bf16[24,3072]{1,0:T(8,128)(2,1)S(1)}, u32[]{:S(2)}, u32[]{:S(2)}) collective-permute-start(bf16[24,3072]{1,0:T(8,128)(2,1)S(1)} %hop_sum.19), channel_id=1, source_target_pairs={{0,2},{1,15},{2,4},{3,1},{4,6},{5,3},{6,8},{7,5},{8,10},{9,7},{10,... | collective-permute-start | bytes 442376 | tf_op jit(solution)/shard_map/ppermute | solution.py:51
  109.8 9.8 %collective-permute-start.38 = (bf16[24,6144]{1,0:T(8,128)(2,1)S(1)}, bf16[24,6144]{1,0:T(8,128)(2,1)S(1)}, u32[]{:S(2)}, u32[]{:S(2)}) collective-permute-start(bf16[24,6144]{1,0:T(8,128)(2,1)S(1)} %two_sum.1), channel_id=1, source_target_pairs={{0,1},{1,0},{2,3},{3,2},{4,5},{5,4},{6,7},{7,6},{8,9},{9,8},{10,11... | collective-permute-start | bytes 884744 | tf_op jit(solution)/shard_map/ppermute | solution.py:38
  111.4 28.1 %copy-start = (s32[4,2]{0,1:T(2,128)S(1)}, s32[4,2]{0,1:T(2,128)}, u32[]{:S(2)}) copy-start(s32[4,2]{0,1:T(2,128)} %param.20) | copy-start | bytes 100
  111.4 28.1 %copy-start.1 = (f32[4,2]{0,1:T(2,128)S(1)}, f32[4,2]{0,1:T(2,128)}, u32[]{:S(2)}) copy-start(f32[4,2]{0,1:T(2,128)} %param.21) | copy-start | bytes 100
  111.4 6.5 %collective-permute-start.24 = (bf16[24,3072]{1,0:T(8,128)(2,1)S(1)}, bf16[24,3072]{1,0:T(8,128)(2,1)S(1)}, u32[]{:S(2)}, u32[]{:S(2)}) collective-permute-start(bf16[24,3072]{1,0:T(8,128)(2,1)S(1)} %hop_sum.16), channel_id=1, source_target_pairs={{0,2},{1,15},{2,4},{3,1},{4,6},{5,3},{6,8},{7,5},{8,10},{9,7},{10,... | collective-permute-start | bytes 442376 | tf_op jit(solution)/shard_map/ppermute | solution.py:51
  113.0 6.5 %collective-permute-start.28 = (bf16[24,3072]{1,0:T(8,128)(2,1)S(1)}, bf16[24,3072]{1,0:T(8,128)(2,1)S(1)}, u32[]{:S(2)}, u32[]{:S(2)}) collective-permute-start(bf16[24,3072]{1,0:T(8,128)(2,1)S(1)} %hop_sum.20), channel_id=1, source_target_pairs={{0,2},{1,15},{2,4},{3,1},{4,6},{5,3},{6,8},{7,5},{8,10},{9,7},{10,... | collective-permute-start | bytes 442376 | tf_op jit(solution)/shard_map/ppermute | solution.py:51
  117.9 6.5 %collective-permute-start.25 = (bf16[24,3072]{1,0:T(8,128)(2,1)S(1)}, bf16[24,3072]{1,0:T(8,128)(2,1)S(1)}, u32[]{:S(2)}, u32[]{:S(2)}) collective-permute-start(bf16[24,3072]{1,0:T(8,128)(2,1)S(1)} %hop_sum.17), channel_id=1, source_target_pairs={{0,2},{1,15},{2,4},{3,1},{4,6},{5,3},{6,8},{7,5},{8,10},{9,7},{10,... | collective-permute-start | bytes 442376 | tf_op jit(solution)/shard_map/ppermute | solution.py:51
  119.5 6.5 %collective-permute-start.29 = (bf16[24,3072]{1,0:T(8,128)(2,1)S(1)}, bf16[24,3072]{1,0:T(8,128)(2,1)S(1)}, u32[]{:S(2)}, u32[]{:S(2)}) collective-permute-start(bf16[24,3072]{1,0:T(8,128)(2,1)S(1)} %hop_sum.21), channel_id=1, source_target_pairs={{0,2},{1,15},{2,4},{3,1},{4,6},{5,3},{6,8},{7,5},{8,10},{9,7},{10,... | collective-permute-start | bytes 442376 | tf_op jit(solution)/shard_map/ppermute | solution.py:51

commit v7 on v5

--- a/solution.py
+++ b/solution.py
@@ -108,36 +108,24 @@
 
 
 def scattered(far, each, own, other, kept, got):
-    half = own.shape[1] // 2
+    width = own.shape[1]
+    half = width // 2
     moving = {}
+
+    def hop(step, part, col, cols):
+        terms = [(x, (row, col)) for x, row in (kept[step, part], got[step, part])]
+        if (part, col) in moving:
+            terms.append((moving[part, col], (0, 0)))
+        parcel = hop_sum(each, cols, *terms)
+        moving[part, col] = passed_on(parcel)
+
     for step in range(far, 0, -1):
-        for part in (0, 1) if step < far else (1,):
-            for side in (0, 1):
-                terms = [(x, (row, side * half)) for x, row in (kept[step, part], got[step, part])]
-                if (part, side) in moving:
-                    terms.append((moving[part, side], (0, 0)))
-                parcel = hop_sum(each, half, *terms)
-                moving[part, side] = passed_on(parcel)
-    return own, moving[1, 0], moving[1, 1], swapped(two_sum(other, moving[0, 0], moving[0, 1]))
-
-
-def two_kernel(whole_ref, left_ref, right_ref, out_ref):
-    half = left_ref.shape[1]
-    for side, ref in enumerate((left_ref, right_ref)):
-        cols = slice(side * half, (side + 1) * half)
-        out_ref[:, cols] = (whole_ref[:, cols].astype(jnp.float32) + ref[...].astype(jnp.float32)).astype(out_ref.dtype)
-
-
-def two_sum(whole, left, right):
-    vm = pl.BlockSpec(memory_space=pltpu.VMEM)
-    return pl.pallas_call(
-        two_kernel,
-        out_shape=jax.ShapeDtypeStruct(whole.shape, whole.dtype),
-        in_specs=[vm] * 3,
-        out_specs=vm,
-        compiler_params=pltpu.CompilerParams(vmem_limit_bytes=8 * 1024 * 1024),
-        name="two_sum",
-    )(whole, left, right)
+        if step > 1:
+            hop(step - 1, 0, 0, width)
+        for side in (0, 1):
+            hop(step, 1, side * half, half)
+    leaving = hop_sum(each, width, (other, (0, 0)), (moving[0, 0], (0, 0)))
+    return own, moving[1, 0], moving[1, half], swapped(leaving)
 
 
 def multiplied(pieces, gate, up, down, outs, ready):

time: 140 us -> 141 us (level)
  waiting for transfers between devices: 72.4 us -> 74.6 us
    ppermute x25 -> x22, waiting for transfers between devices: 64.9 us -> 68.1 us  [passed_on(): return lax.ppermute(value, ('dev_1', 'dev_2'), pairs)]
    ppermute x25 -> x22, starting transfers between devices: 3.2 us -> 1.73 us  [passed_on(): return lax.ppermute(value, ('dev_1', 'dev_2'), pairs)]
  transfers between devices with their start and end apart: 39 -> 36, of which waited for: 26 -> 22; matrix products, arithmetic and copies ran while one was open for 0% -> 0% of each run, Pallas kernels for 5% -> 4%
where the time goes in v7:
time: 141 us
  waiting for transfers between devices  74.6 us (53%)
  blocking collectives  33.1 us (23%)
  starting transfers between devices  19.1 us (14%)
  Pallas kernels  13.9 us (10%)
    ppermute x22, waiting for transfers between devices, passed_on(): return lax.ppermute(value, ('dev_1', 'dev_2'), pairs)  68.1 us
    all_to_all x1, blocking collectives, layer(): lax.all_to_all(leaving, 'dev_0', 0, 0, tiled=True)  19.9 us
    all_to_all x1, blocking collectives, layer(): lax.all_to_all(packed_sum(*last_terms, rows_x), 'dev_0', 0, 0, tiled=True)  13.3 us
    ppermute x1, starting transfers between devices, passed_along(): lax.ppermute(value, axis, [(source, source + steps) for source in range(l...  13.1 us
    pallas_call x1, Pallas kernels, early_products(): pl.pallas_call(functools.partial(early_kernel, len(pieces)), out_shape=ou...  4.9 us
    pallas_call x1, Pallas kernels, attended(): pl.pallas_call(attend_kernel, out_shape=[jax.ShapeDtypeStruct((reqs, widt...  4.61 us
    ppermute x13, starting transfers between devices, shifted(): lax.ppermute(value, axis, [(place, (place + steps) % count) for place in...  4.27 us
    ppermute x1, waiting for transfers between devices, passed_along(): lax.ppermute(value, axis, [(source, source + steps) for source in range(l...  4.18 us
  transfers between devices with their start and end apart: 36, of which 22 were waited for; matrix products, arithmetic and copies ran while one was open for 0% of the time, Pallas kernels for 4%

profile of v7, /device:TPU:514, one launch (start us, length us, event | category | flops | bytes accessed | tf_op | source)
XLA Modules:
  0.0 141.1 jit_solution(18026978712073841894)
XLA Ops:
  0.0 13.1 %collective-permute-start = (bf16[64,2048]{1,0:T(8,128)(2,1)}, bf16[64,2048]{1,0:T(8,128)(2,1)S(1)}, u32[]{:S(2)}, u32[]{:S(2)}) collective-permute-start(bf16[64,2048]{1,0:T(8,128)(2,1)} %refs_7_.1), channel_id=1, source_target_pairs={{1,0},{2,1},{3,2},{4,3},{5,4},{6,5},{7,6},{8,7},{9,8},{10,9},{11,1... | collective-permute-start | bytes 786440 | tf_op jit(solution)/shard_map/ppermute | solution.py:33
  13.2 4.2 %collective-permute-done.refs_0_ = bf16[64,2048]{1,0:T(8,128)(2,1)S(1)} collective-permute-done((bf16[64,2048]{1,0:T(8,128)(2,1)}, bf16[64,2048]{1,0:T(8,128)(2,1)S(1)}, u32[]{:S(2)}, u32[]{:S(2)}) %collective-permute-start) | collective-permute-done | bytes 262176 | tf_op jit(solution)/shard_map/ppermute | solution.py:33
  17.3 4.6 %attended.1 = (f32[4,6144]{1,0:T(4,128)S(1)}, bf16[8,144,128]{2,1,0:T(8,128)(2,1)S(1)}) custom-call(s32[1]{0:T(128)} %bitcast.2.me_ref, bf16[64,2048]{1,0:T(8,128)(2,1)S(1)} %collective-permute-done.refs_0_, s32[4]{0:T(128)} %refs_1_.1, s32[2,4]{1,0:T(2,128)} %bitcast.5, s32[1,128]{1,0:T(1,128)} %bitcast.9, bf16[4,6144]{1,0:T(4,128)(2,1)} %refs_4_.1, ...), custom_call_target="tpu_custom_call" | custom-call | flops 77070336 | bytes 2097152 | tf_op jit(solution)/shard_map/attended/pallas_call | solution.py:326
  21.9 19.9 %all_to_all.10.came_ref = bf16[8,144,128]{2,1,0:T(8,128)(2,1)S(1)} all-to-all(bf16[8,144,128]{2,1,0:T(8,128)(2,1)S(1)} %get-tuple-element.24), channel_id=1, replica_groups=mesh['groups'=2,'dev_0'=8,'dev_1'=8,'dev_2'=2] {'dev_0'}, dimensions={0} | all-to-all | bytes 589824 | tf_op jit(solution)/shard_map/all_to_all | solution.py:475
  41.8 0.3 unpacked.1
  42.1 0.1 collective-permute-start.1
  42.2 1.6 %collective-permute-done.1.refs_1_ = bf16[24,6144]{1,0:T(8,128)(2,1)S(1)} collective-permute-done((bf16[24,6144]{1,0:T(8,128)(2,1)S(1)}, bf16[24,6144]{1,0:T(8,128)(2,1)S(1)}, u32[]{:S(2)}, u32[]{:S(2)}) %collective-permute-start.1) | collective-permute-done | bytes 294944 | tf_op jit(solution)/shard_map/ppermute | solution.py:38
  43.8 0.0 collective-permute-start.4
  43.8 9.5 %collective-permute-done.2.left_ref = bf16[24,3072]{1,0:T(8,128)(2,1)S(1)} collective-permute-done((bf16[24,3072]{1,0:T(8,128)(2,1)S(1)}, bf16[24,3072]{1,0:T(8,128)(2,1)S(1)}, u32[]{:S(2)}, u32[]{:S(2)}) %collective-permute-start.2) | collective-permute-done | bytes 147488 | tf_op jit(solution)/shard_map/ppermute | solution.py:51
  53.3 1.6 %collective-permute-done.4.right_ref = bf16[24,3072]{1,0:T(8,128)(2,1)S(1)} collective-permute-done((bf16[24,3072]{1,0:T(8,128)(2,1)S(1)}, bf16[24,3072]{1,0:T(8,128)(2,1)S(1)}, u32[]{:S(2)}, u32[]{:S(2)}) %collective-permute-start.4) | collective-permute-done | bytes 147488 | tf_op jit(solution)/shard_map/ppermute | solution.py:51
  54.9 0.0 collective-permute-start.9
  54.9 4.7 %collective-permute-done.3.left_ref = bf16[24,3072]{1,0:T(8,128)(2,1)S(1)} collective-permute-done((bf16[24,3072]{1,0:T(8,128)(2,1)S(1)}, bf16[24,3072]{1,0:T(8,128)(2,1)S(1)}, u32[]{:S(2)}, u32[]{:S(2)}) %collective-permute-start.3) | collective-permute-done | bytes 147488 | tf_op jit(solution)/shard_map/ppermute | solution.py:51
  59.7 1.6 %collective-permute-done.5.right_ref = bf16[24,3072]{1,0:T(8,128)(2,1)S(1)} collective-permute-done((bf16[24,3072]{1,0:T(8,128)(2,1)S(1)}, bf16[24,3072]{1,0:T(8,128)(2,1)S(1)}, u32[]{:S(2)}, u32[]{:S(2)}) %collective-permute-start.5) | collective-permute-done | bytes 147488 | tf_op jit(solution)/shard_map/ppermute | solution.py:51
  61.2 4.8 %collective-permute-done.13.left_ref = bf16[24,3072]{1,0:T(8,128)(2,1)S(1)} collective-permute-done((bf16[24,3072]{1,0:T(8,128)(2,1)S(1)}, bf16[24,3072]{1,0:T(8,128)(2,1)S(1)}, u32[]{:S(2)}, u32[]{:S(2)}) %collective-permute-start.13) | collective-permute-done | bytes 147488 | tf_op jit(solution)/shard_map/ppermute | solution.py:51
  66.0 1.6 %collective-permute-done.15.right_ref = bf16[24,3072]{1,0:T(8,128)(2,1)S(1)} collective-permute-done((bf16[24,3072]{1,0:T(8,128)(2,1)S(1)}, bf16[24,3072]{1,0:T(8,128)(2,1)S(1)}, u32[]{:S(2)}, u32[]{:S(2)}) %collective-permute-start.15) | collective-permute-done | bytes 147488 | tf_op jit(solution)/shard_map/ppermute | solution.py:51
  67.6 0.1 collective-permute-start.7
  67.8 0.6 collective-permute-start.6
  68.4 4.0 %collective-permute-done.14.left_ref = bf16[24,3072]{1,0:T(8,128)(2,1)S(1)} collective-permute-done((bf16[24,3072]{1,0:T(8,128)(2,1)S(1)}, bf16[24,3072]{1,0:T(8,128)(2,1)S(1)}, u32[]{:S(2)}, u32[]{:S(2)}) %collective-permute-start.14) | collective-permute-done | bytes 147488 | tf_op jit(solution)/shard_map/ppermute | solution.py:51
  72.4 1.6 %collective-permute-done.16.right_ref = bf16[24,3072]{1,0:T(8,128)(2,1)S(1)} collective-permute-done((bf16[24,3072]{1,0:T(8,128)(2,1)S(1)}, bf16[24,3072]{1,0:T(8,128)(2,1)S(1)}, u32[]{:S(2)}, u32[]{:S(2)}) %collective-permute-start.16) | collective-permute-done | bytes 147488 | tf_op jit(solution)/shard_map/ppermute | solution.py:51
  74.0 0.6 collective-permute-start.19
  74.6 0.2 collective-permute-start.20
  74.8 2.3 %collective-permute-done.17.refs_4_ = bf16[24,6144]{1,0:T(8,128)(2,1)S(1)} collective-permute-done((bf16[24,6144]{1,0:T(8,128)(2,1)S(1)}, bf16[24,6144]{1,0:T(8,128)(2,1)S(1)}, u32[]{:S(2)}, u32[]{:S(2)}) %collective-permute-start.17) | collective-permute-done | bytes 294944 | tf_op jit(solution)/shard_map/ppermute | solution.py:51
  77.1 4.9 %early.1 = (bf16[24,6144]{1,0:T(8,128)(2,1)S(1)}, bf16[24,6144]{1,0:T(8,128)(2,1)S(1)}, bf16[48,6144]{1,0:T(8,128)(2,1)S(1)}, bf16[48,6144]{1,0:T(8,128)(2,1)S(1...) custom-call(bf16[24,6144]{1,0:T(8,128)(2,1)S(1)} %get-tuple-element., ...), custom_call_target="tpu_custom_call" | custom-call | flops 2264924160 | bytes 9437184 | tf_op jit(solution)/shard_map/early/pallas_call | solution.py:194
  82.0 1.7 %late.1 = (bf16[24,6144]{1,0:T(8,128)(2,1)S(1)}, bf16[24,6144]{1,0:T(8,128)(2,1)S(1)}, bf16[24,6144]{1,0:T(8,128)(2,1)S(1)}, bf16[48,6144]{1,0:T(8,128)(2,1)S(1)}, bf16[24,6144]{1,0:T(8,128)(2,1)S(1)}) custom-call(bf16[24,6144]{1,0:T(8,128)(2,1)S(1)} %joined.6.refs_0_, bf16[24,6144]{1,0:T(8,128)(2,1)S(1)} %collective-permute-done.18.refs_1_, ...), custom_call_target="tpu_custom_call" | custom-call | flops 1358954496 | bytes 9437184 | tf_op jit(solution)/shard_map/late/pallas_call | solution.py:209
  83.7 0.6 collective-permute-start.31
  84.4 0.1 collective-permute-start.30
  84.5 0.4 collective-permute-start.21
  84.9 0.7 collective-permute-done.31.refs_1_
  85.6 0.1 hop_sum.20
  85.6 0.1 collective-permute-start.32
  85.8 1.3 collective-permute-start.12
  87.1 6.6 %collective-permute-done.32.refs_2_ = bf16[24,6144]{1,0:T(8,128)(2,1)S(1)} collective-permute-done((bf16[24,6144]{1,0:T(8,128)(2,1)S(1)}, bf16[24,6144]{1,0:T(8,128)(2,1)S(1)}, u32[]{:S(2)}, u32[]{:S(2)}) %collective-permute-start.32) | collective-permute-done | bytes 294944 | tf_op jit(solution)/shard_map/ppermute | solution.py:51
  93.7 0.1 hop_sum.21
  93.8 0.1 collective-permute-start.33
  94.0 0.4 collective-permute-start.26
  94.4 0.1 collective-permute-start.22
  94.5 7.3 %collective-permute-done.33.refs_2_ = bf16[24,6144]{1,0:T(8,128)(2,1)S(1)} collective-permute-done((bf16[24,6144]{1,0:T(8,128)(2,1)S(1)}, bf16[24,6144]{1,0:T(8,128)(2,1)S(1)}, u32[]{:S(2)}, u32[]{:S(2)}) %collective-permute-start.33) | collective-permute-done | bytes 294944 | tf_op jit(solution)/shard_map/ppermute | solution.py:51
  101.8 0.1 hop_sum.22
  102.0 0.1 collective-permute-start.34
  102.1 1.3 collective-permute-done.26.refs_2_
  103.4 0.1 hop_sum.17
  103.5 0.1 collective-permute-start.27
  103.6 1.4 collective-permute-done.22.refs_2_
  105.0 0.1 hop_sum.13
  105.1 0.1 collective-permute-start.23
  105.2 6.4 %collective-permute-done.27.refs_2_ = bf16[24,3072]{1,0:T(8,128)(2,1)S(1)} collective-permute-done((bf16[24,3072]{1,0:T(8,128)(2,1)S(1)}, bf16[24,3072]{1,0:T(8,128)(2,1)S(1)}, u32[]{:S(2)}, u32[]{:S(2)}) %collective-permute-start.27) | collective-permute-done | bytes 147488 | tf_op jit(solution)/shard_map/ppermute | solution.py:51
  111.6 0.1 hop_sum.18
  111.6 0.1 collective-permute-start.28
  111.8 1.4 collective-permute-done.23.refs_2_
  113.2 0.1 hop_sum.14
  113.2 0.1 collective-permute-start.24
  113.4 0.1 hop_sum.23
  113.5 0.1 collective-permute-start.35
  113.6 4.5 %collective-permute-done.28.refs_2_ = bf16[24,3072]{1,0:T(8,128)(2,1)S(1)} collective-permute-done((bf16[24,3072]{1,0:T(8,128)(2,1)S(1)}, bf16[24,3072]{1,0:T(8,128)(2,1)S(1)}, u32[]{:S(2)}, u32[]{:S(2)}) %collective-permute-start.28) | collective-permute-done | bytes 147488 | tf_op jit(solution)/shard_map/ppermute | solution.py:51
  118.1 0.1 hop_sum.19
  118.2 0.1 collective-permute-start.29
  118.3 1.4 collective-permute-done.24.refs_2_
  119.7 0.1 hop_sum.15
  119.8 0.1 collective-permute-start.25
  119.9 4.7 %collective-permute-done.29.right_ref = bf16[24,3072]{1,0:T(8,128)(2,1)S(1)} collective-permute-done((bf16[24,3072]{1,0:T(8,128)(2,1)S(1)}, bf16[24,3072]{1,0:T(8,128)(2,1)S(1)}, u32[]{:S(2)}, u32[]{:S(2)}) %collective-permute-start.29) | collective-permute-done | bytes 147488 | tf_op jit(solution)/shard_map/ppermute | solution.py:51
  124.6 1.6 %collective-permute-done.25.left_ref = bf16[24,3072]{1,0:T(8,128)(2,1)S(1)} collective-permute-done((bf16[24,3072]{1,0:T(8,128)(2,1)S(1)}, bf16[24,3072]{1,0:T(8,128)(2,1)S(1)}, u32[]{:S(2)}, u32[]{:S(2)}) %collective-permute-start.25) | collective-permute-done | bytes 147488 | tf_op jit(solution)/shard_map/ppermute | solution.py:51
  126.2 0.3 packed_sum.1
  126.5 13.3 %all_to_all.11.home_ref = bf16[8,144,128]{2,1,0:T(8,128)(2,1)S(1)} all-to-all(bf16[8,144,128]{2,1,0:T(8,128)(2,1)S(1)} %packed_sum.1), channel_id=1, replica_groups=mesh['groups'=2,'dev_0'=8,'dev_1'=8,'dev_2'=2] {'dev_0'}, dimensions={0} | all-to-all | bytes 589824 | tf_op jit(solution)/shard_map/all_to_all | solution.py:507
  139.8 1.4 mixed_in.1
  (36 shorter events, 0.2 us)
Async XLA Ops:
  0.0 17.3 %collective-permute-start = (bf16[64,2048]{1,0:T(8,128)(2,1)}, bf16[64,2048]{1,0:T(8,128)(2,1)S(1)}, u32[]{:S(2)}, u32[]{:S(2)}) collective-permute-start(bf16[64,2048]{1,0:T(8,128)(2,1)} %refs_7_.1), channel_id=1, source_target_pairs={{1,0},{2,1},{3,2},{4,3},{5,4},{6,5},{7,6},{8,7},{9,8},{10,9},{11,1... | collective-permute-start | bytes 786440 | tf_op jit(solution)/shard_map/ppermute | solution.py:33
  42.1 1.7 %collective-permute-start.1 = (bf16[24,6144]{1,0:T(8,128)(2,1)S(1)}, bf16[24,6144]{1,0:T(8,128)(2,1)S(1)}, u32[]{:S(2)}, u32[]{:S(2)}) collective-permute-start(bf16[24,6144]{1,0:T(8,128)(2,1)S(1)} %get-tuple-element.25.refs_0_), channel_id=1, source_target_pairs={{0,1},{1,0},{2,3},{3,2},{4,5},{5,4},{6,7},{7,6},{8,9},{9,8},{10,11... | collective-permute-start | bytes 884744 | tf_op jit(solution)/shard_map/ppermute | solution.py:38
  43.8 11.1 %collective-permute-start.8 = (bf16[24,6144]{1,0:T(8,128)(2,1)S(1)}, bf16[24,6144]{1,0:T(8,128)(2,1)S(1)}, u32[]{:S(2)}, u32[]{:S(2)}) collective-permute-start(bf16[24,6144]{1,0:T(8,128)(2,1)S(1)} %collective-permute-done.1.refs_1_), channel_id=1, source_target_pairs={{0,2},{1,15},{2,4},{3,1},{4,6},{5,3},{6,8},{7,5},{8,10},{9,7},{10,... | collective-permute-start | bytes 884744 | tf_op jit(solution)/shard_map/ppermute | solution.py:51
  43.8 9.5 %collective-permute-start.2 = (bf16[24,3072]{1,0:T(8,128)(2,1)S(1)}, bf16[24,3072]{1,0:T(8,128)(2,1)S(1)}, u32[]{:S(2)}, u32[]{:S(2)}) collective-permute-start(bf16[24,3072]{1,0:T(8,128)(2,1)S(1)} %get-tuple-element.26), channel_id=1, source_target_pairs={{0,2},{1,15},{2,4},{3,1},{4,6},{5,3},{6,8},{7,5},{8,10},{9,7},{10,... | collective-permute-start | bytes 442376 | tf_op jit(solution)/shard_map/ppermute | solution.py:51
  43.8 11.1 %collective-permute-start.4 = (bf16[24,3072]{1,0:T(8,128)(2,1)S(1)}, bf16[24,3072]{1,0:T(8,128)(2,1)S(1)}, u32[]{:S(2)}, u32[]{:S(2)}) collective-permute-start(bf16[24,3072]{1,0:T(8,128)(2,1)S(1)} %get-tuple-element.27), channel_id=1, source_target_pairs={{0,2},{1,15},{2,4},{3,1},{4,6},{5,3},{6,8},{7,5},{8,10},{9,7},{10,... | collective-permute-start | bytes 442376 | tf_op jit(solution)/shard_map/ppermute | solution.py:51
  53.3 6.4 %collective-permute-start.3 = (bf16[24,3072]{1,0:T(8,128)(2,1)S(1)}, bf16[24,3072]{1,0:T(8,128)(2,1)S(1)}, u32[]{:S(2)}, u32[]{:S(2)}) collective-permute-start(bf16[24,3072]{1,0:T(8,128)(2,1)S(1)} %collective-permute-done.2.left_ref), channel_id=1, source_target_pairs={{0,2},{1,15},{2,4},{3,1},{4,6},{5,3},{6,8},{7,5},{8,10},{9,7},{10,... | collective-permute-start | bytes 442376 | tf_op jit(solution)/shard_map/ppermute | solution.py:51
  54.9 6.4 %collective-permute-start.5 = (bf16[24,3072]{1,0:T(8,128)(2,1)S(1)}, bf16[24,3072]{1,0:T(8,128)(2,1)S(1)}, u32[]{:S(2)}, u32[]{:S(2)}) collective-permute-start(bf16[24,3072]{1,0:T(8,128)(2,1)S(1)} %collective-permute-done.4.right_ref), channel_id=1, source_target_pairs={{0,2},{1,15},{2,4},{3,1},{4,6},{5,3},{6,8},{7,5},{8,10},{9,7},{10,... | collective-permute-start | bytes 442376 | tf_op jit(solution)/shard_map/ppermute | solution.py:51
  54.9 13.5 %collective-permute-start.9 = (bf16[24,6144]{1,0:T(8,128)(2,1)S(1)}, bf16[24,6144]{1,0:T(8,128)(2,1)S(1)}, u32[]{:S(2)}, u32[]{:S(2)}) collective-permute-start(bf16[24,6144]{1,0:T(8,128)(2,1)S(1)} %collective-permute-done.8.refs_9_), channel_id=1, source_target_pairs={{0,2},{1,15},{2,4},{3,1},{4,6},{5,3},{6,8},{7,5},{8,10},{9,7},{10,... | collective-permute-start | bytes 884744 | tf_op jit(solution)/shard_map/ppermute | solution.py:51
  59.6 6.4 %collective-permute-start.13 = (bf16[24,3072]{1,0:T(8,128)(2,1)S(1)}, bf16[24,3072]{1,0:T(8,128)(2,1)S(1)}, u32[]{:S(2)}, u32[]{:S(2)}) collective-permute-start(bf16[24,3072]{1,0:T(8,128)(2,1)S(1)} %collective-permute-done.3.left_ref), channel_id=1, source_target_pairs={{0,2},{1,15},{2,4},{3,1},{4,6},{5,3},{6,8},{7,5},{8,10},{9,7},{10,... | collective-permute-start | bytes 442376 | tf_op jit(solution)/shard_map/ppermute | solution.py:51
  61.2 6.4 %collective-permute-start.15 = (bf16[24,3072]{1,0:T(8,128)(2,1)S(1)}, bf16[24,3072]{1,0:T(8,128)(2,1)S(1)}, u32[]{:S(2)}, u32[]{:S(2)}) collective-permute-start(bf16[24,3072]{1,0:T(8,128)(2,1)S(1)} %collective-permute-done.5.right_ref), channel_id=1, source_target_pairs={{0,2},{1,15},{2,4},{3,1},{4,6},{5,3},{6,8},{7,5},{8,10},{9,7},{10,... | collective-permute-start | bytes 442376 | tf_op jit(solution)/shard_map/ppermute | solution.py:51
  66.0 6.4 %collective-permute-start.14 = (bf16[24,3072]{1,0:T(8,128)(2,1)S(1)}, bf16[24,3072]{1,0:T(8,128)(2,1)S(1)}, u32[]{:S(2)}, u32[]{:S(2)}) collective-permute-start(bf16[24,3072]{1,0:T(8,128)(2,1)S(1)} %collective-permute-done.13.left_ref), channel_id=1, source_target_pairs={{0,2},{1,15},{2,4},{3,1},{4,6},{5,3},{6,8},{7,5},{8,10},{9,7},{10,... | collective-permute-start | bytes 442376 | tf_op jit(solution)/shard_map/ppermute | solution.py:51
  67.6 6.4 %collective-permute-start.16 = (bf16[24,3072]{1,0:T(8,128)(2,1)S(1)}, bf16[24,3072]{1,0:T(8,128)(2,1)S(1)}, u32[]{:S(2)}, u32[]{:S(2)}) collective-permute-start(bf16[24,3072]{1,0:T(8,128)(2,1)S(1)} %collective-permute-done.15.right_ref), channel_id=1, source_target_pairs={{0,2},{1,15},{2,4},{3,1},{4,6},{5,3},{6,8},{7,5},{8,10},{9,7},{10,... | collective-permute-start | bytes 442376 | tf_op jit(solution)/shard_map/ppermute | solution.py:51
  67.6 6.4 %collective-permute-start.7 = (bf16[24,6144]{1,0:T(8,128)(2,1)S(1)}, bf16[24,6144]{1,0:T(8,128)(2,1)S(1)}, u32[]{:S(2)}, u32[]{:S(2)}) collective-permute-start(bf16[24,6144]{1,0:T(8,128)(2,1)S(1)} %joined.5.refs_7_), channel_id=1, source_target_pairs={{0,1},{1,0},{2,3},{3,2},{4,5},{5,4},{6,7},{7,6},{8,9},{9,8},{10,11... | collective-permute-start | bytes 884744 | tf_op jit(solution)/shard_map/ppermute | solution.py:38
  67.8 6.8 %collective-permute-start.6 = (bf16[24,6144]{1,0:T(8,128)(2,1)S(1)}, bf16[24,6144]{1,0:T(8,128)(2,1)S(1)}, u32[]{:S(2)}, u32[]{:S(2)}) collective-permute-start(bf16[24,6144]{1,0:T(8,128)(2,1)S(1)} %joined.4.refs_6_), channel_id=1, source_target_pairs={{0,1},{1,0},{2,3},{3,2},{4,5},{5,4},{6,7},{7,6},{8,9},{9,8},{10,11... | collective-permute-start | bytes 884744 | tf_op jit(solution)/shard_map/ppermute | solution.py:38
  68.4 8.7 %collective-permute-start.17 = (bf16[24,6144]{1,0:T(8,128)(2,1)S(1)}, bf16[24,6144]{1,0:T(8,128)(2,1)S(1)}, u32[]{:S(2)}, u32[]{:S(2)}) collective-permute-start(bf16[24,6144]{1,0:T(8,128)(2,1)S(1)} %collective-permute-done.9.refs_8_), channel_id=1, source_target_pairs={{0,2},{1,15},{2,4},{3,1},{4,6},{5,3},{6,8},{7,5},{8,10},{9,7},{10,... | collective-permute-start | bytes 884744 | tf_op jit(solution)/shard_map/ppermute | solution.py:51
  72.4 4.7 %collective-permute-start.11 = (bf16[24,6144]{1,0:T(8,128)(2,1)S(1)}, bf16[24,6144]{1,0:T(8,128)(2,1)S(1)}, u32[]{:S(2)}, u32[]{:S(2)}) collective-permute-start(bf16[24,6144]{1,0:T(8,128)(2,1)S(1)} %collective-permute-done.8.refs_9_), channel_id=1, source_target_pairs={{0,1},{1,0},{2,3},{3,2},{4,5},{5,4},{6,7},{7,6},{8,9},{9,8},{10,11... | collective-permute-start | bytes 884744 | tf_op jit(solution)/shard_map/ppermute | solution.py:38
  73.9 3.2 %collective-permute-start.10 = (bf16[24,6144]{1,0:T(8,128)(2,1)S(1)}, bf16[24,6144]{1,0:T(8,128)(2,1)S(1)}, u32[]{:S(2)}, u32[]{:S(2)}) collective-permute-start(bf16[24,6144]{1,0:T(8,128)(2,1)S(1)} %collective-permute-done.9.refs_8_), channel_id=1, source_target_pairs={{0,1},{1,0},{2,3},{3,2},{4,5},{5,4},{6,7},{7,6},{8,9},{9,8},{10,11... | collective-permute-start | bytes 884744 | tf_op jit(solution)/shard_map/ppermute | solution.py:38
  74.0 8.0 %collective-permute-start.19 = (bf16[24,6144]{1,0:T(8,128)(2,1)S(1)}, bf16[24,6144]{1,0:T(8,128)(2,1)S(1)}, u32[]{:S(2)}, u32[]{:S(2)}) collective-permute-start(bf16[24,6144]{1,0:T(8,128)(2,1)S(1)} %joined.7.refs_5_), channel_id=1, source_target_pairs={{0,1},{1,0},{2,3},{3,2},{4,5},{5,4},{6,7},{7,6},{8,9},{9,8},{10,11... | collective-permute-start | bytes 884744 | tf_op jit(solution)/shard_map/ppermute | solution.py:38
  74.6 7.4 %collective-permute-start.20 = (bf16[24,6144]{1,0:T(8,128)(2,1)S(1)}, bf16[24,6144]{1,0:T(8,128)(2,1)S(1)}, u32[]{:S(2)}, u32[]{:S(2)}) collective-permute-start(bf16[24,6144]{1,0:T(8,128)(2,1)S(1)} %joined.6.refs_0_), channel_id=1, source_target_pairs={{0,1},{1,0},{2,3},{3,2},{4,5},{5,4},{6,7},{7,6},{8,9},{9,8},{10,11... | collective-permute-start | bytes 884744 | tf_op jit(solution)/shard_map/ppermute | solution.py:38
  77.1 4.9 %collective-permute-start.18 = (bf16[24,6144]{1,0:T(8,128)(2,1)S(1)}, bf16[24,6144]{1,0:T(8,128)(2,1)S(1)}, u32[]{:S(2)}, u32[]{:S(2)}) collective-permute-start(bf16[24,6144]{1,0:T(8,128)(2,1)S(1)} %collective-permute-done.17.refs_4_), channel_id=1, source_target_pairs={{0,1},{1,0},{2,3},{3,2},{4,5},{5,4},{6,7},{7,6},{8,9},{9,8},{10,11... | collective-permute-start | bytes 884744 | tf_op jit(solution)/shard_map/ppermute | solution.py:38
  83.7 1.8 %collective-permute-start.31 = (bf16[24,6144]{1,0:T(8,128)(2,1)S(1)}, bf16[24,6144]{1,0:T(8,128)(2,1)S(1)}, u32[]{:S(2)}, u32[]{:S(2)}) collective-permute-start(bf16[24,6144]{1,0:T(8,128)(2,1)S(1)} %get-tuple-element.41), channel_id=1, source_target_pairs={{0,1},{1,0},{2,3},{3,2},{4,5},{5,4},{6,7},{7,6},{8,9},{9,8},{10,11... | collective-permute-start | bytes 884744 | tf_op jit(solution)/shard_map/ppermute | solution.py:38
  84.4 2.7 %collective-permute-start.30 = (bf16[48,6144]{1,0:T(8,128)(2,1)S(1)}, bf16[48,6144]{1,0:T(8,128)(2,1)S(1)}, u32[]{:S(2)}, u32[]{:S(2)}) collective-permute-start(bf16[48,6144]{1,0:T(8,128)(2,1)S(1)} %get-tuple-element.39), channel_id=1, source_target_pairs={{0,1},{1,0},{2,3},{3,2},{4,5},{5,4},{6,7},{7,6},{8,9},{9,8},{10,11... | collective-permute-start | bytes 1769480 | tf_op jit(solution)/shard_map/ppermute | solution.py:38
  84.5 9.4 %collective-permute-start.21 = (bf16[48,6144]{1,0:T(8,128)(2,1)S(1)}, bf16[48,6144]{1,0:T(8,128)(2,1)S(1)}, u32[]{:S(2)}, u32[]{:S(2)}) collective-permute-start(bf16[48,6144]{1,0:T(8,128)(2,1)S(1)} %get-tuple-element.35), channel_id=1, source_target_pairs={{0,1},{1,0},{2,3},{3,2},{4,5},{5,4},{6,7},{7,6},{8,9},{9,8},{10,11... | collective-permute-start | bytes 1769480 | tf_op jit(solution)/shard_map/ppermute | solution.py:38
  85.6 8.0 %collective-permute-start.32 = (bf16[24,6144]{1,0:T(8,128)(2,1)S(1)}, bf16[24,6144]{1,0:T(8,128)(2,1)S(1)}, u32[]{:S(2)}, u32[]{:S(2)}) collective-permute-start(bf16[24,6144]{1,0:T(8,128)(2,1)S(1)} %hop_sum.20), channel_id=1, source_target_pairs={{0,2},{1,15},{2,4},{3,1},{4,6},{5,3},{6,8},{7,5},{8,10},{9,7},{10,... | collective-permute-start | bytes 884744 | tf_op jit(solution)/shard_map/ppermute | solution.py:51
  85.8 19.4 %collective-permute-start.12 = (bf16[48,6144]{1,0:T(8,128)(2,1)S(1)}, bf16[48,6144]{1,0:T(8,128)(2,1)S(1)}, u32[]{:S(2)}, u32[]{:S(2)}) collective-permute-start(bf16[48,6144]{1,0:T(8,128)(2,1)S(1)} %get-tuple-element.30), channel_id=1, source_target_pairs={{0,1},{1,0},{2,3},{3,2},{4,5},{5,4},{6,7},{7,6},{8,9},{9,8},{10,11... | collective-permute-start | bytes 1769480 | tf_op jit(solution)/shard_map/ppermute | solution.py:38
  93.8 8.0 %collective-permute-start.33 = (bf16[24,6144]{1,0:T(8,128)(2,1)S(1)}, bf16[24,6144]{1,0:T(8,128)(2,1)S(1)}, u32[]{:S(2)}, u32[]{:S(2)}) collective-permute-start(bf16[24,6144]{1,0:T(8,128)(2,1)S(1)} %hop_sum.21), channel_id=1, source_target_pairs={{0,2},{1,15},{2,4},{3,1},{4,6},{5,3},{6,8},{7,5},{8,10},{9,7},{10,... | collective-permute-start | bytes 884744 | tf_op jit(solution)/shard_map/ppermute | solution.py:51
  94.0 9.4 %collective-permute-start.26 = (bf16[24,3072]{1,0:T(8,128)(2,1)S(1)}, bf16[24,3072]{1,0:T(8,128)(2,1)S(1)}, u32[]{:S(2)}, u32[]{:S(2)}) collective-permute-start(bf16[24,3072]{1,0:T(8,128)(2,1)S(1)} %hop_sum.16), channel_id=1, source_target_pairs={{0,2},{1,15},{2,4},{3,1},{4,6},{5,3},{6,8},{7,5},{8,10},{9,7},{10,... | collective-permute-start | bytes 442376 | tf_op jit(solution)/shard_map/ppermute | solution.py:51
  94.4 10.6 %collective-permute-start.22 = (bf16[24,3072]{1,0:T(8,128)(2,1)S(1)}, bf16[24,3072]{1,0:T(8,128)(2,1)S(1)}, u32[]{:S(2)}, u32[]{:S(2)}) collective-permute-start(bf16[24,3072]{1,0:T(8,128)(2,1)S(1)} %hop_sum.12), channel_id=1, source_target_pairs={{0,2},{1,15},{2,4},{3,1},{4,6},{5,3},{6,8},{7,5},{8,10},{9,7},{10,... | collective-permute-start | bytes 442376 | tf_op jit(solution)/shard_map/ppermute | solution.py:51
  102.0 11.4 %collective-permute-start.34 = (bf16[24,6144]{1,0:T(8,128)(2,1)S(1)}, bf16[24,6144]{1,0:T(8,128)(2,1)S(1)}, u32[]{:S(2)}, u32[]{:S(2)}) collective-permute-start(bf16[24,6144]{1,0:T(8,128)(2,1)S(1)} %hop_sum.22), channel_id=1, source_target_pairs={{0,2},{1,15},{2,4},{3,1},{4,6},{5,3},{6,8},{7,5},{8,10},{9,7},{10,... | collective-permute-start | bytes 884744 | tf_op jit(solution)/shard_map/ppermute | solution.py:51
  103.5 8.1 %collective-permute-start.27 = (bf16[24,3072]{1,0:T(8,128)(2,1)S(1)}, bf16[24,3072]{1,0:T(8,128)(2,1)S(1)}, u32[]{:S(2)}, u32[]{:S(2)}) collective-permute-start(bf16[24,3072]{1,0:T(8,128)(2,1)S(1)} %hop_sum.17), channel_id=1, source_target_pairs={{0,2},{1,15},{2,4},{3,1},{4,6},{5,3},{6,8},{7,5},{8,10},{9,7},{10,... | collective-permute-start | bytes 442376 | tf_op jit(solution)/shard_map/ppermute | solution.py:51
  105.1 8.1 %collective-permute-start.23 = (bf16[24,3072]{1,0:T(8,128)(2,1)S(1)}, bf16[24,3072]{1,0:T(8,128)(2,1)S(1)}, u32[]{:S(2)}, u32[]{:S(2)}) collective-permute-start(bf16[24,3072]{1,0:T(8,128)(2,1)S(1)} %hop_sum.13), channel_id=1, source_target_pairs={{0,2},{1,15},{2,4},{3,1},{4,6},{5,3},{6,8},{7,5},{8,10},{9,7},{10,... | collective-permute-start | bytes 442376 | tf_op jit(solution)/shard_map/ppermute | solution.py:51
  111.6 6.5 %collective-permute-start.28 = (bf16[24,3072]{1,0:T(8,128)(2,1)S(1)}, bf16[24,3072]{1,0:T(8,128)(2,1)S(1)}, u32[]{:S(2)}, u32[]{:S(2)}) collective-permute-start(bf16[24,3072]{1,0:T(8,128)(2,1)S(1)} %hop_sum.18), channel_id=1, source_target_pairs={{0,2},{1,15},{2,4},{3,1},{4,6},{5,3},{6,8},{7,5},{8,10},{9,7},{10,... | collective-permute-start | bytes 442376 | tf_op jit(solution)/shard_map/ppermute | solution.py:51
  113.2 26.5 %copy-start = (s32[4,2]{0,1:T(2,128)S(1)}, s32[4,2]{0,1:T(2,128)}, u32[]{:S(2)}) copy-start(s32[4,2]{0,1:T(2,128)} %param.20) | copy-start | bytes 100
  113.2 26.5 %copy-start.1 = (f32[4,2]{0,1:T(2,128)S(1)}, f32[4,2]{0,1:T(2,128)}, u32[]{:S(2)}) copy-start(f32[4,2]{0,1:T(2,128)} %param.21) | copy-start | bytes 100
  113.2 6.5 %collective-permute-start.24 = (bf16[24,3072]{1,0:T(8,128)(2,1)S(1)}, bf16[24,3072]{1,0:T(8,128)(2,1)S(1)}, u32[]{:S(2)}, u32[]{:S(2)}) collective-permute-start(bf16[24,3072]{1,0:T(8,128)(2,1)S(1)} %hop_sum.14), channel_id=1, source_target_pairs={{0,2},{1,15},{2,4},{3,1},{4,6},{5,3},{6,8},{7,5},{8,10},{9,7},{10,... | collective-permute-start | bytes 442376 | tf_op jit(solution)/shard_map/ppermute | solution.py:51
  113.5 12.8 %collective-permute-start.35 = (bf16[24,6144]{1,0:T(8,128)(2,1)S(1)}, bf16[24,6144]{1,0:T(8,128)(2,1)S(1)}, u32[]{:S(2)}, u32[]{:S(2)}) collective-permute-start(bf16[24,6144]{1,0:T(8,128)(2,1)S(1)} %hop_sum.23), channel_id=1, source_target_pairs={{0,1},{1,0},{2,3},{3,2},{4,5},{5,4},{6,7},{7,6},{8,9},{9,8},{10,11... | collective-permute-start | bytes 884744 | tf_op jit(solution)/shard_map/ppermute | solution.py:38
  118.2 6.5 %collective-permute-start.29 = (bf16[24,3072]{1,0:T(8,128)(2,1)S(1)}, bf16[24,3072]{1,0:T(8,128)(2,1)S(1)}, u32[]{:S(2)}, u32[]{:S(2)}) collective-permute-start(bf16[24,3072]{1,0:T(8,128)(2,1)S(1)} %hop_sum.19), channel_id=1, source_target_pairs={{0,2},{1,15},{2,4},{3,1},{4,6},{5,3},{6,8},{7,5},{8,10},{9,7},{10,... | collective-permute-start | bytes 442376 | tf_op jit(solution)/shard_map/ppermute | solution.py:51
  119.8 6.5 %collective-permute-start.25 = (bf16[24,3072]{1,0:T(8,128)(2,1)S(1)}, bf16[24,3072]{1,0:T(8,128)(2,1)S(1)}, u32[]{:S(2)}, u32[]{:S(2)}) collective-permute-start(bf16[24,3072]{1,0:T(8,128)(2,1)S(1)} %hop_sum.15), channel_id=1, source_target_pairs={{0,2},{1,15},{2,4},{3,1},{4,6},{5,3},{6,8},{7,5},{8,10},{9,7},{10,... | collective-permute-start | bytes 442376 | tf_op jit(solution)/shard_map/ppermute | solution.py:51

commit v8 on v5

--- a/solution.py
+++ b/solution.py
@@ -51,38 +51,38 @@
     return lax.ppermute(value, ("dev_1", "dev_2"), pairs)
 
 
-def join_kernel(left_ref, right_ref, out_ref):
-    half = left_ref.shape[1]
-    out_ref[:, :half] = left_ref[...]
-    out_ref[:, half:] = right_ref[...]
-
-
-def joined(left, right):
-    rows, half = left.shape
+def join_kernel(*refs):
+    out = refs[-1]
+    rows, half = refs[0].shape
+    for i, ref in enumerate(refs[:-1]):
+        row, col = i // 2 * rows, i % 2 * half
+        out[row : row + rows, col : col + half] = ref[...]
+
+
+def joined(*sides):
+    rows, half = sides[0].shape
     vm = pl.BlockSpec(memory_space=pltpu.VMEM)
     return pl.pallas_call(
         join_kernel,
-        out_shape=jax.ShapeDtypeStruct((rows, 2 * half), left.dtype),
-        in_specs=[vm] * 2,
+        out_shape=jax.ShapeDtypeStruct((len(sides) // 2 * rows, 2 * half), sides[0].dtype),
+        in_specs=[vm] * len(sides),
         out_specs=vm,
         compiler_params=pltpu.CompilerParams(vmem_limit_bytes=8 * 1024 * 1024),
         name="joined",
-    )(left, right)
-
-
-def gathered(own, left, right):
-    other = swapped(own)
+    )(*sides)
+
+
+def gathered(left, right):
     far = lax.axis_size("dev_1") // 2
+    sides = {0: [left, right], 1: [swapped(x) for x in (left, right)]}
+    other = joined(*sides[1])
     came, theirs = {}, {}
-    sides, whole = (left, right), other
     for step in range(1, far + 1):
-        sides = [passed_on(x) for x in sides]
-        came[step, 0] = joined(*sides)
-        if step < far:
-            whole = passed_on(whole)
-            came[step, 1] = whole
-        for part in (0, 1) if step < far else (0,):
-            theirs[step, part] = swapped(came[step, part])
+        parts = (1, 0) if step < far else (0,)
+        for part in reversed(parts):
+            sides[part] = [passed_on(x) for x in sides[part]]
+        came[step] = joined(*[x for part in parts for x in sides[part]])
+        theirs[step] = swapped(came[step])
     return other, came, theirs
 
 
@@ -485,36 +485,28 @@
         rows_x,
     )
     own_block, *own_sides = unpacked(lax.all_to_all(leaving, "dev_0", 0, 0, tiled=True))
-    other, came, theirs = gathered(own_block, *own_sides)
+    other, came, theirs = gathered(*own_sides)
     far = lax.axis_size("dev_1") // 2
     each = rows_x * MOST
+    last = far - 1
     near = range(far - 2, 0, -1)
-    pieces = [own_block, other]
-    for group in (theirs, came):
+    pieces = [own_block, other] + [group[step] for group in (theirs, came) for step in near]
+    home_own, home_other, *near_kept, near_sent, gate, up, down = early_products(
+        pieces, (w_gate, w_up, w_down), [each, each] + [2 * each] * len(near) + [2 * len(near) * each]
+    )
+    kept, got = {}, {}
+    near_got = swapped(near_sent)
+    for i, step in enumerate(near):
         for part in (0, 1):
-            pieces += [group[step, part] for step in near]
-    home_own, home_other, *groups, gate, up, down = early_products(
-        pieces, (w_gate, w_up, w_down), [each, each] + [len(near) * each] * 4
+            row = (1 - part) * each
+            kept[step, part] = (near_kept[i], row)
+            got[step, part] = (near_got, 2 * i * each + row)
+    far_kept, last_kept, sent = late_products(
+        [came[far], theirs[last], theirs[far], came[last]], (gate, up, down), [each, 2 * each, 3 * each]
     )
-    last = far - 1
-    pieces = [
-        came[far, 0],
-        theirs[last, 1],
-        theirs[last, 0],
-        theirs[far, 0],
-        came[last, 1],
-        came[last, 0],
-    ]
-    kept, got = {}, {}
-    sent = [swapped(groups[2 + part]) for part in (0, 1)]
-    for part in (0, 1):
-        for i, step in enumerate(near):
-            kept[step, part] = (groups[part], i * each)
-            got[step, part] = (sent[part], i * each)
-    *stay, sent_1, sent_0 = late_products(pieces, (gate, up, down), [each, each, each, 2 * each, each])
-    kept[far, 1], kept[last, 1], kept[last, 0] = [(x, 0) for x in stay]
-    first = swapped(sent_1)
-    got[far, 1], got[last, 1], got[last, 0] = (first, 0), (first, each), (swapped(sent_0), 0)
+    kept[far, 1], kept[last, 1], kept[last, 0] = (far_kept, 0), (last_kept, 0), (last_kept, each)
+    first = swapped(sent)
+    got[far, 1], got[last, 1], got[last, 0] = (first, 0), (first, each), (first, 2 * each)
     last_terms = scattered(far, each, home_own, home_other, kept, got)
     home = lax.all_to_all(packed_sum(*last_terms, rows_x), "dev_0", 0, 0, tiled=True)
     return mixed_in(expert_ids.T, route_weights.T, home, hidden_state)

time: 140 us -> 134 us (0.957)
  waiting for transfers between devices: 72.4 us -> 65.7 us
    ppermute x25 -> x28, waiting for transfers between devices: 64.9 us -> 58 us  [passed_on(): return lax.ppermute(value, ('dev_1', 'dev_2'), pairs)]
    ppermute x25 -> x28, starting transfers between devices: 3.2 us -> 5.68 us  [passed_on(): return lax.ppermute(value, ('dev_1', 'dev_2'), pairs)]
    ppermute x13 -> x9, starting transfers between devices: 3.22 us -> 2.1 us  [shifted(): lax.ppermute(value, axis, [(place, (place + steps) % count) for place in...]
    ppermute x13 -> x9, waiting for transfers between devices: 3.35 us -> 3.46 us  [shifted(): lax.ppermute(value, axis, [(place, (place + steps) % count) for place in...]
  transfers between devices with their start and end apart: 39 -> 38, of which waited for: 26 -> 32; matrix products, arithmetic and copies ran while one was open for 0% -> 0% of each run, Pallas kernels for 5% -> 6%
where the time goes in v8:
time: 134 us
  waiting for transfers between devices  65.7 us (49%)
  blocking collectives  33.1 us (25%)
  starting transfers between devices  20.9 us (16%)
  Pallas kernels  14 us (10%)
    ppermute x28, waiting for transfers between devices, passed_on(): return lax.ppermute(value, ('dev_1', 'dev_2'), pairs)  58 us
    all_to_all x1, blocking collectives, layer(): lax.all_to_all(leaving, 'dev_0', 0, 0, tiled=True)  19.9 us
    all_to_all x1, blocking collectives, layer(): lax.all_to_all(packed_sum(*last_terms, rows_x), 'dev_0', 0, 0, tiled=True)  13.2 us
    ppermute x1, starting transfers between devices, passed_along(): lax.ppermute(value, axis, [(source, source + steps) for source in range(l...  13.1 us
    ppermute x28, starting transfers between devices, passed_on(): return lax.ppermute(value, ('dev_1', 'dev_2'), pairs)  5.68 us
    pallas_call x1, Pallas kernels, early_products(): pl.pallas_call(functools.partial(early_kernel, len(pieces)), out_shape=ou...  4.89 us
    pallas_call x1, Pallas kernels, attended(): pl.pallas_call(attend_kernel, out_shape=[jax.ShapeDtypeStruct((reqs, widt...  4.61 us
    ppermute x1, waiting for transfers between devices, passed_along(): lax.ppermute(value, axis, [(source, source + steps) for source in range(l...  4.18 us
  transfers between devices with their start and end apart: 38, of which 32 were waited for; matrix products, arithmetic and copies ran while one was open for 0% of the time, Pallas kernels for 6%

profile of v8, /device:TPU:514, one launch (start us, length us, event | category | flops | bytes accessed | tf_op | source)
XLA Modules:
  0.0 134.0 jit_solution(7624946439628264014)
XLA Ops:
  0.0 13.1 %collective-permute-start = (bf16[64,2048]{1,0:T(8,128)(2,1)}, bf16[64,2048]{1,0:T(8,128)(2,1)S(1)}, u32[]{:S(2)}, u32[]{:S(2)}) collective-permute-start(bf16[64,2048]{1,0:T(8,128)(2,1)} %refs_7_.2), channel_id=1, source_target_pairs={{1,0},{2,1},{3,2},{4,3},{5,4},{6,5},{7,6},{8,7},{9,8},{10,9},{11,1... | collective-permute-start | bytes 786440 | tf_op jit(solution)/shard_map/ppermute | solution.py:33
  13.2 4.2 %collective-permute-done.refs_0_ = bf16[64,2048]{1,0:T(8,128)(2,1)S(1)} collective-permute-done((bf16[64,2048]{1,0:T(8,128)(2,1)}, bf16[64,2048]{1,0:T(8,128)(2,1)S(1)}, u32[]{:S(2)}, u32[]{:S(2)}) %collective-permute-start) | collective-permute-done | bytes 262176 | tf_op jit(solution)/shard_map/ppermute | solution.py:33
  17.3 4.6 %attended.1 = (f32[4,6144]{1,0:T(4,128)S(1)}, bf16[8,144,128]{2,1,0:T(8,128)(2,1)S(1)}) custom-call(s32[1]{0:T(128)} %bitcast.2.me_ref, bf16[64,2048]{1,0:T(8,128)(2,1)S(1)} %collective-permute-done.refs_0_, s32[4]{0:T(128)} %refs_1_.1, s32[2,4]{1,0:T(2,128)} %bitcast.5, s32[1,128]{1,0:T(1,128)} %bitcast.9, bf16[4,6144]{1,0:T(4,128)(2,1)} %refs_4_.1, ...), custom_call_target="tpu_custom_call" | custom-call | flops 77070336 | bytes 2097152 | tf_op jit(solution)/shard_map/attended/pallas_call | solution.py:338
  21.9 19.9 %all_to_all.10.came_ref = bf16[8,144,128]{2,1,0:T(8,128)(2,1)S(1)} all-to-all(bf16[8,144,128]{2,1,0:T(8,128)(2,1)S(1)} %get-tuple-element.21), channel_id=1, replica_groups=mesh['groups'=2,'dev_0'=8,'dev_1'=8,'dev_2'=2] {'dev_0'}, dimensions={0} | all-to-all | bytes 589824 | tf_op jit(solution)/shard_map/all_to_all | solution.py:487
  41.8 0.3 unpacked.1
  42.1 0.1 collective-permute-start.1
  42.2 0.5 collective-permute-start.2
  42.7 0.9 collective-permute-done.1.refs_0_
  43.6 0.2 collective-permute-done.2.refs_1_
  43.8 5.3 %collective-permute-done.7.refs_2_ = bf16[24,3072]{1,0:T(8,128)(2,1)S(1)} collective-permute-done((bf16[24,3072]{1,0:T(8,128)(2,1)S(1)}, bf16[24,3072]{1,0:T(8,128)(2,1)S(1)}, u32[]{:S(2)}, u32[]{:S(2)}) %collective-permute-start.7) | collective-permute-done | bytes 147488 | tf_op jit(solution)/shard_map/ppermute | solution.py:51
  49.1 1.6 %collective-permute-done.9.refs_3_ = bf16[24,3072]{1,0:T(8,128)(2,1)S(1)} collective-permute-done((bf16[24,3072]{1,0:T(8,128)(2,1)S(1)}, bf16[24,3072]{1,0:T(8,128)(2,1)S(1)}, u32[]{:S(2)}, u32[]{:S(2)}) %collective-permute-start.9) | collective-permute-done | bytes 147488 | tf_op jit(solution)/shard_map/ppermute | solution.py:51
  50.6 1.6 %collective-permute-done.3.refs_0_ = bf16[24,3072]{1,0:T(8,128)(2,1)S(1)} collective-permute-done((bf16[24,3072]{1,0:T(8,128)(2,1)S(1)}, bf16[24,3072]{1,0:T(8,128)(2,1)S(1)}, u32[]{:S(2)}, u32[]{:S(2)}) %collective-permute-start.3) | collective-permute-done | bytes 147488 | tf_op jit(solution)/shard_map/ppermute | solution.py:51
  52.2 1.6 %collective-permute-done.5.refs_1_ = bf16[24,3072]{1,0:T(8,128)(2,1)S(1)} collective-permute-done((bf16[24,3072]{1,0:T(8,128)(2,1)S(1)}, bf16[24,3072]{1,0:T(8,128)(2,1)S(1)}, u32[]{:S(2)}, u32[]{:S(2)}) %collective-permute-start.5) | collective-permute-done | bytes 147488 | tf_op jit(solution)/shard_map/ppermute | solution.py:51
  53.8 1.6 %collective-permute-done.8.refs_2_ = bf16[24,3072]{1,0:T(8,128)(2,1)S(1)} collective-permute-done((bf16[24,3072]{1,0:T(8,128)(2,1)S(1)}, bf16[24,3072]{1,0:T(8,128)(2,1)S(1)}, u32[]{:S(2)}, u32[]{:S(2)}) %collective-permute-start.8) | collective-permute-done | bytes 147488 | tf_op jit(solution)/shard_map/ppermute | solution.py:51
  55.5 0.1 collective-permute-start.12
  55.6 1.4 %collective-permute-done.10.refs_3_ = bf16[24,3072]{1,0:T(8,128)(2,1)S(1)} collective-permute-done((bf16[24,3072]{1,0:T(8,128)(2,1)S(1)}, bf16[24,3072]{1,0:T(8,128)(2,1)S(1)}, u32[]{:S(2)}, u32[]{:S(2)}) %collective-permute-start.10) | collective-permute-done | bytes 147488 | tf_op jit(solution)/shard_map/ppermute | solution.py:51
  57.0 1.6 %collective-permute-done.4.refs_0_ = bf16[24,3072]{1,0:T(8,128)(2,1)S(1)} collective-permute-done((bf16[24,3072]{1,0:T(8,128)(2,1)S(1)}, bf16[24,3072]{1,0:T(8,128)(2,1)S(1)}, u32[]{:S(2)}, u32[]{:S(2)}) %collective-permute-start.4) | collective-permute-done | bytes 147488 | tf_op jit(solution)/shard_map/ppermute | solution.py:51
  58.6 1.6 %collective-permute-done.6.refs_1_ = bf16[24,3072]{1,0:T(8,128)(2,1)S(1)} collective-permute-done((bf16[24,3072]{1,0:T(8,128)(2,1)S(1)}, bf16[24,3072]{1,0:T(8,128)(2,1)S(1)}, u32[]{:S(2)}, u32[]{:S(2)}) %collective-permute-start.6) | collective-permute-done | bytes 147488 | tf_op jit(solution)/shard_map/ppermute | solution.py:51
  60.2 0.1 collective-permute-start.11
  60.4 0.3 collective-permute-start.16
  60.7 0.1 collective-permute-start.18
  60.8 1.0 collective-permute-done.14.refs_2_
  61.8 5.2 %collective-permute-done.16.refs_3_ = bf16[24,3072]{1,0:T(8,128)(2,1)S(1)} collective-permute-done((bf16[24,3072]{1,0:T(8,128)(2,1)S(1)}, bf16[24,3072]{1,0:T(8,128)(2,1)S(1)}, u32[]{:S(2)}, u32[]{:S(2)}) %collective-permute-start.16) | collective-permute-done | bytes 147488 | tf_op jit(solution)/shard_map/ppermute | solution.py:51
  67.0 1.6 %collective-permute-done.18.refs_0_ = bf16[24,3072]{1,0:T(8,128)(2,1)S(1)} collective-permute-done((bf16[24,3072]{1,0:T(8,128)(2,1)S(1)}, bf16[24,3072]{1,0:T(8,128)(2,1)S(1)}, u32[]{:S(2)}, u32[]{:S(2)}) %collective-permute-start.18) | collective-permute-done | bytes 147488 | tf_op jit(solution)/shard_map/ppermute | solution.py:51
  68.6 1.6 %collective-permute-done.19.refs_1_ = bf16[24,3072]{1,0:T(8,128)(2,1)S(1)} collective-permute-done((bf16[24,3072]{1,0:T(8,128)(2,1)S(1)}, bf16[24,3072]{1,0:T(8,128)(2,1)S(1)}, u32[]{:S(2)}, u32[]{:S(2)}) %collective-permute-start.19) | collective-permute-done | bytes 147488 | tf_op jit(solution)/shard_map/ppermute | solution.py:51
  70.2 0.1 collective-permute-start.20
  70.3 0.1 collective-permute-start.15
  70.5 0.1 collective-permute-start.17
  70.6 6.2 %collective-permute-done.15.refs_0_ = bf16[24,3072]{1,0:T(8,128)(2,1)S(1)} collective-permute-done((bf16[24,3072]{1,0:T(8,128)(2,1)S(1)}, bf16[24,3072]{1,0:T(8,128)(2,1)S(1)}, u32[]{:S(2)}, u32[]{:S(2)}) %collective-permute-start.15) | collective-permute-done | bytes 147488 | tf_op jit(solution)/shard_map/ppermute | solution.py:51
  76.8 1.6 %collective-permute-done.17.refs_1_ = bf16[24,3072]{1,0:T(8,128)(2,1)S(1)} collective-permute-done((bf16[24,3072]{1,0:T(8,128)(2,1)S(1)}, bf16[24,3072]{1,0:T(8,128)(2,1)S(1)}, u32[]{:S(2)}, u32[]{:S(2)}) %collective-permute-start.17) | collective-permute-done | bytes 147488 | tf_op jit(solution)/shard_map/ppermute | solution.py:51
  78.4 0.1 collective-permute-start.21
  78.6 4.9 %early.1 = (bf16[24,6144]{1,0:T(8,128)(2,1)S(1)}, bf16[24,6144]{1,0:T(8,128)(2,1)S(1)}, bf16[48,6144]{1,0:T(8,128)(2,1)S(1)}, bf16[48,6144]{1,0:T(8,128)(2,1)S(1...) custom-call(bf16[24,6144]{1,0:T(8,128)(2,1)S(1)} %get-tuple-element., ...), custom_call_target="tpu_custom_call" | custom-call | flops 2264924160 | bytes 9437184 | tf_op jit(solution)/shard_map/early/pallas_call | solution.py:206
  83.5 0.6 collective-permute-start.13
  84.1 1.7 %late.1 = (bf16[24,6144]{1,0:T(8,128)(2,1)S(1)}, bf16[48,6144]{1,0:T(8,128)(2,1)S(1)}, bf16[72,6144]{1,0:T(8,128)(2,1)S(1)}) custom-call(bf16[24,6144]{1,0:T(8,128)(2,1)S(1)} %joined.8.refs_0_, bf16[48,6144]{1,0:T(8,128)(2,1)S(1)} %collective-permute-done.20.refs_1_, bf16[24,6144]{1,0:T(8,128)(2,1)S(1)} %collective-permute-done.21.refs_2_, ...), custom_call_target="tpu_custom_call" | custom-call | flops 1358954496 | bytes 9437184 | tf_op jit(solution)/shard_map/late/pallas_call | solution.py:221
  85.8 0.2 collective-permute-start.22
  86.0 2.4 %collective-permute-done.22.refs_1_ = bf16[72,6144]{1,0:T(8,128)(2,1)S(1)} collective-permute-done((bf16[72,6144]{1,0:T(8,128)(2,1)S(1)}, bf16[72,6144]{1,0:T(8,128)(2,1)S(1)}, u32[]{:S(2)}, u32[]{:S(2)}) %collective-permute-start.22) | collective-permute-done | bytes 884768 | tf_op jit(solution)/shard_map/ppermute | solution.py:38
  88.4 0.1 collective-permute-start.34
  88.6 0.1 collective-permute-start.31
  88.8 0.2 collective-permute-start.27
  89.0 3.1 %collective-permute-start.23 = (bf16[24,3072]{1,0:T(8,128)(2,1)S(1)}, bf16[24,3072]{1,0:T(8,128)(2,1)S(1)}, u32[]{:S(2)}, u32[]{:S(2)}) collective-permute-start(bf16[24,3072]{1,0:T(8,128)(2,1)S(1)} %hop_sum.14), channel_id=1, source_target_pairs={{0,2},{1,15},{2,4},{3,1},{4,6},{5,3},{6,8},{7,5},{8,10},{9,7},{10,... | collective-permute-start | bytes 442376 | tf_op jit(solution)/shard_map/ppermute | solution.py:51
  92.2 2.7 %collective-permute-done.34.refs_2_ = bf16[24,3072]{1,0:T(8,128)(2,1)S(1)} collective-permute-done((bf16[24,3072]{1,0:T(8,128)(2,1)S(1)}, bf16[24,3072]{1,0:T(8,128)(2,1)S(1)}, u32[]{:S(2)}, u32[]{:S(2)}) %collective-permute-start.34) | collective-permute-done | bytes 147488 | tf_op jit(solution)/shard_map/ppermute | solution.py:51
  94.9 0.1 collective-permute-start.35
  95.1 1.4 %collective-permute-done.31.refs_2_ = bf16[24,3072]{1,0:T(8,128)(2,1)S(1)} collective-permute-done((bf16[24,3072]{1,0:T(8,128)(2,1)S(1)}, bf16[24,3072]{1,0:T(8,128)(2,1)S(1)}, u32[]{:S(2)}, u32[]{:S(2)}) %collective-permute-start.31) | collective-permute-done | bytes 147488 | tf_op jit(solution)/shard_map/ppermute | solution.py:51
  96.5 0.1 collective-permute-start.32
  96.6 1.4 %collective-permute-done.27.refs_2_ = bf16[24,3072]{1,0:T(8,128)(2,1)S(1)} collective-permute-done((bf16[24,3072]{1,0:T(8,128)(2,1)S(1)}, bf16[24,3072]{1,0:T(8,128)(2,1)S(1)}, u32[]{:S(2)}, u32[]{:S(2)}) %collective-permute-start.27) | collective-permute-done | bytes 147488 | tf_op jit(solution)/shard_map/ppermute | solution.py:51
  98.2 1.4 %collective-permute-done.23.refs_2_ = bf16[24,3072]{1,0:T(8,128)(2,1)S(1)} collective-permute-done((bf16[24,3072]{1,0:T(8,128)(2,1)S(1)}, bf16[24,3072]{1,0:T(8,128)(2,1)S(1)}, u32[]{:S(2)}, u32[]{:S(2)}) %collective-permute-start.23) | collective-permute-done | bytes 147488 | tf_op jit(solution)/shard_map/ppermute | solution.py:51
  99.8 1.6 %collective-permute-done.35.refs_2_ = bf16[24,3072]{1,0:T(8,128)(2,1)S(1)} collective-permute-done((bf16[24,3072]{1,0:T(8,128)(2,1)S(1)}, bf16[24,3072]{1,0:T(8,128)(2,1)S(1)}, u32[]{:S(2)}, u32[]{:S(2)}) %collective-permute-start.35) | collective-permute-done | bytes 147488 | tf_op jit(solution)/shard_map/ppermute | solution.py:51
  101.5 0.1 collective-permute-start.36
  101.6 1.4 %collective-permute-done.32.refs_2_ = bf16[24,3072]{1,0:T(8,128)(2,1)S(1)} collective-permute-done((bf16[24,3072]{1,0:T(8,128)(2,1)S(1)}, bf16[24,3072]{1,0:T(8,128)(2,1)S(1)}, u32[]{:S(2)}, u32[]{:S(2)}) %collective-permute-start.32) | collective-permute-done | bytes 147488 | tf_op jit(solution)/shard_map/ppermute | solution.py:51
  103.0 0.1 collective-permute-start.33
  103.2 1.4 %collective-permute-done.28.refs_2_ = bf16[24,3072]{1,0:T(8,128)(2,1)S(1)} collective-permute-done((bf16[24,3072]{1,0:T(8,128)(2,1)S(1)}, bf16[24,3072]{1,0:T(8,128)(2,1)S(1)}, u32[]{:S(2)}, u32[]{:S(2)}) %collective-permute-start.28) | collective-permute-done | bytes 147488 | tf_op jit(solution)/shard_map/ppermute | solution.py:51
  104.6 0.1 collective-permute-start.29
  104.8 1.4 %collective-permute-done.24.refs_2_ = bf16[24,3072]{1,0:T(8,128)(2,1)S(1)} collective-permute-done((bf16[24,3072]{1,0:T(8,128)(2,1)S(1)}, bf16[24,3072]{1,0:T(8,128)(2,1)S(1)}, u32[]{:S(2)}, u32[]{:S(2)}) %collective-permute-start.24) | collective-permute-done | bytes 147488 | tf_op jit(solution)/shard_map/ppermute | solution.py:51
  106.2 0.1 collective-permute-start.25
  106.3 1.6 %collective-permute-done.36.right_ref = bf16[24,3072]{1,0:T(8,128)(2,1)S(1)} collective-permute-done((bf16[24,3072]{1,0:T(8,128)(2,1)S(1)}, bf16[24,3072]{1,0:T(8,128)(2,1)S(1)}, u32[]{:S(2)}, u32[]{:S(2)}) %collective-permute-start.36) | collective-permute-done | bytes 147488 | tf_op jit(solution)/shard_map/ppermute | solution.py:51
  107.9 1.6 %collective-permute-done.33.left_ref = bf16[24,3072]{1,0:T(8,128)(2,1)S(1)} collective-permute-done((bf16[24,3072]{1,0:T(8,128)(2,1)S(1)}, bf16[24,3072]{1,0:T(8,128)(2,1)S(1)}, u32[]{:S(2)}, u32[]{:S(2)}) %collective-permute-start.33) | collective-permute-done | bytes 147488 | tf_op jit(solution)/shard_map/ppermute | solution.py:51
  109.6 0.1 collective-permute-start.37
  109.7 1.3 collective-permute-done.29.refs_2_
  111.3 1.4 %collective-permute-done.25.refs_2_ = bf16[24,3072]{1,0:T(8,128)(2,1)S(1)} collective-permute-done((bf16[24,3072]{1,0:T(8,128)(2,1)S(1)}, bf16[24,3072]{1,0:T(8,128)(2,1)S(1)}, u32[]{:S(2)}, u32[]{:S(2)}) %collective-permute-start.25) | collective-permute-done | bytes 147488 | tf_op jit(solution)/shard_map/ppermute | solution.py:51
  112.9 4.7 %collective-permute-done.30.right_ref = bf16[24,3072]{1,0:T(8,128)(2,1)S(1)} collective-permute-done((bf16[24,3072]{1,0:T(8,128)(2,1)S(1)}, bf16[24,3072]{1,0:T(8,128)(2,1)S(1)}, u32[]{:S(2)}, u32[]{:S(2)}) %collective-permute-start.30) | collective-permute-done | bytes 147488 | tf_op jit(solution)/shard_map/ppermute | solution.py:51
  117.6 1.6 %collective-permute-done.26.left_ref = bf16[24,3072]{1,0:T(8,128)(2,1)S(1)} collective-permute-done((bf16[24,3072]{1,0:T(8,128)(2,1)S(1)}, bf16[24,3072]{1,0:T(8,128)(2,1)S(1)}, u32[]{:S(2)}, u32[]{:S(2)}) %collective-permute-start.26) | collective-permute-done | bytes 147488 | tf_op jit(solution)/shard_map/ppermute | solution.py:51
  119.2 0.3 packed_sum.1
  119.5 13.2 %all_to_all.11.home_ref = bf16[8,144,128]{2,1,0:T(8,128)(2,1)S(1)} all-to-all(bf16[8,144,128]{2,1,0:T(8,128)(2,1)S(1)} %packed_sum.1), channel_id=1, replica_groups=mesh['groups'=2,'dev_0'=8,'dev_1'=8,'dev_2'=2] {'dev_0'}, dimensions={0} | all-to-all | bytes 589824 | tf_op jit(solution)/shard_map/all_to_all | solution.py:511
  132.7 1.4 %mixed_in.1 = bf16[4,6144]{1,0:T(4,128)(2,1)} custom-call(s32[2,4]{1,0:T(2,128)S(1)} %bitcast.6, f32[2,4]{1,0:T(2,128)S(1)} %bitcast.7, bf16[8,144,128]{2,1,0:T(8,128)(2,1)S(1)} %all_to_all.11.home_ref, f32[4,6144]{1,0:T(4,128)S(1)} %get-tuple-element.36.hidden_ref), custom_call_target="tpu_custom_call" | custom-call | tf_op jit(solution)/shard_map/mixed_in/pallas_call | solution.py:443
  (44 shorter events, 1.5 us)
Async XLA Ops:
  0.0 17.3 %collective-permute-start = (bf16[64,2048]{1,0:T(8,128)(2,1)}, bf16[64,2048]{1,0:T(8,128)(2,1)S(1)}, u32[]{:S(2)}, u32[]{:S(2)}) collective-permute-start(bf16[64,2048]{1,0:T(8,128)(2,1)} %refs_7_.2), channel_id=1, source_target_pairs={{1,0},{2,1},{3,2},{4,3},{5,4},{6,5},{7,6},{8,7},{9,8},{10,9},{11,1... | collective-permute-start | bytes 786440 | tf_op jit(solution)/shard_map/ppermute | solution.py:33
  42.1 1.5 %collective-permute-start.1 = (bf16[24,3072]{1,0:T(8,128)(2,1)S(1)}, bf16[24,3072]{1,0:T(8,128)(2,1)S(1)}, u32[]{:S(2)}, u32[]{:S(2)}) collective-permute-start(bf16[24,3072]{1,0:T(8,128)(2,1)S(1)} %get-tuple-element.23), channel_id=1, source_target_pairs={{0,1},{1,0},{2,3},{3,2},{4,5},{5,4},{6,7},{7,6},{8,9},{9,8},{10,11... | collective-permute-start | bytes 442376 | tf_op jit(solution)/shard_map/ppermute | solution.py:38
  42.2 1.6 %collective-permute-start.2 = (bf16[24,3072]{1,0:T(8,128)(2,1)S(1)}, bf16[24,3072]{1,0:T(8,128)(2,1)S(1)}, u32[]{:S(2)}, u32[]{:S(2)}) collective-permute-start(bf16[24,3072]{1,0:T(8,128)(2,1)S(1)} %get-tuple-element.24), channel_id=1, source_target_pairs={{0,1},{1,0},{2,3},{3,2},{4,5},{5,4},{6,7},{7,6},{8,9},{9,8},{10,11... | collective-permute-start | bytes 442376 | tf_op jit(solution)/shard_map/ppermute | solution.py:38
  42.7 6.4 %collective-permute-start.7 = (bf16[24,3072]{1,0:T(8,128)(2,1)S(1)}, bf16[24,3072]{1,0:T(8,128)(2,1)S(1)}, u32[]{:S(2)}, u32[]{:S(2)}) collective-permute-start(bf16[24,3072]{1,0:T(8,128)(2,1)S(1)} %get-tuple-element.23), channel_id=1, source_target_pairs={{0,2},{1,15},{2,4},{3,1},{4,6},{5,3},{6,8},{7,5},{8,10},{9,7},{10,... | collective-permute-start | bytes 442376 | tf_op jit(solution)/shard_map/ppermute | solution.py:51
  42.7 7.9 %collective-permute-start.9 = (bf16[24,3072]{1,0:T(8,128)(2,1)S(1)}, bf16[24,3072]{1,0:T(8,128)(2,1)S(1)}, u32[]{:S(2)}, u32[]{:S(2)}) collective-permute-start(bf16[24,3072]{1,0:T(8,128)(2,1)S(1)} %get-tuple-element.24), channel_id=1, source_target_pairs={{0,2},{1,15},{2,4},{3,1},{4,6},{5,3},{6,8},{7,5},{8,10},{9,7},{10,... | collective-permute-start | bytes 442376 | tf_op jit(solution)/shard_map/ppermute | solution.py:51
  43.6 8.7 %collective-permute-start.3 = (bf16[24,3072]{1,0:T(8,128)(2,1)S(1)}, bf16[24,3072]{1,0:T(8,128)(2,1)S(1)}, u32[]{:S(2)}, u32[]{:S(2)}) collective-permute-start(bf16[24,3072]{1,0:T(8,128)(2,1)S(1)} %collective-permute-done.1.refs_0_), channel_id=1, source_target_pairs={{0,2},{1,15},{2,4},{3,1},{4,6},{5,3},{6,8},{7,5},{8,10},{9,7},{10,... | collective-permute-start | bytes 442376 | tf_op jit(solution)/shard_map/ppermute | solution.py:51
  43.8 10.0 %collective-permute-start.5 = (bf16[24,3072]{1,0:T(8,128)(2,1)S(1)}, bf16[24,3072]{1,0:T(8,128)(2,1)S(1)}, u32[]{:S(2)}, u32[]{:S(2)}) collective-permute-start(bf16[24,3072]{1,0:T(8,128)(2,1)S(1)} %collective-permute-done.2.refs_1_), channel_id=1, source_target_pairs={{0,2},{1,15},{2,4},{3,1},{4,6},{5,3},{6,8},{7,5},{8,10},{9,7},{10,... | collective-permute-start | bytes 442376 | tf_op jit(solution)/shard_map/ppermute | solution.py:51
  49.1 6.4 %collective-permute-start.8 = (bf16[24,3072]{1,0:T(8,128)(2,1)S(1)}, bf16[24,3072]{1,0:T(8,128)(2,1)S(1)}, u32[]{:S(2)}, u32[]{:S(2)}) collective-permute-start(bf16[24,3072]{1,0:T(8,128)(2,1)S(1)} %collective-permute-done.7.refs_2_), channel_id=1, source_target_pairs={{0,2},{1,15},{2,4},{3,1},{4,6},{5,3},{6,8},{7,5},{8,10},{9,7},{10,... | collective-permute-start | bytes 442376 | tf_op jit(solution)/shard_map/ppermute | solution.py:51
  50.6 6.4 %collective-permute-start.10 = (bf16[24,3072]{1,0:T(8,128)(2,1)S(1)}, bf16[24,3072]{1,0:T(8,128)(2,1)S(1)}, u32[]{:S(2)}, u32[]{:S(2)}) collective-permute-start(bf16[24,3072]{1,0:T(8,128)(2,1)S(1)} %collective-permute-done.9.refs_3_), channel_id=1, source_target_pairs={{0,2},{1,15},{2,4},{3,1},{4,6},{5,3},{6,8},{7,5},{8,10},{9,7},{10,... | collective-permute-start | bytes 442376 | tf_op jit(solution)/shard_map/ppermute | solution.py:51
  52.2 6.4 %collective-permute-start.4 = (bf16[24,3072]{1,0:T(8,128)(2,1)S(1)}, bf16[24,3072]{1,0:T(8,128)(2,1)S(1)}, u32[]{:S(2)}, u32[]{:S(2)}) collective-permute-start(bf16[24,3072]{1,0:T(8,128)(2,1)S(1)} %collective-permute-done.3.refs_0_), channel_id=1, source_target_pairs={{0,2},{1,15},{2,4},{3,1},{4,6},{5,3},{6,8},{7,5},{8,10},{9,7},{10,... | collective-permute-start | bytes 442376 | tf_op jit(solution)/shard_map/ppermute | solution.py:51
  53.8 6.4 %collective-permute-start.6 = (bf16[24,3072]{1,0:T(8,128)(2,1)S(1)}, bf16[24,3072]{1,0:T(8,128)(2,1)S(1)}, u32[]{:S(2)}, u32[]{:S(2)}) collective-permute-start(bf16[24,3072]{1,0:T(8,128)(2,1)S(1)} %collective-permute-done.5.refs_1_), channel_id=1, source_target_pairs={{0,2},{1,15},{2,4},{3,1},{4,6},{5,3},{6,8},{7,5},{8,10},{9,7},{10,... | collective-permute-start | bytes 442376 | tf_op jit(solution)/shard_map/ppermute | solution.py:51
  55.4 6.4 %collective-permute-start.14 = (bf16[24,3072]{1,0:T(8,128)(2,1)S(1)}, bf16[24,3072]{1,0:T(8,128)(2,1)S(1)}, u32[]{:S(2)}, u32[]{:S(2)}) collective-permute-start(bf16[24,3072]{1,0:T(8,128)(2,1)S(1)} %collective-permute-done.8.refs_2_), channel_id=1, source_target_pairs={{0,2},{1,15},{2,4},{3,1},{4,6},{5,3},{6,8},{7,5},{8,10},{9,7},{10,... | collective-permute-start | bytes 442376 | tf_op jit(solution)/shard_map/ppermute | solution.py:51
  55.5 23.1 %collective-permute-start.12 = (bf16[48,6144]{1,0:T(8,128)(2,1)S(1)}, bf16[48,6144]{1,0:T(8,128)(2,1)S(1)}, u32[]{:S(2)}, u32[]{:S(2)}) collective-permute-start(bf16[48,6144]{1,0:T(8,128)(2,1)S(1)} %joined.7.refs_5_), channel_id=1, source_target_pairs={{0,1},{1,0},{2,3},{3,2},{4,5},{5,4},{6,7},{7,6},{8,9},{9,8},{10,11... | collective-permute-start | bytes 1769480 | tf_op jit(solution)/shard_map/ppermute | solution.py:38
  60.2 18.4 %collective-permute-start.11 = (bf16[48,6144]{1,0:T(8,128)(2,1)S(1)}, bf16[48,6144]{1,0:T(8,128)(2,1)S(1)}, u32[]{:S(2)}, u32[]{:S(2)}) collective-permute-start(bf16[48,6144]{1,0:T(8,128)(2,1)S(1)} %joined.6.refs_4_), channel_id=1, source_target_pairs={{0,1},{1,0},{2,3},{3,2},{4,5},{5,4},{6,7},{7,6},{8,9},{9,8},{10,11... | collective-permute-start | bytes 1769480 | tf_op jit(solution)/shard_map/ppermute | solution.py:38
  60.4 6.6 %collective-permute-start.16 = (bf16[24,3072]{1,0:T(8,128)(2,1)S(1)}, bf16[24,3072]{1,0:T(8,128)(2,1)S(1)}, u32[]{:S(2)}, u32[]{:S(2)}) collective-permute-start(bf16[24,3072]{1,0:T(8,128)(2,1)S(1)} %collective-permute-done.10.refs_3_), channel_id=1, source_target_pairs={{0,2},{1,15},{2,4},{3,1},{4,6},{5,3},{6,8},{7,5},{8,10},{9,7},{10,... | collective-permute-start | bytes 442376 | tf_op jit(solution)/shard_map/ppermute | solution.py:51
  60.7 7.9 %collective-permute-start.18 = (bf16[24,3072]{1,0:T(8,128)(2,1)S(1)}, bf16[24,3072]{1,0:T(8,128)(2,1)S(1)}, u32[]{:S(2)}, u32[]{:S(2)}) collective-permute-start(bf16[24,3072]{1,0:T(8,128)(2,1)S(1)} %collective-permute-done.4.refs_0_), channel_id=1, source_target_pairs={{0,2},{1,15},{2,4},{3,1},{4,6},{5,3},{6,8},{7,5},{8,10},{9,7},{10,... | collective-permute-start | bytes 442376 | tf_op jit(solution)/shard_map/ppermute | solution.py:51
  61.8 8.4 %collective-permute-start.19 = (bf16[24,3072]{1,0:T(8,128)(2,1)S(1)}, bf16[24,3072]{1,0:T(8,128)(2,1)S(1)}, u32[]{:S(2)}, u32[]{:S(2)}) collective-permute-start(bf16[24,3072]{1,0:T(8,128)(2,1)S(1)} %collective-permute-done.6.refs_1_), channel_id=1, source_target_pairs={{0,2},{1,15},{2,4},{3,1},{4,6},{5,3},{6,8},{7,5},{8,10},{9,7},{10,... | collective-permute-start | bytes 442376 | tf_op jit(solution)/shard_map/ppermute | solution.py:51
  70.2 13.9 %collective-permute-start.20 = (bf16[48,6144]{1,0:T(8,128)(2,1)S(1)}, bf16[48,6144]{1,0:T(8,128)(2,1)S(1)}, u32[]{:S(2)}, u32[]{:S(2)}) collective-permute-start(bf16[48,6144]{1,0:T(8,128)(2,1)S(1)} %joined.9.refs_3_), channel_id=1, source_target_pairs={{0,1},{1,0},{2,3},{3,2},{4,5},{5,4},{6,7},{7,6},{8,9},{9,8},{10,11... | collective-permute-start | bytes 1769480 | tf_op jit(solution)/shard_map/ppermute | solution.py:38
  70.3 6.5 %collective-permute-start.15 = (bf16[24,3072]{1,0:T(8,128)(2,1)S(1)}, bf16[24,3072]{1,0:T(8,128)(2,1)S(1)}, u32[]{:S(2)}, u32[]{:S(2)}) collective-permute-start(bf16[24,3072]{1,0:T(8,128)(2,1)S(1)} %collective-permute-done.14.refs_2_), channel_id=1, source_target_pairs={{0,2},{1,15},{2,4},{3,1},{4,6},{5,3},{6,8},{7,5},{8,10},{9,7},{10,... | collective-permute-start | bytes 442376 | tf_op jit(solution)/shard_map/ppermute | solution.py:51
  70.5 7.9 %collective-permute-start.17 = (bf16[24,3072]{1,0:T(8,128)(2,1)S(1)}, bf16[24,3072]{1,0:T(8,128)(2,1)S(1)}, u32[]{:S(2)}, u32[]{:S(2)}) collective-permute-start(bf16[24,3072]{1,0:T(8,128)(2,1)S(1)} %collective-permute-done.16.refs_3_), channel_id=1, source_target_pairs={{0,2},{1,15},{2,4},{3,1},{4,6},{5,3},{6,8},{7,5},{8,10},{9,7},{10,... | collective-permute-start | bytes 442376 | tf_op jit(solution)/shard_map/ppermute | solution.py:51
  78.4 5.7 %collective-permute-start.21 = (bf16[24,6144]{1,0:T(8,128)(2,1)S(1)}, bf16[24,6144]{1,0:T(8,128)(2,1)S(1)}, u32[]{:S(2)}, u32[]{:S(2)}) collective-permute-start(bf16[24,6144]{1,0:T(8,128)(2,1)S(1)} %joined.8.refs_0_), channel_id=1, source_target_pairs={{0,1},{1,0},{2,3},{3,2},{4,5},{5,4},{6,7},{7,6},{8,9},{9,8},{10,11... | collective-permute-start | bytes 884744 | tf_op jit(solution)/shard_map/ppermute | solution.py:38
  83.5 11.3 %collective-permute-start.13 = (bf16[96,6144]{1,0:T(8,128)(2,1)S(1)}, bf16[96,6144]{1,0:T(8,128)(2,1)S(1)}, u32[]{:S(2)}, u32[]{:S(2)}) collective-permute-start(bf16[96,6144]{1,0:T(8,128)(2,1)S(1)} %get-tuple-element.27), channel_id=1, source_target_pairs={{0,1},{1,0},{2,3},{3,2},{4,5},{5,4},{6,7},{7,6},{8,9},{9,8},{10,11... | collective-permute-start | bytes 3538952 | tf_op jit(solution)/shard_map/ppermute | solution.py:38
  85.8 2.5 %collective-permute-start.22 = (bf16[72,6144]{1,0:T(8,128)(2,1)S(1)}, bf16[72,6144]{1,0:T(8,128)(2,1)S(1)}, u32[]{:S(2)}, u32[]{:S(2)}) collective-permute-start(bf16[72,6144]{1,0:T(8,128)(2,1)S(1)} %get-tuple-element.33), channel_id=1, source_target_pairs={{0,1},{1,0},{2,3},{3,2},{4,5},{5,4},{6,7},{7,6},{8,9},{9,8},{10,11... | collective-permute-start | bytes 2654216 | tf_op jit(solution)/shard_map/ppermute | solution.py:38
  88.4 6.5 %collective-permute-start.34 = (bf16[24,3072]{1,0:T(8,128)(2,1)S(1)}, bf16[24,3072]{1,0:T(8,128)(2,1)S(1)}, u32[]{:S(2)}, u32[]{:S(2)}) collective-permute-start(bf16[24,3072]{1,0:T(8,128)(2,1)S(1)} %hop_sum.25), channel_id=1, source_target_pairs={{0,2},{1,15},{2,4},{3,1},{4,6},{5,3},{6,8},{7,5},{8,10},{9,7},{10,... | collective-permute-start | bytes 442376 | tf_op jit(solution)/shard_map/ppermute | solution.py:51
  88.6 7.9 %collective-permute-start.31 = (bf16[24,3072]{1,0:T(8,128)(2,1)S(1)}, bf16[24,3072]{1,0:T(8,128)(2,1)S(1)}, u32[]{:S(2)}, u32[]{:S(2)}) collective-permute-start(bf16[24,3072]{1,0:T(8,128)(2,1)S(1)} %hop_sum.22), channel_id=1, source_target_pairs={{0,2},{1,15},{2,4},{3,1},{4,6},{5,3},{6,8},{7,5},{8,10},{9,7},{10,... | collective-permute-start | bytes 442376 | tf_op jit(solution)/shard_map/ppermute | solution.py:51
  88.8 9.3 %collective-permute-start.27 = (bf16[24,3072]{1,0:T(8,128)(2,1)S(1)}, bf16[24,3072]{1,0:T(8,128)(2,1)S(1)}, u32[]{:S(2)}, u32[]{:S(2)}) collective-permute-start(bf16[24,3072]{1,0:T(8,128)(2,1)S(1)} %hop_sum.18), channel_id=1, source_target_pairs={{0,2},{1,15},{2,4},{3,1},{4,6},{5,3},{6,8},{7,5},{8,10},{9,7},{10,... | collective-permute-start | bytes 442376 | tf_op jit(solution)/shard_map/ppermute | solution.py:51
  89.0 10.6 %collective-permute-start.23 = (bf16[24,3072]{1,0:T(8,128)(2,1)S(1)}, bf16[24,3072]{1,0:T(8,128)(2,1)S(1)}, u32[]{:S(2)}, u32[]{:S(2)}) collective-permute-start(bf16[24,3072]{1,0:T(8,128)(2,1)S(1)} %hop_sum.14), channel_id=1, source_target_pairs={{0,2},{1,15},{2,4},{3,1},{4,6},{5,3},{6,8},{7,5},{8,10},{9,7},{10,... | collective-permute-start | bytes 442376 | tf_op jit(solution)/shard_map/ppermute | solution.py:51
  94.9 6.5 %collective-permute-start.35 = (bf16[24,3072]{1,0:T(8,128)(2,1)S(1)}, bf16[24,3072]{1,0:T(8,128)(2,1)S(1)}, u32[]{:S(2)}, u32[]{:S(2)}) collective-permute-start(bf16[24,3072]{1,0:T(8,128)(2,1)S(1)} %hop_sum.26), channel_id=1, source_target_pairs={{0,2},{1,15},{2,4},{3,1},{4,6},{5,3},{6,8},{7,5},{8,10},{9,7},{10,... | collective-permute-start | bytes 442376 | tf_op jit(solution)/shard_map/ppermute | solution.py:51
  96.5 6.5 %collective-permute-start.32 = (bf16[24,3072]{1,0:T(8,128)(2,1)S(1)}, bf16[24,3072]{1,0:T(8,128)(2,1)S(1)}, u32[]{:S(2)}, u32[]{:S(2)}) collective-permute-start(bf16[24,3072]{1,0:T(8,128)(2,1)S(1)} %hop_sum.23), channel_id=1, source_target_pairs={{0,2},{1,15},{2,4},{3,1},{4,6},{5,3},{6,8},{7,5},{8,10},{9,7},{10,... | collective-permute-start | bytes 442376 | tf_op jit(solution)/shard_map/ppermute | solution.py:51
  98.1 6.5 %collective-permute-start.28 = (bf16[24,3072]{1,0:T(8,128)(2,1)S(1)}, bf16[24,3072]{1,0:T(8,128)(2,1)S(1)}, u32[]{:S(2)}, u32[]{:S(2)}) collective-permute-start(bf16[24,3072]{1,0:T(8,128)(2,1)S(1)} %hop_sum.19), channel_id=1, source_target_pairs={{0,2},{1,15},{2,4},{3,1},{4,6},{5,3},{6,8},{7,5},{8,10},{9,7},{10,... | collective-permute-start | bytes 442376 | tf_op jit(solution)/shard_map/ppermute | solution.py:51
  99.7 6.5 %collective-permute-start.24 = (bf16[24,3072]{1,0:T(8,128)(2,1)S(1)}, bf16[24,3072]{1,0:T(8,128)(2,1)S(1)}, u32[]{:S(2)}, u32[]{:S(2)}) collective-permute-start(bf16[24,3072]{1,0:T(8,128)(2,1)S(1)} %hop_sum.15), channel_id=1, source_target_pairs={{0,2},{1,15},{2,4},{3,1},{4,6},{5,3},{6,8},{7,5},{8,10},{9,7},{10,... | collective-permute-start | bytes 442376 | tf_op jit(solution)/shard_map/ppermute | solution.py:51
  101.5 6.5 %collective-permute-start.36 = (bf16[24,3072]{1,0:T(8,128)(2,1)S(1)}, bf16[24,3072]{1,0:T(8,128)(2,1)S(1)}, u32[]{:S(2)}, u32[]{:S(2)}) collective-permute-start(bf16[24,3072]{1,0:T(8,128)(2,1)S(1)} %hop_sum.27), channel_id=1, source_target_pairs={{0,2},{1,15},{2,4},{3,1},{4,6},{5,3},{6,8},{7,5},{8,10},{9,7},{10,... | collective-permute-start | bytes 442376 | tf_op jit(solution)/shard_map/ppermute | solution.py:51
  103.0 6.5 %collective-permute-start.33 = (bf16[24,3072]{1,0:T(8,128)(2,1)S(1)}, bf16[24,3072]{1,0:T(8,128)(2,1)S(1)}, u32[]{:S(2)}, u32[]{:S(2)}) collective-permute-start(bf16[24,3072]{1,0:T(8,128)(2,1)S(1)} %hop_sum.24), channel_id=1, source_target_pairs={{0,2},{1,15},{2,4},{3,1},{4,6},{5,3},{6,8},{7,5},{8,10},{9,7},{10,... | collective-permute-start | bytes 442376 | tf_op jit(solution)/shard_map/ppermute | solution.py:51
  104.6 6.5 %collective-permute-start.29 = (bf16[24,3072]{1,0:T(8,128)(2,1)S(1)}, bf16[24,3072]{1,0:T(8,128)(2,1)S(1)}, u32[]{:S(2)}, u32[]{:S(2)}) collective-permute-start(bf16[24,3072]{1,0:T(8,128)(2,1)S(1)} %hop_sum.20), channel_id=1, source_target_pairs={{0,2},{1,15},{2,4},{3,1},{4,6},{5,3},{6,8},{7,5},{8,10},{9,7},{10,... | collective-permute-start | bytes 442376 | tf_op jit(solution)/shard_map/ppermute | solution.py:51
  106.2 6.5 %collective-permute-start.25 = (bf16[24,3072]{1,0:T(8,128)(2,1)S(1)}, bf16[24,3072]{1,0:T(8,128)(2,1)S(1)}, u32[]{:S(2)}, u32[]{:S(2)}) collective-permute-start(bf16[24,3072]{1,0:T(8,128)(2,1)S(1)} %hop_sum.16), channel_id=1, source_target_pairs={{0,2},{1,15},{2,4},{3,1},{4,6},{5,3},{6,8},{7,5},{8,10},{9,7},{10,... | collective-permute-start | bytes 442376 | tf_op jit(solution)/shard_map/ppermute | solution.py:51
  109.6 23.1 %copy-start = (s32[4,2]{0,1:T(2,128)S(1)}, s32[4,2]{0,1:T(2,128)}, u32[]{:S(2)}) copy-start(s32[4,2]{0,1:T(2,128)} %param.20) | copy-start | bytes 100
  109.6 23.1 %copy-start.1 = (f32[4,2]{0,1:T(2,128)S(1)}, f32[4,2]{0,1:T(2,128)}, u32[]{:S(2)}) copy-start(f32[4,2]{0,1:T(2,128)} %param.21) | copy-start | bytes 100
  109.6 9.6 %collective-permute-start.37 = (bf16[24,6144]{1,0:T(8,128)(2,1)S(1)}, bf16[24,6144]{1,0:T(8,128)(2,1)S(1)}, u32[]{:S(2)}, u32[]{:S(2)}) collective-permute-start(bf16[24,6144]{1,0:T(8,128)(2,1)S(1)} %two_sum.1), channel_id=1, source_target_pairs={{0,1},{1,0},{2,3},{3,2},{4,5},{5,4},{6,7},{7,6},{8,9},{9,8},{10,11... | collective-permute-start | bytes 884744 | tf_op jit(solution)/shard_map/ppermute | solution.py:38
  111.1 6.5 %collective-permute-start.30 = (bf16[24,3072]{1,0:T(8,128)(2,1)S(1)}, bf16[24,3072]{1,0:T(8,128)(2,1)S(1)}, u32[]{:S(2)}, u32[]{:S(2)}) collective-permute-start(bf16[24,3072]{1,0:T(8,128)(2,1)S(1)} %hop_sum.21), channel_id=1, source_target_pairs={{0,2},{1,15},{2,4},{3,1},{4,6},{5,3},{6,8},{7,5},{8,10},{9,7},{10,... | collective-permute-start | bytes 442376 | tf_op jit(solution)/shard_map/ppermute | solution.py:51
  112.7 6.5 %collective-permute-start.26 = (bf16[24,3072]{1,0:T(8,128)(2,1)S(1)}, bf16[24,3072]{1,0:T(8,128)(2,1)S(1)}, u32[]{:S(2)}, u32[]{:S(2)}) collective-permute-start(bf16[24,3072]{1,0:T(8,128)(2,1)S(1)} %hop_sum.17), channel_id=1, source_target_pairs={{0,2},{1,15},{2,4},{3,1},{4,6},{5,3},{6,8},{7,5},{8,10},{9,7},{10,... | collective-permute-start | bytes 442376 | tf_op jit(solution)/shard_map/ppermute | solution.py:51
